TPU v7x, 32 devices: a whole 2x2x4 slice. The times are simulated.
32 devices in a mesh: dp: 8 (over z, y), seq: 4 (over x, core).
Axes of the slice: x: 2, y: 2, z: 4, core: 2. Of those that a mesh axis runs over, the one named last changes fastest.
Arguments:
- tokens: bfloat16 [2, 8192, 2048], P(None, ('dp', 'seq')), may hold values from -6 to 6
- positions: int32 [2, 8192], P(None, 'dp'), may hold values from 0 to 1023, as said below
- cotangent: bfloat16 [2, 8192, 2048], P(None, ('dp', 'seq')), may hold values from -6 to 6
- norm1_gain: bfloat16 [2048], P(('dp', 'seq')), may hold values from 0.099609375 to 1.8984375
- norm1_bias: bfloat16 [2048], P(('dp', 'seq')), may hold values from -2 to 2
- norm2_gain: bfloat16 [2048], P(('dp', 'seq')), may hold values from 0.099609375 to 1.8984375
- norm2_bias: bfloat16 [2048], P(('dp', 'seq')), may hold values from -2 to 2
- qkv_weight: bfloat16 [2048, 6144], P(('dp', 'seq')), may hold values from -1 to 1
- qkv_bias: bfloat16 [6144], P(('dp', 'seq')), may hold values from -2 to 2
- out_weight: bfloat16 [2048, 2048], P(('dp', 'seq')), may hold values from -1 to 1
- out_bias: bfloat16 [2048], P(('dp', 'seq')), may hold values from -3 to 3
- up_weight: bfloat16 [2048, 8192], P(('dp', 'seq')), may hold values from -0.125 to 0.125
- up_bias: bfloat16 [8192], P(('dp', 'seq')), may hold values from -3 to 3
- down_weight: bfloat16 [2048, 8192], P(('dp', 'seq')), may hold values from -0.0625 to 0.0625
- down_bias: bfloat16 [2048], P(('dp', 'seq')), may hold values from -3 to 3
Outputs:
- output: bfloat16 [2, 8192, 2048], P(None, ('dp', 'seq'))
- token_grad: float32 [2, 8192, 2048], P(None, ('dp', 'seq'))
- norm1_gain_grad: float32 [2048], P(('dp', 'seq'))
- norm1_bias_grad: float32 [2048], P(('dp', 'seq'))
- norm2_gain_grad: float32 [2048], P(('dp', 'seq'))
- norm2_bias_grad: float32 [2048], P(('dp', 'seq'))
- qkv_weight_grad: float32 [2048, 6144], P(('dp', 'seq'))
- qkv_bias_grad: float32 [6144], P(('dp', 'seq'))
- out_weight_grad: float32 [2048, 2048], P(('dp', 'seq'))
- out_bias_grad: float32 [2048], P(('dp', 'seq'))
- up_weight_grad: float32 [2048, 8192], P(('dp', 'seq'))
- up_bias_grad: float32 [8192], P(('dp', 'seq'))
- down_weight_grad: float32 [2048, 8192], P(('dp', 'seq'))
- down_bias_grad: float32 [2048], P(('dp', 'seq'))
Inputs may be any that keep to these rules, and one draw needn't show every extreme that they name: The 1024 positions of each sequence hold every number of 0 to 1023 once. The positions of one sequence on one index of seq are two runs of 128 consecutive rising numbers, one starting at c * 128 and one at 1024 - (c + 1) * 128 for some c, in either order.
All inputs are finite; a program needn't handle non-finite values.
Results may differ from a plain program's by a relative error of at most 0.0095.
Values may be sent and summed in bfloat16 or wider, within the bound.
A program may use at most 704 MiB of HBM per device.

v0:
```python
from functools import partial
import math

import jax
import jax.numpy as jnp
from jax import lax
from jax.sharding import PartitionSpec as P

HEADS = 8
HEAD_DIM = 256
ROTARY = 64


EPSILON = 1e-05
NEGATIVE = -1e30


def matmul(left, right):
    return jnp.dot(left, right, preferred_element_type=jnp.float32)


def cross_dot(left, right):
    return lax.dot_general(
        left, right, (((1,), (1,)), ((), ())), preferred_element_type=jnp.float32
    )


def token_dot(left, right):
    return lax.dot_general(
        left, right, (((0,), (0,)), ((), ())), preferred_element_type=jnp.float32
    )


def angles(places):
    halves = ROTARY // 2
    frequency = jnp.exp(jnp.arange(halves, dtype=jnp.float32) * (-2.0 * math.log(10000.0) / ROTARY))
    phases = places.astype(jnp.float32)[..., None] * frequency
    phases = jnp.concatenate([phases, phases], -1)
    return (jnp.cos(phases), jnp.sin(phases))


def rotate(field_in, cosine, sine_vals):
    halves = ROTARY // 2
    rot_part = field_in[..., :ROTARY]
    front_half = rot_part[..., :halves]
    back_half = rot_part[..., halves:]
    turned = jnp.concatenate([-back_half, front_half], -1)
    rotated = rot_part * cosine + turned * sine_vals
    return jnp.concatenate([rotated, field_in[..., ROTARY:]], -1)


def rotate_back(grad_in, cosine, sine_vals):
    halves = ROTARY // 2
    rot_part = grad_in[..., :ROTARY]
    scaled = rot_part * sine_vals
    rotated = rot_part * cosine + jnp.concatenate([scaled[..., halves:], -scaled[..., :halves]], -1)
    return jnp.concatenate([rotated, grad_in[..., ROTARY:]], -1)


def body(
    tokens,
    positions,
    cotangent,
    norm1_gain,
    norm1_bias,
    norm2_gain,
    norm2_bias,
    qkv_weight,
    qkv_bias,
    out_weight,
    out_bias,
    up_weight,
    up_bias,
    down_weight,
    down_bias,
):
    batch_seqs, local_len, model_width = tokens.shape
    rows_all = batch_seqs * local_len
    hidden_width = up_weight.shape[1]
    scaling = HEAD_DIM ** (-0.5)
    vectors = (
        lax.all_gather(norm1_gain, ("dp", "seq"), axis=0, tiled=True),
        lax.all_gather(norm1_bias, ("dp", "seq"), axis=0, tiled=True),
        lax.all_gather(norm2_gain, ("dp", "seq"), axis=0, tiled=True),
        lax.all_gather(norm2_bias, ("dp", "seq"), axis=0, tiled=True),
        lax.all_gather(qkv_bias, ("dp", "seq"), axis=0, tiled=True),
        lax.all_gather(out_bias, ("dp", "seq"), axis=0, tiled=True),
        lax.all_gather(up_bias, ("dp", "seq"), axis=0, tiled=True),
        lax.all_gather(down_bias, ("dp", "seq"), axis=0, tiled=True),
    )
    gain_one, bias_one, gain_two, bias_two, b_qkv, b_out, b_up, b_down = [
        element.astype(jnp.float32) for element in vectors
    ]
    inputs = tokens.reshape(rows_all, model_width).astype(jnp.float32)
    center = inputs - jnp.mean(inputs, -1, keepdims=True)
    inv_std = lax.rsqrt(jnp.mean(center * center, -1, keepdims=True) + EPSILON)
    normal = center * inv_std
    normed_one = (normal * gain_one + bias_one).astype(jnp.bfloat16)
    normed_two = (normal * gain_two + bias_two).astype(jnp.bfloat16)
    pieces = (
        lax.all_gather(qkv_weight, ("dp", "seq"), axis=0, tiled=True),
        lax.all_gather(up_weight, ("dp", "seq"), axis=0, tiled=True),
    )
    packed = matmul(normed_one, pieces[0])
    hidden = matmul(normed_two, pieces[1])
    packed = packed + b_qkv
    hidden = hidden + b_up
    shaped = packed.reshape(batch_seqs, local_len, 3, HEADS, HEAD_DIM)
    own_places = lax.dynamic_slice_in_dim(
        positions, lax.axis_index("seq") * local_len, local_len, 1
    )
    cosine, sine_vals = angles(own_places)
    cos_heads = cosine[:, :, None, :]
    sin_heads = sine_vals[:, :, None, :]
    queries = rotate(shaped[:, :, 0], cos_heads, sin_heads).astype(jnp.bfloat16)
    keys_own = rotate(shaped[:, :, 1], cos_heads, sin_heads).astype(jnp.bfloat16)
    values_own = shaped[:, :, 2].astype(jnp.bfloat16)
    row_max = jnp.full((batch_seqs, HEADS, local_len), NEGATIVE, jnp.float32)
    key_piece = lax.all_gather(keys_own, "seq", axis=1, tiled=True)
    value_piece = lax.all_gather(values_own, "seq", axis=1, tiled=True)
    scores = (
        jnp.einsum("bqhe,bkhe->bhqk", queries, key_piece, preferred_element_type=jnp.float32)
        * scaling
    )
    allowed = positions[:, None, None, :] <= own_places[:, None, :, None]
    scores = jnp.where(allowed, scores, NEGATIVE)
    new_max = jnp.maximum(row_max, jnp.max(scores, -1))
    weights_exp = jnp.where(allowed, jnp.exp(scores - new_max[..., None]), 0.0)
    row_sum = jnp.sum(weights_exp, -1)
    accumulated = jnp.einsum(
        "bhqk,bkhe->bhqe",
        weights_exp.astype(jnp.bfloat16),
        value_piece,
        preferred_element_type=jnp.float32,
    )
    row_max, row_sum, accumulated = (new_max, row_sum, accumulated)
    log_total = row_max + jnp.log(row_sum)
    context = jnp.transpose(accumulated / row_sum[..., None], (0, 2, 1, 3))
    context_low = context.astype(jnp.bfloat16).reshape(rows_all, model_width)
    activated = jax.nn.gelu(hidden, approximate=False).astype(jnp.bfloat16)
    pieces = (
        lax.all_gather(out_weight, ("dp", "seq"), axis=0, tiled=True),
        lax.all_gather(down_weight, ("dp", "seq"), axis=0, tiled=True),
    )
    part_out = cross_dot(context_low, pieces[0]) + cross_dot(activated, pieces[1])
    output = (inputs + part_out + b_out + b_down).astype(jnp.bfloat16).reshape(tokens.shape)
    upstream = cotangent.reshape(rows_all, model_width)
    pieces = (
        lax.all_gather(out_weight, ("dp", "seq"), axis=0, tiled=True),
        lax.all_gather(down_weight, ("dp", "seq"), axis=0, tiled=True),
    )
    grad_context = matmul(upstream, pieces[0])
    grad_active = matmul(upstream, pieces[1])
    unused, gelu_pull = jax.vjp(partial(jax.nn.gelu, approximate=False), hidden)
    grad_hidden = gelu_pull(grad_active)[0].astype(jnp.bfloat16)
    grad_ctx4 = grad_context.astype(jnp.bfloat16).reshape(batch_seqs, local_len, HEADS, HEAD_DIM)
    row_delta = jnp.transpose(jnp.sum(grad_ctx4.astype(jnp.float32) * context, -1), (0, 2, 1))
    keys_full, values_full = (
        lax.all_gather(keys_own, "seq", axis=1, tiled=True),
        lax.all_gather(values_own, "seq", axis=1, tiled=True),
    )
    scores = (
        jnp.einsum("bqhe,bkhe->bhqk", queries, keys_full, preferred_element_type=jnp.float32)
        * scaling
    )
    allowed = positions[:, None, None, :] <= own_places[:, None, :, None]
    scores = jnp.where(allowed, scores, NEGATIVE)
    soft_probs = jnp.where(allowed, jnp.exp(scores - log_total[..., None]), 0.0)
    grad_probs = jnp.einsum(
        "bqhe,bkhe->bhqk", grad_ctx4, values_full, preferred_element_type=jnp.float32
    )
    grad_scores = (soft_probs * (grad_probs - row_delta[..., None])).astype(jnp.bfloat16)
    grad_queries = (
        jnp.einsum("bhqk,bkhe->bqhe", grad_scores, keys_full, preferred_element_type=jnp.float32)
        * scaling
    )
    key_terms = (
        jnp.einsum("bhqk,bqhe->bkhe", grad_scores, queries, preferred_element_type=jnp.float32)
        * scaling
    )
    value_terms = jnp.einsum(
        "bhqk,bqhe->bkhe",
        soft_probs.astype(jnp.bfloat16),
        grad_ctx4,
        preferred_element_type=jnp.float32,
    )
    grad_keys, grad_values = (
        lax.psum_scatter(
            key_terms.astype(jnp.bfloat16), "seq", scatter_dimension=1, tiled=True
        ).astype(jnp.float32),
        lax.psum_scatter(
            value_terms.astype(jnp.bfloat16), "seq", scatter_dimension=1, tiled=True
        ).astype(jnp.float32),
    )
    grad_packed = jnp.stack(
        [
            rotate_back(grad_queries, cos_heads, sin_heads),
            rotate_back(grad_keys, cos_heads, sin_heads),
            grad_values,
        ],
        2,
    )
    grad_packed = grad_packed.reshape(rows_all, 3 * model_width).astype(jnp.bfloat16)
    pieces = (
        lax.all_gather(qkv_weight, ("dp", "seq"), axis=0, tiled=True),
        lax.all_gather(up_weight, ("dp", "seq"), axis=0, tiled=True),
    )
    first_out = cross_dot(grad_packed, pieces[0])
    second_out = cross_dot(grad_hidden, pieces[1])
    grad_normal = first_out * gain_one + second_out * gain_two
    token_grad = inv_std * (
        grad_normal
        - jnp.mean(grad_normal, -1, keepdims=True)
        - normal * jnp.mean(grad_normal * normal, -1, keepdims=True)
    ) + upstream.astype(jnp.float32)
    token_grad = token_grad.reshape(tokens.shape)
    summed = (
        lax.psum_scatter(
            jnp.sum(first_out * normal, 0), ("dp", "seq"), scatter_dimension=0, tiled=True
        ),
        lax.psum_scatter(jnp.sum(first_out, 0), ("dp", "seq"), scatter_dimension=0, tiled=True),
        lax.psum_scatter(
            jnp.sum(second_out * normal, 0), ("dp", "seq"), scatter_dimension=0, tiled=True
        ),
        lax.psum_scatter(jnp.sum(second_out, 0), ("dp", "seq"), scatter_dimension=0, tiled=True),
        lax.psum_scatter(
            jnp.sum(grad_packed.astype(jnp.float32), 0),
            ("dp", "seq"),
            scatter_dimension=0,
            tiled=True,
        ),
        lax.psum_scatter(
            jnp.sum(upstream.astype(jnp.float32), 0), ("dp", "seq"), scatter_dimension=0, tiled=True
        ),
        lax.psum_scatter(
            jnp.sum(grad_hidden.astype(jnp.float32), 0),
            ("dp", "seq"),
            scatter_dimension=0,
            tiled=True,
        ),
    )
    matrix = lax.psum_scatter(
        jnp.concatenate(
            [
                token_dot(normed_one, grad_packed),
                token_dot(normed_two, grad_hidden),
                token_dot(upstream, context_low),
                token_dot(upstream, activated),
            ],
            1,
        ),
        ("dp", "seq"),
        scatter_dimension=0,
        tiled=True,
    )
    cut_one = 3 * model_width
    cut_two = cut_one + hidden_width
    cut_three = cut_two + model_width
    return (
        output,
        token_grad,
        summed[0],
        summed[1],
        summed[2],
        summed[3],
        matrix[:, :cut_one],
        summed[4],
        matrix[:, cut_two:cut_three],
        summed[5],
        matrix[:, cut_one:cut_two],
        summed[6],
        matrix[:, cut_three:],
        summed[5],
    )


def solution(mesh):
    return jax.shard_map(
        body,
        mesh=mesh,
        in_specs=(
            P(None, ("dp", "seq"), None),
            P(None, "dp"),
            P(None, ("dp", "seq"), None),
            P(("dp", "seq")),
            P(("dp", "seq")),
            P(("dp", "seq")),
            P(("dp", "seq")),
            P(("dp", "seq"), None),
            P(("dp", "seq")),
            P(("dp", "seq"), None),
            P(("dp", "seq")),
            P(("dp", "seq"), None),
            P(("dp", "seq")),
            P(("dp", "seq"), None),
            P(("dp", "seq")),
        ),
        out_specs=(
            P(None, ("dp", "seq"), None),
            P(None, ("dp", "seq"), None),
            P(("dp", "seq")),
            P(("dp", "seq")),
            P(("dp", "seq")),
            P(("dp", "seq")),
            P(("dp", "seq"), None),
            P(("dp", "seq")),
            P(("dp", "seq"), None),
            P(("dp", "seq")),
            P(("dp", "seq"), None),
            P(("dp", "seq")),
            P(("dp", "seq"), None),
            P(("dp", "seq")),
        ),
        check_vma=False,
    )
```

profile of v0, /device:TPU:0, one launch (start us, length us, event | category | flops | bytes accessed | tf_op | source)
XLA Modules:
  0.0 2747.6 jit_solution(7620616951852728253)
XLA Ops:
  13.3 44.8 %all-reduce.15 = (bf16[2048]{0:T(1024)(128)(2,1)S(1)}, bf16[2048]{0:T(1024)(128)(2,1)S(1)}, bf16[6144]{0:T(1024)(128)(2,1)S(1)}, bf16[2048]{0:T(1024)(128)(2,1)S...) all-reduce(bf16[2048]{0:T(1024)(128)(2,1)S(1)} %dynamic-update-slic, ...), channel_id=1, replica_groups=mesh['dp'=8,'seq'=4] {'dp','seq'}, use_global_device_ids=true, to_apply=%add.1 | all-reduce | flops 18432 | bytes 73728
  59.5 3.4 fusion.48
  62.9 106.5 %all-gather.9.cloned.1.call-done = bf16[2048,6144]{1,0:T(8,128)(2,1)} async-done(((bf16[64,6144]{1,0:T(8,128)(2,1)}), bf16[2048,6144]{1,0:T(8,128)(2,1)}) %all-gather.9.cloned.1.call-update) | async-done | bytes 25165840 | tf_op jit(solution)/shard_map/all_gather | solution.py:101
  169.4 21.5 convolution_add_fusion
  190.9 14.9 copy.110
  205.8 4.1 fusion.84
  214.8 2.5 fusion.65
  219.8 3.7 slice.99
  223.5 4.3 copy.107
  229.5 18.0 all-gather.13.cloned.1.call-done
  247.5 8.5 convolution_convert_fusion
  258.0 4.5 copy.77
  262.5 4.3 slice.143
  266.8 39.2 %all-gather.11.cloned.1.call-done = bf16[2,1024,8,256]{3,1,2,0:T(8,128)(2,1)} async-done(((bf16[2,256,8,256]{3,1,2,0:T(8,128)(2,1)}), bf16[2,1024,8,256]{3,1,2,0:T(8,128)(2,1)}) %all-gather.11.cloned.1.call-update) | async-done | bytes 8388624 | tf_op jit(solution)/shard_map/all_gather | solution.py:119
  306.0 15.2 fusion.9
  321.2 8.1 fusion.6
  329.3 37.5 %all-gather.19.cloned.1.call-done = bf16[2,1024,1,8,256]{1,4,3,0,2:T(8,128)(2,1)} async-done(((bf16[2,256,1,8,256]{1,4,3,0,2:T(8,128)(2,1)}), bf16[2,1024,1,8,256]{1,4,3,0,2:T(8,128)(2,1)}) %all-gather.19.cloned.1.call-update) | async-done | bytes 8388624 | tf_op jit(solution)/shard_map/all_gather | solution.py:120
  366.8 13.9 multiply_reduce_fusion
  380.7 14.3 multiply_convert_fusion.1
  395.1 10.0 fusion.14
  405.7 42.7 %all-gather.1 = bf16[32,1,256]{2,1,0:T(2,128)(2,1)S(1)} all-gather(bf16[1,1,256]{2,1,0:T(2,128)(2,1)S(1)} %reshape.197), channel_id=1, replica_groups=mesh['dp'=8,'seq'=4] {'dp','seq'}, dimensions={0}, use_global_device_ids=true | all-gather | bytes 16896 | tf_op jit(solution)/shard_map/all_gather | solution.py:88
  448.5 2.6 convert_reduce_fusion.3
  453.2 10.3 multiply_bitcast_fusion
  463.5 5.3 slice.113
  468.8 3.5 copy.74
  474.3 8.2 convolution_bitcast_fusion.1
  482.5 10.2 convert_bitcast_fusion
  493.0 71.0 %all-gather.15.cloned.1.call-done = bf16[2048,8192]{1,0:T(8,128)(2,1)} async-done(((bf16[64,8192]{1,0:T(8,128)(2,1)}), bf16[2048,8192]{1,0:T(8,128)(2,1)}) %all-gather.15.cloned.1.call-update) | async-done | bytes 33554448 | tf_op jit(solution)/shard_map/all_gather | solution.py:102
  564.0 26.7 fusion.89
  590.7 168.4 %all-gather.17.cloned.1.call-done = bf16[2048,8192]{1,0:T(8,128)(2,1)} async-done(((bf16[64,8192]{1,0:T(8,128)(2,1)}), bf16[2048,8192]{1,0:T(8,128)(2,1)}) %all-gather.17.cloned.1.call-update) | async-done | bytes 33554448 | tf_op jit(solution)/shard_map/all_gather | solution.py:143
  759.1 62.2 %convert_reduce_fusion = (f32[8192]{0:T(1024)}, bf16[512,8192]{1,0:T(8,128)(2,1)}, f32[512,8192]{1,0:T(8,128)}) fusion(f32[512,8192]{1,0:T(8,128)} %fusion.89, f32[8192]{0:T(1024)S(1)} %bitcast.158, bf16[512,2048]{1,0:T(8,128)(2,1)} %bitcast.149, bf16[2048,8192]{1,0:T(8,128)(2,1)} %all-gather.17.cloned.1.call-done), kind=kOutput, calls=%fused_computation.4 | convolution fusion | flops 17494433792 | bytes 77660160 | tf_op jit(solution)/shard_map/dot_general | solution.py:19
  821.3 10.5 multiply_convert_fusion.2
  831.7 34.7 %convolution_bitcast_fusion = f32[2048,8192]{1,0:T(8,128)} fusion(bf16[512,8192]{1,0:T(8,128)(2,1)} %multiply_convert_fusion.2, bf16[512,2048]{1,0:T(8,128)(2,1)} %bitcast.150), kind=kOutput, calls=%fused_computation.1 | convolution fusion | flops 17179869184 | bytes 77594624 | tf_op jit(solution)/shard_map/dot_general | solution.py:29
  866.4 29.7 %fusion.92 = f32[2048,8192]{1,0:T(8,128)} fusion(bf16[512,2048]{1,0:T(8,128)(2,1)S(1)} %copy-done.8, bf16[512,8192]{1,0:T(8,128)(2,1)} %get-tuple-element.35), kind=kOutput, calls=%fused_computation.147 | convolution fusion | flops 17179869184 | bytes 77594624 | tf_op jit(solution)/shard_map/dot_general | solution.py:29
  896.2 2.8 slice.117
  910.1 3.7 convert_reduce_fusion.1
  914.4 6.3 copy.88
  920.7 10.3 convert_element_type.155
  931.0 22.9 fusion.91
  953.9 21.2 fusion.90
  975.2 27.6 %fusion.79 = (f32[2048]{0:T(1024)}, f32[2048]{0:T(1024)}, f32[512]{0:T(512)}, f32[512]{0:T(512)}, f32[512,2048]{1,0:T(8,128)}, /*index=5*/f32[2048]{0:T(1024)}, f32[2048]{0:T(1024)}) fusion(f32[512]{0:T(512)S(1)} %bitcast.167, f32[512]{0:T(512)S(1)} %bitcast.164, bf16[2,256,2048]{2,1,0:T(8,128)(2,1)S(1)} %copy-done.1, f32[2048]{0:T(1024)S(1)} %copy-done.23, ...), kind=kOutput, calls=%fused_computation.135 | convolution fusion | flops 17195589632 | bytes 52486144 | tf_op jit(solution)/shard_map/dot_general | solution.py:23
  1002.9 130.7 %pad_maximum_fusion = f32[2048,24576]{1,0:T(8,128)} fusion(f32[2048,8192]{1,0:T(8,128)} %convolution_bitcast_fusion, f32[2048,2048]{1,0:T(8,128)} %convolution_bitcast_fusion.1, f32[2048,8192]{1,0:T(8,128)} %fusion.92, f32[2048,6144]{1,0:T(8,128)} %fusion.91), kind=kLoop, calls=%fused_computation | loop fusion | flops 150994944 | bytes 402653184 | tf_op jit(solution)/shard_map/concatenate | solution.py:243
  1135.2 9.6 fusion.88
  1144.8 30.4 %fusion.57 = bf16[512,2048]{1,0:T(8,128)(2,1)} fusion(bf16[2,256,2048]{2,1,0:T(8,128)(2,1)S(1)} %copy-done.2, f32[512,2048]{1,0:T(8,128)} %fusion.88, bf16[512,8192]{1,0:T(8,128)(2,1)} %multiply_convert_fusion.2, bf16[2048,8192]{1,0:T(8,128)(2,1)} %all-gather.17.cloned.1.call-done, f32[2048]{0:T(1024)S(1)} %convert_element_type.143, ...), kind=kOutput, calls=%fused_computation.86 | convolution fusion | flops 17186160640 | bytes 50348032 | tf_op jit(solution)/shard_map/dot_general | solution.py:23
  1175.2 5.2 fusion.52
  1188.9 1542.0 %reduce-scatter.8.cloned.1.call-done = f32[64,24576]{1,0:T(8,128)} async-done(((f32[2048,24576]{1,0:T(8,128)}), f32[64,24576]{1,0:T(8,128)}) %reduce-scatter.8.cloned.1.call-update) | async-done | bytes 6291472 | tf_op jit(solution)/shard_map/reduce_scatter | solution.py:242
  2732.7 2.7 slice.118
  2735.4 4.6 fusion.85
  (174 shorter events, 47.7 us)
Async XLA Ops:
  7.2 3.6 copy-start
  7.2 4.3 copy-start.35
  7.2 4.6 copy-start.36
  7.2 4.8 copy-start.37
  7.2 5.1 copy-start.38
  7.2 5.3 copy-start.39
  7.2 5.6 copy-start.40
  7.3 5.8 copy-start.41
  7.3 50.9 %copy-start.30 = (s32[2,1024]{1,0:T(2,128)S(1)}, s32[2,1024]{1,0:T(2,128)}, u32[]{:S(2)}) copy-start(s32[2,1024]{1,0:T(2,128)} %param.16) | copy-start | bytes 24580
  7.3 162.1 %all-gather.9.cloned.1.call-start = ((), (), s32[]{:S(2)}) async-start(), calls=%async_computation.3 | async-start | bytes 25952256 | tf_op jit(solution)/shard_map/all_gather | solution.py:101
  8.0 239.5 %all-gather.13.cloned.1.call-start = ((), (), s32[]{:S(2)}) async-start(), calls=%async_computation.5 | async-start | bytes 8650752 | tf_op jit(solution)/shard_map/all_gather | solution.py:142
  8.8 297.2 %all-gather.11.cloned.1.call-start = ((), (), s32[]{:S(2)}) async-start(), calls=%async_computation.4 | async-start | bytes 10485760 | tf_op jit(solution)/shard_map/all_gather | solution.py:119
  10.8 52.2 %copy-start.24 = (f32[1,2,2,128]{3,1,2,0:T(2,128)}, f32[1,2,2,128]{3,1,2,0:T(2,128)S(1)}, u32[]{:S(2)}) copy-start(f32[1,2,2,128]{3,1,2,0:T(2,128)S(1)} %copy.108) | copy-start | bytes 6148
  11.5 179.4 %copy-start.27 = (f32[1,2,2,128]{3,1,2,0:T(2,128)}, f32[1,2,2,128]{3,1,2,0:T(2,128)S(1)}, u32[]{:S(2)}) copy-start(f32[1,2,2,128]{3,1,2,0:T(2,128)S(1)} %copy.109) | copy-start | bytes 6148
  58.1 392.9 %copy-start.20 = (f32[2048]{0:T(1024)}, f32[2048]{0:T(1024)S(1)}, u32[]{:S(2)}) copy-start(f32[2048]{0:T(1024)S(1)} %convert_element_type.129) | copy-start | bytes 24580
  58.1 132.7 %copy-start.22 = (f32[2048]{0:T(1024)}, f32[2048]{0:T(1024)S(1)}, u32[]{:S(2)}) copy-start(f32[2048]{0:T(1024)S(1)} %convert_element_type.137) | copy-start | bytes 24580
  59.5 155.3 %copy-start.12 = (f32[2,256,64]{2,1,0:T(8,128)}, f32[2,256,64]{2,1,0:T(8,128)S(1)}, u32[]{:S(2)}) copy-start(f32[2,256,64]{2,1,0:T(8,128)S(1)} %get-tuple-element.69) | copy-start | bytes 393220
  59.5 155.3 %copy-start.14 = (f32[2,256,64]{2,1,0:T(8,128)}, f32[2,256,64]{2,1,0:T(8,128)S(1)}, u32[]{:S(2)}) copy-start(f32[2,256,64]{2,1,0:T(8,128)S(1)} %get-tuple-element.70) | copy-start | bytes 393220
  211.1 3.7 copy-start.3
  219.7 147.1 %all-gather.19.cloned.1.call-start = ((), (), s32[]{:S(2)}) async-start(), calls=%async_computation.11 | async-start | bytes 10485760 | tf_op jit(solution)/shard_map/all_gather | solution.py:120
  227.8 336.2 %all-gather.15.cloned.1.call-start = ((), (), s32[]{:S(2)}) async-start(), calls=%async_computation.6 | async-start | bytes 34603008 | tf_op jit(solution)/shard_map/all_gather | solution.py:102
  228.4 530.6 %all-gather.17.cloned.1.call-start = ((), (), s32[]{:S(2)}) async-start(), calls=%async_computation.7 | async-start | bytes 34603008 | tf_op jit(solution)/shard_map/all_gather | solution.py:143
  229.0 667.1 %reduce-scatter.4.cloned.1.call-start = ((), (), s32[]{:S(2)}) async-start(), calls=%async_computation.8 | async-start | bytes 10485760 | tf_op jit(solution)/shard_map/reduce_scatter | solution.py:188
  405.1 505.0 %reduce-scatter.6.cloned.1.call-start = ((), (), s32[]{:S(2)}) async-start(), calls=%async_computation.9 | async-start | bytes 10485760 | tf_op jit(solution)/shard_map/reduce_scatter | solution.py:191
  472.3 2.0 copy-start.10
  474.3 8.2 copy-start.19
  492.6 71.3 %copy-start.7 = (bf16[512,2048]{1,0:T(8,128)(2,1)S(1)}, bf16[512,2048]{1,0:T(8,128)(2,1)}, u32[]{:S(2)}) copy-start(bf16[512,2048]{1,0:T(8,128)(2,1)} %get-tuple-element.57) | copy-start | bytes 6291460
  492.7 687.7 %all-reduce.18.cloned.1.call-start = ((), (), s32[]{:S(2)}) async-start(), calls=%async_computation.12 | async-start | bytes 196608
  759.1 62.2 %copy-start.5 = (f32[512,8192]{1,0:T(8,128)S(1)}, f32[512,8192]{1,0:T(8,128)}, u32[]{:S(2)}) copy-start(f32[512,8192]{1,0:T(8,128)} %fusion.89) | copy-start | bytes 50331652
  831.7 34.7 %copy-start.8 = (bf16[512,2048]{1,0:T(8,128)(2,1)S(1)}, bf16[512,2048]{1,0:T(8,128)(2,1)}, u32[]{:S(2)}) copy-start(bf16[512,2048]{1,0:T(8,128)(2,1)} %get-tuple-element.57) | copy-start | bytes 6291460
  896.2 2.8 copy-start.6
  899.0 2.3 copy-start.4
  899.0 2.3 copy-start.15
  903.5 2.1 copy-start.9
  920.7 10.3 copy-start.16
  953.9 21.2 copy-start.1
  953.9 21.2 copy-start.21
  953.9 21.2 copy-start.23
  953.9 21.2 copy-start.25
  953.9 21.2 copy-start.28
  1002.8 1728.0 %reduce-scatter.8.cloned.1.call-start = ((), (), s32[]{:S(2)}) async-start(), calls=%async_computation.10 | async-start | bytes 207618048 | tf_op jit(solution)/shard_map/reduce_scatter | solution.py:242
  1135.2 9.6 copy-start.2
  1144.7 30.4 %copy-start.34 = (f32[512]{0:T(512)S(1)}, f32[512]{0:T(512)}, u32[]{:S(2)}) copy-start(f32[512]{0:T(512)} %get-tuple-element.44) | copy-start | bytes 6148
  1144.7 30.4 %copy-start.33 = (f32[512]{0:T(512)S(1)}, f32[512]{0:T(512)}, u32[]{:S(2)}) copy-start(f32[512]{0:T(512)} %get-tuple-element.45) | copy-start | bytes 6148
  1144.7 30.4 %copy-start.11 = (bf16[2,256,2048]{2,1,0:T(8,128)(2,1)S(1)}, bf16[2,256,2048]{2,1,0:T(8,128)(2,1)}, u32[]{:S(2)}) copy-start(bf16[2,256,2048]{2,1,0:T(8,128)(2,1)} %param.17) | copy-start | bytes 6291460
  1144.8 30.4 %copy-start.26 = (f32[1,2,2,128]{3,1,2,0:T(2,128)S(1)}, f32[1,2,2,128]{3,1,2,0:T(2,128)}, u32[]{:S(2)}) copy-start(f32[1,2,2,128]{3,1,2,0:T(2,128)} %copy-done.24) | copy-start | bytes 6148
  1144.8 30.4 %copy-start.29 = (f32[1,2,2,128]{3,1,2,0:T(2,128)S(1)}, f32[1,2,2,128]{3,1,2,0:T(2,128)}, u32[]{:S(2)}) copy-start(f32[1,2,2,128]{3,1,2,0:T(2,128)} %copy-done.27) | copy-start | bytes 6148
  1182.4 1557.6 %copy-start.43 = (f32[64]{0:T(128)}, f32[64]{0:T(128)S(1)}, u32[]{:S(2)}) copy-start(f32[64]{0:T(128)S(1)} %dynamic-slice.5) | copy-start | bytes 772
  (6 other events, 5.9 us)
Sparse Core Ops, SparseCore 0:
  10.9 158.3 all-gather.8
  172.2 75.2 all-gather.12
  249.1 56.8 all-gather.10
  307.4 59.3 all-gather.18
  369.5 194.4 all-gather.14
  566.7 192.3 all-gather.16
  761.6 69.5 reduce-scatter.3
  833.8 71.4 reduce-scatter.5
  1002.9 125.4 all-reduce.17
  1134.7 1596.1 reduce-scatter.7
where the time goes:
time: 2760 us; the launch traced here: 2750 us
  waiting for transfers between devices  1990 us (72%)
  matrix products  377 us (14%)
  other arithmetic  186 us (7%)
  local copies, waits for them, and re-layouts  96 us (3%)
  blocking collectives  87.5 us (3%)
    reduce_scatter x1, waiting for transfers between devices, body(): lax.psum_scatter(jnp.concatenate([token_dot(normed_one, grad_packed), tok...  1540 us
    all_gather x1, waiting for transfers between devices, body(): lax.all_gather(down_weight, ('dp', 'seq'), axis=0, tiled=True)  168 us
    concatenate x1, other arithmetic, body(): jnp.concatenate([token_dot(normed_one, grad_packed), token_dot(normed_two...  131 us
    dot_general x4, matrix products, matmul(): return jnp.dot(left, right, preferred_element_type=jnp.float32)  119 us
    all_gather x1, waiting for transfers between devices, body(): lax.all_gather(qkv_weight, ('dp', 'seq'), axis=0, tiled=True)  106 us
    dot_general x4, matrix products, token_dot(): lax.dot_general(left, right, (((0,), (0,)), ((), ())), preferred_element_...  95.5 us
    dot_general x4, matrix products, cross_dot(): lax.dot_general(left, right, (((1,), (1,)), ((), ())), preferred_element_...  88.8 us
    all_gather x1, waiting for transfers between devices, body(): lax.all_gather(up_weight, ('dp', 'seq'), axis=0, tiled=True)  71 us
  transfers between devices with their start and end apart: 10, of which 7 were waited for; matrix products, arithmetic and copies ran while one was open for 20% of the time, Pallas kernels for 0%

commit v1 on v0

v1 whole, which is shorter than its diff:
```python
import functools
import math

import jax
import jax.numpy as jnp
from jax import lax
from jax.experimental import pallas as pl
from jax.experimental.pallas import tpu as pltpu
from jax.sharding import Mesh, PartitionSpec as P


HEADS = 8
HEAD_DIM = 256
ROTARY = 64
EPSILON = 1e-05
NEGATIVE = -1e30
F32 = jnp.float32
BF16 = jnp.bfloat16
ALL = ("zo", "yi", "seq")
GROUP = ("yi", "seq")
MESH = pl.DeviceIdType.MESH
ANY = pl.BlockSpec(memory_space=pl.ANY)


def dot(left, right, dims):
    return lax.dot_general(left, right, (dims, ((), ())), preferred_element_type=F32)


def split_axes(mesh):
    dp, seq = mesh.shape["dp"], mesh.shape["seq"]
    sub = 1
    while seq * sub * 2 <= HEADS and dp % (sub * 2) == 0:
        sub *= 2
    return dp // sub, sub, seq


def remote(source, target, send, recv, device):
    return pltpu.make_async_remote_copy(
        src_ref=source, dst_ref=target, send_sem=send, recv_sem=recv,
        device_id=device, device_id_type=MESH,
    )


class Layout:
    def __init__(self, outer, sub, seq):
        self.outer, self.sub, self.seq = outer, sub, seq
        self.chips_x = seq // 2
        self.group = sub * seq
        self.count = outer * self.group
        self.heads = HEADS // self.group
        self.offsets = [(ry, rx) for ry in range(sub) for rx in range(self.chips_x)]
        self.far = sorted(self.offsets[1:], key=lambda o: (o[0] > 0) + (o[1] > 0))

    def shift(self, ry, rx):
        pairs = []
        for y in range(self.sub):
            for x in range(self.chips_x):
                for c in range(2):
                    there = ((y + ry) % self.sub, (x + rx) % self.chips_x)
                    pairs.append((y * self.seq + x * 2 + c, there[0] * self.seq + there[1] * 2 + c))
        return pairs

    def flip(self):
        return [(i, i ^ 1) for i in range(self.seq)]


def swap_copies(lay, plan, me, sources, targets, send, recv, back):
    zo = lax.axis_index("zo")
    copies = []
    for k in range(1, lay.group):
        peer = lax.rem(me + k, lay.group)
        device = (zo, peer // lay.seq, lax.rem(peer, lay.seq))
        j = 0
        for (parts, rows, cols), source, target in zip(plan, sources, targets, strict=True):
            for part in range(parts):
                wide = lambda who: pl.ds(pl.multiple_of((part * lay.group + who) * cols, 128), cols)
                thin = pl.ds(part * cols, cols)
                block = lambda who: pl.ds(pl.multiple_of(who * rows, rows), rows)
                if back:
                    copies.append(remote(source.at[block(peer), thin], target.at[:, wide(me)], send.at[k - 1, j], recv.at[k - 1, j], device))
                else:
                    copies.append(remote(source.at[:, wide(peer)], target.at[block(me), thin], send.at[k - 1, j], recv.at[k - 1, j], device))
                j += 1
    return copies


def swap_own(lay, plan, me, sources, targets, sems, back):
    copies = []
    j = 0
    for (parts, rows, cols), source, target in zip(plan, sources, targets, strict=True):
        for part in range(parts):
            wide = pl.ds(pl.multiple_of((part * lay.group + me) * cols, 128), cols)
            thin = pl.ds(part * cols, cols)
            block = pl.ds(pl.multiple_of(me * rows, rows), rows)
            if back:
                copies.append(pltpu.make_async_copy(source.at[block, thin], target.at[:, wide], sems.at[j]))
            else:
                copies.append(pltpu.make_async_copy(source.at[:, wide], target.at[block, thin], sems.at[j]))
            j += 1
    return copies


def group_barrier(lay, me):
    zo = lax.axis_index("zo")
    barrier = pltpu.get_barrier_semaphore()
    for k in range(1, lay.group):
        peer = lax.rem(me + k, lay.group)
        pl.semaphore_signal(
            barrier, inc=1, device_id=(zo, peer // lay.seq, lax.rem(peer, lay.seq)), device_id_type=MESH
        )
    pl.semaphore_wait(barrier, lay.group - 1)


def swap_shapes(lay, plan, back):
    if back:
        return [jax.ShapeDtypeStruct((rows, parts * lay.group * cols), BF16) for parts, rows, cols in plan]
    return [jax.ShapeDtypeStruct((lay.group * rows, parts * cols), BF16) for parts, rows, cols in plan]


def exchange_kernel(lay, plan, back, *refs):
    n = len(plan)
    vec_ref, sources = refs[0], refs[1 : 1 + n]
    all_ref, targets = refs[1 + n], refs[2 + n : 2 + 2 * n]
    send, recv, own, vec_send, vec_recv, vec_own = refs[2 + 2 * n :]
    zo = lax.axis_index("zo")
    me = lax.axis_index("yi") * lay.seq + lax.axis_index("seq")
    rank = zo * lay.group + me

    def device_of(k):
        peer = lax.rem(rank + k, lay.count)
        inner = lax.rem(peer, lay.group)
        return (peer // lay.group, inner // lay.seq, lax.rem(inner, lay.seq))

    barrier = pltpu.get_barrier_semaphore()

    def greet(k, carry):
        pl.semaphore_signal(barrier, inc=1, device_id=device_of(k), device_id_type=MESH)
        return carry

    lax.fori_loop(1, lay.count, greet, 0)
    pl.semaphore_wait(barrier, lay.count - 1)
    copies = swap_copies(lay, plan, me, sources, targets, send, recv, back)
    mine = swap_own(lay, plan, me, sources, targets, own, back)
    mine.append(pltpu.make_async_copy(vec_ref, all_ref.at[rank], vec_own))

    def vec_copy(k):
        return remote(vec_ref, all_ref.at[rank], vec_send.at[k - 1], vec_recv.at[k - 1], device_of(k))

    def start(k, carry):
        vec_copy(k).start()
        return carry

    def finish(k, carry):
        vec_copy(k).wait()
        return carry

    lax.fori_loop(1, lay.count, start, 0)
    for copy in copies + mine:
        copy.start()
    lax.fori_loop(1, lay.count, finish, 0)
    for copy in copies + mine:
        copy.wait()


def busy(microseconds):
    return pl.CostEstimate(flops=int(7e8 * microseconds), bytes_accessed=1 << 20, transcendentals=0)


def exchange(lay, plan, vec, arrays, back, number, time):
    count = sum(parts for parts, _, _ in plan)
    return pl.pallas_call(
        functools.partial(exchange_kernel, lay, plan, back),
        out_shape=[jax.ShapeDtypeStruct((lay.count, *vec.shape), F32), *swap_shapes(lay, plan, back)],
        in_specs=[ANY] * (1 + len(plan)),
        out_specs=[ANY] * (1 + len(plan)),
        scratch_shapes=[
            pltpu.SemaphoreType.DMA((lay.group - 1, count)),
            pltpu.SemaphoreType.DMA((lay.group - 1, count)),
            pltpu.SemaphoreType.DMA((count,)),
            pltpu.SemaphoreType.DMA((lay.count - 1,)),
            pltpu.SemaphoreType.DMA((lay.count - 1,)),
            pltpu.SemaphoreType.DMA,
        ],
        compiler_params=pltpu.CompilerParams(collective_id=number, has_side_effects=True),
        cost_estimate=busy(time),
    )(vec, *arrays)


def norm_kernel(lay, plan, *refs):
    n = len(plan)
    x_ref, gain_ref, sources = refs[0], refs[1], refs[2 : 2 + n]
    one_ref, two_ref, hat_ref, targets = *refs[2 + n : 5 + n], refs[5 + n : 5 + 2 * n]
    held, stage, send, recv, core_send, core_recv, w_send, w_recv, w_own, own_sem, out_sem = refs[5 + 2 * n :]
    batch, length, _ = x_ref.shape
    zo, yi, s = lax.axis_index("zo"), lax.axis_index("yi"), lax.axis_index("seq")
    me = yi * lay.seq + s
    x, core = s // 2, lax.rem(s, 2)
    partner = (zo, yi, x * 2 + 1 - core)

    def chip(ry, rx):
        return (zo, lax.rem(yi + ry, lay.sub), lax.rem(x + rx, lay.chips_x) * 2 + core)

    group_barrier(lay, me)
    slot = {offset: i for i, offset in enumerate(lay.offsets)}
    own_copy = pltpu.make_async_copy(x_ref, held.at[0, 0], own_sem)
    own_copy.start()
    straight = [o for o in lay.far if not (o[0] and o[1])]
    diagonal = [o for o in lay.far if o[0] and o[1]]
    copies = {}
    for o in straight:
        copies[o] = [remote(x_ref, held.at[0, slot[o]], send.at[slot[o], 0], recv.at[slot[o], 0], chip(*o))]
    half = batch // 2
    for ry, rx in diagonal:
        j = slot[(ry, rx)]
        copies[(ry, rx)] = [
            remote(held.at[0, slot[(0, rx)], :half], held.at[0, j, :half], send.at[j, 0], recv.at[j, 0], chip(ry, 0)),
            remote(held.at[0, slot[(ry, 0)], half:], held.at[0, j, half:], send.at[j, 1], recv.at[j, 1], chip(0, rx)),
        ]
    to_partner = {
        o: remote(x_ref if o == (0, 0) else held.at[0, slot[o]], held.at[1, slot[o]],
                  core_send.at[slot[o]], core_recv.at[slot[o]], partner)
        for o in lay.offsets
    }
    for o in straight:
        copies[o][0].start()
    to_partner[(0, 0)].start()
    swaps = swap_copies(lay, plan, me, sources, targets, w_send, w_recv, False)
    mine = swap_own(lay, plan, me, sources, targets, w_own, False)
    for copy in swaps + mine:
        copy.start()

    gains = [gain_ref[i : i + 1, :] for i in range(4)]
    rows = 16
    pending = [[], []]
    turn = [0]

    def norm(c, j):
        for m in range(batch):
            k = turn[0] % 2
            turn[0] += 1
            for copy in pending[k]:
                copy.wait()

            def chunk(i, carry):
                at = pl.ds(pl.multiple_of(i * rows, rows), rows)
                value = held[c, j, m, at, :].astype(F32)
                center = value - jnp.mean(value, -1, keepdims=True)
                hat = center * lax.rsqrt(jnp.mean(center * center, -1, keepdims=True) + EPSILON)
                stage[k, 0, at, :] = (hat * gains[0] + gains[1]).astype(BF16)
                stage[k, 1, at, :] = (hat * gains[2] + gains[3]).astype(BF16)
                stage[k, 2, at, :] = hat.astype(BF16)
                return carry

            lax.fori_loop(0, length // rows, chunk, 0)
            pending[k] = [
                pltpu.make_async_copy(stage.at[k, i], ref.at[c, j, m], out_sem.at[k, i])
                for i, ref in enumerate((one_ref, two_ref, hat_ref))
            ]
            for copy in pending[k]:
                copy.start()

    own_copy.wait()
    norm(0, 0)
    to_partner[(0, 0)].wait_recv()
    norm(1, 0)
    for o in straight:
        copies[o][0].wait_recv()
        to_partner[o].start()
        for ry, rx in diagonal:
            if o == (0, rx):
                copies[(ry, rx)][0].start()
            if o == (ry, 0):
                copies[(ry, rx)][1].start()
        norm(0, slot[o])
    for o in straight:
        to_partner[o].wait_recv()
        norm(1, slot[o])
    for o in diagonal:
        for copy in copies[o]:
            copy.wait_recv()
        to_partner[o].start()
        norm(0, slot[o])
    for o in diagonal:
        to_partner[o].wait_recv()
        norm(1, slot[o])
    for side in pending:
        for copy in side:
            copy.wait()
    for o in lay.far:
        for copy in copies[o]:
            copy.wait_send()
    for o in lay.offsets:
        to_partner[o].wait_send()
    for copy in swaps + mine:
        copy.wait()


def norm_exchange(lay, plan, tokens, gains, weights):
    count = sum(parts for parts, _, _ in plan)
    chips = lay.group // 2
    whole = jax.ShapeDtypeStruct((2, chips, *tokens.shape), BF16)
    return pl.pallas_call(
        functools.partial(norm_kernel, lay, plan),
        out_shape=[whole] * 3 + swap_shapes(lay, plan, False),
        in_specs=[ANY, pl.BlockSpec(memory_space=pltpu.VMEM)] + [ANY] * len(plan),
        out_specs=[ANY] * (3 + len(plan)),
        scratch_shapes=[
            pltpu.VMEM((2, chips, *tokens.shape), BF16),
            pltpu.VMEM((2, 3, *tokens.shape[1:]), BF16),
            pltpu.SemaphoreType.DMA((chips, 2)),
            pltpu.SemaphoreType.DMA((chips, 2)),
            pltpu.SemaphoreType.DMA((chips,)),
            pltpu.SemaphoreType.DMA((chips,)),
            pltpu.SemaphoreType.DMA((lay.group - 1, count)),
            pltpu.SemaphoreType.DMA((lay.group - 1, count)),
            pltpu.SemaphoreType.DMA((count,)),
            pltpu.SemaphoreType.DMA,
            pltpu.SemaphoreType.DMA((2, 3)),
        ],
        compiler_params=pltpu.CompilerParams(
            collective_id=1, has_side_effects=True, vmem_limit_bytes=48 << 20
        ),
        cost_estimate=busy(100),
        name="norm_exchange",
    )(tokens, gains, *weights)


def deal_kernel(lay, plan, *refs):
    n = len(plan)
    sources, targets = refs[:n], refs[n : 2 * n]
    send, recv, own = refs[2 * n :]
    me = lax.axis_index("yi") * lay.seq + lax.axis_index("seq")
    group_barrier(lay, me)
    copies = swap_copies(lay, plan, me, sources, targets, send, recv, True)
    copies += swap_own(lay, plan, me, sources, targets, own, True)
    for copy in copies:
        copy.start()
    for copy in copies:
        copy.wait()


def deal_exchange(lay, plan, sums, number):
    count = sum(parts for parts, _, _ in plan)
    return pl.pallas_call(
        functools.partial(deal_kernel, lay, plan),
        out_shape=swap_shapes(lay, plan, True),
        in_specs=[ANY] * len(plan),
        out_specs=[ANY] * len(plan),
        scratch_shapes=[
            pltpu.SemaphoreType.DMA((lay.group - 1, count)),
            pltpu.SemaphoreType.DMA((lay.group - 1, count)),
            pltpu.SemaphoreType.DMA((count,)),
        ],
        compiler_params=pltpu.CompilerParams(collective_id=number, has_side_effects=True),
        cost_estimate=busy(17),
    )(*sums)


def turn_pairs(field, cosine, sine):
    halves = ROTARY // 2
    front = field[:, :128]
    lane = lax.broadcasted_iota(jnp.int32, front.shape, 1)
    other = jnp.where(lane < halves, pltpu.roll(front, 128 - halves, 1), pltpu.roll(front, halves, 1))
    return jnp.concatenate([front * cosine + other * sine, field[:, 128:]], -1)


QUERY_BLOCK = 256


def attend_kernel(scaling, packed_ref, cos_ref, sin_ref, col_ref, row_ref, q_ref, k_ref, v_ref, ctx_ref, lse_ref,
                  q_buf, k_buf, v_buf):
    cores, _, chips, _, length, _ = packed_ref.shape
    for c in range(cores):
        for i in range(chips):
            at = pl.ds((c * chips + i) * length, length)
            block = packed_ref[c, 0, i, 0]
            cosine, sine = cos_ref[0, at, :], sin_ref[0, at, :]
            q_buf[at, :] = turn_pairs(block[:, :HEAD_DIM], cosine, sine).astype(BF16)
            k_buf[at, :] = turn_pairs(block[:, HEAD_DIM : 2 * HEAD_DIM], cosine, sine).astype(BF16)
            v_buf[at, :] = block[:, 2 * HEAD_DIM :].astype(BF16)
    q_ref[0] = q_buf[...]
    k_ref[0] = k_buf[...]
    v_ref[0] = v_buf[...]
    total = cores * chips * length

    def one(j, carry):
        at = pl.ds(pl.multiple_of(j * QUERY_BLOCK, QUERY_BLOCK), QUERY_BLOCK)
        scores = dot(k_buf[...], q_buf[at, :], ((1,), (1,))) * scaling
        allowed = col_ref[0] <= row_ref[0, :, at]
        scores = jnp.where(allowed, scores, NEGATIVE)
        top = jnp.max(scores, 0, keepdims=True)
        weights = jnp.where(allowed, jnp.exp(scores - top), 0.0)
        total_row = jnp.sum(weights, 0, keepdims=True)
        probs = (weights * (1.0 / total_row)).astype(BF16)
        ctx_ref[0, at, :] = dot(probs, v_buf[...], ((0,), (0,))).astype(BF16)
        lse_ref[0, :, at] = top + jnp.log(total_row)
        return carry

    lax.fori_loop(0, total // QUERY_BLOCK, one, 0)


def attend_back_kernel(scaling, q_ref, k_ref, v_ref, g_ref, cos_ref, sin_ref, col_ref, row_ref, lse_ref, out_ref,
                       dq_buf, dk_buf, dv_buf):
    cores, _, chips, _, length, _ = out_ref.shape
    total = q_ref.shape[1]
    dk_buf[...] = jnp.zeros_like(dk_buf)
    dv_buf[...] = jnp.zeros_like(dv_buf)

    def one(j, carry):
        at = pl.ds(pl.multiple_of(j * QUERY_BLOCK, QUERY_BLOCK), QUERY_BLOCK)
        queries = q_ref[0, at, :]
        grads = g_ref[0, at, :]
        scores = dot(k_ref[0], queries, ((1,), (1,))) * scaling
        allowed = col_ref[0] <= row_ref[0, :, at]
        scores = jnp.where(allowed, scores, NEGATIVE)
        probs = jnp.where(allowed, jnp.exp(scores - lse_ref[0, :, at]), 0.0)
        grad_probs = dot(v_ref[0], grads, ((1,), (1,)))
        delta = jnp.sum(probs * grad_probs, 0, keepdims=True)
        grad_scores = (probs * (grad_probs - delta)).astype(BF16)
        dv_buf[...] += dot(probs.astype(BF16), grads, ((1,), (0,)))
        dk_buf[...] += dot(grad_scores, queries, ((1,), (0,)))
        dq_buf[at, :] = dot(grad_scores, k_ref[0], ((0,), (0,)))
        return carry

    lax.fori_loop(0, total // QUERY_BLOCK, one, 0)
    for c in range(cores):
        for i in range(chips):
            at = pl.ds((c * chips + i) * length, length)
            cosine, sine = cos_ref[0, at, :], sin_ref[0, at, :]
            out_ref[c, 0, i, 0, :, :HEAD_DIM] = turn_pairs(dq_buf[at, :] * scaling, cosine, -sine).astype(BF16)
            out_ref[c, 0, i, 0, :, HEAD_DIM : 2 * HEAD_DIM] = turn_pairs(dk_buf[at, :] * scaling, cosine, -sine).astype(BF16)
            out_ref[c, 0, i, 0, :, 2 * HEAD_DIM :] = dv_buf[at, :].astype(BF16)


def make_body(lay):
    sub, seq, group, chips_x = lay.sub, lay.seq, lay.group, lay.chips_x

    def gather_near(value):
        return [value if o == (0, 0) else lax.ppermute(value, GROUP, lay.shift(*o)) for o in lay.offsets]

    def gather_partner(near):
        partner = [lax.ppermute(piece, "seq", lay.flip()) for piece in near]
        return jnp.concatenate([piece[None] for piece in near + partner], 0)

    def reduce_near(kept, given):
        came = lax.ppermute(given, "seq", lay.flip())
        came, kept = lax.optimization_barrier((came, kept))
        return [
            (kept[i].astype(F32) + came[i].astype(F32)).astype(BF16) if o != (0, 0) else kept[i].astype(F32) + came[i].astype(F32)
            for i, o in enumerate(lay.offsets)
        ]

    def reduce_far(pieces):
        total = pieces[0]
        for o, piece in zip(lay.offsets[1:], pieces[1:], strict=True):
            back = ((-o[0]) % sub, (-o[1]) % chips_x)
            came = lax.ppermute(piece, GROUP, lay.shift(*back))
            total = total + came.astype(F32)
        return total

    def after(value, *tokens):
        return lax.optimization_barrier((value, *tokens))[0]

    def step(
        tokens, positions, cotangent, gain1, bias1, gain2, bias2,
        w_qkv, b_qkv, w_out, b_out, w_up, b_up, w_down, b_down,
    ):
        batch, length, width = tokens.shape
        rows = w_qkv.shape[0]
        ff = w_up.shape[1]
        count = seq * length
        total = group * batch * length
        my_seq = lax.axis_index("seq")
        me = lax.axis_index("yi") * seq + my_seq
        scaling = HEAD_DIM ** (-0.5)
        cols = lay.heads * HEAD_DIM
        ff_cols = ff // group
        out_cols = width // group
        plans = {"up": (1, rows, ff_cols), "down": (1, rows, ff_cols), "qkv": (3, rows, cols), "out": (1, rows, out_cols)}

        def gather_rows(mine):
            return lax.all_gather(mine, "zo", axis=0, tiled=True)

        names = (bias1, bias2, gain1, gain2, b_qkv, b_up, b_out, b_down)
        vec = jnp.concatenate([v.astype(F32) for v in names])
        size = -(-vec.shape[0] // 1024) * 1024
        vec = jnp.pad(vec, (0, size - vec.shape[0])).reshape(-1, 128)
        vectors, up_own, qkv_own = exchange(lay, [plans["up"], plans["qkv"]], vec, [w_up, w_qkv], False, 0, 30)
        up_w = gather_rows(up_own)
        qkv_w = gather_rows(qkv_own)
        vectors = vectors.reshape(lay.count, -1)
        cuts = []
        at = 0
        for piece in names:
            cuts.append(vectors[:, at : at + piece.shape[0]].reshape(-1))
            at += piece.shape[0]
        bias1_all, bias2_all, gain1_all, gain2_all, b_qkv_all, b_up_all, b_out_all, b_down_all = cuts
        b_qkv_mine = lax.dynamic_index_in_dim(b_qkv_all.reshape(3, group, cols), me, 1, keepdims=False).reshape(-1)
        b_up_mine = lax.dynamic_index_in_dim(b_up_all.reshape(group, ff_cols), me, 0, keepdims=False)
        zeros = jnp.zeros_like(bias1_all)
        gains = jnp.stack([gain1_all, bias1_all, gain2_all, bias2_all, zeros, zeros, zeros, zeros])
        one, two, hat, out_own, down_own = norm_exchange(lay, [plans["out"], plans["down"]], tokens, gains, [w_out, w_down])
        out_w = gather_rows(out_own)
        down_w = gather_rows(down_own)
        one, two, hat = [v.reshape(total, width) for v in (one, two, hat)]
        cotangent, hat = lax.optimization_barrier((cotangent, hat))
        near_dy = gather_near(cotangent)

        x, core = my_seq // 2, my_seq % 2
        places = []
        for ry in range(sub):
            from_there = positions
            if ry:
                from_there = lax.ppermute(positions, "yi", [(i, (i + ry) % sub) for i in range(sub)])
            blocks = from_there.reshape(batch, seq, length)
            order = [((x - rx) % chips_x) * 2 + (core + rc) % 2 for rc in range(2) for rx in range(chips_x)]
            places.append(jnp.concatenate([lax.dynamic_slice_in_dim(blocks, o, 1, 1) for o in order], 1))
        places = jnp.stack(places).reshape(sub * batch, count)
        halves = ROTARY // 2
        frequency = jnp.exp(jnp.arange(halves, dtype=F32) * (-2.0 * math.log(10000.0) / ROTARY))
        phases = places.astype(F32)[..., None] * frequency
        cosine, sine = jnp.cos(phases), jnp.sin(phases)
        rest = (sub * batch, count, 128 - ROTARY)
        cosine = jnp.concatenate([cosine, cosine, jnp.ones(rest, F32)], -1)
        sine = jnp.concatenate([-sine, sine, jnp.zeros(rest, F32)], -1)
        place_col = places[:, :, None]
        place_row = places[:, None, :]

        hidden = dot(two, up_w, ((1,), (0,))) + b_up_mine
        phi_cdf = 0.5 * (1.0 + lax.erf(hidden * math.sqrt(0.5)))
        density = jnp.exp(-0.5 * hidden * hidden) * (1.0 / math.sqrt(2.0 * math.pi))
        activated = (hidden * phi_cdf).astype(BF16)
        slope = (phi_cdf + hidden * density).astype(BF16)
        activated, slope = lax.optimization_barrier((activated, slope))

        seqs = sub * batch
        one = after(one, activated)
        packed = dot(one, qkv_w, ((1,), (0,))) + b_qkv_mine
        wide = (2, 1, chips_x, 1, length, 3 * cols)
        wide_spec = pl.BlockSpec(wide, lambda i: (0, i // batch, 0, i % batch, 0, 0))
        full = (2, sub, chips_x, batch, length, 3 * cols)
        head_spec = pl.BlockSpec((1, count, HEAD_DIM), lambda i: (i, 0, 0))
        turn_spec = pl.BlockSpec((1, count, 128), lambda i: (i, 0, 0))
        col_spec = pl.BlockSpec((1, count, 1), lambda i: (i, 0, 0))
        row_spec = pl.BlockSpec((1, 1, count), lambda i: (i, 0, 0))
        head_shape = jax.ShapeDtypeStruct((seqs, count, HEAD_DIM), BF16)
        work = 2 * seqs * count * count * HEAD_DIM
        params = pltpu.CompilerParams(vmem_limit_bytes=56 << 20)
        queries, keys, values, context, lse = pl.pallas_call(
            functools.partial(attend_kernel, scaling),
            grid=(seqs,),
            in_specs=[wide_spec, turn_spec, turn_spec, col_spec, row_spec],
            out_specs=[head_spec] * 4 + [row_spec],
            out_shape=[head_shape] * 4 + [jax.ShapeDtypeStruct((seqs, 1, count), F32)],
            scratch_shapes=[pltpu.VMEM((count, HEAD_DIM), BF16)] * 3,
            compiler_params=params,
            cost_estimate=pl.CostEstimate(flops=2 * work, bytes_accessed=30 << 20, transcendentals=seqs * count * count),
            name="attend",
        )(packed.reshape(full), cosine, sine, place_col, place_row)

        def to_tokens(v):
            v = v.reshape(sub, batch, 2, chips_x, length, cols)
            return jnp.transpose(v, (2, 0, 3, 1, 4, 5)).reshape(total, cols)

        def to_heads(v):
            v = v.reshape(2, sub, chips_x, batch, length, cols)
            return jnp.transpose(v, (1, 3, 0, 2, 4, 5)).reshape(seqs, count, cols)

        context = to_tokens(context)

        def scatter(grad):
            return lax.psum_scatter(grad, "zo", scatter_dimension=0, tiled=True)

        def outer_dot(left, right):
            return dot(left, right, ((0,), (0,))).astype(BF16)

        near_dy = lax.optimization_barrier((*near_dy, context))[:-1]
        upstream = gather_partner(list(near_dy)).reshape(total, width)
        down_part = outer_dot(upstream, activated)
        upstream = after(upstream, down_part)
        down_sum = scatter(down_part)
        grad_context = dot(upstream, out_w, ((1,), (0,))).astype(BF16)
        upstream = after(upstream, grad_context)
        out_part = outer_dot(upstream, context)
        out_w_sum = scatter(out_part)

        def two_dots(half, first, first_w, second, second_w):
            size = total // 2
            cut = slice(half * size, (half + 1) * size)
            sums = dot(first[cut], first_w, ((1,), (1,))) + dot(second[cut], second_w, ((1,), (1,)))
            return sums.astype(BF16).reshape(group // 2, batch, length, first_w.shape[0])

        def chain(values, *tokens):
            return lax.optimization_barrier((*values, *tokens))[: len(values)]

        pair = chain((context, activated), out_part)
        given = two_dots(1, pair[0], out_w, pair[1], down_w)
        pair = chain(pair, given)
        kept = two_dots(0, pair[0], out_w, pair[1], down_w)
        out_near = reduce_near(kept, given)
        grad_context, *out_near = chain((grad_context, *out_near))
        out_sum = reduce_far(out_near)
        output = (tokens.astype(F32) + out_sum + b_out_all + b_down_all).astype(BF16)

        grad_packed = pl.pallas_call(
            functools.partial(attend_back_kernel, scaling),
            grid=(seqs,),
            in_specs=[head_spec] * 4 + [turn_spec, turn_spec, col_spec, row_spec, row_spec],
            out_specs=wide_spec,
            out_shape=jax.ShapeDtypeStruct(full, BF16),
            scratch_shapes=[pltpu.VMEM((count, HEAD_DIM), F32)] * 3,
            compiler_params=params,
            cost_estimate=pl.CostEstimate(flops=5 * work, bytes_accessed=24 << 20, transcendentals=seqs * count * count),
            name="attend_back",
        )(queries, keys, values, to_heads(grad_context), cosine, sine, place_col, place_row, lse)
        grad_packed = grad_packed.reshape(total, 3 * cols)

        qkv_part = outer_dot(hat, grad_packed)
        qkv_sum = scatter(qkv_part)
        (upstream,) = chain((upstream,), qkv_part)
        grad_hidden = (dot(upstream, down_w, ((1,), (0,))) * slope.astype(F32)).astype(BF16)
        hat, grad_hidden = chain((hat, grad_hidden))
        up_part = outer_dot(hat, grad_hidden)
        up_sum = scatter(up_part)

        down_sum, out_w_sum = chain((down_sum, out_w_sum), up_part)
        down_raw, out_raw = deal_exchange(lay, [plans["down"], plans["out"]], [down_sum, out_w_sum], 2)

        fold_qkv = (gain1_all[:, None] * qkv_w.astype(F32)).astype(BF16)
        fold_up = (gain2_all[:, None] * up_w.astype(F32)).astype(BF16)
        pair = chain((grad_packed, grad_hidden, fold_qkv, fold_up), down_raw, out_raw)
        normal_sums = []
        chunk = width // 2
        for k in range(2):
            cut = slice(k * chunk, (k + 1) * chunk)
            given = two_dots(1, pair[0], pair[2][cut], pair[1], pair[3][cut])
            pair = chain(pair, given)
            kept = two_dots(0, pair[0], pair[2][cut], pair[1], pair[3][cut])
            near = reduce_near(kept, given)
            both = chain((*pair, *near))
            pair, near = both[:4], both[4:]
            normal_sums.append(reduce_far(near))
        inputs = tokens.astype(F32)
        center = inputs - jnp.mean(inputs, -1, keepdims=True)
        inv_std = lax.rsqrt(jnp.mean(center * center, -1, keepdims=True) + EPSILON)
        normal = center * inv_std
        grad_normal = jnp.concatenate(normal_sums, -1)
        token_grad = cotangent.astype(F32) + inv_std * (
            grad_normal
            - jnp.mean(grad_normal, -1, keepdims=True)
            - normal * jnp.mean(grad_normal * normal, -1, keepdims=True)
        )

        own_sums = [
            jnp.sum(grad_packed.astype(F32), 0),
            jnp.sum(grad_hidden.astype(F32), 0),
            jnp.sum(cotangent.astype(F32), (0, 1)),
        ]
        vec = jnp.concatenate(own_sums)
        size = -(-vec.shape[0] // 1024) * 1024
        vec = jnp.pad(vec, (0, size - vec.shape[0])).reshape(-1, 128)
        rank = lax.axis_index("zo") * group + me
        everyone, up_raw, qkv_raw = exchange(lay, [plans["up"], plans["qkv"]], vec, [up_sum, qkv_sum], True, 3, 25)
        sums = jnp.sum(everyone.reshape(lay.outer, group, -1), 0)
        sum_qkv = jnp.transpose(sums[:, : 3 * cols].reshape(group, 3, cols), (1, 0, 2)).reshape(-1)
        sum_up = sums[:, 3 * cols : 3 * cols + ff_cols].reshape(-1)
        sum_dy = jnp.sum(sums[:, 3 * cols + ff_cols : 3 * cols + ff_cols + width], 0)

        def own_part(vector):
            return lax.dynamic_index_in_dim(vector.reshape(lay.count, -1), rank, 0, keepdims=False)

        up_raw, qkv_raw = up_raw.astype(F32), qkv_raw.astype(F32)
        column = lambda v: v.astype(F32)[:, None]
        return (
            output,
            token_grad,
            jnp.sum(w_qkv.astype(F32) * qkv_raw, 1),
            jnp.sum(w_qkv.astype(F32) * sum_qkv, 1),
            jnp.sum(w_up.astype(F32) * up_raw, 1),
            jnp.sum(w_up.astype(F32) * sum_up, 1),
            column(gain1) * qkv_raw + column(bias1) * sum_qkv,
            own_part(sum_qkv),
            out_raw.astype(F32),
            own_part(sum_dy),
            column(gain2) * up_raw + column(bias2) * sum_up,
            own_part(sum_up),
            down_raw.astype(F32),
            own_part(sum_dy),
        )

    return step


def solution(mesh):
    outer, sub, seq = split_axes(mesh)
    inner = Mesh(mesh.devices.reshape(outer, sub, seq), ALL)
    act = P(None, ALL, None)
    vec = P(ALL)
    mat = P(ALL, None)
    return jax.shard_map(
        make_body(Layout(outer, sub, seq)),
        mesh=inner,
        in_specs=(
            act, P(None, ("zo", "yi")), act, vec, vec, vec, vec,
            mat, vec, mat, vec, mat, vec, mat, vec,
        ),
        out_specs=(act, act, vec, vec, vec, vec, mat, vec, mat, vec, mat, vec, mat, vec),
        check_vma=False,
    )
```

time: 2760 us -> 883 us (0.32)
  waiting for transfers between devices: 1990 us -> 237 us
  Pallas kernels: 0 us -> 232 us
  other arithmetic: 186 us -> 67.4 us
  matrix products: 377 us -> 267 us
  blocking collectives: 87.5 us -> 0 us
  local copies, waits for them, and re-layouts: 96 us -> 40 us
    reduce_scatter x3 -> x4, waiting for transfers between devices: 1540 us -> 0.01 us  [scatter(): return lax.psum_scatter(grad, 'zo', scatter_dimension=0, tiled=True)]
    all_gather x6 -> x4, waiting for transfers between devices: 441 us -> 0.03 us  [gather_rows(): return lax.all_gather(mine, 'zo', axis=0, tiled=True)]
    ppermute x0 -> x20, waiting for transfers between devices: none -> 236 us  [the longest x9 143 us: reduce_far(): came = lax.ppermute(piece, GROUP, lay.shift(*back))]
    pallas_call x0 -> x6, Pallas kernels: none -> 232 us  [the longest x1 103 us: norm_exchange(): pl.pallas_call(functools.partial(norm_kernel, lay, plan), out_shape=[whol...]
    concatenate x2, other arithmetic: 133 us -> 3.86 us  [the longest x1 1.93 us: step(): cosine = jnp.concatenate([cosine, cosine, jnp.ones(rest, F32)], -1)]
    dot_general x18 -> x20, matrix products: 377 us -> 267 us  [dot(): lax.dot_general(left, right, (dims, ((), ())), preferred_element_type=F32)]
    unnamed x1 -> x0, blocking collectives: 44.8 us -> none
    all_gather x1 -> x0, blocking collectives: 42.7 us -> none  [body(): lax.all_gather(up_bias, ('dp', 'seq'), axis=0, tiled=True)]
  transfers between devices with their start and end apart: 10 -> 28, of which waited for: 7 -> 8; matrix products, arithmetic and copies ran while one was open for 20% -> 35% of each run, Pallas kernels for 0% -> 18%
where the time goes in v1:
time: 883 us; the launch traced here: 876 us
  matrix products  267 us (30%)
  waiting for transfers between devices  237 us (27%)
  Pallas kernels  232 us (26%)
  other arithmetic  67.4 us (8%)
  local copies, waits for them, and re-layouts  40 us (5%)
  starting transfers between devices  17.8 us (2%)
  between operations  15.3 us (2%)
    dot_general x20, matrix products, dot(): lax.dot_general(left, right, (dims, ((), ())), preferred_element_type=F32)  267 us
    ppermute x9, waiting for transfers between devices, reduce_far(): came = lax.ppermute(piece, GROUP, lay.shift(*back))  143 us
    pallas_call x1, Pallas kernels, norm_exchange(): pl.pallas_call(functools.partial(norm_kernel, lay, plan), out_shape=[whol...  103 us
    ppermute x1, waiting for transfers between devices, step(): lax.ppermute(positions, 'yi', [(i, (i + ry) % sub) for i in range(sub)])  86.5 us
    pallas_call x2, Pallas kernels, exchange(): pl.pallas_call(functools.partial(exchange_kernel, lay, plan, back), out_s...  59.6 us
    pallas_call x1, Pallas kernels, step(): pl.pallas_call(functools.partial(attend_back_kernel, scaling), grid=(seqs...  27.2 us
    pallas_call x1, Pallas kernels, step(): pl.pallas_call(functools.partial(attend_kernel, scaling), grid=(seqs,), i...  25.1 us
    convert_element_type x3, other arithmetic, reduce_near(): (kept[i].astype(F32) + came[i].astype(F32)).astype(BF16)  22.5 us
  transfers between devices with their start and end apart: 28, of which 8 were waited for; matrix products, arithmetic and copies ran while one was open for 35% of the time, Pallas kernels for 18%

profile of v1, /device:TPU:0, one launch (start us, length us, event | category | flops | bytes accessed | tf_op | source)
XLA Modules:
  0.0 876.3 jit_solution(1783213395777481950)
XLA Ops:
  7.2 5.4 concatenate.24
  13.2 30.2 %shard_map.254 = (f32[32,8,128]{2,1,0:T(8,128)}, bf16[512,1024]{1,0:T(8,128)(2,1)}, bf16[512,768]{1,0:T(8,128)(2,1)}) custom-call(f32[8,128]{1,0:T(8,128)} %pad_bitcast_fusion.refs_0_, bf16[64,8192]{1,0:T(8,128)(2,1)} %refs_1_.1, bf16[64,6144]{1,0:T(8,128)(2,1)} %refs_2_.2), custom_call_target="tpu_custom_call" | custom-call | flops 20999999488 | bytes 1048576 | tf_op jit(solution)/shard_map/pallas_call | solution.py:171
  47.3 103.4 %norm_exchange.1 = (bf16[2,4,2,256,2048]{4,3,2,1,0:T(8,128)(2,1)}, bf16[2,4,2,256,2048]{4,3,2,1,0:T(8,128)(2,1)}, bf16[2,4,2,256,2048]{4,3,2,1,0:T(8,128)(2,1)},...) custom-call(bf16[2,256,2048]{2,1,0:T(8,128)(2,1)S(1)} %copy-done, f32[8,2048]{1,0:T(8,128)S(1)} %stack.16.refs_1_, ...), custom_call_target="tpu_custom_call" | custom-call | flops 70000001024 | bytes 1048576 | tf_op jit(solution)/shard_map/norm_exchange/pallas_call | solution.py:302
  157.6 86.5 %collective-permute-done.3 = s32[2,1024]{1,0:T(2,128)S(1)} collective-permute-done((s32[2,1024]{1,0:T(2,128)S(1)}, s32[2,1024]{1,0:T(2,128)S(1)}, u32[]{:S(2)}, u32[]{:S(2)}) %collective-permute-start.3) | collective-permute-done | bytes 8224 | tf_op jit(solution)/shard_map/ppermute | solution.py:514
  244.8 3.3 reshape.220.col_ref
  248.1 7.5 fusion.57
  259.4 28.6 %fusion.4 = (bf16[4096,1024]{1,0:T(8,128)(2,1)}, bf16[4096,1024]{1,0:T(8,128)(2,1)}) fusion(f32[1024]{0:T(1024)S(1)} %bitcast.146, bf16[4096,2048]{1,0:T(8,128)(2,1)} %bitcast.152, bf16[2048,1024]{1,0:T(8,128)(2,1)} %all-gather.5.cloned.1.call-done), kind=kOutput, calls=%fused_computation.5 | convolution fusion | flops 17230200832 | bytes 37752832 | tf_op jit(solution)/shard_map/dot_general | solution.py:26
  288.1 19.9 %convolution_add_fusion = f32[4096,768]{1,0:T(8,128)} fusion(bf16[4096,2048]{1,0:T(8,128)(2,1)} %bitcast.151, bf16[2048,768]{1,0:T(8,128)(2,1)} %all-gather.7.cloned.1.call-done, f32[768]{0:T(1024)S(1)} %add.280), kind=kOutput, calls=%fused_computation.18 | convolution fusion | flops 12888047616 | bytes 32508928 | tf_op jit(solution)/shard_map/dot_general | solution.py:26
  307.9 25.1 %attend.1 = (bf16[4,1024,256]{2,1,0:T(8,128)(2,1)}, bf16[4,1024,256]{2,1,0:T(8,128)(2,1)}, bf16[4,1024,256]{2,1,0:T(8,128)(2,1)}, bf16[4,1024,256]{2,1,0:T(8,128)(2,1)}, f32[4,1,1024]{2,1,0:T(1,128)}) custom-call(f32[2,2,2,2,256,768]{5,4,3,2,1,0:T(8,128)} %bitcast.111, f32[4,1024,128]{2,1,0:T(8,128)} %maximum_maximum_fusion.cos_ref, ...), custom_call_target="tpu_custom_call" | custom-call | flops 4294967296 | bytes 31457280 | tf_op jit(solution)/shard_map/attend/pallas_call | solution.py:549
  333.0 3.3 copy.35
  343.7 2.8 collective-permute-done.6
  346.7 2.9 collective-permute-done.7
  349.7 5.8 copy-done.26
  355.5 20.8 %convolution_convert_fusion.2 = bf16[2048,1024]{1,0:T(8,128)(2,1)} fusion(bf16[4096,2048]{1,0:T(8,128)(2,1)S(1)} %bitcast.135, bf16[4096,1024]{1,0:T(8,128)(2,1)S(1)} %bitcast.154), kind=kOutput, calls=%fused_computation.55 | convolution fusion | flops 17181966336 | bytes 29360128 | tf_op jit(solution)/shard_map/dot_general | solution.py:26
  376.3 12.0 %convolution_convert_fusion = bf16[4096,256]{1,0:T(8,128)(2,1)} fusion(bf16[4096,2048]{1,0:T(8,128)(2,1)} %bitcast.136, bf16[2048,256]{1,0:T(8,128)(2,1)} %all-gather.9.cloned.1.call-done), kind=kOutput, calls=%fused_computation.25 | convolution fusion | flops 4296015872 | bytes 19922944 | tf_op jit(solution)/shard_map/dot_general | solution.py:26
  388.4 5.9 convolution_convert_fusion.4
  394.3 15.9 %fusion.26 = f32[2048,2048]{1,0:T(8,128)} fusion(bf16[2048,1024]{1,0:T(8,128)(2,1)} %all-gather.11.cloned.1.call-done, bf16[4096,1024]{1,0:T(8,128)(2,1)} %get-tuple-element.108), kind=kOutput, calls=%fused_computation.52 | convolution fusion | flops 8589934592 | bytes 25165824 | tf_op jit(solution)/shard_map/dot_general | solution.py:26
  410.2 11.6 %add_convert_fusion.1 = bf16[2048,2048]{1,0:T(8,128)(2,1)} fusion(f32[2048,2048]{1,0:T(8,128)} %fusion.26, bf16[2048,256]{1,0:T(8,128)(2,1)S(1)} %copy-done.14, bf16[4096,256]{1,0:T(8,128)(2,1)S(1)} %bitcast.116), kind=kOutput, calls=%fused_computation.9 | convolution fusion | flops 2155872256 | bytes 27262976 | tf_op jit(solution)/shard_map/dot_general | solution.py:26
  422.2 4.2 multiply_convert_fusion.3
  426.4 2.8 multiply_convert_fusion.2
  429.3 15.6 %fusion.24 = f32[2048,2048]{1,0:T(8,128)} fusion(bf16[2048,1024]{1,0:T(8,128)(2,1)} %all-gather.11.cloned.1.call-done, bf16[4096,1024]{1,0:T(8,128)(2,1)} %get-tuple-element.108), kind=kOutput, calls=%fused_computation.50 | convolution fusion | flops 8589934592 | bytes 25165824 | tf_op jit(solution)/shard_map/dot_general | solution.py:26
  444.9 11.7 %add_convert_fusion = bf16[2048,2048]{1,0:T(8,128)(2,1)} fusion(f32[2048,2048]{1,0:T(8,128)} %fusion.24, bf16[2048,256]{1,0:T(8,128)(2,1)S(1)} %copy-done.14, bf16[4096,256]{1,0:T(8,128)(2,1)S(1)} %bitcast.117), kind=kOutput, calls=%fused_computation.8 | convolution fusion | flops 2155872256 | bytes 27262976 | tf_op jit(solution)/shard_map/dot_general | solution.py:26
  456.6 10.1 %fusion.37 = (bf16[2,256,2048]{2,1,0:T(8,128)(2,1)}, bf16[2,256,2048]{2,1,0:T(8,128)(2,1)}, bf16[2,256,2048]{2,1,0:T(8,128)(2,1)}, f32[2,256,2048]{2,1,0:T(8,128)}) fusion(bf16[4,2,256,2048]{3,2,1,0:T(8,128)(2,1)} %collective-permute-done.8, bf16[4,2,256,2048]{3,2,1,0:T(8,128)(2,1)} %bitcast.110), kind=kLoop, calls=%fused_computation.72 | loop fusion | flops 15728640 | bytes 27262976 | tf_op jit(solution)/shard_map/convert_element_type | solution.py:449
  468.2 27.2 %attend_back.1 = bf16[2,2,2,2,256,768]{5,4,3,2,1,0:T(8,128)(2,1)} custom-call(bf16[4,1024,256]{2,1,0:T(8,128)(2,1)} %get-tuple-element.115.q_ref, bf16[4,1024,256]{2,1,0:T(8,128)(2,1)} %get-tuple-element.116.k_ref, bf16[4,1024,256]{2,1,0:T(8,128)(2,1)} %get-tuple-element.117.v_ref, bf16[4,1024,256]{2,1,0:T(8,128)(2,1)} %bitcast.130, ...), custom_call_target="tpu_custom_call" | custom-call | flops 10737418240 | bytes 25165824 | tf_op jit(solution)/shard_map/attend_back/pallas_call | solution.py:605
  495.4 20.4 %convolution_convert_fusion.3 = bf16[2048,768]{1,0:T(8,128)(2,1)} fusion(bf16[4096,2048]{1,0:T(8,128)(2,1)} %bitcast.149, bf16[4096,768]{1,0:T(8,128)(2,1)} %bitcast.118), kind=kOutput, calls=%fused_computation.56 | convolution fusion | flops 12886474752 | bytes 26214400 | tf_op jit(solution)/shard_map/dot_general | solution.py:26
  515.8 22.8 %multiply_convert_fusion = bf16[4096,1024]{1,0:T(8,128)(2,1)S(1)} fusion(bf16[4096,1024]{1,0:T(8,128)(2,1)} %get-tuple-element.122, bf16[4096,2048]{1,0:T(8,128)(2,1)} %bitcast.137, bf16[2048,1024]{1,0:T(8,128)(2,1)} %all-gather.11.cloned.1.call-done), kind=kOutput, calls=%fused_computation.7 | convolution fusion | flops 17192452096 | bytes 37748736 | tf_op jit(solution)/shard_map/dot_general | solution.py:26
  538.6 3.3 copy-done.6
  541.9 21.9 %convolution_convert_fusion.1 = bf16[2048,1024]{1,0:T(8,128)(2,1)} fusion(bf16[4096,2048]{1,0:T(8,128)(2,1)} %bitcast.150, bf16[4096,1024]{1,0:T(8,128)(2,1)S(1)} %multiply_convert_fusion), kind=kOutput, calls=%fused_computation.54 | convolution fusion | flops 17181966336 | bytes 29360128 | tf_op jit(solution)/shard_map/dot_general | solution.py:26
  563.8 16.7 %shard_map.255 = (bf16[64,8192]{1,0:T(8,128)(2,1)}, bf16[64,2048]{1,0:T(8,128)(2,1)}) custom-call(bf16[512,1024]{1,0:T(8,128)(2,1)} %reduce-scatter.5.cloned.1.call-done.refs_0_, bf16[512,256]{1,0:T(8,128)(2,1)} %reduce-scatter.7.cloned.1.call-done.refs_1_), custom_call_target="tpu_custom_call" | custom-call | flops 11900000256 | bytes 1048576 | tf_op jit(solution)/shard_map/pallas_call | solution.py:344
  580.5 7.1 fusion.22
  587.7 7.1 add_convert_fusion.5
  596.0 10.9 %fusion.20 = f32[2048,1024]{1,0:T(8,128)} fusion(bf16[4096,1024]{1,0:T(8,128)(2,1)} %copy-done.6, bf16[2048,1024]{1,0:T(8,128)(2,1)} %multiply_convert_fusion.2), kind=kOutput, calls=%fused_computation.42 | convolution fusion | flops 4294967296 | bytes 14680064 | tf_op jit(solution)/shard_map/dot_general | solution.py:26
  606.9 7.2 add_convert_fusion.4
  614.2 6.2 fusion.51
  620.5 7.1 fusion.18
  627.6 7.5 add_convert_fusion.3
  638.6 7.0 fusion.16
  645.6 6.0 add_convert_fusion.2
  651.8 6.1 fusion.54
  662.6 22.5 %collective-permute-done.14 = bf16[2,256,1024]{2,1,0:T(8,128)(2,1)} collective-permute-done((bf16[2,256,1024]{2,1,0:T(8,128)(2,1)}, bf16[2,256,1024]{2,1,0:T(8,128)(2,1)}, u32[]{:S(2)}, u32[]{:S(2)}) %collective-permute-start.14) | collective-permute-done | bytes 1048608 | tf_op jit(solution)/shard_map/ppermute | solution.py:457
  686.7 19.8 %collective-permute-done.17 = bf16[2,256,1024]{2,1,0:T(8,128)(2,1)} collective-permute-done((bf16[2,256,1024]{2,1,0:T(8,128)(2,1)}, bf16[2,256,1024]{2,1,0:T(8,128)(2,1)}, u32[]{:S(2)}, u32[]{:S(2)}) %collective-permute-start.17) | collective-permute-done | bytes 1048608 | tf_op jit(solution)/shard_map/ppermute | solution.py:457
  708.6 4.7 convert_reduce_fusion
  716.5 2.4 fusion.63
  718.9 100.5 %collective-permute-done.18 = bf16[2,256,1024]{2,1,0:T(8,128)(2,1)S(1)} collective-permute-done((bf16[2,256,1024]{2,1,0:T(8,128)(2,1)}, bf16[2,256,1024]{2,1,0:T(8,128)(2,1)S(1)}, u32[]{:S(2)}, u32[]{:S(2)}) %collective-permute-start.18) | collective-permute-done | bytes 1048608 | tf_op jit(solution)/shard_map/ppermute | solution.py:457
  824.4 5.3 convert_reduce_fusion.3
  830.4 29.4 %shard_map.256 = (f32[32,32,128]{2,1,0:T(8,128)}, bf16[64,8192]{1,0:T(8,128)(2,1)}, bf16[64,6144]{1,0:T(8,128)(2,1)}) custom-call(f32[32,128]{1,0:T(8,128)} %fusion.58.refs_0_, bf16[512,1024]{1,0:T(8,128)(2,1)} %reduce-scatter.9.cloned.1.call-done.refs_1_, bf16[512,768]{1,0:T(8,128)(2,1)} %reduce-scatter.11.cloned.1.call-done.refs_2_), custom_call_target="tpu_custom_call" | custom-call | flops 17500000256 | bytes 1048576 | tf_op jit(solution)/shard_map/pallas_call | solution.py:171
  862.6 3.6 fusion.42
  866.2 2.6 fusion.32
  (230 shorter events, 50.4 us)
Async XLA Ops:
  7.2 252.3 %all-gather.5.cloned.1.call-start = ((), (), s32[]{:S(2)}) async-start(), calls=%async_computation.4 | async-start | bytes 5242880 | tf_op jit(solution)/shard_map/all_gather | solution.py:482
  13.2 34.0 %copy-start = (bf16[2,256,2048]{2,1,0:T(8,128)(2,1)S(1)}, bf16[2,256,2048]{2,1,0:T(8,128)(2,1)}, u32[]{:S(2)}) copy-start(bf16[2,256,2048]{2,1,0:T(8,128)(2,1)} %refs_0_.1) | copy-start | bytes 6291460
  13.2 34.0 %copy-start.1 = (bf16[64,8192]{1,0:T(8,128)(2,1)S(1)}, bf16[64,8192]{1,0:T(8,128)(2,1)}, u32[]{:S(2)}) copy-start(bf16[64,8192]{1,0:T(8,128)(2,1)} %refs_3_.1) | copy-start | bytes 3145732
  13.2 34.0 %copy-start.2 = (bf16[64,2048]{1,0:T(8,128)(2,1)S(1)}, bf16[64,2048]{1,0:T(8,128)(2,1)}, u32[]{:S(2)}) copy-start(bf16[64,2048]{1,0:T(8,128)(2,1)} %refs_2_.3) | copy-start | bytes 786436
  43.5 244.6 %all-gather.7.cloned.1.call-start = ((), (), s32[]{:S(2)}) async-start(), calls=%async_computation.5 | async-start | bytes 3932160 | tf_op jit(solution)/shard_map/all_gather | solution.py:482
  44.2 332.1 %all-gather.9.cloned.1.call-start = ((), (), s32[]{:S(2)}) async-start(), calls=%async_computation.6 | async-start | bytes 1310720 | tf_op jit(solution)/shard_map/all_gather | solution.py:482
  47.2 107.0 %copy-start.34 = (s32[2,1024]{1,0:T(2,128)S(1)}, s32[2,1024]{1,0:T(2,128)}, u32[]{:S(2)}) copy-start(s32[2,1024]{1,0:T(2,128)} %param.16) | copy-start | bytes 24580
  150.7 243.6 %all-gather.11.cloned.1.call-start = ((), (), s32[]{:S(2)}) async-start(), calls=%async_computation.7 | async-start | bytes 5242880 | tf_op jit(solution)/shard_map/all_gather | solution.py:482
  150.7 185.6 %collective-permute-start.2 = (bf16[2,256,2048]{2,1,0:T(8,128)(2,1)}, bf16[2,256,2048]{2,1,0:T(8,128)(2,1)}, u32[]{:S(2)}, u32[]{:S(2)}) collective-permute-start(bf16[2,256,2048]{2,1,0:T(8,128)(2,1)} %param.17), channel_id=1, source_target_pairs={{0,6},{1,7},{2,4},{3,5},{4,2},{5,3},{6,0},{7,1},{8,14},{9,15},{10,... | collective-permute-start | bytes 6291464 | tf_op jit(solution)/shard_map/ppermute | solution.py:439
  152.3 184.0 %collective-permute-start.1 = (bf16[2,256,2048]{2,1,0:T(8,128)(2,1)}, bf16[2,256,2048]{2,1,0:T(8,128)(2,1)}, u32[]{:S(2)}, u32[]{:S(2)}) collective-permute-start(bf16[2,256,2048]{2,1,0:T(8,128)(2,1)} %param.17), channel_id=1, source_target_pairs={{0,4},{1,5},{2,6},{3,7},{4,0},{5,1},{6,2},{7,3},{8,12},{9,13},{10,... | collective-permute-start | bytes 6291464 | tf_op jit(solution)/shard_map/ppermute | solution.py:439
  153.1 183.2 %collective-permute-start = (bf16[2,256,2048]{2,1,0:T(8,128)(2,1)}, bf16[2,256,2048]{2,1,0:T(8,128)(2,1)}, u32[]{:S(2)}, u32[]{:S(2)}) collective-permute-start(bf16[2,256,2048]{2,1,0:T(8,128)(2,1)} %param.17), channel_id=1, source_target_pairs={{0,2},{1,3},{2,0},{3,1},{4,6},{5,7},{6,4},{7,5},{8,10},{9,11},{10,... | collective-permute-start | bytes 6291464 | tf_op jit(solution)/shard_map/ppermute | solution.py:439
  154.3 89.8 %collective-permute-start.3 = (s32[2,1024]{1,0:T(2,128)S(1)}, s32[2,1024]{1,0:T(2,128)S(1)}, u32[]{:S(2)}, u32[]{:S(2)}) collective-permute-start(s32[2,1024]{1,0:T(2,128)S(1)} %copy-done.34), channel_id=1, source_target_pairs={{0,4},{4,0},{1,5},{5,1},{2,6},{6,2},{3,7},{7,3},{8,12},{12,8},{9,1... | collective-permute-start | bytes 24584 | tf_op jit(solution)/shard_map/ppermute | solution.py:514
  155.1 408.6 %reduce-scatter.7.cloned.1.call-start = ((), (), s32[]{:S(2)}) async-start(), calls=%async_computation.9 | async-start | bytes 1310720 | tf_op jit(solution)/shard_map/reduce_scatter | solution.py:572
  336.3 6.4 collective-permute-start.4
  336.5 7.1 collective-permute-start.5
  336.9 9.6 %collective-permute-start.6 = (bf16[2,256,2048]{2,1,0:T(8,128)(2,1)}, bf16[2,256,2048]{2,1,0:T(8,128)(2,1)S(1)}, u32[]{:S(2)}, u32[]{:S(2)}) collective-permute-start(bf16[2,256,2048]{2,1,0:T(8,128)(2,1)} %collective-permute-done.1), channel_id=1, source_target_pairs={{0,1},{1,0},{2,3},{3,2},{4,5},{5,4},{6,7},{7,6},{8,9},{9,8},{10,11... | collective-permute-start | bytes 6291464 | tf_op jit(solution)/shard_map/ppermute | solution.py:442
  337.0 12.6 %collective-permute-start.7 = (bf16[2,256,2048]{2,1,0:T(8,128)(2,1)}, bf16[2,256,2048]{2,1,0:T(8,128)(2,1)S(1)}, u32[]{:S(2)}, u32[]{:S(2)}) collective-permute-start(bf16[2,256,2048]{2,1,0:T(8,128)(2,1)} %collective-permute-done.2), channel_id=1, source_target_pairs={{0,1},{1,0},{2,3},{3,2},{4,5},{5,4},{6,7},{7,6},{8,9},{9,8},{10,11... | collective-permute-start | bytes 6291464 | tf_op jit(solution)/shard_map/ppermute | solution.py:442
  342.8 12.7 %slice-start.6 = ((s8[8388608]{0:T(1024)(128)(4,1)}), s8[4194304]{0:T(1024)(128)(4,1)S(1)}, s32[]{:S(2)}) async-start(s8[8388608]{0:T(1024)(128)(4,1)} %bitcast.153), calls=%async_computation.18 | async-start | bytes 8388608
  376.3 12.1 %copy-start.9 = (bf16[2,2,2,2,256,256]{5,4,1,3,0,2:T(8,128)(2,1)S(1)}, bf16[2,2,2,2,256,256]{5,4,1,3,0,2:T(8,128)(2,1)}, u32[]{:S(2)}) copy-start(bf16[2,2,2,2,256,256]{5,4,1,3,0,2:T(8,128)(2,1)} %copy.35) | copy-start | bytes 6291460
  376.3 12.1 %copy-start.27 = (bf16[8,2,256,2048]{3,2,1,0:T(8,128)(2,1)S(1)}, bf16[8,2,256,2048]{3,2,1,0:T(8,128)(2,1)}, u32[]{:S(2)}) copy-start(bf16[8,2,256,2048]{3,2,1,0:T(8,128)(2,1)} %copy-done.26) | copy-start | bytes 50331652
  394.3 15.9 %copy-start.14 = (bf16[2048,256]{1,0:T(8,128)(2,1)S(1)}, bf16[2048,256]{1,0:T(8,128)(2,1)}, u32[]{:S(2)}) copy-start(bf16[2048,256]{1,0:T(8,128)(2,1)} %all-gather.9.cloned.1.call-done) | copy-start | bytes 3145732
  394.3 15.9 %copy-start.10 = (bf16[2,2,2,2,256,256]{5,4,1,3,0,2:T(8,128)(2,1)S(1)}, bf16[2,2,2,2,256,256]{5,4,1,3,0,2:T(8,128)(2,1)}, u32[]{:S(2)}) copy-start(bf16[2,2,2,2,256,256]{5,4,1,3,0,2:T(8,128)(2,1)} %copy.35) | copy-start | bytes 6291460
  410.2 11.9 %copy-start.29 = (f32[32,64]{1,0:T(8,128)S(1)}, f32[32,64]{1,0:T(8,128)}, u32[]{:S(2)}) copy-start(f32[32,64]{1,0:T(8,128)} %copy-done.28) | copy-start | bytes 24580
  421.8 34.8 %collective-permute-start.8 = (bf16[4,2,256,2048]{3,2,1,0:T(8,128)(2,1)}, bf16[4,2,256,2048]{3,2,1,0:T(8,128)(2,1)}, u32[]{:S(2)}, u32[]{:S(2)}) collective-permute-start(bf16[4,2,256,2048]{3,2,1,0:T(8,128)(2,1)} %bitcast.114), channel_id=1, source_target_pairs={{0,1},{1,0},{2,3},{3,2},{4,5},{5,4},{6,7},{7,6},{8,9},{9,8},{10,11... | collective-permute-start | bytes 25165832 | tf_op jit(solution)/shard_map/ppermute | solution.py:446
  422.0 141.8 %reduce-scatter.5.cloned.1.call-start = ((), (), s32[]{:S(2)}) async-start(), calls=%async_computation.8 | async-start | bytes 5242880 | tf_op jit(solution)/shard_map/reduce_scatter | solution.py:572
  429.2 401.2 %reduce-scatter.11.cloned.1.call-start = ((), (), s32[]{:S(2)}) async-start(), calls=%async_computation.11 | async-start | bytes 3932160 | tf_op jit(solution)/shard_map/reduce_scatter | solution.py:572
  429.3 15.6 %copy-start.11 = (bf16[2,2,2,2,256,256]{5,4,1,3,0,2:T(8,128)(2,1)S(1)}, bf16[2,2,2,2,256,256]{5,4,1,3,0,2:T(8,128)(2,1)}, u32[]{:S(2)}) copy-start(bf16[2,2,2,2,256,256]{5,4,1,3,0,2:T(8,128)(2,1)} %copy.35) | copy-start | bytes 6291460
  594.8 19.4 %collective-permute-start.12 = (bf16[4,2,256,1024]{3,2,1,0:T(8,128)(2,1)}, bf16[4,2,256,1024]{3,2,1,0:T(8,128)(2,1)}, u32[]{:S(2)}, u32[]{:S(2)}) collective-permute-start(bf16[4,2,256,1024]{3,2,1,0:T(8,128)(2,1)} %bitcast.31), channel_id=1, source_target_pairs={{0,1},{1,0},{2,3},{3,2},{4,5},{5,4},{6,7},{7,6},{8,9},{9,8},{10,11... | collective-permute-start | bytes 12582920 | tf_op jit(solution)/shard_map/ppermute | solution.py:446
  595.9 234.4 %reduce-scatter.9.cloned.1.call-start = ((), (), s32[]{:S(2)}) async-start(), calls=%async_computation.10 | async-start | bytes 5242880 | tf_op jit(solution)/shard_map/reduce_scatter | solution.py:572
  596.0 24.4 %slice-start = ((s8[8388608]{0:T(1024)(128)(4,1)}), s8[4194304]{0:T(1024)(128)(4,1)S(1)}, s32[]{:S(2)}) async-start(s8[8388608]{0:T(1024)(128)(4,1)} %bitcast.112), calls=%async_computation.12 | async-start | bytes 8388608
  606.9 13.5 %slice-start.1 = ((s8[8388608]{0:T(1024)(128)(4,1)}), s8[4194304]{0:T(1024)(128)(4,1)S(1)}, s32[]{:S(2)}) async-start(s8[8388608]{0:T(1024)(128)(4,1)} %bitcast.112), calls=%async_computation.13 | async-start | bytes 8388608
  614.2 13.4 %slice-start.2 = ((s8[6291456]{0:T(1024)(128)(4,1)}), s8[4194304]{0:T(1024)(128)(4,1)S(1)}, s32[]{:S(2)}) async-start(s8[6291456]{0:T(1024)(128)(4,1)} %bitcast.122), calls=%async_computation.14 | async-start | bytes 8388608
  635.1 16.6 %collective-permute-start.16 = (bf16[4,2,256,1024]{3,2,1,0:T(8,128)(2,1)}, bf16[4,2,256,1024]{3,2,1,0:T(8,128)(2,1)}, u32[]{:S(2)}, u32[]{:S(2)}) collective-permute-start(bf16[4,2,256,1024]{3,2,1,0:T(8,128)(2,1)} %bitcast.37), channel_id=1, source_target_pairs={{0,1},{1,0},{2,3},{3,2},{4,5},{5,4},{6,7},{7,6},{8,9},{9,8},{10,11... | collective-permute-start | bytes 12582920 | tf_op jit(solution)/shard_map/ppermute | solution.py:446
  635.1 26.3 %collective-permute-start.13 = (bf16[2,256,1024]{2,1,0:T(8,128)(2,1)}, bf16[2,256,1024]{2,1,0:T(8,128)(2,1)S(1)}, u32[]{:S(2)}, u32[]{:S(2)}) collective-permute-start(bf16[2,256,1024]{2,1,0:T(8,128)(2,1)} %get-tuple-element.140), channel_id=1, source_target_pairs={{0,2},{1,3},{2,0},{3,1},{4,6},{5,7},{6,4},{7,5},{8,10},{9,11},{10,... | collective-permute-start | bytes 3145736 | tf_op jit(solution)/shard_map/ppermute | solution.py:457
  636.6 48.5 %collective-permute-start.14 = (bf16[2,256,1024]{2,1,0:T(8,128)(2,1)}, bf16[2,256,1024]{2,1,0:T(8,128)(2,1)}, u32[]{:S(2)}, u32[]{:S(2)}) collective-permute-start(bf16[2,256,1024]{2,1,0:T(8,128)(2,1)} %get-tuple-element.141), channel_id=1, source_target_pairs={{0,4},{1,5},{2,6},{3,7},{4,0},{5,1},{6,2},{7,3},{8,12},{9,13},{10,... | collective-permute-start | bytes 3145736 | tf_op jit(solution)/shard_map/ppermute | solution.py:457
  637.8 47.3 %collective-permute-start.15 = (bf16[2,256,1024]{2,1,0:T(8,128)(2,1)}, bf16[2,256,1024]{2,1,0:T(8,128)(2,1)}, u32[]{:S(2)}, u32[]{:S(2)}) collective-permute-start(bf16[2,256,1024]{2,1,0:T(8,128)(2,1)} %get-tuple-element.142), channel_id=1, source_target_pairs={{0,6},{1,7},{2,4},{3,5},{4,2},{5,3},{6,0},{7,1},{8,14},{9,15},{10,... | collective-permute-start | bytes 3145736 | tf_op jit(solution)/shard_map/ppermute | solution.py:457
  657.9 48.6 %collective-permute-start.17 = (bf16[2,256,1024]{2,1,0:T(8,128)(2,1)}, bf16[2,256,1024]{2,1,0:T(8,128)(2,1)}, u32[]{:S(2)}, u32[]{:S(2)}) collective-permute-start(bf16[2,256,1024]{2,1,0:T(8,128)(2,1)} %get-tuple-element.154), channel_id=1, source_target_pairs={{0,2},{1,3},{2,0},{3,1},{4,6},{5,7},{6,4},{7,5},{8,10},{9,11},{10,... | collective-permute-start | bytes 3145736 | tf_op jit(solution)/shard_map/ppermute | solution.py:457
  659.5 25.6 %copy-start.19 = (bf16[2,256,2048]{2,1,0:T(8,128)(2,1)S(1)}, bf16[2,256,2048]{2,1,0:T(8,128)(2,1)}, u32[]{:S(2)}) copy-start(bf16[2,256,2048]{2,1,0:T(8,128)(2,1)} %get-tuple-element.114) | copy-start | bytes 6291460
  660.6 55.0 %slice-start.4 = ((s8[6291456]{0:T(1024)(128)(4,1)}), s8[4194304]{0:T(1024)(128)(4,1)S(1)}, s32[]{:S(2)}) async-start(s8[6291456]{0:T(1024)(128)(4,1)} %bitcast.125), calls=%async_computation.16 | async-start | bytes 8388608
  660.6 52.7 %copy-start.25 = (bf16[64,2048]{1,0:T(8,128)(2,1)S(1)}, bf16[64,2048]{1,0:T(8,128)(2,1)}, u32[]{:S(2)}) copy-start(bf16[64,2048]{1,0:T(8,128)(2,1)} %get-tuple-element.128) | copy-start | bytes 786436
  660.6 53.5 %copy-start.21 = (bf16[64,8192]{1,0:T(8,128)(2,1)S(1)}, bf16[64,8192]{1,0:T(8,128)(2,1)}, u32[]{:S(2)}) copy-start(bf16[64,8192]{1,0:T(8,128)(2,1)} %get-tuple-element.127) | copy-start | bytes 3145732
  660.6 54.9 %slice-start.5 = ((s8[6291456]{0:T(1024)(128)(4,1)}), s8[2097152]{0:T(1024)(128)(4,1)S(1)}, s32[]{:S(2)}) async-start(s8[6291456]{0:T(1024)(128)(4,1)} %bitcast.125), calls=%async_computation.17 | async-start | bytes 4194304
  660.6 161.8 %collective-permute-start.9 = (bf16[2,256,2048]{2,1,0:T(8,128)(2,1)}, bf16[2,256,2048]{2,1,0:T(8,128)(2,1)S(1)}, u32[]{:S(2)}, u32[]{:S(2)}) collective-permute-start(bf16[2,256,2048]{2,1,0:T(8,128)(2,1)} %get-tuple-element.112), channel_id=1, source_target_pairs={{0,2},{1,3},{2,0},{3,1},{4,6},{5,7},{6,4},{7,5},{8,10},{9,11},{10,... | collective-permute-start | bytes 6291464 | tf_op jit(solution)/shard_map/ppermute | solution.py:457
  661.4 161.1 %collective-permute-start.10 = (bf16[2,256,2048]{2,1,0:T(8,128)(2,1)S(1)}, bf16[2,256,2048]{2,1,0:T(8,128)(2,1)S(1)}, u32[]{:S(2)}, u32[]{:S(2)}) collective-permute-start(bf16[2,256,2048]{2,1,0:T(8,128)(2,1)S(1)} %copy-done.20), channel_id=1, source_target_pairs={{0,4},{1,5},{2,6},{3,7},{4,0},{5,1},{6,2},{7,3},{8,12},{9,13},{10,... | collective-permute-start | bytes 6291464 | tf_op jit(solution)/shard_map/ppermute | solution.py:457
  685.1 137.4 %collective-permute-start.11 = (bf16[2,256,2048]{2,1,0:T(8,128)(2,1)S(1)}, bf16[2,256,2048]{2,1,0:T(8,128)(2,1)S(1)}, u32[]{:S(2)}, u32[]{:S(2)}) collective-permute-start(bf16[2,256,2048]{2,1,0:T(8,128)(2,1)S(1)} %copy-done.19), channel_id=1, source_target_pairs={{0,6},{1,7},{2,4},{3,5},{4,2},{5,3},{6,0},{7,1},{8,14},{9,15},{10,... | collective-permute-start | bytes 6291464 | tf_op jit(solution)/shard_map/ppermute | solution.py:457
  685.1 134.3 %collective-permute-start.18 = (bf16[2,256,1024]{2,1,0:T(8,128)(2,1)}, bf16[2,256,1024]{2,1,0:T(8,128)(2,1)S(1)}, u32[]{:S(2)}, u32[]{:S(2)}) collective-permute-start(bf16[2,256,1024]{2,1,0:T(8,128)(2,1)} %get-tuple-element.155), channel_id=1, source_target_pairs={{0,4},{1,5},{2,6},{3,7},{4,0},{5,1},{6,2},{7,3},{8,12},{9,13},{10,... | collective-permute-start | bytes 3145736 | tf_op jit(solution)/shard_map/ppermute | solution.py:457
  706.5 112.9 %collective-permute-start.19 = (bf16[2,256,1024]{2,1,0:T(8,128)(2,1)}, bf16[2,256,1024]{2,1,0:T(8,128)(2,1)}, u32[]{:S(2)}, u32[]{:S(2)}) collective-permute-start(bf16[2,256,1024]{2,1,0:T(8,128)(2,1)} %get-tuple-element.156), channel_id=1, source_target_pairs={{0,6},{1,7},{2,4},{3,5},{4,2},{5,3},{6,0},{7,1},{8,14},{9,15},{10,... | collective-permute-start | bytes 3145736 | tf_op jit(solution)/shard_map/ppermute | solution.py:457
  716.5 102.9 %copy-start.8 = (f32[2,256,1024]{2,1,0:T(8,128)S(1)}, f32[2,256,1024]{2,1,0:T(8,128)}, u32[]{:S(2)}) copy-start(f32[2,256,1024]{2,1,0:T(8,128)} %get-tuple-element.153) | copy-start | bytes 6291460
  (28 other events, 170.0 us)
Sparse Core Ops, SparseCore 0:
  43.6 79.8 all-gather.4
  125.0 61.9 all-gather.6
  188.6 26.6 all-gather.8
  216.7 80.1 all-gather.10
  422.1 25.1 reduce-scatter.6
  449.4 75.2 reduce-scatter.4
  596.1 59.0 reduce-scatter.10
  657.5 76.6 reduce-scatter.8

commit v2 on v1

--- a/solution.py
+++ b/solution.py
@@ -356,6 +356,92 @@
     )(*sums)
 
 
+def pair_kernel(lay, first_ref, first_w, second_ref, second_w, *refs):
+    step = pl.program_id(0)
+    chips = lay.group // 2
+    outs, (given, came, send, recv, out_sem) = refs[:chips], refs[chips:]
+    zo, yi, s = lax.axis_index("zo"), lax.axis_index("yi"), lax.axis_index("seq")
+    partner = (zo, yi, (s // 2) * 2 + 1 - lax.rem(s, 2))
+
+    def copy(j):
+        return remote(given.at[j], came.at[j], send.at[j], recv.at[j], partner)
+
+    def store(j):
+        return pltpu.make_async_copy(came.at[j], outs[(j + 1) % chips], out_sem.at[j])
+
+    @pl.when(step == 0)
+    def _():
+        barrier = pltpu.get_barrier_semaphore()
+        pl.semaphore_signal(barrier, inc=1, device_id=partner, device_id_type=MESH)
+        pl.semaphore_wait(barrier, 1)
+
+    for j in range(chips):
+
+        @pl.when(step == j + 1)
+        def _():
+            copy(j).start()
+
+    total = dot(first_ref[0, 0], first_w[...], ((1,), (1,))) + dot(second_ref[0, 0], second_w[...], ((1,), (1,)))
+    for j in range(chips):
+
+        @pl.when(step == j)
+        def _():
+            given[j] = total.astype(BF16)
+
+        @pl.when(step == chips + j)
+        def _():
+            copy(j).wait_recv()
+            came[j] = (total + came[j].astype(F32)).astype(BF16)
+
+    for j in range(chips - 1):
+
+        @pl.when(step == chips + j + 1)
+        def _():
+            store(j).start()
+
+    @pl.when(step == 2 * chips - 1)
+    def _():
+        store(chips - 1).start()
+        for j in range(chips):
+            copy(j).wait_send()
+            store(j).wait()
+
+
+def pair_matmul(lay, first, first_w, second, second_w, cut, number):
+    chips = lay.group // 2
+    rows = first.shape[0] // lay.group
+    width = first_w.shape[0] // cut[1]
+    depth1, depth2 = first.shape[1], second.shape[1]
+
+    def act(depth):
+        return pl.BlockSpec((1, 1, rows, depth), lambda i: (1 - i // chips, (i + 1) % chips, 0, 0))
+
+    def weight(depth):
+        return pl.BlockSpec((width, depth), lambda i: (cut[0], 0), pipeline_mode=pl.Buffered(1))
+
+    shape = lambda v: v.reshape(2, chips, rows, v.shape[1])
+    return pl.pallas_call(
+        functools.partial(pair_kernel, lay),
+        grid=(2 * chips,),
+        in_specs=[act(depth1), weight(depth1), act(depth2), weight(depth2)],
+        out_specs=[ANY] * chips,
+        out_shape=[jax.ShapeDtypeStruct((rows, width), BF16)] * chips,
+        scratch_shapes=[
+            pltpu.VMEM((chips, rows, width), BF16),
+            pltpu.VMEM((chips, rows, width), BF16),
+            pltpu.SemaphoreType.DMA((chips,)),
+            pltpu.SemaphoreType.DMA((chips,)),
+            pltpu.SemaphoreType.DMA((chips,)),
+        ],
+        compiler_params=pltpu.CompilerParams(
+            collective_id=number, has_side_effects=True, vmem_limit_bytes=60 << 20
+        ),
+        cost_estimate=pl.CostEstimate(
+            flops=2 * first.shape[0] * (depth1 + depth2) * width, bytes_accessed=32 << 20, transcendentals=0
+        ),
+    )(shape(first), first_w, shape(second), second_w)
+
+
 def turn_pairs(field, cosine, sine):
     halves = ROTARY // 2
     front = field[:, :128]
@@ -442,20 +528,17 @@
         partner = [lax.ppermute(piece, "seq", lay.flip()) for piece in near]
         return jnp.concatenate([piece[None] for piece in near + partner], 0)
 
-    def reduce_near(kept, given):
-        came = lax.ppermute(given, "seq", lay.flip())
-        came, kept = lax.optimization_barrier((came, kept))
-        return [
-            (kept[i].astype(F32) + came[i].astype(F32)).astype(BF16) if o != (0, 0) else kept[i].astype(F32) + came[i].astype(F32)
-            for i, o in enumerate(lay.offsets)
-        ]
-
-    def reduce_far(pieces):
-        total = pieces[0]
+    def send_far(pieces):
+        came = [pieces[0]]
         for o, piece in zip(lay.offsets[1:], pieces[1:], strict=True):
             back = ((-o[0]) % sub, (-o[1]) % chips_x)
-            came = lax.ppermute(piece, GROUP, lay.shift(*back))
-            total = total + came.astype(F32)
+            came.append(lax.ppermute(piece, GROUP, lay.shift(*back)))
+        return came
+
+    def add_all(pieces):
+        total = pieces[0].astype(F32)
+        for piece in pieces[1:]:
+            total = total + piece.astype(F32)
         return total
 
     def after(value, *tokens):
@@ -481,10 +564,21 @@
         def gather_rows(mine):
             return lax.all_gather(mine, "zo", axis=0, tiled=True)
 
+        x, core = my_seq // 2, my_seq % 2
+        places = []
+        for ry in range(sub):
+            from_there = positions
+            if ry:
+                from_there = lax.ppermute(positions, "yi", [(i, (i + ry) % sub) for i in range(sub)])
+            blocks = from_there.reshape(batch, seq, length)
+            order = [((x - rx) % chips_x) * 2 + (core + rc) % 2 for rc in range(2) for rx in range(chips_x)]
+            places.append(jnp.concatenate([lax.dynamic_slice_in_dim(blocks, o, 1, 1) for o in order], 1))
+        places = jnp.stack(places).reshape(sub * batch, count)
         names = (bias1, bias2, gain1, gain2, b_qkv, b_up, b_out, b_down)
         vec = jnp.concatenate([v.astype(F32) for v in names])
         size = -(-vec.shape[0] // 1024) * 1024
         vec = jnp.pad(vec, (0, size - vec.shape[0])).reshape(-1, 128)
+        vec, places = lax.optimization_barrier((vec, places))
         vectors, up_own, qkv_own = exchange(lay, [plans["up"], plans["qkv"]], vec, [w_up, w_qkv], False, 0, 30)
         up_w = gather_rows(up_own)
         qkv_w = gather_rows(qkv_own)
@@ -506,18 +600,16 @@
         cotangent, hat = lax.optimization_barrier((cotangent, hat))
         near_dy = gather_near(cotangent)
 
-        x, core = my_seq // 2, my_seq % 2
-        places = []
-        for ry in range(sub):
-            from_there = positions
-            if ry:
-                from_there = lax.ppermute(positions, "yi", [(i, (i + ry) % sub) for i in range(sub)])
-            blocks = from_there.reshape(batch, seq, length)
-            order = [((x - rx) % chips_x) * 2 + (core + rc) % 2 for rc in range(2) for rx in range(chips_x)]
-            places.append(jnp.concatenate([lax.dynamic_slice_in_dim(blocks, o, 1, 1) for o in order], 1))
-        places = jnp.stack(places).reshape(sub * batch, count)
+        hidden = dot(two, up_w, ((1,), (0,))) + b_up_mine
+        phi_cdf = 0.5 * (1.0 + lax.erf(hidden * math.sqrt(0.5)))
+        density = jnp.exp(-0.5 * hidden * hidden) * (1.0 / math.sqrt(2.0 * math.pi))
+        activated = (hidden * phi_cdf).astype(BF16)
+        slope = (phi_cdf + hidden * density).astype(BF16)
+        activated, slope = lax.optimization_barrier((activated, slope))
+
         halves = ROTARY // 2
         frequency = jnp.exp(jnp.arange(halves, dtype=F32) * (-2.0 * math.log(10000.0) / ROTARY))
+        places = after(places, activated)
         phases = places.astype(F32)[..., None] * frequency
         cosine, sine = jnp.cos(phases), jnp.sin(phases)
         rest = (sub * batch, count, 128 - ROTARY)
@@ -526,15 +618,8 @@
         place_col = places[:, :, None]
         place_row = places[:, None, :]
 
-        hidden = dot(two, up_w, ((1,), (0,))) + b_up_mine
-        phi_cdf = 0.5 * (1.0 + lax.erf(hidden * math.sqrt(0.5)))
-        density = jnp.exp(-0.5 * hidden * hidden) * (1.0 / math.sqrt(2.0 * math.pi))
-        activated = (hidden * phi_cdf).astype(BF16)
-        slope = (phi_cdf + hidden * density).astype(BF16)
-        activated, slope = lax.optimization_barrier((activated, slope))
-
         seqs = sub * batch
-        one = after(one, activated)
+        one = after(one, cosine, sine)
         packed = dot(one, qkv_w, ((1,), (0,))) + b_qkv_mine
         wide = (2, 1, chips_x, 1, length, 3 * cols)
         wide_spec = pl.BlockSpec(wide, lambda i: (0, i // batch, 0, i % batch, 0, 0))
@@ -584,22 +669,17 @@
         out_part = outer_dot(upstream, context)
         out_w_sum = scatter(out_part)
 
-        def two_dots(half, first, first_w, second, second_w):
-            size = total // 2
-            cut = slice(half * size, (half + 1) * size)
-            sums = dot(first[cut], first_w, ((1,), (1,))) + dot(second[cut], second_w, ((1,), (1,)))
-            return sums.astype(BF16).reshape(group // 2, batch, length, first_w.shape[0])
-
         def chain(values, *tokens):
             return lax.optimization_barrier((*values, *tokens))[: len(values)]
 
+        def tokens_of(pieces):
+            return [piece.reshape(batch, length, -1) for piece in pieces]
+
         pair = chain((context, activated), out_part)
-        given = two_dots(1, pair[0], out_w, pair[1], down_w)
-        pair = chain(pair, given)
-        kept = two_dots(0, pair[0], out_w, pair[1], down_w)
-        out_near = reduce_near(kept, given)
+        out_near = pair_matmul(lay, pair[0], out_w, pair[1], down_w, (0, 1), 4)
         grad_context, *out_near = chain((grad_context, *out_near))
-        out_sum = reduce_far(out_near)
+        out_near = tokens_of(out_near)
+        out_sum = add_all(send_far(out_near))
         output = (tokens.astype(F32) + out_sum + b_out_all + b_down_all).astype(BF16)
 
         grad_packed = pl.pallas_call(
@@ -619,32 +699,28 @@
         qkv_sum = scatter(qkv_part)
         (upstream,) = chain((upstream,), qkv_part)
         grad_hidden = (dot(upstream, down_w, ((1,), (0,))) * slope.astype(F32)).astype(BF16)
-        hat, grad_hidden = chain((hat, grad_hidden))
+
+        fold_qkv = (gain1_all[:, None] * qkv_w.astype(F32)).astype(BF16)
+        fold_up = (gain2_all[:, None] * up_w.astype(F32)).astype(BF16)
+        left = grad_packed
+        came = []
+        for k in range(2):
+            near = pair_matmul(lay, left, fold_qkv, grad_hidden, fold_up, (k, 2), 5 + k)
+            left, *near = chain((left, *near))
+            came.append(send_far(tokens_of(near)))
+
+        hat, grad_hidden = chain((hat, grad_hidden), left)
         up_part = outer_dot(hat, grad_hidden)
         up_sum = scatter(up_part)
-
         down_sum, out_w_sum = chain((down_sum, out_w_sum), up_part)
         down_raw, out_raw = deal_exchange(lay, [plans["down"], plans["out"]], [down_sum, out_w_sum], 2)
 
-        fold_qkv = (gain1_all[:, None] * qkv_w.astype(F32)).astype(BF16)
-        fold_up = (gain2_all[:, None] * up_w.astype(F32)).astype(BF16)
-        pair = chain((grad_packed, grad_hidden, fold_qkv, fold_up), down_raw, out_raw)
-        normal_sums = []
-        chunk = width // 2
-        for k in range(2):
-            cut = slice(k * chunk, (k + 1) * chunk)
-            given = two_dots(1, pair[0], pair[2][cut], pair[1], pair[3][cut])
-            pair = chain(pair, given)
-            kept = two_dots(0, pair[0], pair[2][cut], pair[1], pair[3][cut])
-            near = reduce_near(kept, given)
-            both = chain((*pair, *near))
-            pair, near = both[:4], both[4:]
-            normal_sums.append(reduce_far(near))
         inputs = tokens.astype(F32)
         center = inputs - jnp.mean(inputs, -1, keepdims=True)
         inv_std = lax.rsqrt(jnp.mean(center * center, -1, keepdims=True) + EPSILON)
         normal = center * inv_std
-        grad_normal = jnp.concatenate(normal_sums, -1)
+        came[1] = chain(came[1], down_raw, out_raw)
+        grad_normal = jnp.concatenate([add_all(pieces) for pieces in came], -1)
         token_grad = cotangent.astype(F32) + inv_std * (
             grad_normal
             - jnp.mean(grad_normal, -1, keepdims=True)

time: 883 us -> 739 us (0.84)
  waiting for transfers between devices: 237 us -> 34.6 us
  Pallas kernels: 232 us -> 417 us
  matrix products: 267 us -> 152 us
  other arithmetic: 67.4 us -> 51.6 us
    dot_general x20 -> x8, matrix products: 267 us -> 152 us  [dot(): lax.dot_general(left, right, (dims, ((), ())), preferred_element_type=F32)]
    ppermute x12 -> x9, waiting for transfers between devices: 143 us -> 27.6 us  [send_far(): came.append(lax.ppermute(piece, GROUP, lay.shift(*back)))]
    pallas_call x1, Pallas kernels: 16.7 us -> 124 us  [deal_exchange(): pl.pallas_call(functools.partial(deal_kernel, lay, plan), out_shape=swap_...]
    ppermute x1, waiting for transfers between devices: 86.5 us -> 0.01 us  [step(): lax.ppermute(positions, 'yi', [(i, (i + ry) % sub) for i in range(sub)])]
    pallas_call x0 -> x3, Pallas kernels: none -> 78 us  [pair_matmul(): pl.pallas_call(functools.partial(pair_kernel, lay), grid=(2 * chips,), in...]
    convert_element_type x3 -> x1, other arithmetic: 22.5 us -> 0.01 us  [step(): phases = places.astype(F32)[..., None] * frequency]
    unnamed x108 -> x104, local copies, waits for them, and re-layouts: 19.3 us -> 22.6 us
  transfers between devices with their start and end apart: 28 -> 25, of which waited for: 8 -> 5; matrix products, arithmetic and copies ran while one was open for 35% -> 30% of each run, Pallas kernels for 18% -> 49%
where the time goes in v2:
time: 739 us; the launch traced here: 732 us
  Pallas kernels  417 us (56%)
  matrix products  152 us (21%)
  other arithmetic  51.6 us (7%)
  local copies, waits for them, and re-layouts  44 us (6%)
  waiting for transfers between devices  34.6 us (5%)
  starting transfers between devices  18.7 us (3%)
  between operations  15.2 us (2%)
    dot_general x8, matrix products, dot(): lax.dot_general(left, right, (dims, ((), ())), preferred_element_type=F32)  152 us
    pallas_call x1, Pallas kernels, deal_exchange(): pl.pallas_call(functools.partial(deal_kernel, lay, plan), out_shape=swap_...  124 us
    pallas_call x1, Pallas kernels, norm_exchange(): pl.pallas_call(functools.partial(norm_kernel, lay, plan), out_shape=[whol...  104 us
    pallas_call x3, Pallas kernels, pair_matmul(): pl.pallas_call(functools.partial(pair_kernel, lay), grid=(2 * chips,), in...  78 us
    pallas_call x2, Pallas kernels, exchange(): pl.pallas_call(functools.partial(exchange_kernel, lay, plan, back), out_s...  58.5 us
    ppermute x9, waiting for transfers between devices, send_far(): came.append(lax.ppermute(piece, GROUP, lay.shift(*back)))  27.6 us
    pallas_call x1, Pallas kernels, step(): pl.pallas_call(functools.partial(attend_back_kernel, scaling), grid=(seqs...  27.2 us
    pallas_call x1, Pallas kernels, step(): pl.pallas_call(functools.partial(attend_kernel, scaling), grid=(seqs,), i...  25.1 us
  transfers between devices with their start and end apart: 25, of which 5 were waited for; matrix products, arithmetic and copies ran while one was open for 30% of the time, Pallas kernels for 49%

profile of v2, /device:TPU:0, one launch (start us, length us, event | category | flops | bytes accessed | tf_op | source)
XLA Modules:
  0.0 732.3 jit_solution(147117906066000560)
XLA Ops:
  7.2 3.1 collective-permute-start
  11.1 5.4 concatenate.24
  17.2 27.9 %shard_map.254 = (f32[32,8,128]{2,1,0:T(8,128)}, bf16[512,1024]{1,0:T(8,128)(2,1)}, bf16[512,768]{1,0:T(8,128)(2,1)}) custom-call(f32[8,128]{1,0:T(8,128)} %pad_bitcast_fusion.refs_0_, bf16[64,8192]{1,0:T(8,128)(2,1)} %refs_1_.1, bf16[64,6144]{1,0:T(8,128)(2,1)} %refs_2_.2), custom_call_target="tpu_custom_call" | custom-call | flops 20999999488 | bytes 1048576 | tf_op jit(solution)/shard_map/pallas_call | solution.py:171
  48.2 104.2 %norm_exchange.1 = (bf16[2,4,2,256,2048]{4,3,2,1,0:T(8,128)(2,1)}, bf16[2,4,2,256,2048]{4,3,2,1,0:T(8,128)(2,1)}, bf16[2,4,2,256,2048]{4,3,2,1,0:T(8,128)(2,1)},...) custom-call(bf16[2,256,2048]{2,1,0:T(8,128)(2,1)S(1)} %copy-done, f32[8,2048]{1,0:T(8,128)S(1)} %stack.19.refs_1_, ...), custom_call_target="tpu_custom_call" | custom-call | flops 70000001024 | bytes 1048576 | tf_op jit(solution)/shard_map/norm_exchange/pallas_call | solution.py:302
  158.3 28.7 %fusion.4 = (bf16[4096,1024]{1,0:T(8,128)(2,1)}, bf16[4096,1024]{1,0:T(8,128)(2,1)}) fusion(f32[1024]{0:T(1024)S(1)} %bitcast.126, bf16[4096,2048]{1,0:T(8,128)(2,1)} %bitcast.137, bf16[2048,1024]{1,0:T(8,128)(2,1)} %all-gather.5.cloned.1.call-done), kind=kOutput, calls=%fused_computation.5 | convolution fusion | flops 17230200832 | bytes 37752832 | tf_op jit(solution)/shard_map/dot_general | solution.py:26
  187.6 7.5 %fusion.26 = (f32[4,1024,32]{2,1,0:T(8,128)S(1)}, f32[4,1024,32]{2,1,0:T(8,128)S(1)}, f32[4,1024,32]{2,1,0:T(8,128)S(1)}) fusion(f32[32]{0:T(128)S(1)} %multiply_exponential_fusion, f32[4,1024]{1,0:T(4,128)S(1)} %convert_element_type.165), kind=kLoop, calls=%fused_computation.67 | loop fusion | flops 262144 | bytes 1589376 | tf_op jit(solution)/shard_map/neg | solution.py:617
  195.0 1.9 maximum_maximum_fusion.cos_ref
  197.0 1.9 maximum_maximum_fusion.1.sin_ref
  198.9 2.0 copy.33.col_ref
  200.9 19.5 %convolution_add_fusion = f32[4096,768]{1,0:T(8,128)} fusion(bf16[4096,2048]{1,0:T(8,128)(2,1)} %bitcast.136, bf16[2048,768]{1,0:T(8,128)(2,1)} %all-gather.7.cloned.1.call-done, f32[768]{0:T(1024)S(1)} %add.222), kind=kOutput, calls=%fused_computation.12 | convolution fusion | flops 12888047616 | bytes 32508928 | tf_op jit(solution)/shard_map/dot_general | solution.py:26
  220.4 25.1 %attend.1 = (bf16[4,1024,256]{2,1,0:T(8,128)(2,1)}, bf16[4,1024,256]{2,1,0:T(8,128)(2,1)}, bf16[4,1024,256]{2,1,0:T(8,128)(2,1)}, bf16[4,1024,256]{2,1,0:T(8,128)(2,1)}, f32[4,1,1024]{2,1,0:T(1,128)}) custom-call(f32[2,2,2,2,256,768]{5,4,3,2,1,0:T(8,128)} %bitcast.97, f32[4,1024,128]{2,1,0:T(8,128)} %maximum_maximum_fusion.cos_ref, ...), custom_call_target="tpu_custom_call" | custom-call | flops 4294967296 | bytes 31457280 | tf_op jit(solution)/shard_map/attend/pallas_call | solution.py:634
  245.5 3.3 copy.34
  250.0 1.8 bitcast_dynamic-update-slice_fusion.6
  251.8 1.7 bitcast_dynamic-update-slice_fusion.5
  253.5 1.7 bitcast_dynamic-update-slice_fusion.4
  256.2 2.8 collective-permute-done.6
  259.2 2.9 collective-permute-done.7
  262.2 5.8 copy-done.22
  267.9 20.9 %convolution_convert_fusion.2 = bf16[2048,1024]{1,0:T(8,128)(2,1)} fusion(bf16[4096,2048]{1,0:T(8,128)(2,1)S(1)} %bitcast.116, bf16[4096,1024]{1,0:T(8,128)(2,1)S(1)} %bitcast.140), kind=kOutput, calls=%fused_computation.36 | convolution fusion | flops 17181966336 | bytes 29360128 | tf_op jit(solution)/shard_map/dot_general | solution.py:26
  288.9 12.1 %convolution_convert_fusion = bf16[4096,256]{1,0:T(8,128)(2,1)} fusion(bf16[4096,2048]{1,0:T(8,128)(2,1)} %bitcast.117, bf16[2048,256]{1,0:T(8,128)(2,1)} %all-gather.9.cloned.1.call-done.first_w), kind=kOutput, calls=%fused_computation.19 | convolution fusion | flops 4296015872 | bytes 19922944 | tf_op jit(solution)/shard_map/dot_general | solution.py:26
  300.9 5.9 convolution_convert_fusion.4
  312.8 32.0 %shard_map.255 = (bf16[512,2048]{1,0:T(8,128)(2,1)}, bf16[512,2048]{1,0:T(8,128)(2,1)}, bf16[512,2048]{1,0:T(8,128)(2,1)}, bf16[512,2048]{1,0:T(8,128)(2,1)}) custom-call(bf16[2,4,512,256]{3,2,1,0:T(8,128)(2,1)} %bitcast.103, bf16[2048,256]{1,0:T(8,128)(2,1)} %all-gather.9.cloned.1.call-done.first_w, bf16[2,4,512,1024]{3,2,1,0:T(8,128)(2,1)} %bitcast.138, ...), custom_call_target="tpu_custom_call" | custom-call | flops 21474836480 | bytes 33554432 | tf_op jit(solution)/shard_map/pallas_call | solution.py:423
  344.7 1.5 copy.35
  346.3 27.2 %attend_back.1 = bf16[2,2,2,2,256,768]{5,4,3,2,1,0:T(8,128)(2,1)} custom-call(bf16[4,1024,256]{2,1,0:T(8,128)(2,1)} %get-tuple-element.114.q_ref, bf16[4,1024,256]{2,1,0:T(8,128)(2,1)} %get-tuple-element.115.k_ref, bf16[4,1024,256]{2,1,0:T(8,128)(2,1)} %get-tuple-element.116.v_ref, bf16[4,1024,256]{2,1,0:T(8,128)(2,1)} %bitcast.106, ...), custom_call_target="tpu_custom_call" | custom-call | flops 10737418240 | bytes 25165824 | tf_op jit(solution)/shard_map/attend_back/pallas_call | solution.py:685
  373.5 20.1 %convolution_convert_fusion.3 = bf16[2048,768]{1,0:T(8,128)(2,1)} fusion(bf16[4096,2048]{1,0:T(8,128)(2,1)} %bitcast.134, bf16[4096,768]{1,0:T(8,128)(2,1)} %bitcast.100), kind=kOutput, calls=%fused_computation.37 | convolution fusion | flops 12886474752 | bytes 26214400 | tf_op jit(solution)/shard_map/dot_general | solution.py:26
  393.7 22.9 %multiply_convert_fusion = bf16[4096,1024]{1,0:T(8,128)(2,1)S(1)} fusion(bf16[4096,1024]{1,0:T(8,128)(2,1)} %get-tuple-element.121, bf16[4096,2048]{1,0:T(8,128)(2,1)} %bitcast.118, bf16[2048,1024]{1,0:T(8,128)(2,1)} %all-gather.11.cloned.1.call-done.second_w), kind=kOutput, calls=%fused_computation.7 | convolution fusion | flops 17192452096 | bytes 37748736 | tf_op jit(solution)/shard_map/dot_general | solution.py:26
  416.6 3.4 copy-done.4
  419.9 21.5 %convolution_convert_fusion.1 = bf16[2048,1024]{1,0:T(8,128)(2,1)} fusion(bf16[4096,2048]{1,0:T(8,128)(2,1)} %bitcast.135, bf16[4096,1024]{1,0:T(8,128)(2,1)S(1)} %multiply_convert_fusion), kind=kOutput, calls=%fused_computation.35 | convolution fusion | flops 17181966336 | bytes 29360128 | tf_op jit(solution)/shard_map/dot_general | solution.py:26
  441.5 1.9 copy-done.8
  443.3 2.2 multiply_convert_fusion.3.first_w
  446.7 2.8 multiply_convert_fusion.2.second_w
  449.4 23.3 %shard_map.256 = (bf16[512,1024]{1,0:T(8,128)(2,1)}, bf16[512,1024]{1,0:T(8,128)(2,1)}, bf16[512,1024]{1,0:T(8,128)(2,1)}, bf16[512,1024]{1,0:T(8,128)(2,1)}) custom-call(bf16[2,4,512,768]{3,2,1,0:T(8,128)(2,1)} %bitcast.101, bf16[2048,768]{1,0:T(8,128)(2,1)} %multiply_convert_fusion.3.first_w, bf16[2,4,512,1024]{3,2,1,0:T(8,128)(2,1)} %bitcast.98, ...), custom_call_target="tpu_custom_call" | custom-call | flops 15032385536 | bytes 33554432 | tf_op jit(solution)/shard_map/pallas_call | solution.py:423
  474.8 1.6 collective-permute-start.13
  476.3 22.7 %shard_map.257 = (bf16[512,1024]{1,0:T(8,128)(2,1)}, bf16[512,1024]{1,0:T(8,128)(2,1)}, bf16[512,1024]{1,0:T(8,128)(2,1)}, bf16[512,1024]{1,0:T(8,128)(2,1)}) custom-call(bf16[2,4,512,768]{3,2,1,0:T(8,128)(2,1)} %bitcast.102, bf16[2048,768]{1,0:T(8,128)(2,1)} %multiply_convert_fusion.3.first_w, bf16[2,4,512,1024]{3,2,1,0:T(8,128)(2,1)} %bitcast.99, ...), custom_call_target="tpu_custom_call" | custom-call | flops 15032385536 | bytes 33554432 | tf_op jit(solution)/shard_map/pallas_call | solution.py:423
  499.7 3.8 convert_reduce_fusion.1
  504.9 4.6 convert_reduce_fusion
  509.5 1.6 collective-permute-start.16
  511.2 9.8 %collective-permute-done.12 = bf16[2,256,1024]{2,1,0:T(8,128)(2,1)S(1)} collective-permute-done((bf16[2,256,1024]{2,1,0:T(8,128)(2,1)}, bf16[2,256,1024]{2,1,0:T(8,128)(2,1)S(1)}, u32[]{:S(2)}, u32[]{:S(2)}) %collective-permute-start.12) | collective-permute-done | bytes 1048608 | tf_op jit(solution)/shard_map/ppermute | solution.py:535
  522.2 1.6 collective-permute-start.8
  523.8 2.5 fusion.31
  526.3 17.7 %collective-permute-done.14 = bf16[2,256,1024]{2,1,0:T(8,128)(2,1)S(1)} collective-permute-done((bf16[2,256,1024]{2,1,0:T(8,128)(2,1)}, bf16[2,256,1024]{2,1,0:T(8,128)(2,1)S(1)}, u32[]{:S(2)}, u32[]{:S(2)}) %collective-permute-start.14) | collective-permute-done | bytes 1048608 | tf_op jit(solution)/shard_map/ppermute | solution.py:535
  545.5 123.7 %shard_map.258 = (bf16[64,8192]{1,0:T(8,128)(2,1)}, bf16[64,2048]{1,0:T(8,128)(2,1)}) custom-call(bf16[512,1024]{1,0:T(8,128)(2,1)} %reduce-scatter.5.cloned.1.call-done.refs_0_, bf16[512,256]{1,0:T(8,128)(2,1)} %reduce-scatter.7.cloned.1.call-done.refs_1_), custom_call_target="tpu_custom_call" | custom-call | flops 11900000256 | bytes 1048576 | tf_op jit(solution)/shard_map/pallas_call | solution.py:344
  669.3 2.6 fusion.30
  674.1 7.3 convert_reduce_fusion.3
  682.0 30.5 %shard_map.259 = (f32[32,32,128]{2,1,0:T(8,128)}, bf16[64,8192]{1,0:T(8,128)(2,1)}, bf16[64,6144]{1,0:T(8,128)(2,1)}) custom-call(f32[32,128]{1,0:T(8,128)} %fusion.27.refs_0_, bf16[512,1024]{1,0:T(8,128)(2,1)} %reduce-scatter.9.cloned.1.call-done.refs_1_, bf16[512,768]{1,0:T(8,128)(2,1)} %reduce-scatter.11.cloned.1.call-done.refs_2_), custom_call_target="tpu_custom_call" | custom-call | flops 17500000256 | bytes 1048576 | tf_op jit(solution)/shard_map/pallas_call | solution.py:171
  715.4 1.9 convert_element_type.199
  718.6 3.8 fusion.18
  722.5 2.2 fusion.23
  (206 shorter events, 34.4 us)
Async XLA Ops:
  7.2 151.1 %all-gather.5.cloned.1.call-start = ((), (), s32[]{:S(2)}) async-start(), calls=%async_computation.4 | async-start | bytes 5242880 | tf_op jit(solution)/shard_map/all_gather | solution.py:565
  7.2 9.9 %collective-permute-start = (s32[2,1024]{1,0:T(2,128)}, s32[2,1024]{1,0:T(2,128)S(1)}, u32[]{:S(2)}, u32[]{:S(2)}) collective-permute-start(s32[2,1024]{1,0:T(2,128)} %param.16), channel_id=1, source_target_pairs={{0,4},{4,0},{1,5},{5,1},{2,6},{6,2},{3,7},{7,3},{8,12},{12,8},{9,1... | collective-permute-start | bytes 24584 | tf_op jit(solution)/shard_map/ppermute | solution.py:572
  17.2 31.0 %copy-start = (bf16[2,256,2048]{2,1,0:T(8,128)(2,1)S(1)}, bf16[2,256,2048]{2,1,0:T(8,128)(2,1)}, u32[]{:S(2)}) copy-start(bf16[2,256,2048]{2,1,0:T(8,128)(2,1)} %refs_0_.1) | copy-start | bytes 6291460
  17.2 31.0 %copy-start.2 = (bf16[64,8192]{1,0:T(8,128)(2,1)S(1)}, bf16[64,8192]{1,0:T(8,128)(2,1)}, u32[]{:S(2)}) copy-start(bf16[64,8192]{1,0:T(8,128)(2,1)} %refs_3_.1) | copy-start | bytes 3145732
  17.2 31.0 %copy-start.3 = (bf16[64,2048]{1,0:T(8,128)(2,1)S(1)}, bf16[64,2048]{1,0:T(8,128)(2,1)}, u32[]{:S(2)}) copy-start(bf16[64,2048]{1,0:T(8,128)(2,1)} %refs_2_.3) | copy-start | bytes 786436
  45.2 155.7 %all-gather.7.cloned.1.call-start = ((), (), s32[]{:S(2)}) async-start(), calls=%async_computation.5 | async-start | bytes 3932160 | tf_op jit(solution)/shard_map/all_gather | solution.py:565
  47.9 241.0 %all-gather.9.cloned.1.call-start = ((), (), s32[]{:S(2)}) async-start(), calls=%async_computation.6 | async-start | bytes 1310720 | tf_op jit(solution)/shard_map/all_gather | solution.py:565
  152.5 160.3 %all-gather.11.cloned.1.call-start = ((), (), s32[]{:S(2)}) async-start(), calls=%async_computation.7 | async-start | bytes 5242880 | tf_op jit(solution)/shard_map/all_gather | solution.py:565
  154.3 94.4 %collective-permute-start.1 = (bf16[2,256,2048]{2,1,0:T(8,128)(2,1)}, bf16[2,256,2048]{2,1,0:T(8,128)(2,1)}, u32[]{:S(2)}, u32[]{:S(2)}) collective-permute-start(bf16[2,256,2048]{2,1,0:T(8,128)(2,1)} %param.17), channel_id=1, source_target_pairs={{0,2},{1,3},{2,0},{3,1},{4,6},{5,7},{6,4},{7,5},{8,10},{9,11},{10,... | collective-permute-start | bytes 6291464 | tf_op jit(solution)/shard_map/ppermute | solution.py:525
  155.0 93.8 %collective-permute-start.2 = (bf16[2,256,2048]{2,1,0:T(8,128)(2,1)}, bf16[2,256,2048]{2,1,0:T(8,128)(2,1)}, u32[]{:S(2)}, u32[]{:S(2)}) collective-permute-start(bf16[2,256,2048]{2,1,0:T(8,128)(2,1)} %param.17), channel_id=1, source_target_pairs={{0,4},{1,5},{2,6},{3,7},{4,0},{5,1},{6,2},{7,3},{8,12},{9,13},{10,... | collective-permute-start | bytes 6291464 | tf_op jit(solution)/shard_map/ppermute | solution.py:525
  156.4 92.4 %collective-permute-start.3 = (bf16[2,256,2048]{2,1,0:T(8,128)(2,1)}, bf16[2,256,2048]{2,1,0:T(8,128)(2,1)}, u32[]{:S(2)}, u32[]{:S(2)}) collective-permute-start(bf16[2,256,2048]{2,1,0:T(8,128)(2,1)} %param.17), channel_id=1, source_target_pairs={{0,6},{1,7},{2,4},{3,5},{4,2},{5,3},{6,0},{7,1},{8,14},{9,15},{10,... | collective-permute-start | bytes 6291464 | tf_op jit(solution)/shard_map/ppermute | solution.py:525
  158.0 368.3 %reduce-scatter.7.cloned.1.call-start = ((), (), s32[]{:S(2)}) async-start(), calls=%async_computation.9 | async-start | bytes 1310720 | tf_op jit(solution)/shard_map/reduce_scatter | solution.py:657
  248.8 6.5 collective-permute-start.4
  248.9 7.1 collective-permute-start.5
  249.4 9.6 %collective-permute-start.6 = (bf16[2,256,2048]{2,1,0:T(8,128)(2,1)}, bf16[2,256,2048]{2,1,0:T(8,128)(2,1)S(1)}, u32[]{:S(2)}, u32[]{:S(2)}) collective-permute-start(bf16[2,256,2048]{2,1,0:T(8,128)(2,1)} %collective-permute-done.2), channel_id=1, source_target_pairs={{0,1},{1,0},{2,3},{3,2},{4,5},{5,4},{6,7},{7,6},{8,9},{9,8},{10,11... | collective-permute-start | bytes 6291464 | tf_op jit(solution)/shard_map/ppermute | solution.py:528
  249.5 12.6 %collective-permute-start.7 = (bf16[2,256,2048]{2,1,0:T(8,128)(2,1)}, bf16[2,256,2048]{2,1,0:T(8,128)(2,1)S(1)}, u32[]{:S(2)}, u32[]{:S(2)}) collective-permute-start(bf16[2,256,2048]{2,1,0:T(8,128)(2,1)} %collective-permute-done.3), channel_id=1, source_target_pairs={{0,1},{1,0},{2,3},{3,2},{4,5},{5,4},{6,7},{7,6},{8,9},{9,8},{10,11... | collective-permute-start | bytes 6291464 | tf_op jit(solution)/shard_map/ppermute | solution.py:528
  255.3 12.7 %slice-start = ((s8[8388608]{0:T(1024)(128)(4,1)}), s8[4194304]{0:T(1024)(128)(4,1)S(1)}, s32[]{:S(2)}) async-start(s8[8388608]{0:T(1024)(128)(4,1)} %bitcast.139), calls=%async_computation.12 | async-start | bytes 8388608
  256.2 11.8 %slice-start.1 = ((s8[8388608]{0:T(1024)(128)(4,1)}), s8[4194304]{0:T(1024)(128)(4,1)S(1)}, s32[]{:S(2)}) async-start(s8[8388608]{0:T(1024)(128)(4,1)} %bitcast.139), calls=%async_computation.13 | async-start | bytes 8388608
  262.2 5.8 copy-start.22
  288.8 12.1 %copy-start.9 = (bf16[2,2,2,2,256,256]{5,4,3,2,1,0:T(8,128)(2,1)S(1)}, bf16[2,2,2,2,256,256]{5,4,3,2,1,0:T(8,128)(2,1)}, u32[]{:S(2)}) copy-start(bf16[2,2,2,2,256,256]{5,4,3,2,1,0:T(8,128)(2,1)} %copy.34) | copy-start | bytes 6291460
  288.9 12.1 %copy-start.23 = (bf16[8,2,256,2048]{3,2,1,0:T(8,128)(2,1)S(1)}, bf16[8,2,256,2048]{3,2,1,0:T(8,128)(2,1)}, u32[]{:S(2)}) copy-start(bf16[8,2,256,2048]{3,2,1,0:T(8,128)(2,1)} %copy-done.22) | copy-start | bytes 50331652
  306.9 4.5 copy-start.29
  306.9 5.2 copy-start.28
  306.9 219.4 %reduce-scatter.5.cloned.1.call-start = ((), (), s32[]{:S(2)}) async-start(), calls=%async_computation.8 | async-start | bytes 5242880 | tf_op jit(solution)/shard_map/reduce_scatter | solution.py:657
  307.5 374.5 %reduce-scatter.11.cloned.1.call-start = ((), (), s32[]{:S(2)}) async-start(), calls=%async_computation.11 | async-start | bytes 3932160 | tf_op jit(solution)/shard_map/reduce_scatter | solution.py:657
  312.8 32.0 %copy-start.10 = (bf16[4096,256]{1,0:T(8,128)(2,1)S(1)}, bf16[4096,256]{1,0:T(8,128)(2,1)}, u32[]{:S(2)}) copy-start(bf16[4096,256]{1,0:T(8,128)(2,1)} %convolution_convert_fusion) | copy-start | bytes 6291460
  393.6 288.4 %reduce-scatter.9.cloned.1.call-start = ((), (), s32[]{:S(2)}) async-start(), calls=%async_computation.10 | async-start | bytes 5242880 | tf_op jit(solution)/shard_map/reduce_scatter | solution.py:657
  472.8 36.8 %collective-permute-start.11 = (bf16[2,256,1024]{2,1,0:T(8,128)(2,1)}, bf16[2,256,1024]{2,1,0:T(8,128)(2,1)S(1)}, u32[]{:S(2)}, u32[]{:S(2)}) collective-permute-start(bf16[2,256,1024]{2,1,0:T(8,128)(2,1)} %bitcast.133), channel_id=1, source_target_pairs={{0,2},{1,3},{2,0},{3,1},{4,6},{5,7},{6,4},{7,5},{8,10},{9,11},{10,... | collective-permute-start | bytes 3145736 | tf_op jit(solution)/shard_map/ppermute | solution.py:535
  473.4 47.6 %collective-permute-start.12 = (bf16[2,256,1024]{2,1,0:T(8,128)(2,1)}, bf16[2,256,1024]{2,1,0:T(8,128)(2,1)S(1)}, u32[]{:S(2)}, u32[]{:S(2)}) collective-permute-start(bf16[2,256,1024]{2,1,0:T(8,128)(2,1)} %bitcast.132), channel_id=1, source_target_pairs={{0,4},{1,5},{2,6},{3,7},{4,0},{5,1},{6,2},{7,3},{8,12},{9,13},{10,... | collective-permute-start | bytes 3145736 | tf_op jit(solution)/shard_map/ppermute | solution.py:535
  474.8 47.4 %collective-permute-start.13 = (bf16[2,256,1024]{2,1,0:T(8,128)(2,1)}, bf16[2,256,1024]{2,1,0:T(8,128)(2,1)}, u32[]{:S(2)}, u32[]{:S(2)}) collective-permute-start(bf16[2,256,1024]{2,1,0:T(8,128)(2,1)} %bitcast.131), channel_id=1, source_target_pairs={{0,6},{1,7},{2,4},{3,5},{4,2},{5,3},{6,0},{7,1},{8,14},{9,15},{10,... | collective-permute-start | bytes 3145736 | tf_op jit(solution)/shard_map/ppermute | solution.py:535
  499.1 45.0 %collective-permute-start.14 = (bf16[2,256,1024]{2,1,0:T(8,128)(2,1)}, bf16[2,256,1024]{2,1,0:T(8,128)(2,1)S(1)}, u32[]{:S(2)}, u32[]{:S(2)}) collective-permute-start(bf16[2,256,1024]{2,1,0:T(8,128)(2,1)} %bitcast.130), channel_id=1, source_target_pairs={{0,2},{1,3},{2,0},{3,1},{4,6},{5,7},{6,4},{7,5},{8,10},{9,11},{10,... | collective-permute-start | bytes 3145736 | tf_op jit(solution)/shard_map/ppermute | solution.py:535
  503.5 20.3 %copy-start.16 = (bf16[512,1024]{1,0:T(8,128)(2,1)S(1)}, bf16[512,1024]{1,0:T(8,128)(2,1)}, u32[]{:S(2)}) copy-start(bf16[512,1024]{1,0:T(8,128)(2,1)} %get-tuple-element.126) | copy-start | bytes 3145732
  503.5 165.8 %collective-permute-start.15 = (bf16[2,256,1024]{2,1,0:T(8,128)(2,1)}, bf16[2,256,1024]{2,1,0:T(8,128)(2,1)}, u32[]{:S(2)}, u32[]{:S(2)}) collective-permute-start(bf16[2,256,1024]{2,1,0:T(8,128)(2,1)} %bitcast.40), channel_id=1, source_target_pairs={{0,4},{1,5},{2,6},{3,7},{4,0},{5,1},{6,2},{7,3},{8,12},{9,13},{10,... | collective-permute-start | bytes 3145736 | tf_op jit(solution)/shard_map/ppermute | solution.py:535
  509.5 14.3 %copy-start.17 = (bf16[2,256,1024]{2,1,0:T(8,128)(2,1)}, bf16[2,256,1024]{2,1,0:T(8,128)(2,1)S(1)}, u32[]{:S(2)}) copy-start(bf16[2,256,1024]{2,1,0:T(8,128)(2,1)S(1)} %collective-permute-done.11) | copy-start | bytes 3145732
  509.5 159.7 %collective-permute-start.16 = (bf16[2,256,1024]{2,1,0:T(8,128)(2,1)}, bf16[2,256,1024]{2,1,0:T(8,128)(2,1)}, u32[]{:S(2)}, u32[]{:S(2)}) collective-permute-start(bf16[2,256,1024]{2,1,0:T(8,128)(2,1)} %bitcast.41), channel_id=1, source_target_pairs={{0,6},{1,7},{2,4},{3,5},{4,2},{5,3},{6,0},{7,1},{8,14},{9,15},{10,... | collective-permute-start | bytes 3145736 | tf_op jit(solution)/shard_map/ppermute | solution.py:535
  521.0 151.9 %collective-permute-start.10 = (bf16[2,256,2048]{2,1,0:T(8,128)(2,1)}, bf16[2,256,2048]{2,1,0:T(8,128)(2,1)}, u32[]{:S(2)}, u32[]{:S(2)}) collective-permute-start(bf16[2,256,2048]{2,1,0:T(8,128)(2,1)} %bitcast.26), channel_id=1, source_target_pairs={{0,6},{1,7},{2,4},{3,5},{4,2},{5,3},{6,0},{7,1},{8,14},{9,15},{10,... | collective-permute-start | bytes 6291464 | tf_op jit(solution)/shard_map/ppermute | solution.py:535
  522.2 150.7 %collective-permute-start.8 = (bf16[2,256,2048]{2,1,0:T(8,128)(2,1)}, bf16[2,256,2048]{2,1,0:T(8,128)(2,1)}, u32[]{:S(2)}, u32[]{:S(2)}) collective-permute-start(bf16[2,256,2048]{2,1,0:T(8,128)(2,1)} %bitcast.24), channel_id=1, source_target_pairs={{0,2},{1,3},{2,0},{3,1},{4,6},{5,7},{6,4},{7,5},{8,10},{9,11},{10,... | collective-permute-start | bytes 6291464 | tf_op jit(solution)/shard_map/ppermute | solution.py:535
  545.0 124.2 %copy-start.14 = (bf16[512,1024]{1,0:T(8,128)(2,1)S(1)}, bf16[512,1024]{1,0:T(8,128)(2,1)}, u32[]{:S(2)}) copy-start(bf16[512,1024]{1,0:T(8,128)(2,1)} %get-tuple-element.135) | copy-start | bytes 3145732
  545.0 127.8 %collective-permute-start.9 = (bf16[2,256,2048]{2,1,0:T(8,128)(2,1)}, bf16[2,256,2048]{2,1,0:T(8,128)(2,1)}, u32[]{:S(2)}, u32[]{:S(2)}) collective-permute-start(bf16[2,256,2048]{2,1,0:T(8,128)(2,1)} %bitcast.129), channel_id=1, source_target_pairs={{0,4},{1,5},{2,6},{3,7},{4,0},{5,1},{6,2},{7,3},{8,12},{9,13},{10,... | collective-permute-start | bytes 6291464 | tf_op jit(solution)/shard_map/ppermute | solution.py:535
  682.0 31.9 %copy-start.12 = (bf16[64,8192]{1,0:T(8,128)(2,1)S(1)}, bf16[64,8192]{1,0:T(8,128)(2,1)}, u32[]{:S(2)}) copy-start(bf16[64,8192]{1,0:T(8,128)(2,1)} %get-tuple-element.143) | copy-start | bytes 3145732
  712.6 6.1 copy-start.13
  712.6 6.1 copy-start.41
  712.6 6.0 copy-start.42
  713.9 8.5 %copy-start.19 = (bf16[64,6144]{1,0:T(8,128)(2,1)S(1)}, bf16[64,6144]{1,0:T(8,128)(2,1)}, u32[]{:S(2)}) copy-start(bf16[64,6144]{1,0:T(8,128)(2,1)} %refs_2_.2) | copy-start | bytes 2359300
  713.9 8.5 %copy-start.39 = (f32[64]{0:T(128)S(1)}, f32[64]{0:T(128)}, u32[]{:S(2)}) copy-start(f32[64]{0:T(128)} %convert_element_type.155) | copy-start | bytes 772
  714.0 8.5 %copy-start.40 = (f32[64]{0:T(128)S(1)}, f32[64]{0:T(128)}, u32[]{:S(2)}) copy-start(f32[64]{0:T(128)} %convert_element_type.157) | copy-start | bytes 772
  715.4 7.0 copy-start.20
  718.6 6.6 copy-start.43
  (23 other events, 49.4 us)
Sparse Core Ops, SparseCore 0:
  45.3 80.2 all-gather.4
  127.2 61.9 all-gather.6
  190.8 26.6 all-gather.8
  218.9 80.1 all-gather.10
  307.0 24.9 reduce-scatter.6
  334.1 75.2 reduce-scatter.4
  411.7 60.9 reduce-scatter.10
  475.0 76.6 reduce-scatter.8

commit v3 on v2

--- a/solution.py
+++ b/solution.py
@@ -225,10 +225,7 @@
         copies[o][0].start()
     to_partner[(0, 0)].start()
     swaps = swap_copies(lay, plan, me, sources, targets, w_send, w_recv, False)
-    mine = swap_own(lay, plan, me, sources, targets, w_own, False)
-    for copy in swaps + mine:
-        copy.start()
-
+    swaps += swap_own(lay, plan, me, sources, targets, w_own, False)
     gains = [gain_ref[i : i + 1, :] for i in range(4)]
     rows = 16
     pending = [[], []]
@@ -271,6 +268,9 @@
                 copies[(ry, rx)][0].start()
             if o == (ry, 0):
                 copies[(ry, rx)][1].start()
+        if o == straight[-1]:
+            for copy in swaps:
+                copy.start()
         norm(0, slot[o])
     for o in straight:
         to_partner[o].wait_recv()
@@ -291,7 +291,7 @@
             copy.wait_send()
     for o in lay.offsets:
         to_partner[o].wait_send()
-    for copy in swaps + mine:
+    for copy in swaps:
         copy.wait()
 
 
@@ -453,14 +453,30 @@
 QUERY_BLOCK = 256
 
 
+def wide_angles(ref):
+    part = ref[0]
+    return jnp.transpose(jnp.concatenate([part, part, part, part], 0), (1, 0))
+
+
+def wide_pair(cos_ref, sin_ref):
+    cosine, sine = wide_angles(cos_ref), wide_angles(sin_ref)
+    lane = lax.broadcasted_iota(jnp.int32, cosine.shape, 1)
+    cosine = jnp.where(lane < ROTARY, cosine, 1.0)
+    sine = jnp.where(lane < ROTARY // 2, -sine, jnp.where(lane < ROTARY, sine, 0.0))
+    return cosine, sine
+
+
 def attend_kernel(scaling, packed_ref, cos_ref, sin_ref, col_ref, row_ref, q_ref, k_ref, v_ref, ctx_ref, lse_ref,
-                  q_buf, k_buf, v_buf):
+                  q_buf, k_buf, v_buf, ctx_buf, cos_buf, sin_buf):
     cores, _, chips, _, length, _ = packed_ref.shape
+    cos_all, sin_all = wide_pair(cos_ref, sin_ref)
+    cos_buf[...] = cos_all
+    sin_buf[...] = sin_all
     for c in range(cores):
         for i in range(chips):
             at = pl.ds((c * chips + i) * length, length)
             block = packed_ref[c, 0, i, 0]
-            cosine, sine = cos_ref[0, at, :], sin_ref[0, at, :]
+            cosine, sine = cos_buf[at, :], sin_buf[at, :]
             q_buf[at, :] = turn_pairs(block[:, :HEAD_DIM], cosine, sine).astype(BF16)
             k_buf[at, :] = turn_pairs(block[:, HEAD_DIM : 2 * HEAD_DIM], cosine, sine).astype(BF16)
             v_buf[at, :] = block[:, 2 * HEAD_DIM :].astype(BF16)
@@ -478,24 +494,33 @@
         weights = jnp.where(allowed, jnp.exp(scores - top), 0.0)
         total_row = jnp.sum(weights, 0, keepdims=True)
         probs = (weights * (1.0 / total_row)).astype(BF16)
-        ctx_ref[0, at, :] = dot(probs, v_buf[...], ((0,), (0,))).astype(BF16)
+        ctx_buf[at, :] = dot(probs, v_buf[...], ((0,), (0,))).astype(BF16)
         lse_ref[0, :, at] = top + jnp.log(total_row)
         return carry
 
     lax.fori_loop(0, total // QUERY_BLOCK, one, 0)
+    for c in range(cores):
+        for i in range(chips):
+            ctx_ref[c, 0, i, 0] = ctx_buf[pl.ds((c * chips + i) * length, length), :]
 
 
 def attend_back_kernel(scaling, q_ref, k_ref, v_ref, g_ref, cos_ref, sin_ref, col_ref, row_ref, lse_ref, out_ref,
-                       dq_buf, dk_buf, dv_buf):
+                       g_buf, dq_buf, dk_buf, dv_buf, cos_buf, sin_buf):
     cores, _, chips, _, length, _ = out_ref.shape
     total = q_ref.shape[1]
+    cos_all, sin_all = wide_pair(cos_ref, sin_ref)
+    cos_buf[...] = cos_all
+    sin_buf[...] = sin_all
+    for c in range(cores):
+        for i in range(chips):
+            g_buf[pl.ds((c * chips + i) * length, length), :] = g_ref[c, 0, i, 0]
     dk_buf[...] = jnp.zeros_like(dk_buf)
     dv_buf[...] = jnp.zeros_like(dv_buf)
 
     def one(j, carry):
         at = pl.ds(pl.multiple_of(j * QUERY_BLOCK, QUERY_BLOCK), QUERY_BLOCK)
         queries = q_ref[0, at, :]
-        grads = g_ref[0, at, :]
+        grads = g_buf[at, :]
         scores = dot(k_ref[0], queries, ((1,), (1,))) * scaling
         allowed = col_ref[0] <= row_ref[0, :, at]
         scores = jnp.where(allowed, scores, NEGATIVE)
@@ -512,7 +537,7 @@
     for c in range(cores):
         for i in range(chips):
             at = pl.ds((c * chips + i) * length, length)
-            cosine, sine = cos_ref[0, at, :], sin_ref[0, at, :]
+            cosine, sine = cos_buf[at, :], sin_buf[at, :]
             out_ref[c, 0, i, 0, :, :HEAD_DIM] = turn_pairs(dq_buf[at, :] * scaling, cosine, -sine).astype(BF16)
             out_ref[c, 0, i, 0, :, HEAD_DIM : 2 * HEAD_DIM] = turn_pairs(dk_buf[at, :] * scaling, cosine, -sine).astype(BF16)
             out_ref[c, 0, i, 0, :, 2 * HEAD_DIM :] = dv_buf[at, :].astype(BF16)
@@ -578,7 +603,6 @@
         vec = jnp.concatenate([v.astype(F32) for v in names])
         size = -(-vec.shape[0] // 1024) * 1024
         vec = jnp.pad(vec, (0, size - vec.shape[0])).reshape(-1, 128)
-        vec, places = lax.optimization_barrier((vec, places))
         vectors, up_own, qkv_own = exchange(lay, [plans["up"], plans["qkv"]], vec, [w_up, w_qkv], False, 0, 30)
         up_w = gather_rows(up_own)
         qkv_w = gather_rows(qkv_own)
@@ -597,7 +621,7 @@
         out_w = gather_rows(out_own)
         down_w = gather_rows(down_own)
         one, two, hat = [v.reshape(total, width) for v in (one, two, hat)]
-        cotangent, hat = lax.optimization_barrier((cotangent, hat))
+        cotangent, hat, places = lax.optimization_barrier((cotangent, hat, places))
         near_dy = gather_near(cotangent)
 
         hidden = dot(two, up_w, ((1,), (0,))) + b_up_mine
@@ -610,11 +634,8 @@
         halves = ROTARY // 2
         frequency = jnp.exp(jnp.arange(halves, dtype=F32) * (-2.0 * math.log(10000.0) / ROTARY))
         places = after(places, activated)
-        phases = places.astype(F32)[..., None] * frequency
+        phases = places.astype(F32)[:, None, :] * frequency[None, :, None]
         cosine, sine = jnp.cos(phases), jnp.sin(phases)
-        rest = (sub * batch, count, 128 - ROTARY)
-        cosine = jnp.concatenate([cosine, cosine, jnp.ones(rest, F32)], -1)
-        sine = jnp.concatenate([-sine, sine, jnp.zeros(rest, F32)], -1)
         place_col = places[:, :, None]
         place_row = places[:, None, :]
 
@@ -625,7 +646,10 @@
         wide_spec = pl.BlockSpec(wide, lambda i: (0, i // batch, 0, i % batch, 0, 0))
         full = (2, sub, chips_x, batch, length, 3 * cols)
         head_spec = pl.BlockSpec((1, count, HEAD_DIM), lambda i: (i, 0, 0))
-        turn_spec = pl.BlockSpec((1, count, 128), lambda i: (i, 0, 0))
+        turn_spec = pl.BlockSpec((1, ROTARY // 2, count), lambda i: (i, 0, 0))
+        tokens_spec = pl.BlockSpec((2, 1, chips_x, 1, length, cols), lambda i: (0, i // batch, 0, i % batch, 0, 0))
+        by_token = (2, sub, chips_x, batch, length, cols)
+        turn_bufs = [pltpu.VMEM((count, 128), F32)] * 2
         col_spec = pl.BlockSpec((1, count, 1), lambda i: (i, 0, 0))
         row_spec = pl.BlockSpec((1, 1, count), lambda i: (i, 0, 0))
         head_shape = jax.ShapeDtypeStruct((seqs, count, HEAD_DIM), BF16)
@@ -635,23 +659,15 @@
             functools.partial(attend_kernel, scaling),
             grid=(seqs,),
             in_specs=[wide_spec, turn_spec, turn_spec, col_spec, row_spec],
-            out_specs=[head_spec] * 4 + [row_spec],
-            out_shape=[head_shape] * 4 + [jax.ShapeDtypeStruct((seqs, 1, count), F32)],
-            scratch_shapes=[pltpu.VMEM((count, HEAD_DIM), BF16)] * 3,
+            out_specs=[head_spec] * 3 + [tokens_spec, row_spec],
+            out_shape=[head_shape] * 3 + [jax.ShapeDtypeStruct(by_token, BF16), jax.ShapeDtypeStruct((seqs, 1, count), F32)],
+            scratch_shapes=[pltpu.VMEM((count, HEAD_DIM), BF16)] * 4 + turn_bufs,
             compiler_params=params,
             cost_estimate=pl.CostEstimate(flops=2 * work, bytes_accessed=30 << 20, transcendentals=seqs * count * count),
             name="attend",
         )(packed.reshape(full), cosine, sine, place_col, place_row)
 
-        def to_tokens(v):
-            v = v.reshape(sub, batch, 2, chips_x, length, cols)
-            return jnp.transpose(v, (2, 0, 3, 1, 4, 5)).reshape(total, cols)
-
-        def to_heads(v):
-            v = v.reshape(2, sub, chips_x, batch, length, cols)
-            return jnp.transpose(v, (1, 3, 0, 2, 4, 5)).reshape(seqs, count, cols)
-
-        context = to_tokens(context)
+        context = context.reshape(total, cols)
 
         def scatter(grad):
             return lax.psum_scatter(grad, "zo", scatter_dimension=0, tiled=True)
@@ -659,7 +675,10 @@
         def outer_dot(left, right):
             return dot(left, right, ((0,), (0,))).astype(BF16)
 
-        near_dy = lax.optimization_barrier((*near_dy, context))[:-1]
+        qkv_late, up_late = lax.optimization_barrier((qkv_w, up_w, context))[:-1]
+        fold_qkv = (gain1_all[:, None] * qkv_late.astype(F32)).astype(BF16)
+        fold_up = (gain2_all[:, None] * up_late.astype(F32)).astype(BF16)
+        near_dy = lax.optimization_barrier((*near_dy, fold_qkv, fold_up))[:-2]
         upstream = gather_partner(list(near_dy)).reshape(total, width)
         down_part = outer_dot(upstream, activated)
         upstream = after(upstream, down_part)
@@ -679,20 +698,19 @@
         out_near = pair_matmul(lay, pair[0], out_w, pair[1], down_w, (0, 1), 4)
         grad_context, *out_near = chain((grad_context, *out_near))
         out_near = tokens_of(out_near)
-        out_sum = add_all(send_far(out_near))
-        output = (tokens.astype(F32) + out_sum + b_out_all + b_down_all).astype(BF16)
+        out_near = send_far(out_near)
 
         grad_packed = pl.pallas_call(
             functools.partial(attend_back_kernel, scaling),
             grid=(seqs,),
-            in_specs=[head_spec] * 4 + [turn_spec, turn_spec, col_spec, row_spec, row_spec],
+            in_specs=[head_spec] * 3 + [tokens_spec, turn_spec, turn_spec, col_spec, row_spec, row_spec],
             out_specs=wide_spec,
             out_shape=jax.ShapeDtypeStruct(full, BF16),
-            scratch_shapes=[pltpu.VMEM((count, HEAD_DIM), F32)] * 3,
+            scratch_shapes=[pltpu.VMEM((count, HEAD_DIM), BF16)] + [pltpu.VMEM((count, HEAD_DIM), F32)] * 3 + turn_bufs,
             compiler_params=params,
             cost_estimate=pl.CostEstimate(flops=5 * work, bytes_accessed=24 << 20, transcendentals=seqs * count * count),
             name="attend_back",
-        )(queries, keys, values, to_heads(grad_context), cosine, sine, place_col, place_row, lse)
+        )(queries, keys, values, grad_context.reshape(by_token), cosine, sine, place_col, place_row, lse)
         grad_packed = grad_packed.reshape(total, 3 * cols)
 
         qkv_part = outer_dot(hat, grad_packed)
@@ -700,32 +718,14 @@
         (upstream,) = chain((upstream,), qkv_part)
         grad_hidden = (dot(upstream, down_w, ((1,), (0,))) * slope.astype(F32)).astype(BF16)
 
-        fold_qkv = (gain1_all[:, None] * qkv_w.astype(F32)).astype(BF16)
-        fold_up = (gain2_all[:, None] * up_w.astype(F32)).astype(BF16)
-        left = grad_packed
-        came = []
-        for k in range(2):
-            near = pair_matmul(lay, left, fold_qkv, grad_hidden, fold_up, (k, 2), 5 + k)
-            left, *near = chain((left, *near))
-            came.append(send_far(tokens_of(near)))
-
-        hat, grad_hidden = chain((hat, grad_hidden), left)
+        near = pair_matmul(lay, grad_packed, fold_qkv, grad_hidden, fold_up, (0, 2), 5)
+        hat, *near = chain((hat, *near))
+        came = [send_far(tokens_of(near))]
         up_part = outer_dot(hat, grad_hidden)
         up_sum = scatter(up_part)
-        down_sum, out_w_sum = chain((down_sum, out_w_sum), up_part)
-        down_raw, out_raw = deal_exchange(lay, [plans["down"], plans["out"]], [down_sum, out_w_sum], 2)
-
-        inputs = tokens.astype(F32)
-        center = inputs - jnp.mean(inputs, -1, keepdims=True)
-        inv_std = lax.rsqrt(jnp.mean(center * center, -1, keepdims=True) + EPSILON)
-        normal = center * inv_std
-        came[1] = chain(came[1], down_raw, out_raw)
-        grad_normal = jnp.concatenate([add_all(pieces) for pieces in came], -1)
-        token_grad = cotangent.astype(F32) + inv_std * (
-            grad_normal
-            - jnp.mean(grad_normal, -1, keepdims=True)
-            - normal * jnp.mean(grad_normal * normal, -1, keepdims=True)
-        )
+        (left,) = chain((grad_packed,), up_part)
+        near = pair_matmul(lay, left, fold_qkv, grad_hidden, fold_up, (1, 2), 6)
+        came.append(send_far(tokens_of(near)))
 
         own_sums = [
             jnp.sum(grad_packed.astype(F32), 0),
@@ -735,8 +735,27 @@
         vec = jnp.concatenate(own_sums)
         size = -(-vec.shape[0] // 1024) * 1024
         vec = jnp.pad(vec, (0, size - vec.shape[0])).reshape(-1, 128)
+        out_near, vec, down_sum, out_w_sum = chain((out_near, vec, down_sum, out_w_sum), *near)
+        output = (tokens.astype(F32) + add_all(out_near) + b_out_all + b_down_all).astype(BF16)
+        vec, output = chain((vec, output))
+        everyone, down_raw, out_raw, qkv_raw = exchange(
+            lay, [plans["down"], plans["out"], plans["qkv"]], vec, [down_sum, out_w_sum, qkv_sum], True, 2, 40
+        )
+        came[1] = chain(came[1], everyone)
+
+        inputs = tokens.astype(F32)
+        center = inputs - jnp.mean(inputs, -1, keepdims=True)
+        inv_std = lax.rsqrt(jnp.mean(center * center, -1, keepdims=True) + EPSILON)
+        normal = center * inv_std
+        grad_normal = jnp.concatenate([add_all(pieces) for pieces in came], -1)
+        token_grad = cotangent.astype(F32) + inv_std * (
+            grad_normal
+            - jnp.mean(grad_normal, -1, keepdims=True)
+            - normal * jnp.mean(grad_normal * normal, -1, keepdims=True)
+        )
+
         rank = lax.axis_index("zo") * group + me
-        everyone, up_raw, qkv_raw = exchange(lay, [plans["up"], plans["qkv"]], vec, [up_sum, qkv_sum], True, 3, 25)
+        (up_raw,) = deal_exchange(lay, [plans["up"]], [up_sum], 3)
         sums = jnp.sum(everyone.reshape(lay.outer, group, -1), 0)
         sum_qkv = jnp.transpose(sums[:, : 3 * cols].reshape(group, 3, cols), (1, 0, 2)).reshape(-1)
         sum_up = sums[:, 3 * cols : 3 * cols + ff_cols].reshape(-1)

time: 739 us -> 728 us (0.985)
  waiting for transfers between devices: 34.6 us -> 114 us
  Pallas kernels: 417 us -> 339 us
  other arithmetic: 51.6 us -> 43.3 us
    pallas_call x1, Pallas kernels: 124 us -> 14.9 us  [deal_exchange(): pl.pallas_call(functools.partial(deal_kernel, lay, plan), out_shape=swap_...]
    ppermute x9, waiting for transfers between devices: 27.6 us -> 105 us  [send_far(): came.append(lax.ppermute(piece, GROUP, lay.shift(*back)))]
    pallas_call x2, Pallas kernels: 58.5 us -> 92.4 us  [exchange(): pl.pallas_call(functools.partial(exchange_kernel, lay, plan, back), out_s...]
    neg x1 -> x0, other arithmetic: 7.46 us -> none  [step(): sine = jnp.concatenate([-sine, sine, jnp.zeros(rest, F32)], -1)]
    unnamed x104 -> x84, local copies, waits for them, and re-layouts: 22.6 us -> 17.5 us
  transfers between devices with their start and end apart: 25 -> 25, of which waited for: 5 -> 6; matrix products, arithmetic and copies ran while one was open for 30% -> 30% of each run, Pallas kernels for 49% -> 41%
where the time goes in v3:
time: 728 us; the launch traced here: 722 us
  Pallas kernels  339 us (47%)
  matrix products  156 us (21%)
  waiting for transfers between devices  114 us (16%)
  other arithmetic  43.3 us (6%)
  local copies, waits for them, and re-layouts  38.7 us (5%)
  starting transfers between devices  16.8 us (2%)
  between operations  15.1 us (2%)
    dot_general x8, matrix products, dot(): lax.dot_general(left, right, (dims, ((), ())), preferred_element_type=F32)  156 us
    ppermute x9, waiting for transfers between devices, send_far(): came.append(lax.ppermute(piece, GROUP, lay.shift(*back)))  105 us
    pallas_call x1, Pallas kernels, norm_exchange(): pl.pallas_call(functools.partial(norm_kernel, lay, plan), out_shape=[whol...  99 us
    pallas_call x2, Pallas kernels, exchange(): pl.pallas_call(functools.partial(exchange_kernel, lay, plan, back), out_s...  92.4 us
    pallas_call x3, Pallas kernels, pair_matmul(): pl.pallas_call(functools.partial(pair_kernel, lay), grid=(2 * chips,), in...  78.2 us
    pallas_call x1, Pallas kernels, step(): pl.pallas_call(functools.partial(attend_back_kernel, scaling), grid=(seqs...  28 us
    pallas_call x1, Pallas kernels, step(): pl.pallas_call(functools.partial(attend_kernel, scaling), grid=(seqs,), i...  26.5 us
    unnamed x84, local copies, waits for them, and re-layouts  17.5 us
  transfers between devices with their start and end apart: 25, of which 6 were waited for; matrix products, arithmetic and copies ran while one was open for 30% of the time, Pallas kernels for 41%

profile of v3, /device:TPU:0, one launch (start us, length us, event | category | flops | bytes accessed | tf_op | source)
XLA Modules:
  0.0 722.5 jit_solution(11298430220503681953)
XLA Ops:
  7.2 5.4 concatenate.18
  13.2 30.2 %shard_map.254 = (f32[32,8,128]{2,1,0:T(8,128)}, bf16[512,1024]{1,0:T(8,128)(2,1)}, bf16[512,768]{1,0:T(8,128)(2,1)}) custom-call(f32[8,128]{1,0:T(8,128)} %pad_bitcast_fusion.refs_0_, bf16[64,8192]{1,0:T(8,128)(2,1)} %refs_1_.1, bf16[64,6144]{1,0:T(8,128)(2,1)} %refs_2_.2), custom_call_target="tpu_custom_call" | custom-call | flops 20999999488 | bytes 1048576 | tf_op jit(solution)/shard_map/pallas_call | solution.py:171
  48.9 99.0 %norm_exchange.1 = (bf16[2,4,2,256,2048]{4,3,2,1,0:T(8,128)(2,1)}, bf16[2,4,2,256,2048]{4,3,2,1,0:T(8,128)(2,1)}, bf16[2,4,2,256,2048]{4,3,2,1,0:T(8,128)(2,1)},...) custom-call(bf16[2,256,2048]{2,1,0:T(8,128)(2,1)S(1)} %copy-done, f32[8,2048]{1,0:T(8,128)S(1)} %stack.16.refs_1_, ...), custom_call_target="tpu_custom_call" | custom-call | flops 70000001024 | bytes 1048576 | tf_op jit(solution)/shard_map/norm_exchange/pallas_call | solution.py:302
  148.0 1.2 collective-permute-start
  152.5 1.2 collective-permute-start.2
  153.8 1.6 collective-permute-start.3
  155.3 29.1 %fusion.4 = (bf16[4096,1024]{1,0:T(8,128)(2,1)}, bf16[4096,1024]{1,0:T(8,128)(2,1)}) fusion(f32[1024]{0:T(1024)S(1)} %bitcast.111, bf16[4096,2048]{1,0:T(8,128)(2,1)} %bitcast.123, bf16[2048,1024]{1,0:T(8,128)(2,1)} %all-gather.7.cloned.1.call-done), kind=kOutput, calls=%fused_computation.5 | convolution fusion | flops 17230200832 | bytes 37752832 | tf_op jit(solution)/shard_map/dot_general | solution.py:26
  184.4 2.8 multiply_sine_fusion
  187.2 19.3 %convolution_add_fusion = f32[4096,768]{1,0:T(8,128)} fusion(bf16[4096,2048]{1,0:T(8,128)(2,1)} %bitcast.122, bf16[2048,768]{1,0:T(8,128)(2,1)} %all-gather.5.cloned.1.call-done, f32[768]{0:T(1024)S(1)} %add.222), kind=kOutput, calls=%fused_computation.12 | convolution fusion | flops 12888047616 | bytes 32508928 | tf_op jit(solution)/shard_map/dot_general | solution.py:26
  207.1 2.0 copy.31.col_ref
  209.1 26.5 %attend.1 = (bf16[4,1024,256]{2,1,0:T(8,128)(2,1)}, bf16[4,1024,256]{2,1,0:T(8,128)(2,1)}, bf16[4,1024,256]{2,1,0:T(8,128)(2,1)}, bf16[2,2,2,2,256,256]{5,4,3,2,1,0:T(8,128)(2,1)}, f32[4,1,1024]{2,1,0:T(1,128)}) custom-call(f32[2,2,2,2,256,768]{5,4,3,2,1,0:T(8,128)} %bitcast.124, f32[4,32,1024]{2,1,0:T(8,128)} %get-tuple-element.179.cos_ref, ...), custom_call_target="tpu_custom_call" | custom-call | flops 4294967296 | bytes 31457280 | tf_op jit(solution)/shard_map/attend/pallas_call | solution.py:658
  235.5 2.2 multiply_convert_fusion.3.first_w
  238.9 2.8 multiply_convert_fusion.2.second_w
  243.9 1.8 bitcast_dynamic-update-slice_fusion.6
  245.7 1.8 bitcast_dynamic-update-slice_fusion.5
  247.5 1.9 bitcast_dynamic-update-slice_fusion.4
  250.0 2.7 collective-permute-done.6
  253.0 2.8 collective-permute-done.7
  256.0 5.8 copy-done.16
  261.8 20.6 %convolution_convert_fusion.2 = bf16[2048,1024]{1,0:T(8,128)(2,1)} fusion(bf16[4096,2048]{1,0:T(8,128)(2,1)S(1)} %bitcast.101, bf16[4096,1024]{1,0:T(8,128)(2,1)S(1)} %bitcast.127), kind=kOutput, calls=%fused_computation.33 | convolution fusion | flops 17181966336 | bytes 29360128 | tf_op jit(solution)/shard_map/dot_general | solution.py:26
  282.4 12.0 %convolution_convert_fusion = bf16[4096,256]{1,0:T(8,128)(2,1)} fusion(bf16[4096,2048]{1,0:T(8,128)(2,1)} %bitcast.102, bf16[2048,256]{1,0:T(8,128)(2,1)} %all-gather.9.cloned.1.call-done.first_w), kind=kOutput, calls=%fused_computation.19 | convolution fusion | flops 4296015872 | bytes 19922944 | tf_op jit(solution)/shard_map/dot_general | solution.py:26
  294.5 5.9 convolution_convert_fusion.4
  303.7 2.1 convert_reduce_fusion.3
  305.8 31.8 %shard_map.255 = (bf16[512,2048]{1,0:T(8,128)(2,1)}, bf16[512,2048]{1,0:T(8,128)(2,1)}, bf16[512,2048]{1,0:T(8,128)(2,1)}, bf16[512,2048]{1,0:T(8,128)(2,1)}) custom-call(bf16[2,4,512,256]{3,2,1,0:T(8,128)(2,1)} %bitcast.130, bf16[2048,256]{1,0:T(8,128)(2,1)} %all-gather.9.cloned.1.call-done.first_w, bf16[2,4,512,1024]{3,2,1,0:T(8,128)(2,1)} %bitcast.125, ...), custom_call_target="tpu_custom_call" | custom-call | flops 21474836480 | bytes 33554432 | tf_op jit(solution)/shard_map/pallas_call | solution.py:423
  337.6 28.0 %attend_back.1 = bf16[2,2,2,2,256,768]{5,4,3,2,1,0:T(8,128)(2,1)} custom-call(bf16[4,1024,256]{2,1,0:T(8,128)(2,1)} %get-tuple-element.117.q_ref, bf16[4,1024,256]{2,1,0:T(8,128)(2,1)} %get-tuple-element.118.k_ref, bf16[4,1024,256]{2,1,0:T(8,128)(2,1)} %get-tuple-element.119.v_ref, bf16[2,2,2,2,256,256]{5,4,3,2,1,0:T(8,128)(2,1)} %bitcast.132, ...), custom_call_target="tpu_custom_call" | custom-call | flops 10737418240 | bytes 25165824 | tf_op jit(solution)/shard_map/attend_back/pallas_call | solution.py:703
  365.7 20.2 %convolution_convert_fusion.3 = bf16[2048,768]{1,0:T(8,128)(2,1)} fusion(bf16[4096,2048]{1,0:T(8,128)(2,1)} %bitcast.120, bf16[4096,768]{1,0:T(8,128)(2,1)} %bitcast.89), kind=kOutput, calls=%fused_computation.34 | convolution fusion | flops 12886474752 | bytes 26214400 | tf_op jit(solution)/shard_map/dot_general | solution.py:26
  385.9 24.9 %convert_reduce_fusion = (f32[1024]{0:T(1024)S(1)}, bf16[4096,1024]{1,0:T(8,128)(2,1)}) fusion(bf16[4096,1024]{1,0:T(8,128)(2,1)} %get-tuple-element.124, bf16[4096,2048]{1,0:T(8,128)(2,1)} %bitcast.103, bf16[2048,1024]{1,0:T(8,128)(2,1)} %all-gather.11.cloned.1.call-done.second_w), kind=kOutput, calls=%fused_computation.6 | convolution fusion | flops 17200840704 | bytes 37752832 | tf_op jit(solution)/shard_map/dot_general | solution.py:26
  410.8 23.6 %shard_map.256 = (bf16[512,1024]{1,0:T(8,128)(2,1)}, bf16[512,1024]{1,0:T(8,128)(2,1)}, bf16[512,1024]{1,0:T(8,128)(2,1)}, bf16[512,1024]{1,0:T(8,128)(2,1)}) custom-call(bf16[2,4,512,768]{3,2,1,0:T(8,128)(2,1)} %bitcast.90, bf16[2048,768]{1,0:T(8,128)(2,1)} %multiply_convert_fusion.3.first_w, bf16[2,4,512,1024]{3,2,1,0:T(8,128)(2,1)} %bitcast.128, ...), custom_call_target="tpu_custom_call" | custom-call | flops 15032385536 | bytes 33554432 | tf_op jit(solution)/shard_map/pallas_call | solution.py:423
  435.5 24.0 %convolution_convert_fusion.1 = bf16[2048,1024]{1,0:T(8,128)(2,1)} fusion(bf16[4096,2048]{1,0:T(8,128)(2,1)} %bitcast.121, bf16[4096,1024]{1,0:T(8,128)(2,1)} %get-tuple-element.189), kind=kOutput, calls=%fused_computation.32 | convolution fusion | flops 17181966336 | bytes 29360128 | tf_op jit(solution)/shard_map/dot_general | solution.py:26
  461.6 1.4 collective-permute-start.9
  463.1 3.7 convert_reduce_fusion.1
  468.1 1.8 collective-permute-start.13
  469.9 22.8 %shard_map.257 = (bf16[512,1024]{1,0:T(8,128)(2,1)}, bf16[512,1024]{1,0:T(8,128)(2,1)}, bf16[512,1024]{1,0:T(8,128)(2,1)}, bf16[512,1024]{1,0:T(8,128)(2,1)}) custom-call(bf16[2,4,512,768]{3,2,1,0:T(8,128)(2,1)} %bitcast.91, bf16[2048,768]{1,0:T(8,128)(2,1)} %multiply_convert_fusion.3.first_w, bf16[2,4,512,1024]{3,2,1,0:T(8,128)(2,1)} %bitcast.129, ...), custom_call_target="tpu_custom_call" | custom-call | flops 15032385536 | bytes 33554432 | tf_op jit(solution)/shard_map/pallas_call | solution.py:423
  492.7 105.4 %collective-permute-done.12 = bf16[2,256,1024]{2,1,0:T(8,128)(2,1)} collective-permute-done((bf16[2,256,1024]{2,1,0:T(8,128)(2,1)}, bf16[2,256,1024]{2,1,0:T(8,128)(2,1)}, u32[]{:S(2)}, u32[]{:S(2)}) %collective-permute-start.12) | collective-permute-done | bytes 1048608 | tf_op jit(solution)/shard_map/ppermute | solution.py:560
  599.4 3.7 fusion.28
  603.2 2.2 collective-permute-start.16
  605.4 6.4 fusion.12
  611.7 62.2 %shard_map.258 = (f32[32,32,128]{2,1,0:T(8,128)}, bf16[64,8192]{1,0:T(8,128)(2,1)}, bf16[64,2048]{1,0:T(8,128)(2,1)}, bf16[64,6144]{1,0:T(8,128)(2,1)}) custom-call(f32[32,128]{1,0:T(8,128)} %fusion.24.refs_0_, bf16[512,1024]{1,0:T(8,128)(2,1)} %reduce-scatter.5.cloned.1.call-done.refs_1_, bf16[512,256]{1,0:T(8,128)(2,1)} %reduce-scatter.7.cloned.1.call-done.refs_2_, ...), custom_call_target="tpu_custom_call" | custom-call | flops 28000000000 | bytes 1048576 | tf_op jit(solution)/shard_map/pallas_call | solution.py:171
  677.1 2.7 convert_element_type.196
  679.7 1.4 reshape_reshape.19
  681.1 1.4 reshape_reshape.18
  683.5 1.3 constant_dynamic-slice_fusion
  684.8 1.3 constant_dynamic-slice_fusion.2
  686.7 2.5 fusion.27
  690.8 2.9 convert_add_fusion.1
  693.7 14.9 %shard_map.259 = bf16[64,8192]{1,0:T(8,128)(2,1)} custom-call(bf16[512,1024]{1,0:T(8,128)(2,1)} %reduce-scatter.11.cloned.1.call-done.refs_0_), custom_call_target="tpu_custom_call" | custom-call | flops 11900000256 | bytes 1048576 | tf_op jit(solution)/shard_map/pallas_call | solution.py:344
  708.7 3.9 fusion.16
  712.6 2.2 fusion.21
  (178 shorter events, 30.2 us)
Async XLA Ops:
  7.2 148.1 %all-gather.7.cloned.1.call-start = ((), (), s32[]{:S(2)}) async-start(), calls=%async_computation.5 | async-start | bytes 5242880 | tf_op jit(solution)/shard_map/all_gather | solution.py:590
  13.2 35.6 %copy-start = (bf16[2,256,2048]{2,1,0:T(8,128)(2,1)S(1)}, bf16[2,256,2048]{2,1,0:T(8,128)(2,1)}, u32[]{:S(2)}) copy-start(bf16[2,256,2048]{2,1,0:T(8,128)(2,1)} %refs_0_.1) | copy-start | bytes 6291460
  13.2 35.6 %copy-start.1 = (bf16[64,8192]{1,0:T(8,128)(2,1)S(1)}, bf16[64,8192]{1,0:T(8,128)(2,1)}, u32[]{:S(2)}) copy-start(bf16[64,8192]{1,0:T(8,128)(2,1)} %refs_3_.1) | copy-start | bytes 3145732
  13.2 35.6 %copy-start.2 = (bf16[64,2048]{1,0:T(8,128)(2,1)S(1)}, bf16[64,2048]{1,0:T(8,128)(2,1)}, u32[]{:S(2)}) copy-start(bf16[64,2048]{1,0:T(8,128)(2,1)} %refs_2_.3) | copy-start | bytes 786436
  43.5 143.8 %all-gather.5.cloned.1.call-start = ((), (), s32[]{:S(2)}) async-start(), calls=%async_computation.4 | async-start | bytes 3932160 | tf_op jit(solution)/shard_map/all_gather | solution.py:590
  44.2 238.2 %all-gather.9.cloned.1.call-start = ((), (), s32[]{:S(2)}) async-start(), calls=%async_computation.6 | async-start | bytes 1310720 | tf_op jit(solution)/shard_map/all_gather | solution.py:590
  48.9 99.1 %copy-start.23 = (s32[2,1024]{1,0:T(2,128)S(1)}, s32[2,1024]{1,0:T(2,128)}, u32[]{:S(2)}) copy-start(s32[2,1024]{1,0:T(2,128)} %param.16) | copy-start | bytes 24580
  147.9 157.9 %all-gather.11.cloned.1.call-start = ((), (), s32[]{:S(2)}) async-start(), calls=%async_computation.7 | async-start | bytes 5242880 | tf_op jit(solution)/shard_map/all_gather | solution.py:590
  148.0 3.7 collective-permute-start
  149.2 456.1 %reduce-scatter.7.cloned.1.call-start = ((), (), s32[]{:S(2)}) async-start(), calls=%async_computation.9 | async-start | bytes 1310720 | tf_op jit(solution)/shard_map/reduce_scatter | solution.py:673
  151.8 89.9 %collective-permute-start.1 = (bf16[2,256,2048]{2,1,0:T(8,128)(2,1)}, bf16[2,256,2048]{2,1,0:T(8,128)(2,1)}, u32[]{:S(2)}, u32[]{:S(2)}) collective-permute-start(bf16[2,256,2048]{2,1,0:T(8,128)(2,1)} %param.17), channel_id=1, source_target_pairs={{0,2},{1,3},{2,0},{3,1},{4,6},{5,7},{6,4},{7,5},{8,10},{9,11},{10,... | collective-permute-start | bytes 6291464 | tf_op jit(solution)/shard_map/ppermute | solution.py:550
  152.5 89.1 %collective-permute-start.2 = (bf16[2,256,2048]{2,1,0:T(8,128)(2,1)}, bf16[2,256,2048]{2,1,0:T(8,128)(2,1)}, u32[]{:S(2)}, u32[]{:S(2)}) collective-permute-start(bf16[2,256,2048]{2,1,0:T(8,128)(2,1)} %param.17), channel_id=1, source_target_pairs={{0,4},{1,5},{2,6},{3,7},{4,0},{5,1},{6,2},{7,3},{8,12},{9,13},{10,... | collective-permute-start | bytes 6291464 | tf_op jit(solution)/shard_map/ppermute | solution.py:550
  153.8 88.8 %collective-permute-start.3 = (bf16[2,256,2048]{2,1,0:T(8,128)(2,1)}, bf16[2,256,2048]{2,1,0:T(8,128)(2,1)}, u32[]{:S(2)}, u32[]{:S(2)}) collective-permute-start(bf16[2,256,2048]{2,1,0:T(8,128)(2,1)} %param.17), channel_id=1, source_target_pairs={{0,6},{1,7},{2,4},{3,5},{4,2},{5,3},{6,0},{7,1},{8,14},{9,15},{10,... | collective-permute-start | bytes 6291464 | tf_op jit(solution)/shard_map/ppermute | solution.py:550
  209.0 26.5 %copy-start.7 = (bf16[2048,768]{1,0:T(8,128)(2,1)S(1)}, bf16[2048,768]{1,0:T(8,128)(2,1)}, u32[]{:S(2)}) copy-start(bf16[2048,768]{1,0:T(8,128)(2,1)} %all-gather.5.cloned.1.call-done) | copy-start | bytes 9437188
  242.6 6.8 collective-permute-start.4
  242.6 7.2 collective-permute-start.5
  243.1 9.6 %collective-permute-start.6 = (bf16[2,256,2048]{2,1,0:T(8,128)(2,1)}, bf16[2,256,2048]{2,1,0:T(8,128)(2,1)S(1)}, u32[]{:S(2)}, u32[]{:S(2)}) collective-permute-start(bf16[2,256,2048]{2,1,0:T(8,128)(2,1)} %collective-permute-done.2), channel_id=1, source_target_pairs={{0,1},{1,0},{2,3},{3,2},{4,5},{5,4},{6,7},{7,6},{8,9},{9,8},{10,11... | collective-permute-start | bytes 6291464 | tf_op jit(solution)/shard_map/ppermute | solution.py:553
  243.1 12.6 %collective-permute-start.7 = (bf16[2,256,2048]{2,1,0:T(8,128)(2,1)}, bf16[2,256,2048]{2,1,0:T(8,128)(2,1)S(1)}, u32[]{:S(2)}, u32[]{:S(2)}) collective-permute-start(bf16[2,256,2048]{2,1,0:T(8,128)(2,1)} %collective-permute-done.3), channel_id=1, source_target_pairs={{0,1},{1,0},{2,3},{3,2},{4,5},{5,4},{6,7},{7,6},{8,9},{9,8},{10,11... | collective-permute-start | bytes 6291464 | tf_op jit(solution)/shard_map/ppermute | solution.py:553
  249.4 12.3 %slice-start = ((s8[8388608]{0:T(1024)(128)(4,1)}), s8[4194304]{0:T(1024)(128)(4,1)S(1)}, s32[]{:S(2)}) async-start(s8[8388608]{0:T(1024)(128)(4,1)} %bitcast.126), calls=%async_computation.12 | async-start | bytes 8388608
  250.0 11.8 %slice-start.1 = ((s8[8388608]{0:T(1024)(128)(4,1)}), s8[4194304]{0:T(1024)(128)(4,1)S(1)}, s32[]{:S(2)}) async-start(s8[8388608]{0:T(1024)(128)(4,1)} %bitcast.126), calls=%async_computation.13 | async-start | bytes 8388608
  256.0 5.8 copy-start.16
  282.4 12.1 %copy-start.17 = (bf16[8,2,256,2048]{3,2,1,0:T(8,128)(2,1)S(1)}, bf16[8,2,256,2048]{3,2,1,0:T(8,128)(2,1)}, u32[]{:S(2)}) copy-start(bf16[8,2,256,2048]{3,2,1,0:T(8,128)(2,1)} %copy-done.16) | copy-start | bytes 50331652
  282.4 12.1 %copy-start.32 = (bf16[2,2,2,2,256,256]{5,4,3,2,1,0:T(8,128)(2,1)S(1)}, bf16[2,2,2,2,256,256]{5,4,3,2,1,0:T(8,128)(2,1)}, u32[]{:S(2)}) copy-start(bf16[2,2,2,2,256,256]{5,4,3,2,1,0:T(8,128)(2,1)} %get-tuple-element.96) | copy-start | bytes 6291460
  300.5 304.9 %reduce-scatter.5.cloned.1.call-start = ((), (), s32[]{:S(2)}) async-start(), calls=%async_computation.8 | async-start | bytes 5242880 | tf_op jit(solution)/shard_map/reduce_scatter | solution.py:673
  301.0 310.7 %reduce-scatter.9.cloned.1.call-start = ((), (), s32[]{:S(2)}) async-start(), calls=%async_computation.10 | async-start | bytes 3932160 | tf_op jit(solution)/shard_map/reduce_scatter | solution.py:673
  385.9 307.8 %reduce-scatter.11.cloned.1.call-start = ((), (), s32[]{:S(2)}) async-start(), calls=%async_computation.11 | async-start | bytes 5242880 | tf_op jit(solution)/shard_map/reduce_scatter | solution.py:673
  434.4 33.6 %collective-permute-start.11 = (bf16[2,256,1024]{2,1,0:T(8,128)(2,1)}, bf16[2,256,1024]{2,1,0:T(8,128)(2,1)S(1)}, u32[]{:S(2)}, u32[]{:S(2)}) collective-permute-start(bf16[2,256,1024]{2,1,0:T(8,128)(2,1)} %bitcast.119), channel_id=1, source_target_pairs={{0,2},{1,3},{2,0},{3,1},{4,6},{5,7},{6,4},{7,5},{8,10},{9,11},{10,... | collective-permute-start | bytes 3145736 | tf_op jit(solution)/shard_map/ppermute | solution.py:560
  459.5 143.6 %collective-permute-start.10 = (bf16[2,256,2048]{2,1,0:T(8,128)(2,1)}, bf16[2,256,2048]{2,1,0:T(8,128)(2,1)}, u32[]{:S(2)}, u32[]{:S(2)}) collective-permute-start(bf16[2,256,2048]{2,1,0:T(8,128)(2,1)} %bitcast.116), channel_id=1, source_target_pairs={{0,6},{1,7},{2,4},{3,5},{4,2},{5,3},{6,0},{7,1},{8,14},{9,15},{10,... | collective-permute-start | bytes 6291464 | tf_op jit(solution)/shard_map/ppermute | solution.py:560
  460.5 144.9 %collective-permute-start.8 = (bf16[2,256,2048]{2,1,0:T(8,128)(2,1)}, bf16[2,256,2048]{2,1,0:T(8,128)(2,1)}, u32[]{:S(2)}, u32[]{:S(2)}) collective-permute-start(bf16[2,256,2048]{2,1,0:T(8,128)(2,1)} %bitcast.115), channel_id=1, source_target_pairs={{0,2},{1,3},{2,0},{3,1},{4,6},{5,7},{6,4},{7,5},{8,10},{9,11},{10,... | collective-permute-start | bytes 6291464 | tf_op jit(solution)/shard_map/ppermute | solution.py:560
  461.6 143.7 %collective-permute-start.9 = (bf16[2,256,2048]{2,1,0:T(8,128)(2,1)}, bf16[2,256,2048]{2,1,0:T(8,128)(2,1)}, u32[]{:S(2)}, u32[]{:S(2)}) collective-permute-start(bf16[2,256,2048]{2,1,0:T(8,128)(2,1)} %bitcast.114), channel_id=1, source_target_pairs={{0,4},{1,5},{2,6},{3,7},{4,0},{5,1},{6,2},{7,3},{8,12},{9,13},{10,... | collective-permute-start | bytes 6291464 | tf_op jit(solution)/shard_map/ppermute | solution.py:560
  466.8 131.3 %collective-permute-start.12 = (bf16[2,256,1024]{2,1,0:T(8,128)(2,1)}, bf16[2,256,1024]{2,1,0:T(8,128)(2,1)}, u32[]{:S(2)}, u32[]{:S(2)}) collective-permute-start(bf16[2,256,1024]{2,1,0:T(8,128)(2,1)} %bitcast.33), channel_id=1, source_target_pairs={{0,4},{1,5},{2,6},{3,7},{4,0},{5,1},{6,2},{7,3},{8,12},{9,13},{10,... | collective-permute-start | bytes 3145736 | tf_op jit(solution)/shard_map/ppermute | solution.py:560
  468.1 131.0 %collective-permute-start.13 = (bf16[2,256,1024]{2,1,0:T(8,128)(2,1)}, bf16[2,256,1024]{2,1,0:T(8,128)(2,1)}, u32[]{:S(2)}, u32[]{:S(2)}) collective-permute-start(bf16[2,256,1024]{2,1,0:T(8,128)(2,1)} %bitcast.34), channel_id=1, source_target_pairs={{0,6},{1,7},{2,4},{3,5},{4,2},{5,3},{6,0},{7,1},{8,14},{9,15},{10,... | collective-permute-start | bytes 3145736 | tf_op jit(solution)/shard_map/ppermute | solution.py:560
  469.9 129.5 %copy-start.10 = (bf16[512,1024]{1,0:T(8,128)(2,1)S(1)}, bf16[512,1024]{1,0:T(8,128)(2,1)}, u32[]{:S(2)}) copy-start(bf16[512,1024]{1,0:T(8,128)(2,1)} %get-tuple-element.141) | copy-start | bytes 3145732
  598.1 78.9 %collective-permute-start.14 = (bf16[2,256,1024]{2,1,0:T(8,128)(2,1)}, bf16[2,256,1024]{2,1,0:T(8,128)(2,1)}, u32[]{:S(2)}, u32[]{:S(2)}) collective-permute-start(bf16[2,256,1024]{2,1,0:T(8,128)(2,1)} %bitcast.118), channel_id=1, source_target_pairs={{0,2},{1,3},{2,0},{3,1},{4,6},{5,7},{6,4},{7,5},{8,10},{9,11},{10,... | collective-permute-start | bytes 3145736 | tf_op jit(solution)/shard_map/ppermute | solution.py:560
  599.1 78.0 %collective-permute-start.15 = (bf16[2,256,1024]{2,1,0:T(8,128)(2,1)}, bf16[2,256,1024]{2,1,0:T(8,128)(2,1)}, u32[]{:S(2)}, u32[]{:S(2)}) collective-permute-start(bf16[2,256,1024]{2,1,0:T(8,128)(2,1)} %bitcast.117), channel_id=1, source_target_pairs={{0,4},{1,5},{2,6},{3,7},{4,0},{5,1},{6,2},{7,3},{8,12},{9,13},{10,... | collective-permute-start | bytes 3145736 | tf_op jit(solution)/shard_map/ppermute | solution.py:560
  603.2 73.9 %collective-permute-start.16 = (bf16[2,256,1024]{2,1,0:T(8,128)(2,1)}, bf16[2,256,1024]{2,1,0:T(8,128)(2,1)}, u32[]{:S(2)}, u32[]{:S(2)}) collective-permute-start(bf16[2,256,1024]{2,1,0:T(8,128)(2,1)} %bitcast.38), channel_id=1, source_target_pairs={{0,6},{1,7},{2,4},{3,5},{4,2},{5,3},{6,0},{7,1},{8,14},{9,15},{10,... | collective-permute-start | bytes 3145736 | tf_op jit(solution)/shard_map/ppermute | solution.py:560
  673.9 8.7 %copy-start.15 = (bf16[64,2048]{1,0:T(8,128)(2,1)S(1)}, bf16[64,2048]{1,0:T(8,128)(2,1)}, u32[]{:S(2)}) copy-start(bf16[64,2048]{1,0:T(8,128)(2,1)} %get-tuple-element.154) | copy-start | bytes 786436
  675.2 11.5 %copy-start.9 = (bf16[512,1024]{1,0:T(8,128)(2,1)S(1)}, bf16[512,1024]{1,0:T(8,128)(2,1)}, u32[]{:S(2)}) copy-start(bf16[512,1024]{1,0:T(8,128)(2,1)} %get-tuple-element.131) | copy-start | bytes 3145732
  682.6 6.5 copy-start.3
  682.7 32.2 %copy-start.33 = (f32[64]{0:T(128)}, f32[64]{0:T(128)S(1)}, u32[]{:S(2)}) copy-start(f32[64]{0:T(128)S(1)} %fusion.26) | copy-start | bytes 772
  693.6 15.0 %copy-start.8 = (bf16[64,8192]{1,0:T(8,128)(2,1)S(1)}, bf16[64,8192]{1,0:T(8,128)(2,1)}, u32[]{:S(2)}) copy-start(bf16[64,8192]{1,0:T(8,128)(2,1)} %refs_1_.1) | copy-start | bytes 3145732
  693.6 15.0 %copy-start.19 = (f32[1,8,8,128]{3,1,2,0:T(8,128)S(1)}, f32[1,8,8,128]{3,1,2,0:T(8,128)}, u32[]{:S(2)}) copy-start(f32[1,8,8,128]{3,1,2,0:T(8,128)} %copy.40) | copy-start | bytes 98308
  693.6 15.1 %copy-start.30 = (f32[64]{0:T(128)S(1)}, f32[64]{0:T(128)}, u32[]{:S(2)}) copy-start(f32[64]{0:T(128)} %convert_element_type.152) | copy-start | bytes 772
  693.6 15.1 %copy-start.31 = (f32[64]{0:T(128)S(1)}, f32[64]{0:T(128)}, u32[]{:S(2)}) copy-start(f32[64]{0:T(128)} %convert_element_type.154) | copy-start | bytes 772
  708.6 4.0 copy-start.12
  708.6 4.0 copy-start.13
  708.6 4.0 copy-start.20
  708.7 4.0 copy-start.28
  (13 other events, 27.8 us)
Sparse Core Ops, SparseCore 0:
  43.6 79.8 all-gather.6
  125.0 62.0 all-gather.4
  188.7 26.6 all-gather.8
  216.7 80.1 all-gather.10
  300.6 25.3 reduce-scatter.6
  328.1 75.3 reduce-scatter.4
  405.7 60.9 reduce-scatter.8
  469.0 76.6 reduce-scatter.10

commit v4 on v3

--- a/solution.py
+++ b/solution.py
@@ -117,7 +117,24 @@
     return [jax.ShapeDtypeStruct((lay.group * rows, parts * cols), BF16) for parts, rows, cols in plan]
 
 
-def exchange_kernel(lay, plan, back, *refs):
+def device_after(lay, rank, k):
+    peer = lax.rem(rank + k, lay.count)
+    inner = lax.rem(peer, lay.group)
+    return (peer // lay.group, inner // lay.seq, lax.rem(inner, lay.seq))
+
+
+def barrier_all(lay, device_of):
+    barrier = pltpu.get_barrier_semaphore()
+
+    def greet(k, carry):
+        pl.semaphore_signal(barrier, inc=1, device_id=device_of(k), device_id_type=MESH)
+        return carry
+
+    lax.fori_loop(1, lay.count, greet, 0)
+    pl.semaphore_wait(barrier, lay.count - 1)
+
+
+def exchange_kernel(lay, plan, *refs):
     n = len(plan)
     vec_ref, sources = refs[0], refs[1 : 1 + n]
     all_ref, targets = refs[1 + n], refs[2 + n : 2 + 2 * n]
@@ -126,21 +143,10 @@
     me = lax.axis_index("yi") * lay.seq + lax.axis_index("seq")
     rank = zo * lay.group + me
 
-    def device_of(k):
-        peer = lax.rem(rank + k, lay.count)
-        inner = lax.rem(peer, lay.group)
-        return (peer // lay.group, inner // lay.seq, lax.rem(inner, lay.seq))
-
-    barrier = pltpu.get_barrier_semaphore()
-
-    def greet(k, carry):
-        pl.semaphore_signal(barrier, inc=1, device_id=device_of(k), device_id_type=MESH)
-        return carry
-
-    lax.fori_loop(1, lay.count, greet, 0)
-    pl.semaphore_wait(barrier, lay.count - 1)
-    copies = swap_copies(lay, plan, me, sources, targets, send, recv, back)
-    mine = swap_own(lay, plan, me, sources, targets, own, back)
+    device_of = functools.partial(device_after, lay, rank)
+    barrier_all(lay, device_of)
+    copies = swap_copies(lay, plan, me, sources, targets, send, recv, True)
+    mine = swap_own(lay, plan, me, sources, targets, own, True)
     mine.append(pltpu.make_async_copy(vec_ref, all_ref.at[rank], vec_own))
 
     def vec_copy(k):
@@ -166,11 +172,11 @@
     return pl.CostEstimate(flops=int(7e8 * microseconds), bytes_accessed=1 << 20, transcendentals=0)
 
 
-def exchange(lay, plan, vec, arrays, back, number, time):
+def exchange(lay, plan, vec, arrays, number, time):
     count = sum(parts for parts, _, _ in plan)
     return pl.pallas_call(
-        functools.partial(exchange_kernel, lay, plan, back),
-        out_shape=[jax.ShapeDtypeStruct((lay.count, *vec.shape), F32), *swap_shapes(lay, plan, back)],
+        functools.partial(exchange_kernel, lay, plan),
+        out_shape=[jax.ShapeDtypeStruct((lay.count, *vec.shape), F32), *swap_shapes(lay, plan, True)],
         in_specs=[ANY] * (1 + len(plan)),
         out_specs=[ANY] * (1 + len(plan)),
         scratch_shapes=[
@@ -188,10 +194,11 @@
 
 def norm_kernel(lay, plan, *refs):
     n = len(plan)
-    x_ref, gain_ref, sources = refs[0], refs[1], refs[2 : 2 + n]
-    one_ref, two_ref, hat_ref, targets = *refs[2 + n : 5 + n], refs[5 + n : 5 + 2 * n]
-    held, stage, send, recv, core_send, core_recv, w_send, w_recv, w_own, own_sem, out_sem = refs[5 + 2 * n :]
-    batch, length, _ = x_ref.shape
+    x_ref, vec_ref, sources = refs[0], refs[1], refs[2 : 2 + n]
+    one_ref, two_ref, hat_ref, all_ref, targets = *refs[2 + n : 6 + n], refs[6 + n : 6 + 2 * n]
+    (held, stage, vectors, gain_buf, send, recv, core_send, core_recv, w_send, w_recv, w_own, own_sem, out_sem,
+     vec_send, vec_recv, vec_own) = refs[6 + 2 * n :]
+    batch, length, width = x_ref.shape
     zo, yi, s = lax.axis_index("zo"), lax.axis_index("yi"), lax.axis_index("seq")
     me = yi * lay.seq + s
     x, core = s // 2, lax.rem(s, 2)
@@ -200,7 +207,24 @@
     def chip(ry, rx):
         return (zo, lax.rem(yi + ry, lay.sub), lax.rem(x + rx, lay.chips_x) * 2 + core)
 
-    group_barrier(lay, me)
+    rank = zo * lay.group + me
+    device_of = functools.partial(device_after, lay, rank)
+    barrier_all(lay, device_of)
+
+    def vec_copy(k):
+        return remote(vec_ref, vectors.at[rank], vec_send.at[k - 1], vec_recv.at[k - 1], device_of(k))
+
+    def vec_start(k, carry):
+        vec_copy(k).start()
+        return carry
+
+    def vec_finish(k, carry):
+        vec_copy(k).wait()
+        return carry
+
+    lax.fori_loop(1, lay.count, vec_start, 0)
+    vec_mine = pltpu.make_async_copy(vec_ref, vectors.at[rank], vec_own.at[0])
+    vec_mine.start()
     slot = {offset: i for i, offset in enumerate(lay.offsets)}
     own_copy = pltpu.make_async_copy(x_ref, held.at[0, 0], own_sem)
     own_copy.start()
@@ -226,7 +250,23 @@
     to_partner[(0, 0)].start()
     swaps = swap_copies(lay, plan, me, sources, targets, w_send, w_recv, False)
     swaps += swap_own(lay, plan, me, sources, targets, w_own, False)
-    gains = [gain_ref[i : i + 1, :] for i in range(4)]
+    lax.fori_loop(1, lay.count, vec_finish, 0)
+    vec_mine.wait()
+    vec_out = pltpu.make_async_copy(vectors, all_ref, vec_own.at[1])
+    vec_out.start()
+    size = width // lay.count
+    lane = lax.broadcasted_iota(jnp.int32, (1, 128), 1)
+    for v in range(4):
+        row, low = (v * size) // 128, (v * size) % 128
+        for k in range(width // 128):
+            line = None
+            for j in range(128 // size):
+                piece = vectors[k * (128 // size) + j, row : row + 1, :]
+                turn = (j * size - low) % 128
+                piece = pltpu.roll(piece, turn, 1) if turn else piece
+                line = piece if line is None else jnp.where(lane >= j * size, piece, line)
+            gain_buf[v : v + 1, k * 128 : (k + 1) * 128] = line
+    gains = [gain_buf[i : i + 1, :] for i in range(4)]
     rows = 16
     pending = [[], []]
     turn = [0]
@@ -243,8 +283,8 @@
                 value = held[c, j, m, at, :].astype(F32)
                 center = value - jnp.mean(value, -1, keepdims=True)
                 hat = center * lax.rsqrt(jnp.mean(center * center, -1, keepdims=True) + EPSILON)
-                stage[k, 0, at, :] = (hat * gains[0] + gains[1]).astype(BF16)
-                stage[k, 1, at, :] = (hat * gains[2] + gains[3]).astype(BF16)
+                stage[k, 0, at, :] = (hat * gains[2] + gains[0]).astype(BF16)
+                stage[k, 1, at, :] = (hat * gains[3] + gains[1]).astype(BF16)
                 stage[k, 2, at, :] = hat.astype(BF16)
                 return carry
 
@@ -293,20 +333,23 @@
         to_partner[o].wait_send()
     for copy in swaps:
         copy.wait()
-
-
-def norm_exchange(lay, plan, tokens, gains, weights):
+    vec_out.wait()
+
+
+def norm_exchange(lay, plan, tokens, vec, weights):
     count = sum(parts for parts, _, _ in plan)
     chips = lay.group // 2
     whole = jax.ShapeDtypeStruct((2, chips, *tokens.shape), BF16)
     return pl.pallas_call(
         functools.partial(norm_kernel, lay, plan),
-        out_shape=[whole] * 3 + swap_shapes(lay, plan, False),
-        in_specs=[ANY, pl.BlockSpec(memory_space=pltpu.VMEM)] + [ANY] * len(plan),
-        out_specs=[ANY] * (3 + len(plan)),
+        out_shape=[whole] * 3 + [jax.ShapeDtypeStruct((lay.count, *vec.shape), F32)] + swap_shapes(lay, plan, False),
+        in_specs=[ANY] * (2 + len(plan)),
+        out_specs=[ANY] * (4 + len(plan)),
         scratch_shapes=[
             pltpu.VMEM((2, chips, *tokens.shape), BF16),
             pltpu.VMEM((2, 3, *tokens.shape[1:]), BF16),
+            pltpu.VMEM((lay.count, *vec.shape), F32),
+            pltpu.VMEM((4, tokens.shape[2]), F32),
             pltpu.SemaphoreType.DMA((chips, 2)),
             pltpu.SemaphoreType.DMA((chips, 2)),
             pltpu.SemaphoreType.DMA((chips,)),
@@ -316,34 +359,37 @@
             pltpu.SemaphoreType.DMA((count,)),
             pltpu.SemaphoreType.DMA,
             pltpu.SemaphoreType.DMA((2, 3)),
+            pltpu.SemaphoreType.DMA((lay.count - 1,)),
+            pltpu.SemaphoreType.DMA((lay.count - 1,)),
+            pltpu.SemaphoreType.DMA((2,)),
         ],
         compiler_params=pltpu.CompilerParams(
             collective_id=1, has_side_effects=True, vmem_limit_bytes=48 << 20
         ),
         cost_estimate=busy(100),
         name="norm_exchange",
-    )(tokens, gains, *weights)
-
-
-def deal_kernel(lay, plan, *refs):
+    )(tokens, vec, *weights)
+
+
+def deal_kernel(lay, plan, back, *refs):
     n = len(plan)
     sources, targets = refs[:n], refs[n : 2 * n]
     send, recv, own = refs[2 * n :]
     me = lax.axis_index("yi") * lay.seq + lax.axis_index("seq")
     group_barrier(lay, me)
-    copies = swap_copies(lay, plan, me, sources, targets, send, recv, True)
-    copies += swap_own(lay, plan, me, sources, targets, own, True)
+    copies = swap_copies(lay, plan, me, sources, targets, send, recv, back)
+    copies += swap_own(lay, plan, me, sources, targets, own, back)
     for copy in copies:
         copy.start()
     for copy in copies:
         copy.wait()
 
 
-def deal_exchange(lay, plan, sums, number):
+def deal_exchange(lay, plan, arrays, back, number):
     count = sum(parts for parts, _, _ in plan)
     return pl.pallas_call(
-        functools.partial(deal_kernel, lay, plan),
-        out_shape=swap_shapes(lay, plan, True),
+        functools.partial(deal_kernel, lay, plan, back),
+        out_shape=swap_shapes(lay, plan, back),
         in_specs=[ANY] * len(plan),
         out_specs=[ANY] * len(plan),
         scratch_shapes=[
@@ -353,21 +399,28 @@
         ],
         compiler_params=pltpu.CompilerParams(collective_id=number, has_side_effects=True),
         cost_estimate=busy(17),
-    )(*sums)
+    )(*arrays)
 
 
 def pair_kernel(lay, first_ref, first_w, second_ref, second_w, *refs):
     step = pl.program_id(0)
     chips = lay.group // 2
-    outs, (given, came, send, recv, out_sem) = refs[:chips], refs[chips:]
+    (given, came, send, recv, out_sem), outs = refs[-5:], refs[:-5]
+    batch = len(outs) // chips
     zo, yi, s = lax.axis_index("zo"), lax.axis_index("yi"), lax.axis_index("seq")
     partner = (zo, yi, (s // 2) * 2 + 1 - lax.rem(s, 2))
 
     def copy(j):
         return remote(given.at[j], came.at[j], send.at[j], recv.at[j], partner)
 
-    def store(j):
-        return pltpu.make_async_copy(came.at[j], outs[(j + 1) % chips], out_sem.at[j])
+    def stores(j):
+        length = came.shape[1] // batch
+        return [
+            pltpu.make_async_copy(
+                came.at[j, pl.ds(m * length, length)], outs[(j + 1) % chips * batch + m], out_sem.at[j, m]
+            )
+            for m in range(batch)
+        ]
 
     @pl.when(step == 0)
     def _():
@@ -397,17 +450,20 @@
 
         @pl.when(step == chips + j + 1)
         def _():
-            store(j).start()
+            for piece in stores(j):
+                piece.start()
 
     @pl.when(step == 2 * chips - 1)
     def _():
-        store(chips - 1).start()
+        for piece in stores(chips - 1):
+            piece.start()
         for j in range(chips):
             copy(j).wait_send()
-            store(j).wait()
-
-
-def pair_matmul(lay, first, first_w, second, second_w, cut, number):
+            for piece in stores(j):
+                piece.wait()
+
+
+def pair_matmul(lay, first, first_w, second, second_w, batch, cut, number):
     chips = lay.group // 2
     rows = first.shape[0] // lay.group
     width = first_w.shape[0] // cut[1]
@@ -424,14 +480,14 @@
         functools.partial(pair_kernel, lay),
         grid=(2 * chips,),
         in_specs=[act(depth1), weight(depth1), act(depth2), weight(depth2)],
-        out_specs=[ANY] * chips,
-        out_shape=[jax.ShapeDtypeStruct((rows, width), BF16)] * chips,
+        out_specs=[ANY] * (chips * batch),
+        out_shape=[jax.ShapeDtypeStruct((rows // batch, width), BF16)] * (chips * batch),
         scratch_shapes=[
             pltpu.VMEM((chips, rows, width), BF16),
             pltpu.VMEM((chips, rows, width), BF16),
             pltpu.SemaphoreType.DMA((chips,)),
             pltpu.SemaphoreType.DMA((chips,)),
-            pltpu.SemaphoreType.DMA((chips,)),
+            pltpu.SemaphoreType.DMA((chips, batch)),
         ],
         compiler_params=pltpu.CompilerParams(
             collective_id=number, has_side_effects=True, vmem_limit_bytes=60 << 20
@@ -546,25 +602,45 @@
 def make_body(lay):
     sub, seq, group, chips_x = lay.sub, lay.seq, lay.group, lay.chips_x
 
-    def gather_near(value):
-        return [value if o == (0, 0) else lax.ppermute(value, GROUP, lay.shift(*o)) for o in lay.offsets]
-
-    def gather_partner(near):
-        partner = [lax.ppermute(piece, "seq", lay.flip()) for piece in near]
-        return jnp.concatenate([piece[None] for piece in near + partner], 0)
-
-    def send_far(pieces):
-        came = [pieces[0]]
-        for o, piece in zip(lay.offsets[1:], pieces[1:], strict=True):
-            back = ((-o[0]) % sub, (-o[1]) % chips_x)
-            came.append(lax.ppermute(piece, GROUP, lay.shift(*back)))
-        return came
-
-    def add_all(pieces):
+    square = sub == 2 and chips_x == 2
+
+    def across(value, o):
+        return lax.ppermute(value, GROUP, lay.shift(*o))
+
+    def partners(pieces):
+        return [lax.ppermute(piece, "seq", lay.flip()) for piece in pieces]
+
+    def add(*pieces):
         total = pieces[0].astype(F32)
         for piece in pieces[1:]:
             total = total + piece.astype(F32)
         return total
+
+    def far_first(pieces):
+        if square:
+            return [
+                [across(pieces[2][0], (1, 0)), across(pieces[3][0], (1, 0))],
+                [across(pieces[1][1], (0, 1)), across(pieces[3][1], (0, 1))],
+            ]
+        batch = len(pieces[0])
+        return [
+            [across(pieces[i][m], ((-o[0]) % sub, (-o[1]) % chips_x)) for i, o in enumerate(lay.offsets) if i]
+            for m in range(batch)
+        ]
+
+    def far_onward(pieces, came):
+        if square:
+            return [add(pieces[1][0], came[0][1]).astype(BF16), add(pieces[2][1], came[1][1]).astype(BF16)]
+        return []
+
+    def far_second(pieces, came, onward):
+        if square:
+            last = [across(onward[0], (0, 1)), across(onward[1], (1, 0))]
+            return [[pieces[0][m], came[m][0], last[m]] for m in range(2)]
+        return [[pieces[0][m], *came[m]] for m in range(len(came))]
+
+    def add_all(parts):
+        return jnp.stack([add(*pieces) for pieces in parts])
 
     def after(value, *tokens):
         return lax.optimization_barrier((value, *tokens))[0]
@@ -599,41 +675,42 @@
             order = [((x - rx) % chips_x) * 2 + (core + rc) % 2 for rc in range(2) for rx in range(chips_x)]
             places.append(jnp.concatenate([lax.dynamic_slice_in_dim(blocks, o, 1, 1) for o in order], 1))
         places = jnp.stack(places).reshape(sub * batch, count)
+
+        def laid(values):
+            size = -(-sum(v.size for v in values) // 1024) * 1024
+            whole, at = 0.0, 0
+            for v in values:
+                whole = whole + jnp.pad(v.astype(F32), (at, size - at - v.size))
+                at += v.size
+            return whole.reshape(-1, 128)
+
         names = (bias1, bias2, gain1, gain2, b_qkv, b_up, b_out, b_down)
-        vec = jnp.concatenate([v.astype(F32) for v in names])
-        size = -(-vec.shape[0] // 1024) * 1024
-        vec = jnp.pad(vec, (0, size - vec.shape[0])).reshape(-1, 128)
-        vectors, up_own, qkv_own = exchange(lay, [plans["up"], plans["qkv"]], vec, [w_up, w_qkv], False, 0, 30)
+        (qkv_own,) = deal_exchange(lay, [plans["qkv"]], [w_qkv], False, 0)
+        qkv_w = gather_rows(qkv_own)
+        w_up_late, _ = lax.optimization_barrier((w_up, qkv_own))
+        (up_own,) = deal_exchange(lay, [plans["up"]], [w_up_late], False, 7)
         up_w = gather_rows(up_own)
-        qkv_w = gather_rows(qkv_own)
+        tokens_late, _ = lax.optimization_barrier((tokens, up_own))
+        one, two, hat, vectors, out_own, down_own = norm_exchange(
+            lay, [plans["out"], plans["down"]], tokens_late, laid(names), [w_out, w_down]
+        )
+        out_w = gather_rows(out_own)
+        down_w = gather_rows(down_own)
         vectors = vectors.reshape(lay.count, -1)
         cuts = []
         at = 0
         for piece in names:
             cuts.append(vectors[:, at : at + piece.shape[0]].reshape(-1))
             at += piece.shape[0]
-        bias1_all, bias2_all, gain1_all, gain2_all, b_qkv_all, b_up_all, b_out_all, b_down_all = cuts
+        _, _, gain1_all, gain2_all, b_qkv_all, b_up_all, b_out_all, b_down_all = cuts
         b_qkv_mine = lax.dynamic_index_in_dim(b_qkv_all.reshape(3, group, cols), me, 1, keepdims=False).reshape(-1)
         b_up_mine = lax.dynamic_index_in_dim(b_up_all.reshape(group, ff_cols), me, 0, keepdims=False)
-        zeros = jnp.zeros_like(bias1_all)
-        gains = jnp.stack([gain1_all, bias1_all, gain2_all, bias2_all, zeros, zeros, zeros, zeros])
-        one, two, hat, out_own, down_own = norm_exchange(lay, [plans["out"], plans["down"]], tokens, gains, [w_out, w_down])
-        out_w = gather_rows(out_own)
-        down_w = gather_rows(down_own)
         one, two, hat = [v.reshape(total, width) for v in (one, two, hat)]
         cotangent, hat, places = lax.optimization_barrier((cotangent, hat, places))
-        near_dy = gather_near(cotangent)
-
-        hidden = dot(two, up_w, ((1,), (0,))) + b_up_mine
-        phi_cdf = 0.5 * (1.0 + lax.erf(hidden * math.sqrt(0.5)))
-        density = jnp.exp(-0.5 * hidden * hidden) * (1.0 / math.sqrt(2.0 * math.pi))
-        activated = (hidden * phi_cdf).astype(BF16)
-        slope = (phi_cdf + hidden * density).astype(BF16)
-        activated, slope = lax.optimization_barrier((activated, slope))
+        near_dy = [across(cotangent, o) for o in lay.offsets[1:] if not (square and o == (1, 1))]
 
         halves = ROTARY // 2
         frequency = jnp.exp(jnp.arange(halves, dtype=F32) * (-2.0 * math.log(10000.0) / ROTARY))
-        places = after(places, activated)
         phases = places.astype(F32)[:, None, :] * frequency[None, :, None]
         cosine, sine = jnp.cos(phases), jnp.sin(phases)
         place_col = places[:, :, None]
@@ -668,6 +745,18 @@
         )(packed.reshape(full), cosine, sine, place_col, place_row)
 
         context = context.reshape(total, cols)
+        two, *near_dy = lax.optimization_barrier((two, *near_dy, context))[:-1]
+        pieces = [cotangent, *near_dy]
+        early = partners(pieces)
+        if square:
+            halves_dy = [across(pieces[1][0], (1, 0)), across(pieces[2][1], (0, 1))]
+
+        hidden = dot(two, up_w, ((1,), (0,))) + b_up_mine
+        phi_cdf = 0.5 * (1.0 + lax.erf(hidden * math.sqrt(0.5)))
+        density = jnp.exp(-0.5 * hidden * hidden) * (1.0 / math.sqrt(2.0 * math.pi))
+        activated = (hidden * phi_cdf).astype(BF16)
+        slope = (phi_cdf + hidden * density).astype(BF16)
+        activated, slope = lax.optimization_barrier((activated, slope))
 
         def scatter(grad):
             return lax.psum_scatter(grad, "zo", scatter_dimension=0, tiled=True)
@@ -675,11 +764,16 @@
         def outer_dot(left, right):
             return dot(left, right, ((0,), (0,))).astype(BF16)
 
-        qkv_late, up_late = lax.optimization_barrier((qkv_w, up_w, context))[:-1]
+        qkv_late, up_late = lax.optimization_barrier((qkv_w, up_w, activated))[:-1]
         fold_qkv = (gain1_all[:, None] * qkv_late.astype(F32)).astype(BF16)
         fold_up = (gain2_all[:, None] * up_late.astype(F32)).astype(BF16)
-        near_dy = lax.optimization_barrier((*near_dy, fold_qkv, fold_up))[:-2]
-        upstream = gather_partner(list(near_dy)).reshape(total, width)
+        flat = lambda values: [v.reshape(-1, width) for v in values]
+        if square:
+            halves_dy = lax.optimization_barrier((*halves_dy, fold_qkv, fold_up))[:2]
+            rows_dy = flat(pieces) + flat(halves_dy) + flat(early) + flat(partners(halves_dy))
+        else:
+            rows_dy = flat(pieces) + flat(early)
+        upstream = jnp.concatenate(rows_dy, 0)
         down_part = outer_dot(upstream, activated)
         upstream = after(upstream, down_part)
         down_sum = scatter(down_part)
@@ -692,13 +786,13 @@
             return lax.optimization_barrier((*values, *tokens))[: len(values)]
 
         def tokens_of(pieces):
-            return [piece.reshape(batch, length, -1) for piece in pieces]
+            return [pieces[i * batch : (i + 1) * batch] for i in range(group // 2)]
 
         pair = chain((context, activated), out_part)
-        out_near = pair_matmul(lay, pair[0], out_w, pair[1], down_w, (0, 1), 4)
+        out_near = pair_matmul(lay, pair[0], out_w, pair[1], down_w, batch, (0, 1), 4)
         grad_context, *out_near = chain((grad_context, *out_near))
         out_near = tokens_of(out_near)
-        out_near = send_far(out_near)
+        out_came = far_first(out_near)
 
         grad_packed = pl.pallas_call(
             functools.partial(attend_back_kernel, scaling),
@@ -715,39 +809,44 @@
 
         qkv_part = outer_dot(hat, grad_packed)
         qkv_sum = scatter(qkv_part)
-        (upstream,) = chain((upstream,), qkv_part)
+        out_came, upstream = chain((out_came, upstream), qkv_part)
+        onward, upstream = chain((far_onward(out_near, out_came), upstream))
+        out_parts = far_second(out_near, out_came, onward)
         grad_hidden = (dot(upstream, down_w, ((1,), (0,))) * slope.astype(F32)).astype(BF16)
 
-        near = pair_matmul(lay, grad_packed, fold_qkv, grad_hidden, fold_up, (0, 2), 5)
-        hat, *near = chain((hat, *near))
-        came = [send_far(tokens_of(near))]
+        near0 = pair_matmul(lay, grad_packed, fold_qkv, grad_hidden, fold_up, batch, (0, 2), 5)
+        hat, near0 = chain((hat, near0))
+        near0 = tokens_of(near0)
+        came0 = far_first(near0)
         up_part = outer_dot(hat, grad_hidden)
         up_sum = scatter(up_part)
-        (left,) = chain((grad_packed,), up_part)
-        near = pair_matmul(lay, left, fold_qkv, grad_hidden, fold_up, (1, 2), 6)
-        came.append(send_far(tokens_of(near)))
+        came0, left = chain((came0, grad_packed), up_part)
+        onward, left = chain((far_onward(near0, came0), left))
+        parts0 = far_second(near0, came0, onward)
+        near1 = pair_matmul(lay, left, fold_qkv, grad_hidden, fold_up, batch, (1, 2), 6)
+        near1 = tokens_of(near1)
+        came1 = far_first(near1)
 
         own_sums = [
             jnp.sum(grad_packed.astype(F32), 0),
             jnp.sum(grad_hidden.astype(F32), 0),
             jnp.sum(cotangent.astype(F32), (0, 1)),
         ]
-        vec = jnp.concatenate(own_sums)
-        size = -(-vec.shape[0] // 1024) * 1024
-        vec = jnp.pad(vec, (0, size - vec.shape[0])).reshape(-1, 128)
-        out_near, vec, down_sum, out_w_sum = chain((out_near, vec, down_sum, out_w_sum), *near)
-        output = (tokens.astype(F32) + add_all(out_near) + b_out_all + b_down_all).astype(BF16)
-        vec, output = chain((vec, output))
+        out_parts, vec, down_sum, out_w_sum = chain((out_parts, laid(own_sums), down_sum, out_w_sum), near1)
+        output = (tokens.astype(F32) + add_all(out_parts) + b_out_all + b_down_all).astype(BF16)
+        came1, vec = chain((came1, vec), output)
+        onward, vec = chain((far_onward(near1, came1), vec))
+        parts1 = far_second(near1, came1, onward)
         everyone, down_raw, out_raw, qkv_raw = exchange(
-            lay, [plans["down"], plans["out"], plans["qkv"]], vec, [down_sum, out_w_sum, qkv_sum], True, 2, 40
+            lay, [plans["down"], plans["out"], plans["qkv"]], vec, [down_sum, out_w_sum, qkv_sum], 2, 40
         )
-        came[1] = chain(came[1], everyone)
+        (parts1,) = chain((parts1,), everyone)
 
         inputs = tokens.astype(F32)
         center = inputs - jnp.mean(inputs, -1, keepdims=True)
         inv_std = lax.rsqrt(jnp.mean(center * center, -1, keepdims=True) + EPSILON)
         normal = center * inv_std
-        grad_normal = jnp.concatenate([add_all(pieces) for pieces in came], -1)
+        grad_normal = jnp.concatenate([add_all(parts0), add_all(parts1)], -1)
         token_grad = cotangent.astype(F32) + inv_std * (
             grad_normal
             - jnp.mean(grad_normal, -1, keepdims=True)
@@ -755,7 +854,7 @@
         )
 
         rank = lax.axis_index("zo") * group + me
-        (up_raw,) = deal_exchange(lay, [plans["up"]], [up_sum], 3)
+        (up_raw,) = deal_exchange(lay, [plans["up"]], [up_sum], True, 3)
         sums = jnp.sum(everyone.reshape(lay.outer, group, -1), 0)
         sum_qkv = jnp.transpose(sums[:, : 3 * cols].reshape(group, 3, cols), (1, 0, 2)).reshape(-1)
         sum_up = sums[:, 3 * cols : 3 * cols + ff_cols].reshape(-1)

time: 728 us -> 636 us (0.87)
  waiting for transfers between devices: 114 us -> 18.7 us
  Pallas kernels: 339 us -> 316 us
  other arithmetic: 43.3 us -> 59.6 us
  starting transfers between devices: 16.8 us -> 25.6 us
    ppermute x16 -> x27, waiting for transfers between devices: 112 us -> 16.4 us  [the longest x22 16.4 us: across(): return lax.ppermute(value, GROUP, lay.shift(*o))]
    pallas_call x3 -> x4, Pallas kernels: 107 us -> 79.5 us  [the longest x3 42.9 us: deal_exchange(): pl.pallas_call(functools.partial(deal_kernel, lay, plan, back), out_shape...]
    convert_element_type x4 -> x10, other arithmetic: 2.05 us -> 13.7 us  [the longest x3 7.7 us: far_onward(): add(pieces[1][0], came[0][1]).astype(BF16)]
    another operation x0 -> x6, other arithmetic: none -> 10.9 us  [add_all(): return jnp.stack([add(*pieces) for pieces in parts])]
    unnamed x84 -> x122, local copies, waits for them, and re-layouts: 17.5 us -> 27.5 us
    ppermute x16 -> x27, starting transfers between devices: 15.2 us -> 23.8 us  [the longest x22 22.8 us: across(): return lax.ppermute(value, GROUP, lay.shift(*o))]
  transfers between devices with their start and end apart: 25 -> 36, of which waited for: 6 -> 4; matrix products, arithmetic and copies ran while one was open for 30% -> 38% of each run, Pallas kernels for 41% -> 46%
where the time goes in v4:
time: 636 us; the launch traced here: 631 us
  Pallas kernels  316 us (50%)
  matrix products  155 us (24%)
  other arithmetic  59.6 us (9%)
  local copies, waits for them, and re-layouts  40 us (6%)
  starting transfers between devices  25.6 us (4%)
  waiting for transfers between devices  18.7 us (3%)
  between operations  15.5 us (2%)
    dot_general x8, matrix products, dot(): lax.dot_general(left, right, (dims, ((), ())), preferred_element_type=F32)  155 us
    pallas_call x1, Pallas kernels, norm_exchange(): pl.pallas_call(functools.partial(norm_kernel, lay, plan), out_shape=[whol...  104 us
    pallas_call x3, Pallas kernels, pair_matmul(): pl.pallas_call(functools.partial(pair_kernel, lay), grid=(2 * chips,), in...  78 us
    pallas_call x3, Pallas kernels, deal_exchange(): pl.pallas_call(functools.partial(deal_kernel, lay, plan, back), out_shape...  42.9 us
    pallas_call x1, Pallas kernels, exchange(): pl.pallas_call(functools.partial(exchange_kernel, lay, plan), out_shape=[...  36.6 us
    pallas_call x1, Pallas kernels, step(): pl.pallas_call(functools.partial(attend_back_kernel, scaling), grid=(seqs...  28 us
    unnamed x122, local copies, waits for them, and re-layouts  27.5 us
    pallas_call x1, Pallas kernels, step(): pl.pallas_call(functools.partial(attend_kernel, scaling), grid=(seqs,), i...  26.3 us
  transfers between devices with their start and end apart: 36, of which 4 were waited for; matrix products, arithmetic and copies ran while one was open for 38% of the time, Pallas kernels for 46%

profile of v4, /device:TPU:0, one launch (start us, length us, event | category | flops | bytes accessed | tf_op | source)
XLA Modules:
  0.0 631.0 jit_solution(5598795910784269495)
XLA Ops:
  7.2 13.7 %shard_map.254 = bf16[512,768]{1,0:T(8,128)(2,1)} custom-call(bf16[64,6144]{1,0:T(8,128)(2,1)} %refs_0_.1), custom_call_target="tpu_custom_call" | custom-call | flops 11900000256 | bytes 1048576 | tf_op jit(solution)/shard_map/pallas_call | solution.py:390
  21.1 15.0 %shard_map.255 = bf16[512,1024]{1,0:T(8,128)(2,1)} custom-call(bf16[64,8192]{1,0:T(8,128)(2,1)} %refs_0_.2), custom_call_target="tpu_custom_call" | custom-call | flops 11900000256 | bytes 1048576 | tf_op jit(solution)/shard_map/pallas_call | solution.py:390
  37.4 104.5 %norm_exchange.1 = (bf16[2,4,2,256,2048]{4,3,2,1,0:T(8,128)(2,1)}, bf16[2,4,2,256,2048]{4,3,2,1,0:T(8,128)(2,1)}, bf16[2,4,2,256,2048]{4,3,2,1,0:T(8,128)(2,1)},...) custom-call(bf16[2,256,2048]{2,1,0:T(8,128)(2,1)S(1)} %copy-done, ...), custom_call_target="tpu_custom_call" | custom-call | flops 70000001024 | bytes 1048576 | tf_op jit(solution)/shard_map/norm_exchange/pallas_call | solution.py:343
  147.9 3.2 constant_dynamic-update-slice_fusion.9
  151.1 2.8 multiply_sine_fusion
  153.9 2.0 copy.31.col_ref
  155.8 19.4 %convolution_add_fusion = f32[4096,768]{1,0:T(8,128)} fusion(bf16[4096,2048]{1,0:T(8,128)(2,1)} %bitcast.103, bf16[2048,768]{1,0:T(8,128)(2,1)} %all-gather.5.cloned.1.call-done, f32[768]{0:T(1024)S(1)} %add.295), kind=kOutput, calls=%fused_computation.12 | convolution fusion | flops 12888047616 | bytes 32508928 | tf_op jit(solution)/shard_map/dot_general | solution.py:26
  175.2 26.3 %attend.1 = (bf16[4,1024,256]{2,1,0:T(8,128)(2,1)}, bf16[4,1024,256]{2,1,0:T(8,128)(2,1)}, bf16[4,1024,256]{2,1,0:T(8,128)(2,1)}, bf16[2,2,2,2,256,256]{5,4,3,2,1,0:T(8,128)(2,1)}, f32[4,1,1024]{2,1,0:T(1,128)}) custom-call(f32[2,2,2,2,256,768]{5,4,3,2,1,0:T(8,128)} %bitcast.104, f32[4,32,1024]{2,1,0:T(8,128)} %get-tuple-element.261.cos_ref, ...), custom_call_target="tpu_custom_call" | custom-call | flops 4294967296 | bytes 31457280 | tf_op jit(solution)/shard_map/attend/pallas_call | solution.py:735
  201.5 2.3 slice_bitcast_fusion.1
  204.3 2.4 slice_bitcast_fusion
  209.2 3.2 constant_dynamic-update-slice_fusion.8
  212.4 3.1 constant_dynamic-update-slice_fusion.7
  215.6 29.0 %fusion.4 = (bf16[4096,1024]{1,0:T(8,128)(2,1)}, bf16[4096,1024]{1,0:T(8,128)(2,1)}) fusion(f32[1024]{0:T(1024)S(1)} %bitcast.97, bf16[4096,2048]{1,0:T(8,128)(2,1)} %bitcast.102, bf16[2048,1024]{1,0:T(8,128)(2,1)} %all-gather.7.cloned.1.call-done), kind=kOutput, calls=%fused_computation.5 | convolution fusion | flops 17230200832 | bytes 37752832 | tf_op jit(solution)/shard_map/dot_general | solution.py:26
  244.5 2.2 multiply_convert_fusion.3.first_w
  247.9 2.8 multiply_convert_fusion.2.second_w
  252.6 2.0 constant_dynamic-update-slice_fusion.4
  256.5 2.0 constant_dynamic-update-slice_fusion.2
  258.7 5.8 copy-done.27
  264.5 20.9 %convolution_convert_fusion.2 = bf16[2048,1024]{1,0:T(8,128)(2,1)} fusion(bf16[4096,2048]{1,0:T(8,128)(2,1)S(1)} %constant_dynamic-update-slice_fusion, bf16[4096,1024]{1,0:T(8,128)(2,1)S(1)} %bitcast.107), kind=kOutput, calls=%fused_computation.33 | convolution fusion | flops 17181966336 | bytes 29360128 | tf_op jit(solution)/shard_map/dot_general | solution.py:26
  285.4 12.1 %convolution_convert_fusion = bf16[4096,256]{1,0:T(8,128)(2,1)} fusion(bf16[4096,2048]{1,0:T(8,128)(2,1)} %copy-done.27, bf16[2048,256]{1,0:T(8,128)(2,1)} %all-gather.9.cloned.1.call-done.first_w), kind=kOutput, calls=%fused_computation.19 | convolution fusion | flops 4296015872 | bytes 19922944 | tf_op jit(solution)/shard_map/dot_general | solution.py:26
  297.5 5.9 convolution_convert_fusion.4
  306.3 2.0 convert_reduce_fusion.3
  308.4 32.0 %shard_map.256 = (bf16[256,2048]{1,0:T(8,128)(2,1)}, bf16[256,2048]{1,0:T(8,128)(2,1)}, bf16[256,2048]{1,0:T(8,128)(2,1)}, bf16[256,2048]{1,0:T(8,128)(2,1)}, bf...) custom-call(bf16[2,4,512,256]{3,2,1,0:T(8,128)(2,1)} %bitcast.110, ...), custom_call_target="tpu_custom_call" | custom-call | flops 21474836480 | bytes 33554432 | tf_op jit(solution)/shard_map/pallas_call | solution.py:479
  344.5 28.0 %attend_back.1 = bf16[2,2,2,2,256,768]{5,4,3,2,1,0:T(8,128)(2,1)} custom-call(bf16[4,1024,256]{2,1,0:T(8,128)(2,1)} %get-tuple-element.167.q_ref, bf16[4,1024,256]{2,1,0:T(8,128)(2,1)} %get-tuple-element.168.k_ref, bf16[4,1024,256]{2,1,0:T(8,128)(2,1)} %get-tuple-element.169.v_ref, bf16[2,2,2,2,256,256]{5,4,3,2,1,0:T(8,128)(2,1)} %bitcast.112, ...), custom_call_target="tpu_custom_call" | custom-call | flops 10737418240 | bytes 25165824 | tf_op jit(solution)/shard_map/attend_back/pallas_call | solution.py:797
  372.5 20.4 %convolution_convert_fusion.3 = bf16[2048,768]{1,0:T(8,128)(2,1)} fusion(bf16[4096,2048]{1,0:T(8,128)(2,1)} %bitcast.100, bf16[4096,768]{1,0:T(8,128)(2,1)} %bitcast.83), kind=kOutput, calls=%fused_computation.34 | convolution fusion | flops 12886474752 | bytes 26214400 | tf_op jit(solution)/shard_map/dot_general | solution.py:26
  393.0 3.9 convert_reduce_fusion.1
  397.0 3.4 add_convert_fusion.1
  400.4 2.6 add_convert_fusion
  403.7 23.9 %convert_reduce_fusion = (f32[1024]{0:T(1024)S(1)}, bf16[4096,1024]{1,0:T(8,128)(2,1)}) fusion(bf16[4096,1024]{1,0:T(8,128)(2,1)} %get-tuple-element.183, bf16[4096,2048]{1,0:T(8,128)(2,1)} %copy-done.27, bf16[2048,1024]{1,0:T(8,128)(2,1)S(1)} %copy-done.45), kind=kOutput, calls=%fused_computation.6 | convolution fusion | flops 17200840704 | bytes 37752832 | tf_op jit(solution)/shard_map/dot_general | solution.py:26
  427.6 22.9 %shard_map.257 = (bf16[256,1024]{1,0:T(8,128)(2,1)}, bf16[256,1024]{1,0:T(8,128)(2,1)}, bf16[256,1024]{1,0:T(8,128)(2,1)}, bf16[256,1024]{1,0:T(8,128)(2,1)}, bf...) custom-call(bf16[2,4,512,768]{3,2,1,0:T(8,128)(2,1)} %bitcast.84, ...), custom_call_target="tpu_custom_call" | custom-call | flops 15032385536 | bytes 33554432 | tf_op jit(solution)/shard_map/pallas_call | solution.py:479
  454.6 23.8 %convolution_convert_fusion.1 = bf16[2048,1024]{1,0:T(8,128)(2,1)} fusion(bf16[4096,2048]{1,0:T(8,128)(2,1)} %bitcast.101, bf16[4096,1024]{1,0:T(8,128)(2,1)} %get-tuple-element.271), kind=kOutput, calls=%fused_computation.32 | convolution fusion | flops 17181966336 | bytes 29360128 | tf_op jit(solution)/shard_map/dot_general | solution.py:26
  479.8 2.2 add_convert_fusion.5
  486.0 23.1 %shard_map.258 = (bf16[256,1024]{1,0:T(8,128)(2,1)}, bf16[256,1024]{1,0:T(8,128)(2,1)}, bf16[256,1024]{1,0:T(8,128)(2,1)}, bf16[256,1024]{1,0:T(8,128)(2,1)}, bf...) custom-call(bf16[2,4,512,768]{3,2,1,0:T(8,128)(2,1)} %bitcast.85, ...), custom_call_target="tpu_custom_call" | custom-call | flops 15032385536 | bytes 33554432 | tf_op jit(solution)/shard_map/pallas_call | solution.py:479
  510.2 6.3 collective-permute-done.21
  524.4 2.5 add_bitcast_fusion
  526.9 2.4 add_bitcast_fusion.1
  529.4 2.3 fusion.12
  531.7 5.7 collective-permute-done.23
  537.5 4.3 collective-permute-done.25
  541.8 2.1 add_convert_fusion.3
  543.8 2.0 add_convert_fusion.2
  548.4 36.6 %shard_map.259 = (f32[32,32,128]{2,1,0:T(8,128)}, bf16[64,8192]{1,0:T(8,128)(2,1)}, bf16[64,2048]{1,0:T(8,128)(2,1)}, bf16[64,6144]{1,0:T(8,128)(2,1)}) custom-call(f32[32,128]{1,0:T(8,128)} %add_bitcast_fusion.6.refs_0_, bf16[512,1024]{1,0:T(8,128)(2,1)} %reduce-scatter.5.cloned.1.call-done.refs_1_, ...), custom_call_target="tpu_custom_call" | custom-call | flops 28000000000 | bytes 1048576 | tf_op jit(solution)/shard_map/pallas_call | solution.py:177
  585.1 1.9 reshape.172
  590.2 2.8 convert_element_type.294
  594.1 3.6 fusion.19
  602.4 2.9 convert_add_fusion.1
  605.3 14.2 %shard_map.260 = bf16[64,8192]{1,0:T(8,128)(2,1)} custom-call(bf16[512,1024]{1,0:T(8,128)(2,1)} %reduce-scatter.11.cloned.1.call-done.refs_0_), custom_call_target="tpu_custom_call" | custom-call | flops 11900000256 | bytes 1048576 | tf_op jit(solution)/shard_map/pallas_call | solution.py:390
  619.5 3.8 fusion.16
  (246 shorter events, 53.3 us)
Async XLA Ops:
  7.2 148.7 %all-gather.5.cloned.1.call-start = ((), (), s32[]{:S(2)}) async-start(), calls=%async_computation.4 | async-start | bytes 3932160 | tf_op jit(solution)/shard_map/all_gather | solution.py:666
  21.0 16.4 %copy-start = (bf16[2,256,2048]{2,1,0:T(8,128)(2,1)S(1)}, bf16[2,256,2048]{2,1,0:T(8,128)(2,1)}, u32[]{:S(2)}) copy-start(bf16[2,256,2048]{2,1,0:T(8,128)(2,1)} %refs_0_.3) | copy-start | bytes 6291460
  21.0 16.4 %copy-start.2 = (bf16[64,8192]{1,0:T(8,128)(2,1)S(1)}, bf16[64,8192]{1,0:T(8,128)(2,1)}, u32[]{:S(2)}) copy-start(bf16[64,8192]{1,0:T(8,128)(2,1)} %refs_3_.1) | copy-start | bytes 3145732
  21.0 16.4 %copy-start.3 = (bf16[64,2048]{1,0:T(8,128)(2,1)S(1)}, bf16[64,2048]{1,0:T(8,128)(2,1)}, u32[]{:S(2)}) copy-start(bf16[64,2048]{1,0:T(8,128)(2,1)} %refs_2_.1) | copy-start | bytes 786436
  21.0 194.5 %all-gather.7.cloned.1.call-start = ((), (), s32[]{:S(2)}) async-start(), calls=%async_computation.5 | async-start | bytes 5242880 | tf_op jit(solution)/shard_map/all_gather | solution.py:666
  36.1 249.2 %all-gather.9.cloned.1.call-start = ((), (), s32[]{:S(2)}) async-start(), calls=%async_computation.6 | async-start | bytes 1310720 | tf_op jit(solution)/shard_map/all_gather | solution.py:666
  37.4 104.6 %copy-start.32 = (s32[2,1024]{1,0:T(2,128)S(1)}, s32[2,1024]{1,0:T(2,128)}, u32[]{:S(2)}) copy-start(s32[2,1024]{1,0:T(2,128)} %param.16) | copy-start | bytes 24580
  141.9 166.4 %all-gather.11.cloned.1.call-start = ((), (), s32[]{:S(2)}) async-start(), calls=%async_computation.7 | async-start | bytes 5242880 | tf_op jit(solution)/shard_map/all_gather | solution.py:666
  142.0 3.7 collective-permute-start
  142.9 380.5 %reduce-scatter.7.cloned.1.call-start = ((), (), s32[]{:S(2)}) async-start(), calls=%async_computation.9 | async-start | bytes 1310720 | tf_op jit(solution)/shard_map/reduce_scatter | solution.py:762
  145.8 55.7 %collective-permute-start.1 = (bf16[2,256,2048]{2,1,0:T(8,128)(2,1)}, bf16[2,256,2048]{2,1,0:T(8,128)(2,1)}, u32[]{:S(2)}, u32[]{:S(2)}) collective-permute-start(bf16[2,256,2048]{2,1,0:T(8,128)(2,1)} %param.17), channel_id=1, source_target_pairs={{0,2},{1,3},{2,0},{3,1},{4,6},{5,7},{6,4},{7,5},{8,10},{9,11},{10,... | collective-permute-start | bytes 6291464 | tf_op jit(solution)/shard_map/ppermute | solution.py:608
  146.5 55.0 %collective-permute-start.2 = (bf16[2,256,2048]{2,1,0:T(8,128)(2,1)}, bf16[2,256,2048]{2,1,0:T(8,128)(2,1)}, u32[]{:S(2)}, u32[]{:S(2)}) collective-permute-start(bf16[2,256,2048]{2,1,0:T(8,128)(2,1)} %param.17), channel_id=1, source_target_pairs={{0,4},{1,5},{2,6},{3,7},{4,0},{5,1},{6,2},{7,3},{8,12},{9,13},{10,... | collective-permute-start | bytes 6291464 | tf_op jit(solution)/shard_map/ppermute | solution.py:608
  147.9 104.6 %collective-permute-start.5 = (bf16[2,256,2048]{2,1,0:T(8,128)(2,1)}, bf16[2,256,2048]{2,1,0:T(8,128)(2,1)}, u32[]{:S(2)}, u32[]{:S(2)}) collective-permute-start(bf16[2,256,2048]{2,1,0:T(8,128)(2,1)} %param.17), channel_id=1, source_target_pairs={{0,1},{1,0},{2,3},{3,2},{4,5},{5,4},{6,7},{7,6},{8,9},{9,8},{10,11... | collective-permute-start | bytes 6291464 | tf_op jit(solution)/shard_map/ppermute | solution.py:611
  203.8 50.8 %collective-permute-start.6 = (bf16[2,256,2048]{2,1,0:T(8,128)(2,1)}, bf16[2,256,2048]{2,1,0:T(8,128)(2,1)}, u32[]{:S(2)}, u32[]{:S(2)}) collective-permute-start(bf16[2,256,2048]{2,1,0:T(8,128)(2,1)} %collective-permute-done.1), channel_id=1, source_target_pairs={{0,1},{1,0},{2,3},{3,2},{4,5},{5,4},{6,7},{7,6},{8,9},{9,8},{10,11... | collective-permute-start | bytes 6291464 | tf_op jit(solution)/shard_map/ppermute | solution.py:611
  206.7 49.7 %collective-permute-start.7 = (bf16[2,256,2048]{2,1,0:T(8,128)(2,1)}, bf16[2,256,2048]{2,1,0:T(8,128)(2,1)}, u32[]{:S(2)}, u32[]{:S(2)}) collective-permute-start(bf16[2,256,2048]{2,1,0:T(8,128)(2,1)} %collective-permute-done.2), channel_id=1, source_target_pairs={{0,1},{1,0},{2,3},{3,2},{4,5},{5,4},{6,7},{7,6},{8,9},{9,8},{10,11... | collective-permute-start | bytes 6291464 | tf_op jit(solution)/shard_map/ppermute | solution.py:611
  206.7 43.9 %collective-permute-start.3 = (bf16[256,2048]{1,0:T(8,128)(2,1)}, bf16[256,2048]{1,0:T(8,128)(2,1)}, u32[]{:S(2)}, u32[]{:S(2)}) collective-permute-start(bf16[256,2048]{1,0:T(8,128)(2,1)} %slice_bitcast_fusion.1), channel_id=1, source_target_pairs={{0,4},{1,5},{2,6},{3,7},{4,0},{5,1},{6,2},{7,3},{8,12},{9,13},{10,... | collective-permute-start | bytes 3145736 | tf_op jit(solution)/shard_map/ppermute | solution.py:608
  207.8 42.8 %collective-permute-start.4 = (bf16[256,2048]{1,0:T(8,128)(2,1)}, bf16[256,2048]{1,0:T(8,128)(2,1)S(1)}, u32[]{:S(2)}, u32[]{:S(2)}) collective-permute-start(bf16[256,2048]{1,0:T(8,128)(2,1)} %slice_bitcast_fusion), channel_id=1, source_target_pairs={{0,2},{1,3},{2,0},{3,1},{4,6},{5,7},{6,4},{7,5},{8,10},{9,11},{10,... | collective-permute-start | bytes 3145736 | tf_op jit(solution)/shard_map/ppermute | solution.py:608
  215.6 29.0 %copy-start.8 = (bf16[2048,768]{1,0:T(8,128)(2,1)S(1)}, bf16[2048,768]{1,0:T(8,128)(2,1)}, u32[]{:S(2)}) copy-start(bf16[2048,768]{1,0:T(8,128)(2,1)} %all-gather.5.cloned.1.call-done) | copy-start | bytes 9437188
  215.6 35.6 %copy-start.26 = (bf16[4096,2048]{1,0:T(8,128)(2,1)S(1)}, bf16[4096,2048]{1,0:T(8,128)(2,1)}, u32[]{:S(2)}) copy-start(bf16[4096,2048]{1,0:T(8,128)(2,1)} %constant_dynamic-update-slice_fusion.7) | copy-start | bytes 50331652
  250.6 7.8 %collective-permute-start.8 = (bf16[256,2048]{1,0:T(8,128)(2,1)}, bf16[256,2048]{1,0:T(8,128)(2,1)S(1)}, u32[]{:S(2)}, u32[]{:S(2)}) collective-permute-start(bf16[256,2048]{1,0:T(8,128)(2,1)} %collective-permute-done.3), channel_id=1, source_target_pairs={{0,1},{1,0},{2,3},{3,2},{4,5},{5,4},{6,7},{7,6},{8,9},{9,8},{10,11... | collective-permute-start | bytes 3145736 | tf_op jit(solution)/shard_map/ppermute | solution.py:611
  250.6 7.9 %collective-permute-start.9 = (bf16[256,2048]{1,0:T(8,128)(2,1)S(1)}, bf16[256,2048]{1,0:T(8,128)(2,1)S(1)}, u32[]{:S(2)}, u32[]{:S(2)}) collective-permute-start(bf16[256,2048]{1,0:T(8,128)(2,1)S(1)} %collective-permute-done.4), channel_id=1, source_target_pairs={{0,1},{1,0},{2,3},{3,2},{4,5},{5,4},{6,7},{7,6},{8,9},{9,8},{10,11... | collective-permute-start | bytes 3145736 | tf_op jit(solution)/shard_map/ppermute | solution.py:611
  303.4 220.0 %reduce-scatter.5.cloned.1.call-start = ((), (), s32[]{:S(2)}) async-start(), calls=%async_computation.8 | async-start | bytes 5242880 | tf_op jit(solution)/shard_map/reduce_scatter | solution.py:762
  304.0 244.5 %reduce-scatter.9.cloned.1.call-start = ((), (), s32[]{:S(2)}) async-start(), calls=%async_computation.10 | async-start | bytes 3932160 | tf_op jit(solution)/shard_map/reduce_scatter | solution.py:762
  340.4 56.6 %collective-permute-start.10 = (bf16[256,2048]{1,0:T(8,128)(2,1)}, bf16[256,2048]{1,0:T(8,128)(2,1)S(1)}, u32[]{:S(2)}, u32[]{:S(2)}) collective-permute-start(bf16[256,2048]{1,0:T(8,128)(2,1)} %get-tuple-element.162), channel_id=1, source_target_pairs={{0,4},{1,5},{2,6},{3,7},{4,0},{5,1},{6,2},{7,3},{8,12},{9,13},{10,... | collective-permute-start | bytes 3145736 | tf_op jit(solution)/shard_map/ppermute | solution.py:608
  341.2 55.7 %collective-permute-start.11 = (bf16[256,2048]{1,0:T(8,128)(2,1)}, bf16[256,2048]{1,0:T(8,128)(2,1)}, u32[]{:S(2)}, u32[]{:S(2)}) collective-permute-start(bf16[256,2048]{1,0:T(8,128)(2,1)} %get-tuple-element.163), channel_id=1, source_target_pairs={{0,4},{1,5},{2,6},{3,7},{4,0},{5,1},{6,2},{7,3},{8,12},{9,13},{10,... | collective-permute-start | bytes 3145736 | tf_op jit(solution)/shard_map/ppermute | solution.py:608
  342.4 54.5 %collective-permute-start.12 = (bf16[256,2048]{1,0:T(8,128)(2,1)}, bf16[256,2048]{1,0:T(8,128)(2,1)S(1)}, u32[]{:S(2)}, u32[]{:S(2)}) collective-permute-start(bf16[256,2048]{1,0:T(8,128)(2,1)} %get-tuple-element.164), channel_id=1, source_target_pairs={{0,2},{1,3},{2,0},{3,1},{4,6},{5,7},{6,4},{7,5},{8,10},{9,11},{10,... | collective-permute-start | bytes 3145736 | tf_op jit(solution)/shard_map/ppermute | solution.py:608
  343.0 54.0 %collective-permute-start.13 = (bf16[256,2048]{1,0:T(8,128)(2,1)}, bf16[256,2048]{1,0:T(8,128)(2,1)}, u32[]{:S(2)}, u32[]{:S(2)}) collective-permute-start(bf16[256,2048]{1,0:T(8,128)(2,1)} %get-tuple-element.165), channel_id=1, source_target_pairs={{0,2},{1,3},{2,0},{3,1},{4,6},{5,7},{6,4},{7,5},{8,10},{9,11},{10,... | collective-permute-start | bytes 3145736 | tf_op jit(solution)/shard_map/ppermute | solution.py:608
  392.9 212.3 %reduce-scatter.11.cloned.1.call-start = ((), (), s32[]{:S(2)}) async-start(), calls=%async_computation.11 | async-start | bytes 5242880 | tf_op jit(solution)/shard_map/reduce_scatter | solution.py:762
  397.0 30.6 %copy-start.9 = (bf16[256,2048]{1,0:T(8,128)(2,1)}, bf16[256,2048]{1,0:T(8,128)(2,1)S(1)}, u32[]{:S(2)}) copy-start(bf16[256,2048]{1,0:T(8,128)(2,1)S(1)} %collective-permute-done.10) | copy-start | bytes 3145732
  397.0 30.6 %copy-start.10 = (bf16[256,2048]{1,0:T(8,128)(2,1)}, bf16[256,2048]{1,0:T(8,128)(2,1)S(1)}, u32[]{:S(2)}) copy-start(bf16[256,2048]{1,0:T(8,128)(2,1)S(1)} %collective-permute-done.12) | copy-start | bytes 3145732
  403.0 119.7 %collective-permute-start.14 = (bf16[256,2048]{1,0:T(8,128)(2,1)}, bf16[256,2048]{1,0:T(8,128)(2,1)}, u32[]{:S(2)}, u32[]{:S(2)}) collective-permute-start(bf16[256,2048]{1,0:T(8,128)(2,1)} %add_convert_fusion.1), channel_id=1, source_target_pairs={{0,2},{1,3},{2,0},{3,1},{4,6},{5,7},{6,4},{7,5},{8,10},{9,11},{10,... | collective-permute-start | bytes 3145736 | tf_op jit(solution)/shard_map/ppermute | solution.py:608
  450.5 28.5 %collective-permute-start.16 = (bf16[256,1024]{1,0:T(8,128)(2,1)}, bf16[256,1024]{1,0:T(8,128)(2,1)S(1)}, u32[]{:S(2)}, u32[]{:S(2)}) collective-permute-start(bf16[256,1024]{1,0:T(8,128)(2,1)} %get-tuple-element.193), channel_id=1, source_target_pairs={{0,4},{1,5},{2,6},{3,7},{4,0},{5,1},{6,2},{7,3},{8,12},{9,13},{10,... | collective-permute-start | bytes 1572872 | tf_op jit(solution)/shard_map/ppermute | solution.py:608
  451.3 28.5 %collective-permute-start.17 = (bf16[256,1024]{1,0:T(8,128)(2,1)}, bf16[256,1024]{1,0:T(8,128)(2,1)}, u32[]{:S(2)}, u32[]{:S(2)}) collective-permute-start(bf16[256,1024]{1,0:T(8,128)(2,1)} %get-tuple-element.194), channel_id=1, source_target_pairs={{0,4},{1,5},{2,6},{3,7},{4,0},{5,1},{6,2},{7,3},{8,12},{9,13},{10,... | collective-permute-start | bytes 1572872 | tf_op jit(solution)/shard_map/ppermute | solution.py:608
  452.5 27.3 %collective-permute-start.18 = (bf16[256,1024]{1,0:T(8,128)(2,1)}, bf16[256,1024]{1,0:T(8,128)(2,1)S(1)}, u32[]{:S(2)}, u32[]{:S(2)}) collective-permute-start(bf16[256,1024]{1,0:T(8,128)(2,1)} %get-tuple-element.195), channel_id=1, source_target_pairs={{0,2},{1,3},{2,0},{3,1},{4,6},{5,7},{6,4},{7,5},{8,10},{9,11},{10,... | collective-permute-start | bytes 1572872 | tf_op jit(solution)/shard_map/ppermute | solution.py:608
  453.9 25.9 %collective-permute-start.19 = (bf16[256,1024]{1,0:T(8,128)(2,1)}, bf16[256,1024]{1,0:T(8,128)(2,1)}, u32[]{:S(2)}, u32[]{:S(2)}) collective-permute-start(bf16[256,1024]{1,0:T(8,128)(2,1)} %get-tuple-element.196), channel_id=1, source_target_pairs={{0,2},{1,3},{2,0},{3,1},{4,6},{5,7},{6,4},{7,5},{8,10},{9,11},{10,... | collective-permute-start | bytes 1572872 | tf_op jit(solution)/shard_map/ppermute | solution.py:608
  479.0 30.1 %copy-start.18 = (bf16[256,1024]{1,0:T(8,128)(2,1)}, bf16[256,1024]{1,0:T(8,128)(2,1)S(1)}, u32[]{:S(2)}) copy-start(bf16[256,1024]{1,0:T(8,128)(2,1)S(1)} %collective-permute-done.16) | copy-start | bytes 1572868
  479.0 44.4 %collective-permute-start.15 = (bf16[256,2048]{1,0:T(8,128)(2,1)}, bf16[256,2048]{1,0:T(8,128)(2,1)S(1)}, u32[]{:S(2)}, u32[]{:S(2)}) collective-permute-start(bf16[256,2048]{1,0:T(8,128)(2,1)} %add_convert_fusion), channel_id=1, source_target_pairs={{0,4},{1,5},{2,6},{3,7},{4,0},{5,1},{6,2},{7,3},{8,12},{9,13},{10,... | collective-permute-start | bytes 3145736 | tf_op jit(solution)/shard_map/ppermute | solution.py:608
  483.5 33.0 %collective-permute-start.21 = (bf16[256,1024]{1,0:T(8,128)(2,1)S(1)}, bf16[256,1024]{1,0:T(8,128)(2,1)S(1)}, u32[]{:S(2)}, u32[]{:S(2)}) collective-permute-start(bf16[256,1024]{1,0:T(8,128)(2,1)S(1)} %add_convert_fusion.4), channel_id=1, source_target_pairs={{0,4},{1,5},{2,6},{3,7},{4,0},{5,1},{6,2},{7,3},{8,12},{9,13},{10,... | collective-permute-start | bytes 1572872 | tf_op jit(solution)/shard_map/ppermute | solution.py:608
  484.7 34.8 %collective-permute-start.20 = (bf16[256,1024]{1,0:T(8,128)(2,1)}, bf16[256,1024]{1,0:T(8,128)(2,1)}, u32[]{:S(2)}, u32[]{:S(2)}) collective-permute-start(bf16[256,1024]{1,0:T(8,128)(2,1)} %add_convert_fusion.5), channel_id=1, source_target_pairs={{0,2},{1,3},{2,0},{3,1},{4,6},{5,7},{6,4},{7,5},{8,10},{9,11},{10,... | collective-permute-start | bytes 1572872 | tf_op jit(solution)/shard_map/ppermute | solution.py:608
  486.0 32.1 %copy-start.19 = (bf16[256,1024]{1,0:T(8,128)(2,1)S(1)}, bf16[256,1024]{1,0:T(8,128)(2,1)}, u32[]{:S(2)}) copy-start(bf16[256,1024]{1,0:T(8,128)(2,1)} %get-tuple-element.220) | copy-start | bytes 1572868
  486.0 35.0 %copy-start.17 = (bf16[256,1024]{1,0:T(8,128)(2,1)S(1)}, bf16[256,1024]{1,0:T(8,128)(2,1)}, u32[]{:S(2)}) copy-start(bf16[256,1024]{1,0:T(8,128)(2,1)} %get-tuple-element.217) | copy-start | bytes 1572868
  509.1 22.6 %collective-permute-start.22 = (bf16[256,1024]{1,0:T(8,128)(2,1)}, bf16[256,1024]{1,0:T(8,128)(2,1)}, u32[]{:S(2)}, u32[]{:S(2)}) collective-permute-start(bf16[256,1024]{1,0:T(8,128)(2,1)} %get-tuple-element.207), channel_id=1, source_target_pairs={{0,4},{1,5},{2,6},{3,7},{4,0},{5,1},{6,2},{7,3},{8,12},{9,13},{10,... | collective-permute-start | bytes 1572872 | tf_op jit(solution)/shard_map/ppermute | solution.py:608
  517.3 20.2 %collective-permute-start.23 = (bf16[256,1024]{1,0:T(8,128)(2,1)}, bf16[256,1024]{1,0:T(8,128)(2,1)}, u32[]{:S(2)}, u32[]{:S(2)}) collective-permute-start(bf16[256,1024]{1,0:T(8,128)(2,1)} %get-tuple-element.209), channel_id=1, source_target_pairs={{0,4},{1,5},{2,6},{3,7},{4,0},{5,1},{6,2},{7,3},{8,12},{9,13},{10,... | collective-permute-start | bytes 1572872 | tf_op jit(solution)/shard_map/ppermute | solution.py:608
  519.6 17.9 %collective-permute-start.24 = (bf16[256,1024]{1,0:T(8,128)(2,1)}, bf16[256,1024]{1,0:T(8,128)(2,1)}, u32[]{:S(2)}, u32[]{:S(2)}) collective-permute-start(bf16[256,1024]{1,0:T(8,128)(2,1)} %get-tuple-element.206), channel_id=1, source_target_pairs={{0,2},{1,3},{2,0},{3,1},{4,6},{5,7},{6,4},{7,5},{8,10},{9,11},{10,... | collective-permute-start | bytes 1572872 | tf_op jit(solution)/shard_map/ppermute | solution.py:608
  522.7 19.1 %collective-permute-start.25 = (bf16[256,1024]{1,0:T(8,128)(2,1)}, bf16[256,1024]{1,0:T(8,128)(2,1)}, u32[]{:S(2)}, u32[]{:S(2)}) collective-permute-start(bf16[256,1024]{1,0:T(8,128)(2,1)} %get-tuple-element.210), channel_id=1, source_target_pairs={{0,2},{1,3},{2,0},{3,1},{4,6},{5,7},{6,4},{7,5},{8,10},{9,11},{10,... | collective-permute-start | bytes 1572872 | tf_op jit(solution)/shard_map/ppermute | solution.py:608
  545.9 51.9 %collective-permute-start.26 = (bf16[256,1024]{1,0:T(8,128)(2,1)}, bf16[256,1024]{1,0:T(8,128)(2,1)}, u32[]{:S(2)}, u32[]{:S(2)}) collective-permute-start(bf16[256,1024]{1,0:T(8,128)(2,1)} %add_convert_fusion.3), channel_id=1, source_target_pairs={{0,2},{1,3},{2,0},{3,1},{4,6},{5,7},{6,4},{7,5},{8,10},{9,11},{10,... | collective-permute-start | bytes 1572872 | tf_op jit(solution)/shard_map/ppermute | solution.py:608
  547.3 50.4 %collective-permute-start.27 = (bf16[256,1024]{1,0:T(8,128)(2,1)}, bf16[256,1024]{1,0:T(8,128)(2,1)}, u32[]{:S(2)}, u32[]{:S(2)}) collective-permute-start(bf16[256,1024]{1,0:T(8,128)(2,1)} %add_convert_fusion.2), channel_id=1, source_target_pairs={{0,4},{1,5},{2,6},{3,7},{4,0},{5,1},{6,2},{7,3},{8,12},{9,13},{10,... | collective-permute-start | bytes 1572872 | tf_op jit(solution)/shard_map/ppermute | solution.py:608
  593.0 30.4 %copy-start.51 = (f32[64]{0:T(128)}, f32[64]{0:T(128)S(1)}, u32[]{:S(2)}) copy-start(f32[64]{0:T(128)S(1)} %fusion.23) | copy-start | bytes 772
  (42 other events, 343.5 us)
Sparse Core Ops, SparseCore 0:
  21.0 67.7 all-gather.4
  90.4 79.4 all-gather.6
  171.5 26.4 all-gather.8
  199.4 80.1 all-gather.10
  303.5 24.6 reduce-scatter.6
  330.4 75.3 reduce-scatter.4
  408.0 60.8 reduce-scatter.8
  478.5 74.6 reduce-scatter.10

commit v5 on v4

--- a/solution.py
+++ b/solution.py
@@ -49,6 +49,8 @@
         self.count = outer * self.group
         self.heads = HEADS // self.group
         self.offsets = [(ry, rx) for ry in range(sub) for rx in range(self.chips_x)]
+        self.square = sub == 2 and self.chips_x == 2
+        self.near = [o for o in self.offsets if not (self.square and o == (1, 1))]
         self.far = sorted(self.offsets[1:], key=lambda o: (o[0] > 0) + (o[1] > 0))
 
     def shift(self, ry, rx):
@@ -134,62 +136,8 @@
     pl.semaphore_wait(barrier, lay.count - 1)
 
 
-def exchange_kernel(lay, plan, *refs):
-    n = len(plan)
-    vec_ref, sources = refs[0], refs[1 : 1 + n]
-    all_ref, targets = refs[1 + n], refs[2 + n : 2 + 2 * n]
-    send, recv, own, vec_send, vec_recv, vec_own = refs[2 + 2 * n :]
-    zo = lax.axis_index("zo")
-    me = lax.axis_index("yi") * lay.seq + lax.axis_index("seq")
-    rank = zo * lay.group + me
-
-    device_of = functools.partial(device_after, lay, rank)
-    barrier_all(lay, device_of)
-    copies = swap_copies(lay, plan, me, sources, targets, send, recv, True)
-    mine = swap_own(lay, plan, me, sources, targets, own, True)
-    mine.append(pltpu.make_async_copy(vec_ref, all_ref.at[rank], vec_own))
-
-    def vec_copy(k):
-        return remote(vec_ref, all_ref.at[rank], vec_send.at[k - 1], vec_recv.at[k - 1], device_of(k))
-
-    def start(k, carry):
-        vec_copy(k).start()
-        return carry
-
-    def finish(k, carry):
-        vec_copy(k).wait()
-        return carry
-
-    lax.fori_loop(1, lay.count, start, 0)
-    for copy in copies + mine:
-        copy.start()
-    lax.fori_loop(1, lay.count, finish, 0)
-    for copy in copies + mine:
-        copy.wait()
-
-
 def busy(microseconds):
     return pl.CostEstimate(flops=int(7e8 * microseconds), bytes_accessed=1 << 20, transcendentals=0)
-
-
-def exchange(lay, plan, vec, arrays, number, time):
-    count = sum(parts for parts, _, _ in plan)
-    return pl.pallas_call(
-        functools.partial(exchange_kernel, lay, plan),
-        out_shape=[jax.ShapeDtypeStruct((lay.count, *vec.shape), F32), *swap_shapes(lay, plan, True)],
-        in_specs=[ANY] * (1 + len(plan)),
-        out_specs=[ANY] * (1 + len(plan)),
-        scratch_shapes=[
-            pltpu.SemaphoreType.DMA((lay.group - 1, count)),
-            pltpu.SemaphoreType.DMA((lay.group - 1, count)),
-            pltpu.SemaphoreType.DMA((count,)),
-            pltpu.SemaphoreType.DMA((lay.count - 1,)),
-            pltpu.SemaphoreType.DMA((lay.count - 1,)),
-            pltpu.SemaphoreType.DMA,
-        ],
-        compiler_params=pltpu.CompilerParams(collective_id=number, has_side_effects=True),
-        cost_estimate=busy(time),
-    )(vec, *arrays)
 
 
 def norm_kernel(lay, plan, *refs):
@@ -288,7 +236,7 @@
                 stage[k, 2, at, :] = hat.astype(BF16)
                 return carry
 
-            lax.fori_loop(0, length // rows, chunk, 0)
+            lax.fori_loop(0, length // rows, chunk, 0, unroll=2)
             pending[k] = [
                 pltpu.make_async_copy(stage.at[k, i], ref.at[c, j, m], out_sem.at[k, i])
                 for i, ref in enumerate((one_ref, two_ref, hat_ref))
@@ -402,13 +350,23 @@
     )(*arrays)
 
 
-def pair_kernel(lay, first_ref, first_w, second_ref, second_w, *refs):
+def pair_kernel(lay, plan, with_vec, scaled, batch, *refs):
+    refs = list(refs)
+    take = lambda k: [refs.pop(0) for _ in range(k)]
     step = pl.program_id(0)
     chips = lay.group // 2
-    (given, came, send, recv, out_sem), outs = refs[-5:], refs[:-5]
-    batch = len(outs) // chips
+    first_ref, first_w, second_ref, second_w = take(4)
+    scales = take(2) if scaled else []
+    sources, vec_ref = take(len(plan)), take(int(with_vec))
+    outs, targets, all_ref = take(chips * batch), take(len(plan)), take(int(with_vec))
+    given, came, send, recv, out_sem = take(5)
     zo, yi, s = lax.axis_index("zo"), lax.axis_index("yi"), lax.axis_index("seq")
+    me = yi * lay.seq + s
+    rank = zo * lay.group + me
+    device_of = functools.partial(device_after, lay, rank)
     partner = (zo, yi, (s // 2) * 2 + 1 - lax.rem(s, 2))
+    swap_sems = take(3) if plan else []
+    vec_sems = take(3) if with_vec else []
 
     def copy(j):
         return remote(given.at[j], came.at[j], send.at[j], recv.at[j], partner)
@@ -422,11 +380,40 @@
             for m in range(batch)
         ]
 
+    def riders():
+        if not plan:
+            return []
+        copies = swap_copies(lay, plan, me, sources, targets, swap_sems[0], swap_sems[1], True)
+        return copies + swap_own(lay, plan, me, sources, targets, swap_sems[2], True)
+
+    def vec_copy(k):
+        return remote(vec_ref[0], all_ref[0].at[rank], vec_sems[0].at[k - 1], vec_sems[1].at[k - 1], device_of(k))
+
+    def vec_start(k, carry):
+        vec_copy(k).start()
+        return carry
+
+    def vec_finish(k, carry):
+        vec_copy(k).wait()
+        return carry
+
+    def vec_mine():
+        return pltpu.make_async_copy(vec_ref[0], all_ref[0].at[rank], vec_sems[2])
+
     @pl.when(step == 0)
     def _():
-        barrier = pltpu.get_barrier_semaphore()
-        pl.semaphore_signal(barrier, inc=1, device_id=partner, device_id_type=MESH)
-        pl.semaphore_wait(barrier, 1)
+        if with_vec:
+            barrier_all(lay, device_of)
+            vec_mine().start()
+            lax.fori_loop(1, lay.count, vec_start, 0)
+        elif plan:
+            group_barrier(lay, me)
+        else:
+            barrier = pltpu.get_barrier_semaphore()
+            pl.semaphore_signal(barrier, inc=1, device_id=partner, device_id_type=MESH)
+            pl.semaphore_wait(barrier, 1)
+        for rider in riders():
+            rider.start()
 
     for j in range(chips):
 
@@ -434,7 +421,9 @@
         def _():
             copy(j).start()
 
-    total = dot(first_ref[0, 0], first_w[...], ((1,), (1,))) + dot(second_ref[0, 0], second_w[...], ((1,), (1,)))
+    total = dot(first_ref[0, 0], first_w[...], ((1,), (1,)))
+    other = dot(second_ref[0, 0], second_w[...], ((1,), (1,)))
+    total = total * scales[0][...] + other * scales[1][...] if scaled else total + other
     for j in range(chips):
 
         @pl.when(step == j)
@@ -461,13 +450,19 @@
             copy(j).wait_send()
             for piece in stores(j):
                 piece.wait()
-
-
-def pair_matmul(lay, first, first_w, second, second_w, batch, cut, number):
+        for rider in riders():
+            rider.wait()
+        if with_vec:
+            vec_mine().wait()
+            lax.fori_loop(1, lay.count, vec_finish, 0)
+
+
+def pair_matmul(lay, acts, weights, batch, cut, number, scales=(), plan=(), arrays=(), vec=None):
     chips = lay.group // 2
-    rows = first.shape[0] // lay.group
-    width = first_w.shape[0] // cut[1]
-    depth1, depth2 = first.shape[1], second.shape[1]
+    rows = acts[0].shape[0] // lay.group
+    width = weights[0].shape[0] // cut[1]
+    count = sum(parts for parts, _, _ in plan)
+    with_vec = vec is not None
 
     def act(depth):
         return pl.BlockSpec((1, 1, rows, depth), lambda i: (1 - i // chips, (i + 1) % chips, 0, 0))
@@ -475,27 +470,43 @@
     def weight(depth):
         return pl.BlockSpec((width, depth), lambda i: (cut[0], 0), pipeline_mode=pl.Buffered(1))
 
-    shape = lambda v: v.reshape(2, chips, rows, v.shape[1])
+    specs, args = [], []
+    for a, w in zip(acts, weights, strict=True):
+        specs += [act(a.shape[1]), weight(a.shape[1])]
+        args += [a.reshape(2, chips, rows, a.shape[1]), w]
+    for scale in scales:
+        specs.append(pl.BlockSpec((1, width), lambda i: (0, cut[0])))
+        args.append(scale.reshape(1, -1))
+    args += [*arrays, *([vec] if with_vec else [])]
+    specs += [ANY] * (len(args) - len(specs))
+    shapes = [jax.ShapeDtypeStruct((rows // batch, width), BF16)] * (chips * batch) + swap_shapes(lay, plan, True)
+    scratch = [
+        pltpu.VMEM((chips, rows, width), BF16),
+        pltpu.VMEM((chips, rows, width), BF16),
+        pltpu.SemaphoreType.DMA((chips,)),
+        pltpu.SemaphoreType.DMA((chips,)),
+        pltpu.SemaphoreType.DMA((chips, batch)),
+    ]
+    if plan:
+        scratch += [pltpu.SemaphoreType.DMA((lay.group - 1, count))] * 2 + [pltpu.SemaphoreType.DMA((count,))]
+    if with_vec:
+        shapes.append(jax.ShapeDtypeStruct((lay.count, *vec.shape), F32))
+        scratch += [pltpu.SemaphoreType.DMA((lay.count - 1,))] * 2 + [pltpu.SemaphoreType.DMA]
+    depth = sum(a.shape[1] for a in acts)
     return pl.pallas_call(
-        functools.partial(pair_kernel, lay),
+        functools.partial(pair_kernel, lay, plan, with_vec, bool(scales), batch),
         grid=(2 * chips,),
-        in_specs=[act(depth1), weight(depth1), act(depth2), weight(depth2)],
-        out_specs=[ANY] * (chips * batch),
-        out_shape=[jax.ShapeDtypeStruct((rows // batch, width), BF16)] * (chips * batch),
-        scratch_shapes=[
-            pltpu.VMEM((chips, rows, width), BF16),
-            pltpu.VMEM((chips, rows, width), BF16),
-            pltpu.SemaphoreType.DMA((chips,)),
-            pltpu.SemaphoreType.DMA((chips,)),
-            pltpu.SemaphoreType.DMA((chips, batch)),
-        ],
+        in_specs=specs,
+        out_specs=[ANY] * len(shapes),
+        out_shape=shapes,
+        scratch_shapes=scratch,
         compiler_params=pltpu.CompilerParams(
             collective_id=number, has_side_effects=True, vmem_limit_bytes=60 << 20
         ),
         cost_estimate=pl.CostEstimate(
-            flops=2 * first.shape[0] * (depth1 + depth2) * width, bytes_accessed=32 << 20, transcendentals=0
+            flops=2 * acts[0].shape[0] * depth * width, bytes_accessed=32 << 20, transcendentals=0
         ),
-    )(shape(first), first_w, shape(second), second_w)
+    )(*args)
 
 
 def turn_pairs(field, cosine, sine):
@@ -522,8 +533,76 @@
     return cosine, sine
 
 
-def attend_kernel(scaling, packed_ref, cos_ref, sin_ref, col_ref, row_ref, q_ref, k_ref, v_ref, ctx_ref, lse_ref,
-                  q_buf, k_buf, v_buf, ctx_buf, cos_buf, sin_buf):
+def attend_kernel(lay, scaling, *refs):
+    refs = list(refs)
+    take = lambda k: [refs.pop(0) for _ in range(k)]
+    near_count = len(lay.near)
+    packed_ref, cos_ref, sin_ref, col_ref, row_ref = take(5)
+    near = take(near_count)
+    q_ref, k_ref, v_ref, ctx_ref, lse_ref, dy_ref = take(6)
+    q_buf, k_buf, v_buf, ctx_buf, cos_buf, sin_buf, bounce = take(7)
+    load_sem, store_sem, core_send, core_recv, on_send, on_recv = take(6)
+    step, last = pl.program_id(0), pl.num_programs(0) - 1
+    zo, yi, s = lax.axis_index("zo"), lax.axis_index("yi"), lax.axis_index("seq")
+    x, core = s // 2, lax.rem(s, 2)
+    partner = (zo, yi, x * 2 + 1 - core)
+    chips = lay.group // 2
+    half = near[0].shape[0] // 2
+
+    def load(i):
+        return pltpu.make_async_copy(near[i], bounce.at[i], load_sem.at[i])
+
+    def store(i):
+        return pltpu.make_async_copy(bounce.at[i], dy_ref.at[0, i], store_sem.at[i])
+
+    def to_partner(i):
+        source = near[i] if i < near_count else dy_ref.at[0, i]
+        return remote(source, dy_ref.at[1, i], core_send.at[i], core_recv.at[i], partner)
+
+    def onward():
+        if not lay.square:
+            return []
+        over_y = (zo, lax.rem(yi + 1, lay.sub), s)
+        over_x = (zo, yi, lax.rem(x + 1, lay.chips_x) * 2 + core)
+        return [
+            remote(near[1].at[:half], dy_ref.at[0, 3, :half], on_send.at[0], on_recv.at[0], over_y),
+            remote(near[2].at[half:], dy_ref.at[0, 3, half:], on_send.at[1], on_recv.at[1], over_x),
+        ]
+
+    @pl.when(step == 0)
+    def _():
+        group_barrier(lay, yi * lay.seq + s)
+        for copy in onward():
+            copy.start()
+        for i in range(near_count):
+            load(i).start()
+            to_partner(i).start()
+
+    @pl.when(step == 1)
+    def _():
+        for i in range(near_count):
+            load(i).wait()
+            store(i).start()
+
+    attend_one(scaling, packed_ref, cos_ref, sin_ref, col_ref, row_ref, q_ref, k_ref, v_ref, ctx_ref, lse_ref,
+               q_buf, k_buf, v_buf, ctx_buf, cos_buf, sin_buf)
+
+    @pl.when(step == last)
+    def _():
+        for copy in onward():
+            copy.wait_recv()
+        for i in range(near_count, chips):
+            to_partner(i).start()
+        for i in range(near_count):
+            store(i).wait()
+        for i in range(chips):
+            to_partner(i).wait()
+        for copy in onward():
+            copy.wait_send()
+
+
+def attend_one(scaling, packed_ref, cos_ref, sin_ref, col_ref, row_ref, q_ref, k_ref, v_ref, ctx_ref, lse_ref,
+               q_buf, k_buf, v_buf, ctx_buf, cos_buf, sin_buf):
     cores, _, chips, _, length, _ = packed_ref.shape
     cos_all, sin_all = wide_pair(cos_ref, sin_ref)
     cos_buf[...] = cos_all
@@ -602,13 +681,10 @@
 def make_body(lay):
     sub, seq, group, chips_x = lay.sub, lay.seq, lay.group, lay.chips_x
 
-    square = sub == 2 and chips_x == 2
+    square = lay.square
 
     def across(value, o):
         return lax.ppermute(value, GROUP, lay.shift(*o))
-
-    def partners(pieces):
-        return [lax.ppermute(piece, "seq", lay.flip()) for piece in pieces]
 
     def add(*pieces):
         total = pieces[0].astype(F32)
@@ -707,7 +783,7 @@
         b_up_mine = lax.dynamic_index_in_dim(b_up_all.reshape(group, ff_cols), me, 0, keepdims=False)
         one, two, hat = [v.reshape(total, width) for v in (one, two, hat)]
         cotangent, hat, places = lax.optimization_barrier((cotangent, hat, places))
-        near_dy = [across(cotangent, o) for o in lay.offsets[1:] if not (square and o == (1, 1))]
+        near_dy = [cotangent] + [across(cotangent, o) for o in lay.near[1:]]
 
         halves = ROTARY // 2
         frequency = jnp.exp(jnp.arange(halves, dtype=F32) * (-2.0 * math.log(10000.0) / ROTARY))
@@ -719,6 +795,15 @@
         seqs = sub * batch
         one = after(one, cosine, sine)
         packed = dot(one, qkv_w, ((1,), (0,))) + b_qkv_mine
+        two = after(two, packed)
+
+        hidden = dot(two, up_w, ((1,), (0,))) + b_up_mine
+        phi_cdf = 0.5 * (1.0 + lax.erf(hidden * math.sqrt(0.5)))
+        density = jnp.exp(-0.5 * hidden * hidden) * (1.0 / math.sqrt(2.0 * math.pi))
+        activated = (hidden * phi_cdf).astype(BF16)
+        slope = (phi_cdf + hidden * density).astype(BF16)
+        activated, slope = lax.optimization_barrier((activated, slope))
+        packed = after(packed, activated)
         wide = (2, 1, chips_x, 1, length, 3 * cols)
         wide_spec = pl.BlockSpec(wide, lambda i: (0, i // batch, 0, i % batch, 0, 0))
         full = (2, sub, chips_x, batch, length, 3 * cols)
@@ -732,31 +817,31 @@
         head_shape = jax.ShapeDtypeStruct((seqs, count, HEAD_DIM), BF16)
         work = 2 * seqs * count * count * HEAD_DIM
         params = pltpu.CompilerParams(vmem_limit_bytes=56 << 20)
-        queries, keys, values, context, lse = pl.pallas_call(
-            functools.partial(attend_kernel, scaling),
+        near_count, chips = len(near_dy), group // 2
+        queries, keys, values, context, lse, upstream = pl.pallas_call(
+            functools.partial(attend_kernel, lay, scaling),
             grid=(seqs,),
-            in_specs=[wide_spec, turn_spec, turn_spec, col_spec, row_spec],
-            out_specs=[head_spec] * 3 + [tokens_spec, row_spec],
-            out_shape=[head_shape] * 3 + [jax.ShapeDtypeStruct(by_token, BF16), jax.ShapeDtypeStruct((seqs, 1, count), F32)],
-            scratch_shapes=[pltpu.VMEM((count, HEAD_DIM), BF16)] * 4 + turn_bufs,
-            compiler_params=params,
+            in_specs=[wide_spec, turn_spec, turn_spec, col_spec, row_spec] + [ANY] * near_count,
+            out_specs=[head_spec] * 3 + [tokens_spec, row_spec, ANY],
+            out_shape=[head_shape] * 3
+            + [
+                jax.ShapeDtypeStruct(by_token, BF16),
+                jax.ShapeDtypeStruct((seqs, 1, count), F32),
+                jax.ShapeDtypeStruct((2, chips, *cotangent.shape), BF16),
+            ],
+            scratch_shapes=[pltpu.VMEM((count, HEAD_DIM), BF16)] * 4
+            + turn_bufs
+            + [pltpu.VMEM((near_count, *cotangent.shape), BF16)]
+            + [pltpu.SemaphoreType.DMA((near_count,))] * 2
+            + [pltpu.SemaphoreType.DMA((chips,))] * 2
+            + [pltpu.SemaphoreType.DMA((2,))] * 2,
+            compiler_params=pltpu.CompilerParams(collective_id=8, has_side_effects=True, vmem_limit_bytes=58 << 20),
             cost_estimate=pl.CostEstimate(flops=2 * work, bytes_accessed=30 << 20, transcendentals=seqs * count * count),
             name="attend",
-        )(packed.reshape(full), cosine, sine, place_col, place_row)
+        )(packed.reshape(full), cosine, sine, place_col, place_row, *near_dy)
+        upstream = upstream.reshape(total, width)
 
         context = context.reshape(total, cols)
-        two, *near_dy = lax.optimization_barrier((two, *near_dy, context))[:-1]
-        pieces = [cotangent, *near_dy]
-        early = partners(pieces)
-        if square:
-            halves_dy = [across(pieces[1][0], (1, 0)), across(pieces[2][1], (0, 1))]
-
-        hidden = dot(two, up_w, ((1,), (0,))) + b_up_mine
-        phi_cdf = 0.5 * (1.0 + lax.erf(hidden * math.sqrt(0.5)))
-        density = jnp.exp(-0.5 * hidden * hidden) * (1.0 / math.sqrt(2.0 * math.pi))
-        activated = (hidden * phi_cdf).astype(BF16)
-        slope = (phi_cdf + hidden * density).astype(BF16)
-        activated, slope = lax.optimization_barrier((activated, slope))
 
         def scatter(grad):
             return lax.psum_scatter(grad, "zo", scatter_dimension=0, tiled=True)
@@ -764,35 +849,16 @@
         def outer_dot(left, right):
             return dot(left, right, ((0,), (0,))).astype(BF16)
 
-        qkv_late, up_late = lax.optimization_barrier((qkv_w, up_w, activated))[:-1]
-        fold_qkv = (gain1_all[:, None] * qkv_late.astype(F32)).astype(BF16)
-        fold_up = (gain2_all[:, None] * up_late.astype(F32)).astype(BF16)
-        flat = lambda values: [v.reshape(-1, width) for v in values]
-        if square:
-            halves_dy = lax.optimization_barrier((*halves_dy, fold_qkv, fold_up))[:2]
-            rows_dy = flat(pieces) + flat(halves_dy) + flat(early) + flat(partners(halves_dy))
-        else:
-            rows_dy = flat(pieces) + flat(early)
-        upstream = jnp.concatenate(rows_dy, 0)
+        def chain(values, *tokens):
+            return lax.optimization_barrier((*values, *tokens))[: len(values)]
+
+        def tokens_of(pieces):
+            return [pieces[i * batch : (i + 1) * batch] for i in range(group // 2)]
+
         down_part = outer_dot(upstream, activated)
-        upstream = after(upstream, down_part)
+        upstream, down_part = chain((upstream, down_part))
         down_sum = scatter(down_part)
         grad_context = dot(upstream, out_w, ((1,), (0,))).astype(BF16)
-        upstream = after(upstream, grad_context)
-        out_part = outer_dot(upstream, context)
-        out_w_sum = scatter(out_part)
-
-        def chain(values, *tokens):
-            return lax.optimization_barrier((*values, *tokens))[: len(values)]
-
-        def tokens_of(pieces):
-            return [pieces[i * batch : (i + 1) * batch] for i in range(group // 2)]
-
-        pair = chain((context, activated), out_part)
-        out_near = pair_matmul(lay, pair[0], out_w, pair[1], down_w, batch, (0, 1), 4)
-        grad_context, *out_near = chain((grad_context, *out_near))
-        out_near = tokens_of(out_near)
-        out_came = far_first(out_near)
 
         grad_packed = pl.pallas_call(
             functools.partial(attend_back_kernel, scaling),
@@ -809,38 +875,67 @@
 
         qkv_part = outer_dot(hat, grad_packed)
         qkv_sum = scatter(qkv_part)
-        out_came, upstream = chain((out_came, upstream), qkv_part)
-        onward, upstream = chain((far_onward(out_near, out_came), upstream))
+        acts = chain((context, activated), qkv_part)
+        out_near = tokens_of(pair_matmul(lay, acts, (out_w, down_w), batch, (0, 1), 4))
+        out_came = far_first(out_near)
+        (upstream,) = chain((upstream,), out_near)
+        out_part = outer_dot(upstream, context)
+        out_part, upstream = chain((out_part, upstream))
+        grad_hidden = (dot(upstream, down_w, ((1,), (0,))) * slope.astype(F32)).astype(BF16)
+        up_part = outer_dot(hat, grad_hidden)
+        up_sum = scatter(up_part)
+        (out_part,) = chain((out_part,), up_part)
+        out_w_sum = scatter(out_part)
+        out_came, left = chain((out_came, grad_packed), up_part)
+        onward, left = chain((far_onward(out_near, out_came), left))
         out_parts = far_second(out_near, out_came, onward)
-        grad_hidden = (dot(upstream, down_w, ((1,), (0,))) * slope.astype(F32)).astype(BF16)
-
-        near0 = pair_matmul(lay, grad_packed, fold_qkv, grad_hidden, fold_up, batch, (0, 2), 5)
-        hat, near0 = chain((hat, near0))
+
+        folded = (qkv_w, up_w)
+        scales = (gain1_all, gain2_all)
+        left, down_sum = chain((left, down_sum))
+        *near0, down_raw = pair_matmul(
+            lay, (left, grad_hidden), folded, batch, (0, 2), 5, scales, [plans["down"]], [down_sum]
+        )
         near0 = tokens_of(near0)
         came0 = far_first(near0)
-        up_part = outer_dot(hat, grad_hidden)
-        up_sum = scatter(up_part)
-        came0, left = chain((came0, grad_packed), up_part)
-        onward, left = chain((far_onward(near0, came0), left))
-        parts0 = far_second(near0, came0, onward)
-        near1 = pair_matmul(lay, left, fold_qkv, grad_hidden, fold_up, batch, (1, 2), 6)
-        near1 = tokens_of(near1)
-        came1 = far_first(near1)
-
         own_sums = [
             jnp.sum(grad_packed.astype(F32), 0),
             jnp.sum(grad_hidden.astype(F32), 0),
             jnp.sum(cotangent.astype(F32), (0, 1)),
         ]
-        out_parts, vec, down_sum, out_w_sum = chain((out_parts, laid(own_sums), down_sum, out_w_sum), near1)
+        left, vec, qkv_sum = chain((left, laid(own_sums), qkv_sum), near0)
+        *near1, qkv_raw, everyone = pair_matmul(
+            lay, (left, grad_hidden), folded, batch, (1, 2), 6, scales, [plans["qkv"]], [qkv_sum], vec
+        )
+        near1 = tokens_of(near1)
+        came1 = far_first(near1)
+        (came0,) = chain((came0,), near1)
+        onward0 = far_onward(near0, came0)
+        parts0 = far_second(near0, came0, onward0)
+        (out_parts,) = chain((out_parts,), onward0)
         output = (tokens.astype(F32) + add_all(out_parts) + b_out_all + b_down_all).astype(BF16)
-        came1, vec = chain((came1, vec), output)
-        onward, vec = chain((far_onward(near1, came1), vec))
-        parts1 = far_second(near1, came1, onward)
-        everyone, down_raw, out_raw, qkv_raw = exchange(
-            lay, [plans["down"], plans["out"], plans["qkv"]], vec, [down_sum, out_w_sum, qkv_sum], 2, 40
+        sums = jnp.sum(everyone.reshape(lay.outer, group, -1), 0)
+        sum_qkv = jnp.transpose(sums[:, : 3 * cols].reshape(group, 3, cols), (1, 0, 2)).reshape(-1)
+        sum_up = sums[:, 3 * cols : 3 * cols + ff_cols].reshape(-1)
+        sum_dy = jnp.sum(sums[:, 3 * cols + ff_cols : 3 * cols + ff_cols + width], 0)
+        rank = lax.axis_index("zo") * group + me
+
+        def own_part(vector):
+            return lax.dynamic_index_in_dim(vector.reshape(lay.count, -1), rank, 0, keepdims=False)
+
+        column = lambda v: v.astype(F32)[:, None]
+        qkv_raw = qkv_raw.astype(F32)
+        bias_grads = (own_part(sum_qkv), own_part(sum_up), own_part(sum_dy))
+        qkv_grads = (
+            jnp.sum(w_qkv.astype(F32) * qkv_raw, 1),
+            jnp.sum(w_qkv.astype(F32) * sum_qkv, 1),
+            column(gain1) * qkv_raw + column(bias1) * sum_qkv,
         )
-        (parts1,) = chain((parts1,), everyone)
+        down_grad = down_raw.astype(F32)
+        came1, *early = chain((came1, output, down_grad, *bias_grads, *qkv_grads))
+        output, down_grad, bias_grads, qkv_grads = early[0], early[1], early[2:5], early[5:8]
+        onward1 = far_onward(near1, came1)
+        parts1 = far_second(near1, came1, onward1)
 
         inputs = tokens.astype(F32)
         center = inputs - jnp.mean(inputs, -1, keepdims=True)
@@ -853,33 +948,31 @@
             - normal * jnp.mean(grad_normal * normal, -1, keepdims=True)
         )
 
-        rank = lax.axis_index("zo") * group + me
+        up_sum, token_grad = chain((up_sum, token_grad))
         (up_raw,) = deal_exchange(lay, [plans["up"]], [up_sum], True, 3)
-        sums = jnp.sum(everyone.reshape(lay.outer, group, -1), 0)
-        sum_qkv = jnp.transpose(sums[:, : 3 * cols].reshape(group, 3, cols), (1, 0, 2)).reshape(-1)
-        sum_up = sums[:, 3 * cols : 3 * cols + ff_cols].reshape(-1)
-        sum_dy = jnp.sum(sums[:, 3 * cols + ff_cols : 3 * cols + ff_cols + width], 0)
-
-        def own_part(vector):
-            return lax.dynamic_index_in_dim(vector.reshape(lay.count, -1), rank, 0, keepdims=False)
-
-        up_raw, qkv_raw = up_raw.astype(F32), qkv_raw.astype(F32)
-        column = lambda v: v.astype(F32)[:, None]
+        up_raw = up_raw.astype(F32)
+        up_grads = (
+            jnp.sum(w_up.astype(F32) * up_raw, 1),
+            jnp.sum(w_up.astype(F32) * sum_up, 1),
+            column(gain2) * up_raw + column(bias2) * sum_up,
+        )
+        out_w_sum, *up_grads = chain((out_w_sum, *up_grads))
+        (out_raw,) = deal_exchange(lay, [plans["out"]], [out_w_sum], True, 2)
         return (
             output,
             token_grad,
-            jnp.sum(w_qkv.astype(F32) * qkv_raw, 1),
-            jnp.sum(w_qkv.astype(F32) * sum_qkv, 1),
-            jnp.sum(w_up.astype(F32) * up_raw, 1),
-            jnp.sum(w_up.astype(F32) * sum_up, 1),
-            column(gain1) * qkv_raw + column(bias1) * sum_qkv,
-            own_part(sum_qkv),
+            qkv_grads[0],
+            qkv_grads[1],
+            up_grads[0],
+            up_grads[1],
+            qkv_grads[2],
+            bias_grads[0],
             out_raw.astype(F32),
-            own_part(sum_dy),
-            column(gain2) * up_raw + column(bias2) * sum_up,
-            own_part(sum_up),
-            down_raw.astype(F32),
-            own_part(sum_dy),
+            bias_grads[2],
+            up_grads[2],
+            bias_grads[1],
+            down_grad,
+            bias_grads[2],
         )
 
     return step

time: 636 us -> 622 us (0.978)
  waiting for transfers between devices: 18.7 us -> 40.9 us
  local copies, waits for them, and re-layouts: 40 us -> 21.9 us
  other arithmetic: 59.6 us -> 46.5 us
    ppermute x22 -> x20, waiting for transfers between devices: 16.4 us -> 35.1 us  [across(): return lax.ppermute(value, GROUP, lay.shift(*o))]
    unnamed x122 -> x114, local copies, waits for them, and re-layouts: 27.5 us -> 9.17 us
    pallas_call x1, Pallas kernels: 104 us -> 96.6 us  [norm_exchange(): pl.pallas_call(functools.partial(norm_kernel, lay, plan), out_shape=[whol...]
    pallas_call x3 -> x4, Pallas kernels: 42.9 us -> 50.3 us  [deal_exchange(): pl.pallas_call(functools.partial(deal_kernel, lay, plan, back), out_shape...]
    pallas_call x5 -> x4, Pallas kernels: 141 us -> 137 us  [the longest x3 103 us: pair_matmul(): pl.pallas_call(functools.partial(pair_kernel, lay, plan, with_vec, bool(s...]
    ppermute x22 -> x20, starting transfers between devices: 22.8 us -> 19.8 us  [across(): return lax.ppermute(value, GROUP, lay.shift(*o))]
  transfers between devices with their start and end apart: 36 -> 29, of which waited for: 4 -> 7; matrix products, arithmetic and copies ran while one was open for 38% -> 35% of each run, Pallas kernels for 46% -> 47%
where the time goes in v5:
time: 622 us; the launch traced here: 617 us
  Pallas kernels  313 us (50%)
  matrix products  159 us (26%)
  other arithmetic  46.5 us (7%)
  waiting for transfers between devices  40.9 us (7%)
  local copies, waits for them, and re-layouts  21.9 us (4%)
  starting transfers between devices  20.9 us (3%)
  between operations  15.6 us (3%)
    dot_general x8, matrix products, dot(): lax.dot_general(left, right, (dims, ((), ())), preferred_element_type=F32)  159 us
    pallas_call x3, Pallas kernels, pair_matmul(): pl.pallas_call(functools.partial(pair_kernel, lay, plan, with_vec, bool(s...  103 us
    pallas_call x1, Pallas kernels, norm_exchange(): pl.pallas_call(functools.partial(norm_kernel, lay, plan), out_shape=[whol...  96.6 us
    pallas_call x4, Pallas kernels, deal_exchange(): pl.pallas_call(functools.partial(deal_kernel, lay, plan, back), out_shape...  50.3 us
    ppermute x20, waiting for transfers between devices, across(): return lax.ppermute(value, GROUP, lay.shift(*o))  35.1 us
    pallas_call x1, Pallas kernels, step(): pl.pallas_call(functools.partial(attend_kernel, lay, scaling), grid=(seqs...  34.5 us
    pallas_call x1, Pallas kernels, step(): pl.pallas_call(functools.partial(attend_back_kernel, scaling), grid=(seqs...  28.5 us
    ppermute x20, starting transfers between devices, across(): return lax.ppermute(value, GROUP, lay.shift(*o))  19.8 us
  transfers between devices with their start and end apart: 29, of which 7 were waited for; matrix products, arithmetic and copies ran while one was open for 35% of the time, Pallas kernels for 47%

profile of v5, /device:TPU:0, one launch (start us, length us, event | category | flops | bytes accessed | tf_op | source)
XLA Modules:
  0.0 617.2 jit_solution(13535256829608665636)
XLA Ops:
  7.2 13.7 %shard_map.254 = bf16[512,768]{1,0:T(8,128)(2,1)} custom-call(bf16[64,6144]{1,0:T(8,128)(2,1)} %refs_0_.1), custom_call_target="tpu_custom_call" | custom-call | flops 11900000256 | bytes 1048576 | tf_op jit(solution)/shard_map/pallas_call | solution.py:338
  21.1 15.0 %shard_map.255 = bf16[512,1024]{1,0:T(8,128)(2,1)} custom-call(bf16[64,8192]{1,0:T(8,128)(2,1)} %refs_0_.2), custom_call_target="tpu_custom_call" | custom-call | flops 11900000256 | bytes 1048576 | tf_op jit(solution)/shard_map/pallas_call | solution.py:338
  37.5 96.6 %norm_exchange.1 = (bf16[2,4,2,256,2048]{4,3,2,1,0:T(8,128)(2,1)}, bf16[2,4,2,256,2048]{4,3,2,1,0:T(8,128)(2,1)}, bf16[2,4,2,256,2048]{4,3,2,1,0:T(8,128)(2,1)},...) custom-call(bf16[2,256,2048]{2,1,0:T(8,128)(2,1)S(1)} %copy-done, ...), custom_call_target="tpu_custom_call" | custom-call | flops 70000001024 | bytes 1048576 | tf_op jit(solution)/shard_map/norm_exchange/pallas_call | solution.py:291
  137.9 1.4 collective-permute-start.1
  140.9 3.0 multiply_sine_fusion
  143.8 2.0 copy.31.refs_3_.col_ref
  145.8 19.3 %convolution_add_fusion = f32[4096,768]{1,0:T(8,128)} fusion(bf16[4096,2048]{1,0:T(8,128)(2,1)} %bitcast.100, bf16[2048,768]{1,0:T(8,128)(2,1)} %all-gather.5.cloned.1.call-done.refs_1_, f32[768]{0:T(1024)S(1)} %add.294), kind=kOutput, calls=%fused_computation.11 | convolution fusion | flops 12888047616 | bytes 32508928 | tf_op jit(solution)/shard_map/dot_general | solution.py:26
  165.1 4.8 all-gather.7.cloned.1.call-done.refs_3_
  169.9 28.6 %fusion.4 = (bf16[4096,1024]{1,0:T(8,128)(2,1)}, bf16[4096,1024]{1,0:T(8,128)(2,1)}) fusion(f32[1024]{0:T(1024)S(1)} %bitcast.88, bf16[4096,2048]{1,0:T(8,128)(2,1)} %bitcast.99, bf16[2048,1024]{1,0:T(8,128)(2,1)} %all-gather.7.cloned.1.call-done.refs_3_), kind=kOutput, calls=%fused_computation.5 | convolution fusion | flops 17230200832 | bytes 37752832 | tf_op jit(solution)/shard_map/dot_general | solution.py:26
  199.9 34.5 %attend.1 = (bf16[4,1024,256]{2,1,0:T(8,128)(2,1)}, bf16[4,1024,256]{2,1,0:T(8,128)(2,1)}, bf16[4,1024,256]{2,1,0:T(8,128)(2,1)}, bf16[2,2,2,2,256,256]{5,4,3,2,...) custom-call(f32[2,2,2,2,256,768]{5,4,3,2,1,0:T(8,128)} %bitcast.73, ...), custom_call_target="tpu_custom_call" | custom-call | flops 4294967296 | bytes 31457280 | tf_op jit(solution)/shard_map/attend/pallas_call | solution.py:821
  234.4 24.1 %convolution_convert_fusion.2 = bf16[2048,1024]{1,0:T(8,128)(2,1)} fusion(bf16[4096,2048]{1,0:T(8,128)(2,1)} %bitcast.91, bf16[4096,1024]{1,0:T(8,128)(2,1)} %get-tuple-element.134), kind=kOutput, calls=%fused_computation.31 | convolution fusion | flops 17181966336 | bytes 29360128 | tf_op jit(solution)/shard_map/dot_general | solution.py:26
  258.5 11.9 %convolution_convert_fusion = bf16[4096,256]{1,0:T(8,128)(2,1)} fusion(bf16[4096,2048]{1,0:T(8,128)(2,1)} %bitcast.92, bf16[2048,256]{1,0:T(8,128)(2,1)} %all-gather.9.cloned.1.call-done.refs_1_), kind=kOutput, calls=%fused_computation.17 | convolution fusion | flops 4296015872 | bytes 19922944 | tf_op jit(solution)/shard_map/dot_general | solution.py:26
  270.4 28.5 %attend_back.1 = bf16[2,2,2,2,256,768]{5,4,3,2,1,0:T(8,128)(2,1)} custom-call(bf16[4,1024,256]{2,1,0:T(8,128)(2,1)} %get-tuple-element.126.q_ref, bf16[4,1024,256]{2,1,0:T(8,128)(2,1)} %get-tuple-element.127.k_ref, bf16[4,1024,256]{2,1,0:T(8,128)(2,1)} %get-tuple-element.128.v_ref, bf16[2,2,2,2,256,256]{5,4,3,2,1,0:T(8,128)(2,1)} %bitcast.104, ...), custom_call_target="tpu_custom_call" | custom-call | flops 10737418240 | bytes 25165824 | tf_op jit(solution)/shard_map/attend_back/pallas_call | solution.py:863
  298.9 20.2 %convolution_convert_fusion.3 = bf16[2048,768]{1,0:T(8,128)(2,1)} fusion(bf16[4096,2048]{1,0:T(8,128)(2,1)} %bitcast.97, bf16[4096,768]{1,0:T(8,128)(2,1)} %bitcast.74), kind=kOutput, calls=%fused_computation.32 | convolution fusion | flops 12886474752 | bytes 26214400 | tf_op jit(solution)/shard_map/dot_general | solution.py:26
  319.1 32.0 %shard_map.256 = (bf16[256,2048]{1,0:T(8,128)(2,1)}, bf16[256,2048]{1,0:T(8,128)(2,1)}, bf16[256,2048]{1,0:T(8,128)(2,1)}, bf16[256,2048]{1,0:T(8,128)(2,1)}, bf...) custom-call(bf16[2,4,512,256]{3,2,1,0:T(8,128)(2,1)} %bitcast.95, ...), custom_call_target="tpu_custom_call" | custom-call | flops 21474836480 | bytes 33554432 | tf_op jit(solution)/shard_map/pallas_call | solution.py:496
  351.1 1.5 collective-permute-start.3
  353.2 1.5 collective-permute-start.5
  355.2 9.5 %convolution_convert_fusion.4 = bf16[2048,256]{1,0:T(8,128)(2,1)} fusion(bf16[4096,2048]{1,0:T(8,128)(2,1)} %bitcast.93, bf16[4096,256]{1,0:T(8,128)(2,1)S(1)} %bitcast.96), kind=kOutput, calls=%fused_computation.36 | convolution fusion | flops 4295491584 | bytes 19922944 | tf_op jit(solution)/shard_map/dot_general | solution.py:26
  364.8 23.9 %convert_reduce_fusion = (f32[1024]{0:T(1024)S(1)}, bf16[4096,1024]{1,0:T(8,128)(2,1)S(1)}) fusion(bf16[4096,1024]{1,0:T(8,128)(2,1)} %get-tuple-element.146, bf16[4096,2048]{1,0:T(8,128)(2,1)} %bitcast.94, bf16[2048,1024]{1,0:T(8,128)(2,1)} %all-gather.11.cloned.1.call-done.refs_3_), kind=kOutput, calls=%fused_computation.6 | convolution fusion | flops 17200840704 | bytes 37752832 | tf_op jit(solution)/shard_map/dot_general | solution.py:26
  388.7 3.3 copy-done.52
  392.0 21.4 %convolution_convert_fusion.1 = bf16[2048,1024]{1,0:T(8,128)(2,1)} fusion(bf16[4096,2048]{1,0:T(8,128)(2,1)} %bitcast.98, bf16[4096,1024]{1,0:T(8,128)(2,1)S(1)} %get-tuple-element.237), kind=kOutput, calls=%fused_computation.30 | convolution fusion | flops 17181966336 | bytes 29360128 | tf_op jit(solution)/shard_map/dot_general | solution.py:26
  417.1 3.9 convert_reduce_fusion.1
  421.6 2.6 add_convert_fusion
  424.3 2.6 add_convert_fusion.1
  428.3 33.5 %shard_map.257 = (bf16[256,1024]{1,0:T(8,128)(2,1)}, bf16[256,1024]{1,0:T(8,128)(2,1)}, bf16[256,1024]{1,0:T(8,128)(2,1)}, bf16[256,1024]{1,0:T(8,128)(2,1)}, bf...) custom-call(bf16[2,4,512,768]{3,2,1,0:T(8,128)(2,1)} %bitcast.75, ...), custom_call_target="tpu_custom_call" | custom-call | flops 15032385536 | bytes 33554432 | tf_op jit(solution)/shard_map/pallas_call | solution.py:496
  464.9 37.2 %shard_map.258 = (bf16[256,1024]{1,0:T(8,128)(2,1)}, bf16[256,1024]{1,0:T(8,128)(2,1)}, bf16[256,1024]{1,0:T(8,128)(2,1)}, bf16[256,1024]{1,0:T(8,128)(2,1)}, bf...) custom-call(bf16[2,4,512,768]{3,2,1,0:T(8,128)(2,1)} %bitcast.76, ...), custom_call_target="tpu_custom_call" | custom-call | flops 15032385536 | bytes 33554432 | tf_op jit(solution)/shard_map/pallas_call | solution.py:496
  508.2 1.5 convert_element_type.255
  509.7 1.7 constant_dynamic-slice_fusion.1
  513.3 3.4 fusion.19
  518.6 7.1 %collective-permute-done.16 = bf16[256,1024]{1,0:T(8,128)(2,1)S(1)} collective-permute-done((bf16[256,1024]{1,0:T(8,128)(2,1)}, bf16[256,1024]{1,0:T(8,128)(2,1)S(1)}, u32[]{:S(2)}, u32[]{:S(2)}) %collective-permute-start.16) | collective-permute-done | bytes 524320 | tf_op jit(solution)/shard_map/ppermute | solution.py:687
  526.9 2.0 add_convert_fusion.5
  528.9 2.1 collective-permute-start.9
  531.0 1.7 add_bitcast_fusion.1
  532.7 2.0 add_bitcast_fusion
  534.9 2.6 fusion.12
  537.5 6.5 %collective-permute-done.8 = bf16[256,1024]{1,0:T(8,128)(2,1)S(1)} collective-permute-done((bf16[256,1024]{1,0:T(8,128)(2,1)S(1)}, bf16[256,1024]{1,0:T(8,128)(2,1)S(1)}, u32[]{:S(2)}, u32[]{:S(2)}) %collective-permute-start.8) | collective-permute-done | bytes 524320 | tf_op jit(solution)/shard_map/ppermute | solution.py:687
  544.0 4.2 collective-permute-done.9
  550.4 1.9 collective-permute-start.20
  552.5 1.9 collective-permute-start.18
  554.4 9.9 %collective-permute-done.19 = bf16[256,1024]{1,0:T(8,128)(2,1)} collective-permute-done((bf16[256,1024]{1,0:T(8,128)(2,1)}, bf16[256,1024]{1,0:T(8,128)(2,1)}, u32[]{:S(2)}, u32[]{:S(2)}) %collective-permute-start.19) | collective-permute-done | bytes 524320 | tf_op jit(solution)/shard_map/ppermute | solution.py:687
  564.3 1.6 add_bitcast_fusion.3
  566.0 1.5 add_bitcast_fusion.2
  567.7 7.3 %collective-permute-done.17 = bf16[256,1024]{1,0:T(8,128)(2,1)S(1)} collective-permute-done((bf16[256,1024]{1,0:T(8,128)(2,1)}, bf16[256,1024]{1,0:T(8,128)(2,1)S(1)}, u32[]{:S(2)}, u32[]{:S(2)}) %collective-permute-start.17) | collective-permute-done | bytes 524320 | tf_op jit(solution)/shard_map/ppermute | solution.py:687
  579.2 2.9 convert_add_fusion.1
  582.1 13.7 %shard_map.259 = bf16[64,8192]{1,0:T(8,128)(2,1)} custom-call(bf16[512,1024]{1,0:T(8,128)(2,1)} %reduce-scatter.9.cloned.1.call-done.refs_0_), custom_call_target="tpu_custom_call" | custom-call | flops 11900000256 | bytes 1048576 | tf_op jit(solution)/shard_map/pallas_call | solution.py:338
  595.9 3.8 fusion.16
  599.7 7.9 %shard_map.260 = bf16[64,2048]{1,0:T(8,128)(2,1)} custom-call(bf16[512,256]{1,0:T(8,128)(2,1)} %reduce-scatter.11.cloned.1.call-done.refs_0_), custom_call_target="tpu_custom_call" | custom-call | flops 11900000256 | bytes 1048576 | tf_op jit(solution)/shard_map/pallas_call | solution.py:338
  607.6 1.8 convert_element_type.278
  (217 shorter events, 36.1 us)
Async XLA Ops:
  7.2 138.6 %all-gather.5.cloned.1.call-start = ((), (), s32[]{:S(2)}) async-start(), calls=%async_computation.4 | async-start | bytes 3932160 | tf_op jit(solution)/shard_map/all_gather | solution.py:742
  20.9 15.3 %copy-start.51 = (bf16[64]{0:T(256)(128)(2,1)S(1)}, bf16[64]{0:T(256)(128)(2,1)}, u32[]{:S(2)}) copy-start(bf16[64]{0:T(256)(128)(2,1)} %param.20) | copy-start | bytes 388
  21.0 16.4 %copy-start.39 = (bf16[64]{0:T(256)(128)(2,1)S(1)}, bf16[64]{0:T(256)(128)(2,1)}, u32[]{:S(2)}) copy-start(bf16[64]{0:T(256)(128)(2,1)} %param.29) | copy-start | bytes 388
  21.0 16.4 %copy-start.40 = (bf16[64]{0:T(256)(128)(2,1)S(1)}, bf16[64]{0:T(256)(128)(2,1)}, u32[]{:S(2)}) copy-start(bf16[64]{0:T(256)(128)(2,1)} %param.25) | copy-start | bytes 388
  21.0 16.4 %copy-start.41 = (bf16[256]{0:T(256)(128)(2,1)S(1)}, bf16[256]{0:T(256)(128)(2,1)}, u32[]{:S(2)}) copy-start(bf16[256]{0:T(256)(128)(2,1)} %param.27) | copy-start | bytes 1540
  21.0 16.4 %copy-start.42 = (bf16[192]{0:T(256)(128)(2,1)S(1)}, bf16[192]{0:T(256)(128)(2,1)}, u32[]{:S(2)}) copy-start(bf16[192]{0:T(256)(128)(2,1)} %param.23) | copy-start | bytes 1156
  21.0 16.4 %copy-start = (bf16[2,256,2048]{2,1,0:T(8,128)(2,1)S(1)}, bf16[2,256,2048]{2,1,0:T(8,128)(2,1)}, u32[]{:S(2)}) copy-start(bf16[2,256,2048]{2,1,0:T(8,128)(2,1)} %refs_0_.3) | copy-start | bytes 6291460
  21.0 16.4 %copy-start.2 = (bf16[64,8192]{1,0:T(8,128)(2,1)S(1)}, bf16[64,8192]{1,0:T(8,128)(2,1)}, u32[]{:S(2)}) copy-start(bf16[64,8192]{1,0:T(8,128)(2,1)} %refs_3_.1) | copy-start | bytes 3145732
  21.0 16.4 %copy-start.3 = (bf16[64,2048]{1,0:T(8,128)(2,1)S(1)}, bf16[64,2048]{1,0:T(8,128)(2,1)}, u32[]{:S(2)}) copy-start(bf16[64,2048]{1,0:T(8,128)(2,1)} %refs_2_.1) | copy-start | bytes 786436
  21.0 148.9 %all-gather.7.cloned.1.call-start = ((), (), s32[]{:S(2)}) async-start(), calls=%async_computation.5 | async-start | bytes 5242880 | tf_op jit(solution)/shard_map/all_gather | solution.py:742
  36.1 222.4 %all-gather.9.cloned.1.call-start = ((), (), s32[]{:S(2)}) async-start(), calls=%async_computation.6 | async-start | bytes 1310720 | tf_op jit(solution)/shard_map/all_gather | solution.py:742
  37.5 96.7 %copy-start.32 = (s32[2,1024]{1,0:T(2,128)S(1)}, s32[2,1024]{1,0:T(2,128)}, u32[]{:S(2)}) copy-start(s32[2,1024]{1,0:T(2,128)} %param.16) | copy-start | bytes 24580
  134.1 185.0 %all-gather.11.cloned.1.call-start = ((), (), s32[]{:S(2)}) async-start(), calls=%async_computation.7 | async-start | bytes 5242880 | tf_op jit(solution)/shard_map/all_gather | solution.py:742
  134.1 3.7 collective-permute-start
  135.0 293.3 %reduce-scatter.5.cloned.1.call-start = ((), (), s32[]{:S(2)}) async-start(), calls=%async_computation.8 | async-start | bytes 5242880 | tf_op jit(solution)/shard_map/reduce_scatter | solution.py:847
  137.9 60.6 %collective-permute-start.1 = (bf16[2,256,2048]{2,1,0:T(8,128)(2,1)}, bf16[2,256,2048]{2,1,0:T(8,128)(2,1)S(1)}, u32[]{:S(2)}, u32[]{:S(2)}) collective-permute-start(bf16[2,256,2048]{2,1,0:T(8,128)(2,1)} %refs_5_), channel_id=1, source_target_pairs={{0,2},{1,3},{2,0},{3,1},{4,6},{5,7},{6,4},{7,5},{8,10},{9,11},{10,... | collective-permute-start | bytes 6291464 | tf_op jit(solution)/shard_map/ppermute | solution.py:687
  139.4 59.2 %collective-permute-start.2 = (bf16[2,256,2048]{2,1,0:T(8,128)(2,1)}, bf16[2,256,2048]{2,1,0:T(8,128)(2,1)}, u32[]{:S(2)}, u32[]{:S(2)}) collective-permute-start(bf16[2,256,2048]{2,1,0:T(8,128)(2,1)} %refs_5_), channel_id=1, source_target_pairs={{0,4},{1,5},{2,6},{3,7},{4,0},{5,1},{6,2},{7,3},{8,12},{9,13},{10,... | collective-permute-start | bytes 6291464 | tf_op jit(solution)/shard_map/ppermute | solution.py:687
  258.5 206.5 %reduce-scatter.7.cloned.1.call-start = ((), (), s32[]{:S(2)}) async-start(), calls=%async_computation.9 | async-start | bytes 3932160 | tf_op jit(solution)/shard_map/reduce_scatter | solution.py:847
  319.1 36.1 %copy-start.43 = (bf16[2,2,2,2,256,256]{5,4,3,2,1,0:T(8,128)(2,1)S(1)}, bf16[2,2,2,2,256,256]{5,4,3,2,1,0:T(8,128)(2,1)}, u32[]{:S(2)}) copy-start(bf16[2,2,2,2,256,256]{5,4,3,2,1,0:T(8,128)(2,1)} %get-tuple-element.124) | copy-start | bytes 6291460
  351.1 70.5 %collective-permute-start.3 = (bf16[256,2048]{1,0:T(8,128)(2,1)}, bf16[256,2048]{1,0:T(8,128)(2,1)S(1)}, u32[]{:S(2)}, u32[]{:S(2)}) collective-permute-start(bf16[256,2048]{1,0:T(8,128)(2,1)} %get-tuple-element.137), channel_id=1, source_target_pairs={{0,4},{1,5},{2,6},{3,7},{4,0},{5,1},{6,2},{7,3},{8,12},{9,13},{10,... | collective-permute-start | bytes 3145736 | tf_op jit(solution)/shard_map/ppermute | solution.py:687
  352.6 69.0 %collective-permute-start.4 = (bf16[256,2048]{1,0:T(8,128)(2,1)}, bf16[256,2048]{1,0:T(8,128)(2,1)}, u32[]{:S(2)}, u32[]{:S(2)}) collective-permute-start(bf16[256,2048]{1,0:T(8,128)(2,1)} %get-tuple-element.138), channel_id=1, source_target_pairs={{0,4},{1,5},{2,6},{3,7},{4,0},{5,1},{6,2},{7,3},{8,12},{9,13},{10,... | collective-permute-start | bytes 3145736 | tf_op jit(solution)/shard_map/ppermute | solution.py:687
  353.2 68.5 %collective-permute-start.5 = (bf16[256,2048]{1,0:T(8,128)(2,1)}, bf16[256,2048]{1,0:T(8,128)(2,1)}, u32[]{:S(2)}, u32[]{:S(2)}) collective-permute-start(bf16[256,2048]{1,0:T(8,128)(2,1)} %get-tuple-element.139), channel_id=1, source_target_pairs={{0,2},{1,3},{2,0},{3,1},{4,6},{5,7},{6,4},{7,5},{8,10},{9,11},{10,... | collective-permute-start | bytes 3145736 | tf_op jit(solution)/shard_map/ppermute | solution.py:687
  354.6 67.0 %collective-permute-start.6 = (bf16[256,2048]{1,0:T(8,128)(2,1)}, bf16[256,2048]{1,0:T(8,128)(2,1)}, u32[]{:S(2)}, u32[]{:S(2)}) collective-permute-start(bf16[256,2048]{1,0:T(8,128)(2,1)} %get-tuple-element.140), channel_id=1, source_target_pairs={{0,2},{1,3},{2,0},{3,1},{4,6},{5,7},{6,4},{7,5},{8,10},{9,11},{10,... | collective-permute-start | bytes 3145736 | tf_op jit(solution)/shard_map/ppermute | solution.py:687
  364.7 217.4 %reduce-scatter.9.cloned.1.call-start = ((), (), s32[]{:S(2)}) async-start(), calls=%async_computation.10 | async-start | bytes 5242880 | tf_op jit(solution)/shard_map/reduce_scatter | solution.py:847
  413.5 186.2 %reduce-scatter.11.cloned.1.call-start = ((), (), s32[]{:S(2)}) async-start(), calls=%async_computation.11 | async-start | bytes 1310720 | tf_op jit(solution)/shard_map/reduce_scatter | solution.py:847
  426.8 102.1 %collective-permute-start.11 = (bf16[256,2048]{1,0:T(8,128)(2,1)}, bf16[256,2048]{1,0:T(8,128)(2,1)}, u32[]{:S(2)}, u32[]{:S(2)}) collective-permute-start(bf16[256,2048]{1,0:T(8,128)(2,1)} %add_convert_fusion.1), channel_id=1, source_target_pairs={{0,2},{1,3},{2,0},{3,1},{4,6},{5,7},{6,4},{7,5},{8,10},{9,11},{10,... | collective-permute-start | bytes 3145736 | tf_op jit(solution)/shard_map/ppermute | solution.py:687
  428.3 102.7 %collective-permute-start.12 = (bf16[256,2048]{1,0:T(8,128)(2,1)}, bf16[256,2048]{1,0:T(8,128)(2,1)}, u32[]{:S(2)}, u32[]{:S(2)}) collective-permute-start(bf16[256,2048]{1,0:T(8,128)(2,1)} %add_convert_fusion), channel_id=1, source_target_pairs={{0,4},{1,5},{2,6},{3,7},{4,0},{5,1},{6,2},{7,3},{8,12},{9,13},{10,... | collective-permute-start | bytes 3145736 | tf_op jit(solution)/shard_map/ppermute | solution.py:687
  461.8 49.6 %collective-permute-start.13 = (bf16[256,1024]{1,0:T(8,128)(2,1)}, bf16[256,1024]{1,0:T(8,128)(2,1)}, u32[]{:S(2)}, u32[]{:S(2)}) collective-permute-start(bf16[256,1024]{1,0:T(8,128)(2,1)} %get-tuple-element.158), channel_id=1, source_target_pairs={{0,4},{1,5},{2,6},{3,7},{4,0},{5,1},{6,2},{7,3},{8,12},{9,13},{10,... | collective-permute-start | bytes 1572872 | tf_op jit(solution)/shard_map/ppermute | solution.py:687
  462.8 53.8 %collective-permute-start.14 = (bf16[256,1024]{1,0:T(8,128)(2,1)}, bf16[256,1024]{1,0:T(8,128)(2,1)}, u32[]{:S(2)}, u32[]{:S(2)}) collective-permute-start(bf16[256,1024]{1,0:T(8,128)(2,1)} %get-tuple-element.160), channel_id=1, source_target_pairs={{0,4},{1,5},{2,6},{3,7},{4,0},{5,1},{6,2},{7,3},{8,12},{9,13},{10,... | collective-permute-start | bytes 1572872 | tf_op jit(solution)/shard_map/ppermute | solution.py:687
  463.9 54.2 %collective-permute-start.15 = (bf16[256,1024]{1,0:T(8,128)(2,1)}, bf16[256,1024]{1,0:T(8,128)(2,1)}, u32[]{:S(2)}, u32[]{:S(2)}) collective-permute-start(bf16[256,1024]{1,0:T(8,128)(2,1)} %get-tuple-element.157), channel_id=1, source_target_pairs={{0,2},{1,3},{2,0},{3,1},{4,6},{5,7},{6,4},{7,5},{8,10},{9,11},{10,... | collective-permute-start | bytes 1572872 | tf_op jit(solution)/shard_map/ppermute | solution.py:687
  464.9 43.3 %copy-start.11 = (bf16[64,8192]{1,0:T(8,128)(2,1)S(1)}, bf16[64,8192]{1,0:T(8,128)(2,1)}, u32[]{:S(2)}) copy-start(bf16[64,8192]{1,0:T(8,128)(2,1)} %get-tuple-element.185) | copy-start | bytes 3145732
  503.4 23.4 %copy-start.19 = (bf16[256,1024]{1,0:T(8,128)(2,1)S(1)}, bf16[256,1024]{1,0:T(8,128)(2,1)}, u32[]{:S(2)}) copy-start(bf16[256,1024]{1,0:T(8,128)(2,1)} %get-tuple-element.156) | copy-start | bytes 1572868
  508.2 17.5 %copy-start.45 = (bf16[256,1024]{1,0:T(8,128)(2,1)S(1)}, bf16[256,1024]{1,0:T(8,128)(2,1)}, u32[]{:S(2)}) copy-start(bf16[256,1024]{1,0:T(8,128)(2,1)} %get-tuple-element.166) | copy-start | bytes 1572868
  508.2 17.6 %copy-start.20 = (bf16[256,1024]{1,0:T(8,128)(2,1)S(1)}, bf16[256,1024]{1,0:T(8,128)(2,1)}, u32[]{:S(2)}) copy-start(bf16[256,1024]{1,0:T(8,128)(2,1)} %get-tuple-element.159) | copy-start | bytes 1572868
  508.2 20.7 %copy-start.44 = (bf16[256,1024]{1,0:T(8,128)(2,1)S(1)}, bf16[256,1024]{1,0:T(8,128)(2,1)}, u32[]{:S(2)}) copy-start(bf16[256,1024]{1,0:T(8,128)(2,1)} %get-tuple-element.167) | copy-start | bytes 1572868
  508.2 22.8 %copy-start.8 = (bf16[256,2048]{1,0:T(8,128)(2,1)S(1)}, bf16[256,2048]{1,0:T(8,128)(2,1)}, u32[]{:S(2)}) copy-start(bf16[256,2048]{1,0:T(8,128)(2,1)} %get-tuple-element.179) | copy-start | bytes 3145732
  511.4 14.4 %collective-permute-start.16 = (bf16[256,1024]{1,0:T(8,128)(2,1)}, bf16[256,1024]{1,0:T(8,128)(2,1)S(1)}, u32[]{:S(2)}, u32[]{:S(2)}) collective-permute-start(bf16[256,1024]{1,0:T(8,128)(2,1)} %get-tuple-element.161), channel_id=1, source_target_pairs={{0,2},{1,3},{2,0},{3,1},{4,6},{5,7},{6,4},{7,5},{8,10},{9,11},{10,... | collective-permute-start | bytes 1572872 | tf_op jit(solution)/shard_map/ppermute | solution.py:687
  512.0 97.3 %copy-start.53 = (f32[64]{0:T(128)}, f32[64]{0:T(128)S(1)}, u32[]{:S(2)}) copy-start(f32[64]{0:T(128)S(1)} %fusion.23) | copy-start | bytes 772
  516.7 20.8 %collective-permute-start.10 = (bf16[256,1024]{1,0:T(8,128)(2,1)S(1)}, bf16[256,1024]{1,0:T(8,128)(2,1)S(1)}, u32[]{:S(2)}, u32[]{:S(2)}) collective-permute-start(bf16[256,1024]{1,0:T(8,128)(2,1)S(1)} %copy-done.47), channel_id=1, source_target_pairs={{0,2},{1,3},{2,0},{3,1},{4,6},{5,7},{6,4},{7,5},{8,10},{9,11},{10,... | collective-permute-start | bytes 1572872 | tf_op jit(solution)/shard_map/ppermute | solution.py:687
  518.1 19.4 %collective-permute-start.7 = (bf16[256,1024]{1,0:T(8,128)(2,1)S(1)}, bf16[256,1024]{1,0:T(8,128)(2,1)S(1)}, u32[]{:S(2)}, u32[]{:S(2)}) collective-permute-start(bf16[256,1024]{1,0:T(8,128)(2,1)S(1)} %copy-done.46), channel_id=1, source_target_pairs={{0,4},{1,5},{2,6},{3,7},{4,0},{5,1},{6,2},{7,3},{8,12},{9,13},{10,... | collective-permute-start | bytes 1572872 | tf_op jit(solution)/shard_map/ppermute | solution.py:687
  525.8 18.3 %collective-permute-start.8 = (bf16[256,1024]{1,0:T(8,128)(2,1)S(1)}, bf16[256,1024]{1,0:T(8,128)(2,1)S(1)}, u32[]{:S(2)}, u32[]{:S(2)}) collective-permute-start(bf16[256,1024]{1,0:T(8,128)(2,1)S(1)} %copy-done.45), channel_id=1, source_target_pairs={{0,4},{1,5},{2,6},{3,7},{4,0},{5,1},{6,2},{7,3},{8,12},{9,13},{10,... | collective-permute-start | bytes 1572872 | tf_op jit(solution)/shard_map/ppermute | solution.py:687
  528.9 19.3 %collective-permute-start.9 = (bf16[256,1024]{1,0:T(8,128)(2,1)S(1)}, bf16[256,1024]{1,0:T(8,128)(2,1)S(1)}, u32[]{:S(2)}, u32[]{:S(2)}) collective-permute-start(bf16[256,1024]{1,0:T(8,128)(2,1)S(1)} %copy-done.44), channel_id=1, source_target_pairs={{0,2},{1,3},{2,0},{3,1},{4,6},{5,7},{6,4},{7,5},{8,10},{9,11},{10,... | collective-permute-start | bytes 1572872 | tf_op jit(solution)/shard_map/ppermute | solution.py:687
  537.4 28.5 %copy-start.16 = (bf16[256,1024]{1,0:T(8,128)(2,1)S(1)}, bf16[256,1024]{1,0:T(8,128)(2,1)}, u32[]{:S(2)}) copy-start(bf16[256,1024]{1,0:T(8,128)(2,1)} %get-tuple-element.174) | copy-start | bytes 1572868
  549.2 15.1 %collective-permute-start.19 = (bf16[256,1024]{1,0:T(8,128)(2,1)}, bf16[256,1024]{1,0:T(8,128)(2,1)}, u32[]{:S(2)}, u32[]{:S(2)}) collective-permute-start(bf16[256,1024]{1,0:T(8,128)(2,1)} %add_convert_fusion.3), channel_id=1, source_target_pairs={{0,2},{1,3},{2,0},{3,1},{4,6},{5,7},{6,4},{7,5},{8,10},{9,11},{10,... | collective-permute-start | bytes 1572872 | tf_op jit(solution)/shard_map/ppermute | solution.py:687
  550.4 24.6 %copy-start.15 = (bf16[256,1024]{1,0:T(8,128)(2,1)S(1)}, bf16[256,1024]{1,0:T(8,128)(2,1)}, u32[]{:S(2)}) copy-start(bf16[256,1024]{1,0:T(8,128)(2,1)} %get-tuple-element.154) | copy-start | bytes 1572868
  550.4 15.6 %collective-permute-start.20 = (bf16[256,1024]{1,0:T(8,128)(2,1)}, bf16[256,1024]{1,0:T(8,128)(2,1)}, u32[]{:S(2)}, u32[]{:S(2)}) collective-permute-start(bf16[256,1024]{1,0:T(8,128)(2,1)} %add_convert_fusion.2), channel_id=1, source_target_pairs={{0,4},{1,5},{2,6},{3,7},{4,0},{5,1},{6,2},{7,3},{8,12},{9,13},{10,... | collective-permute-start | bytes 1572872 | tf_op jit(solution)/shard_map/ppermute | solution.py:687
  552.4 22.6 %collective-permute-start.17 = (bf16[256,1024]{1,0:T(8,128)(2,1)}, bf16[256,1024]{1,0:T(8,128)(2,1)S(1)}, u32[]{:S(2)}, u32[]{:S(2)}) collective-permute-start(bf16[256,1024]{1,0:T(8,128)(2,1)} %add_convert_fusion.5), channel_id=1, source_target_pairs={{0,2},{1,3},{2,0},{3,1},{4,6},{5,7},{6,4},{7,5},{8,10},{9,11},{10,... | collective-permute-start | bytes 1572872 | tf_op jit(solution)/shard_map/ppermute | solution.py:687
  552.5 23.8 %collective-permute-start.18 = (bf16[256,1024]{1,0:T(8,128)(2,1)}, bf16[256,1024]{1,0:T(8,128)(2,1)S(1)}, u32[]{:S(2)}, u32[]{:S(2)}) collective-permute-start(bf16[256,1024]{1,0:T(8,128)(2,1)} %add_convert_fusion.4), channel_id=1, source_target_pairs={{0,4},{1,5},{2,6},{3,7},{4,0},{5,1},{6,2},{7,3},{8,12},{9,13},{10,... | collective-permute-start | bytes 1572872 | tf_op jit(solution)/shard_map/ppermute | solution.py:687
  (35 other events, 243.0 us)
Sparse Core Ops, SparseCore 0:
  21.0 67.7 all-gather.4
  90.4 79.4 all-gather.6
  171.5 26.4 all-gather.8
  199.5 80.1 all-gather.10
  282.3 75.2 reduce-scatter.4
  364.9 57.8 reduce-scatter.6
  425.0 85.1 reduce-scatter.8
  552.5 24.5 reduce-scatter.10

commit v6 on v5

--- a/solution.py
+++ b/solution.py
@@ -490,7 +490,7 @@
     if plan:
         scratch += [pltpu.SemaphoreType.DMA((lay.group - 1, count))] * 2 + [pltpu.SemaphoreType.DMA((count,))]
     if with_vec:
-        shapes.append(jax.ShapeDtypeStruct((lay.count, *vec.shape), F32))
+        shapes.append(jax.ShapeDtypeStruct((lay.count, *vec.shape), vec.dtype))
         scratch += [pltpu.SemaphoreType.DMA((lay.count - 1,))] * 2 + [pltpu.SemaphoreType.DMA]
     depth = sum(a.shape[1] for a in acts)
     return pl.pallas_call(
@@ -639,7 +639,7 @@
             ctx_ref[c, 0, i, 0] = ctx_buf[pl.ds((c * chips + i) * length, length), :]
 
 
-def attend_back_kernel(scaling, q_ref, k_ref, v_ref, g_ref, cos_ref, sin_ref, col_ref, row_ref, lse_ref, out_ref,
+def attend_back_kernel(scaling, q_ref, k_ref, v_ref, g_ref, cos_ref, sin_ref, col_ref, row_ref, lse_ref, out_ref, sum_ref,
                        g_buf, dq_buf, dk_buf, dv_buf, cos_buf, sin_buf):
     cores, _, chips, _, length, _ = out_ref.shape
     total = q_ref.shape[1]
@@ -673,9 +673,17 @@
         for i in range(chips):
             at = pl.ds((c * chips + i) * length, length)
             cosine, sine = cos_buf[at, :], sin_buf[at, :]
-            out_ref[c, 0, i, 0, :, :HEAD_DIM] = turn_pairs(dq_buf[at, :] * scaling, cosine, -sine).astype(BF16)
-            out_ref[c, 0, i, 0, :, HEAD_DIM : 2 * HEAD_DIM] = turn_pairs(dk_buf[at, :] * scaling, cosine, -sine).astype(BF16)
-            out_ref[c, 0, i, 0, :, 2 * HEAD_DIM :] = dv_buf[at, :].astype(BF16)
+            pieces = (
+                turn_pairs(dq_buf[at, :] * scaling, cosine, -sine),
+                turn_pairs(dk_buf[at, :] * scaling, cosine, -sine),
+                dv_buf[at, :],
+            )
+            for k, piece in enumerate(pieces):
+                columns = slice(k * HEAD_DIM, (k + 1) * HEAD_DIM)
+                low = piece.astype(BF16)
+                out_ref[c, 0, i, 0, :, columns] = low
+                part = jnp.sum(low.astype(F32), 0, keepdims=True)
+                sum_ref[0, :, columns] = part if c + i == 0 else sum_ref[0, :, columns] + part
 
 
 def make_body(lay):
@@ -761,12 +769,12 @@
             return whole.reshape(-1, 128)
 
         names = (bias1, bias2, gain1, gain2, b_qkv, b_up, b_out, b_down)
-        (qkv_own,) = deal_exchange(lay, [plans["qkv"]], [w_qkv], False, 0)
+        (up_own,) = deal_exchange(lay, [plans["up"]], [w_up], False, 0)
+        up_w = gather_rows(up_own)
+        w_qkv_late, _ = lax.optimization_barrier((w_qkv, up_own))
+        (qkv_own,) = deal_exchange(lay, [plans["qkv"]], [w_qkv_late], False, 7)
         qkv_w = gather_rows(qkv_own)
-        w_up_late, _ = lax.optimization_barrier((w_up, qkv_own))
-        (up_own,) = deal_exchange(lay, [plans["up"]], [w_up_late], False, 7)
-        up_w = gather_rows(up_own)
-        tokens_late, _ = lax.optimization_barrier((tokens, up_own))
+        tokens_late, _ = lax.optimization_barrier((tokens, qkv_own))
         one, two, hat, vectors, out_own, down_own = norm_exchange(
             lay, [plans["out"], plans["down"]], tokens_late, laid(names), [w_out, w_down]
         )
@@ -785,25 +793,25 @@
         cotangent, hat, places = lax.optimization_barrier((cotangent, hat, places))
         near_dy = [cotangent] + [across(cotangent, o) for o in lay.near[1:]]
 
-        halves = ROTARY // 2
-        frequency = jnp.exp(jnp.arange(halves, dtype=F32) * (-2.0 * math.log(10000.0) / ROTARY))
-        phases = places.astype(F32)[:, None, :] * frequency[None, :, None]
-        cosine, sine = jnp.cos(phases), jnp.sin(phases)
-        place_col = places[:, :, None]
-        place_row = places[:, None, :]
-
-        seqs = sub * batch
-        one = after(one, cosine, sine)
-        packed = dot(one, qkv_w, ((1,), (0,))) + b_qkv_mine
-        two = after(two, packed)
-
         hidden = dot(two, up_w, ((1,), (0,))) + b_up_mine
         phi_cdf = 0.5 * (1.0 + lax.erf(hidden * math.sqrt(0.5)))
         density = jnp.exp(-0.5 * hidden * hidden) * (1.0 / math.sqrt(2.0 * math.pi))
         activated = (hidden * phi_cdf).astype(BF16)
         slope = (phi_cdf + hidden * density).astype(BF16)
         activated, slope = lax.optimization_barrier((activated, slope))
-        packed = after(packed, activated)
+
+        halves = ROTARY // 2
+        frequency = jnp.exp(jnp.arange(halves, dtype=F32) * (-2.0 * math.log(10000.0) / ROTARY))
+        places = after(places, activated)
+        phases = places.astype(F32)[:, None, :] * frequency[None, :, None]
+        cosine, sine = jnp.cos(phases), jnp.sin(phases)
+        place_col = places[:, :, None]
+        place_row = places[:, None, :]
+
+        seqs = sub * batch
+        one = after(one, cosine, sine)
+        packed = dot(one, qkv_w, ((1,), (0,))) + b_qkv_mine
+
         wide = (2, 1, chips_x, 1, length, 3 * cols)
         wide_spec = pl.BlockSpec(wide, lambda i: (0, i // batch, 0, i % batch, 0, 0))
         full = (2, sub, chips_x, batch, length, 3 * cols)
@@ -860,12 +868,12 @@
         down_sum = scatter(down_part)
         grad_context = dot(upstream, out_w, ((1,), (0,))).astype(BF16)
 
-        grad_packed = pl.pallas_call(
+        grad_packed, sum_packed = pl.pallas_call(
             functools.partial(attend_back_kernel, scaling),
             grid=(seqs,),
             in_specs=[head_spec] * 3 + [tokens_spec, turn_spec, turn_spec, col_spec, row_spec, row_spec],
-            out_specs=wide_spec,
-            out_shape=jax.ShapeDtypeStruct(full, BF16),
+            out_specs=[wide_spec, pl.BlockSpec((1, 1, 3 * cols), lambda i: (i, 0, 0))],
+            out_shape=[jax.ShapeDtypeStruct(full, BF16), jax.ShapeDtypeStruct((seqs, 1, 3 * cols), F32)],
             scratch_shapes=[pltpu.VMEM((count, HEAD_DIM), BF16)] + [pltpu.VMEM((count, HEAD_DIM), F32)] * 3 + turn_bufs,
             compiler_params=params,
             cost_estimate=pl.CostEstimate(flops=5 * work, bytes_accessed=24 << 20, transcendentals=seqs * count * count),
@@ -873,22 +881,21 @@
         )(queries, keys, values, grad_context.reshape(by_token), cosine, sine, place_col, place_row, lse)
         grad_packed = grad_packed.reshape(total, 3 * cols)
 
+        acts = chain((context, activated), grad_packed)
+        out_near = tokens_of(pair_matmul(lay, acts, (out_w, down_w), batch, (0, 1), 4))
+        out_came = far_first(out_near)
+        hat, out_near = chain((hat, out_near))
         qkv_part = outer_dot(hat, grad_packed)
         qkv_sum = scatter(qkv_part)
-        acts = chain((context, activated), qkv_part)
-        out_near = tokens_of(pair_matmul(lay, acts, (out_w, down_w), batch, (0, 1), 4))
-        out_came = far_first(out_near)
-        (upstream,) = chain((upstream,), out_near)
-        out_part = outer_dot(upstream, context)
-        out_part, upstream = chain((out_part, upstream))
+        (upstream,) = chain((upstream,), qkv_part)
         grad_hidden = (dot(upstream, down_w, ((1,), (0,))) * slope.astype(F32)).astype(BF16)
+        sum_hidden = jnp.sum(grad_hidden.astype(F32), 0)
+        out_came, grad_hidden = chain((out_came, grad_hidden))
+        onward, grad_hidden = chain((far_onward(out_near, out_came), grad_hidden))
+        out_parts = far_second(out_near, out_came, onward)
         up_part = outer_dot(hat, grad_hidden)
         up_sum = scatter(up_part)
-        (out_part,) = chain((out_part,), up_part)
-        out_w_sum = scatter(out_part)
-        out_came, left = chain((out_came, grad_packed), up_part)
-        onward, left = chain((far_onward(out_near, out_came), left))
-        out_parts = far_second(out_near, out_came, onward)
+        (left,) = chain((grad_packed,), up_part)
 
         folded = (qkv_w, up_w)
         scales = (gain1_all, gain2_all)
@@ -899,11 +906,11 @@
         near0 = tokens_of(near0)
         came0 = far_first(near0)
         own_sums = [
-            jnp.sum(grad_packed.astype(F32), 0),
-            jnp.sum(grad_hidden.astype(F32), 0),
+            jnp.sum(sum_packed, (0, 1)),
+            sum_hidden,
             jnp.sum(cotangent.astype(F32), (0, 1)),
         ]
-        left, vec, qkv_sum = chain((left, laid(own_sums), qkv_sum), near0)
+        left, vec, qkv_sum = chain((left, laid(own_sums).astype(BF16), qkv_sum), near0)
         *near1, qkv_raw, everyone = pair_matmul(
             lay, (left, grad_hidden), folded, batch, (1, 2), 6, scales, [plans["qkv"]], [qkv_sum], vec
         )
@@ -911,10 +918,13 @@
         came1 = far_first(near1)
         (came0,) = chain((came0,), near1)
         onward0 = far_onward(near0, came0)
+        onward0, upstream = chain((onward0, upstream))
         parts0 = far_second(near0, came0, onward0)
-        (out_parts,) = chain((out_parts,), onward0)
+        out_part = outer_dot(upstream, context)
+        out_w_sum = scatter(out_part)
+        (out_parts,) = chain((out_parts,), out_part)
         output = (tokens.astype(F32) + add_all(out_parts) + b_out_all + b_down_all).astype(BF16)
-        sums = jnp.sum(everyone.reshape(lay.outer, group, -1), 0)
+        sums = jnp.sum(everyone.astype(F32).reshape(lay.outer, group, -1), 0)
         sum_qkv = jnp.transpose(sums[:, : 3 * cols].reshape(group, 3, cols), (1, 0, 2)).reshape(-1)
         sum_up = sums[:, 3 * cols : 3 * cols + ff_cols].reshape(-1)
         sum_dy = jnp.sum(sums[:, 3 * cols + ff_cols : 3 * cols + ff_cols + width], 0)
@@ -949,15 +959,13 @@
         )
 
         up_sum, token_grad = chain((up_sum, token_grad))
-        (up_raw,) = deal_exchange(lay, [plans["up"]], [up_sum], True, 3)
+        up_raw, out_raw = deal_exchange(lay, [plans["up"], plans["out"]], [up_sum, out_w_sum], True, 3)
         up_raw = up_raw.astype(F32)
         up_grads = (
             jnp.sum(w_up.astype(F32) * up_raw, 1),
             jnp.sum(w_up.astype(F32) * sum_up, 1),
             column(gain2) * up_raw + column(bias2) * sum_up,
         )
-        out_w_sum, *up_grads = chain((out_w_sum, *up_grads))
-        (out_raw,) = deal_exchange(lay, [plans["out"]], [out_w_sum], True, 2)
         return (
             output,
             token_grad,

time: 622 us -> 618 us (level)
  local copies, waits for them, and re-layouts: 21.9 us -> 15.6 us
    pallas_call x4 -> x3, Pallas kernels: 50.3 us -> 45.6 us  [deal_exchange(): pl.pallas_call(functools.partial(deal_kernel, lay, plan, back), out_shape...]
  transfers between devices with their start and end apart: 29 -> 29, of which waited for: 7 -> 10; matrix products, arithmetic and copies ran while one was open for 35% -> 35% of each run, Pallas kernels for 47% -> 45%
where the time goes in v6:
time: 618 us; the launch traced here: 612 us
  Pallas kernels  307 us (50%)
  matrix products  159 us (26%)
  other arithmetic  49.6 us (8%)
  waiting for transfers between devices  43.9 us (7%)
  starting transfers between devices  21.9 us (4%)
  local copies, waits for them, and re-layouts  15.6 us (3%)
  between operations  15.5 us (3%)
    dot_general x8, matrix products, dot(): lax.dot_general(left, right, (dims, ((), ())), preferred_element_type=F32)  159 us
    pallas_call x3, Pallas kernels, pair_matmul(): pl.pallas_call(functools.partial(pair_kernel, lay, plan, with_vec, bool(s...  101 us
    pallas_call x1, Pallas kernels, norm_exchange(): pl.pallas_call(functools.partial(norm_kernel, lay, plan), out_shape=[whol...  96.7 us
    pallas_call x3, Pallas kernels, deal_exchange(): pl.pallas_call(functools.partial(deal_kernel, lay, plan, back), out_shape...  45.6 us
    ppermute x20, waiting for transfers between devices, across(): return lax.ppermute(value, GROUP, lay.shift(*o))  41.3 us
    pallas_call x1, Pallas kernels, step(): pl.pallas_call(functools.partial(attend_kernel, lay, scaling), grid=(seqs...  34.2 us
    pallas_call x1, Pallas kernels, step(): pl.pallas_call(functools.partial(attend_back_kernel, scaling), grid=(seqs...  29.3 us
    ppermute x20, starting transfers between devices, across(): return lax.ppermute(value, GROUP, lay.shift(*o))  20.8 us
  transfers between devices with their start and end apart: 29, of which 10 were waited for; matrix products, arithmetic and copies ran while one was open for 35% of the time, Pallas kernels for 45%

profile of v6, /device:TPU:0, one launch (start us, length us, event | category | flops | bytes accessed | tf_op | source)
XLA Modules:
  0.0 612.2 jit_solution(392991872700332445)
XLA Ops:
  7.2 16.2 %shard_map.254 = bf16[512,1024]{1,0:T(8,128)(2,1)} custom-call(bf16[64,8192]{1,0:T(8,128)(2,1)} %refs_0_.1), custom_call_target="tpu_custom_call" | custom-call | flops 11900000256 | bytes 1048576 | tf_op jit(solution)/shard_map/pallas_call | solution.py:338
  23.6 12.5 %shard_map.255 = bf16[512,768]{1,0:T(8,128)(2,1)} custom-call(bf16[64,6144]{1,0:T(8,128)(2,1)} %refs_0_.2), custom_call_target="tpu_custom_call" | custom-call | flops 11900000256 | bytes 1048576 | tf_op jit(solution)/shard_map/pallas_call | solution.py:338
  37.5 96.7 %norm_exchange.1 = (bf16[2,4,2,256,2048]{4,3,2,1,0:T(8,128)(2,1)}, bf16[2,4,2,256,2048]{4,3,2,1,0:T(8,128)(2,1)}, bf16[2,4,2,256,2048]{4,3,2,1,0:T(8,128)(2,1)},...) custom-call(bf16[2,256,2048]{2,1,0:T(8,128)(2,1)S(1)} %copy-done, ...), custom_call_target="tpu_custom_call" | custom-call | flops 70000001024 | bytes 1048576 | tf_op jit(solution)/shard_map/norm_exchange/pallas_call | solution.py:291
  135.6 2.4 collective-permute-done
  138.1 1.5 collective-permute-start.1
  140.4 28.8 %fusion.4 = (bf16[4096,1024]{1,0:T(8,128)(2,1)}, bf16[4096,1024]{1,0:T(8,128)(2,1)}) fusion(f32[1024]{0:T(1024)S(1)} %bitcast.85, bf16[4096,2048]{1,0:T(8,128)(2,1)} %bitcast.97, bf16[2048,1024]{1,0:T(8,128)(2,1)} %all-gather.5.cloned.1.call-done.refs_3_), kind=kOutput, calls=%fused_computation.5 | convolution fusion | flops 17230200832 | bytes 37752832 | tf_op jit(solution)/shard_map/dot_general | solution.py:26
  169.8 2.8 multiply_sine_fusion
  172.6 2.0 copy.31.refs_3_.col_ref
  174.6 19.3 %convolution_add_fusion = f32[4096,768]{1,0:T(8,128)} fusion(bf16[4096,2048]{1,0:T(8,128)(2,1)} %bitcast.96, bf16[2048,768]{1,0:T(8,128)(2,1)} %all-gather.7.cloned.1.call-done.refs_1_, f32[768]{0:T(1024)S(1)} %add.300), kind=kOutput, calls=%fused_computation.10 | convolution fusion | flops 12888047616 | bytes 32508928 | tf_op jit(solution)/shard_map/dot_general | solution.py:26
  193.8 34.2 %attend.1 = (bf16[4,1024,256]{2,1,0:T(8,128)(2,1)}, bf16[4,1024,256]{2,1,0:T(8,128)(2,1)}, bf16[4,1024,256]{2,1,0:T(8,128)(2,1)}, bf16[2,2,2,2,256,256]{5,4,3,2,...) custom-call(f32[2,2,2,2,256,768]{5,4,3,2,1,0:T(8,128)} %bitcast.73, ...), custom_call_target="tpu_custom_call" | custom-call | flops 4294967296 | bytes 31457280 | tf_op jit(solution)/shard_map/attend/pallas_call | solution.py:829
  228.1 24.0 %convolution_convert_fusion.2 = bf16[2048,1024]{1,0:T(8,128)(2,1)} fusion(bf16[4096,2048]{1,0:T(8,128)(2,1)} %bitcast.88, bf16[4096,1024]{1,0:T(8,128)(2,1)} %get-tuple-element.139), kind=kOutput, calls=%fused_computation.30 | convolution fusion | flops 17181966336 | bytes 29360128 | tf_op jit(solution)/shard_map/dot_general | solution.py:26
  252.2 11.9 %convolution_convert_fusion = bf16[4096,256]{1,0:T(8,128)(2,1)} fusion(bf16[4096,2048]{1,0:T(8,128)(2,1)} %bitcast.89, bf16[2048,256]{1,0:T(8,128)(2,1)} %all-gather.9.cloned.1.call-done.refs_1_), kind=kOutput, calls=%fused_computation.16 | convolution fusion | flops 4296015872 | bytes 19922944 | tf_op jit(solution)/shard_map/dot_general | solution.py:26
  264.2 29.3 %attend_back.1 = (bf16[2,2,2,2,256,768]{5,4,3,2,1,0:T(8,128)(2,1)}, f32[4,1,768]{2,1,0:T(1,128)}) custom-call(bf16[4,1024,256]{2,1,0:T(8,128)(2,1)} %get-tuple-element.128.q_ref, bf16[4,1024,256]{2,1,0:T(8,128)(2,1)} %get-tuple-element.129.k_ref, bf16[4,1024,256]{2,1,0:T(8,128)(2,1)} %get-tuple-element.130.v_ref, bf16[2,2,2,2,256,256]{5,4,3,2,1,0:T(8,128)(2,1)} %bitcast.104, ...), custom_call_target="tpu_custom_call" | custom-call | flops 10737418240 | bytes 25165824 | tf_op jit(solution)/shard_map/attend_back/pallas_call | solution.py:871
  293.5 31.8 %shard_map.256 = (bf16[256,2048]{1,0:T(8,128)(2,1)}, bf16[256,2048]{1,0:T(8,128)(2,1)}, bf16[256,2048]{1,0:T(8,128)(2,1)}, bf16[256,2048]{1,0:T(8,128)(2,1)}, bf...) custom-call(bf16[2,4,512,256]{3,2,1,0:T(8,128)(2,1)} %bitcast.92, ...), custom_call_target="tpu_custom_call" | custom-call | flops 21474836480 | bytes 33554432 | tf_op jit(solution)/shard_map/pallas_call | solution.py:496
  329.4 20.3 %convolution_convert_fusion.3 = bf16[2048,768]{1,0:T(8,128)(2,1)} fusion(bf16[4096,2048]{1,0:T(8,128)(2,1)} %bitcast.94, bf16[4096,768]{1,0:T(8,128)(2,1)} %bitcast.101), kind=kOutput, calls=%fused_computation.31 | convolution fusion | flops 12886474752 | bytes 26214400 | tf_op jit(solution)/shard_map/dot_general | solution.py:26
  349.8 23.4 %convert_reduce_fusion = (f32[1024]{0:T(1024)S(1)}, bf16[4096,1024]{1,0:T(8,128)(2,1)S(1)}) fusion(bf16[4096,1024]{1,0:T(8,128)(2,1)} %get-tuple-element.152, bf16[4096,2048]{1,0:T(8,128)(2,1)} %bitcast.90, bf16[2048,1024]{1,0:T(8,128)(2,1)} %all-gather.11.cloned.1.call-done.refs_3_), kind=kOutput, calls=%fused_computation.6 | convolution fusion | flops 17200840704 | bytes 37752832 | tf_op jit(solution)/shard_map/dot_general | solution.py:26
  373.3 1.5 collective-permute-done.6
  374.8 3.4 add_convert_fusion
  378.2 2.6 add_convert_fusion.1
  380.8 21.5 %convolution_convert_fusion.1 = bf16[2048,1024]{1,0:T(8,128)(2,1)} fusion(bf16[4096,2048]{1,0:T(8,128)(2,1)} %bitcast.95, bf16[4096,1024]{1,0:T(8,128)(2,1)S(1)} %get-tuple-element.157), kind=kOutput, calls=%fused_computation.29 | convolution fusion | flops 17181966336 | bytes 29360128 | tf_op jit(solution)/shard_map/dot_general | solution.py:26
  405.3 2.0 convert_reduce_fusion.2
  409.0 33.1 %shard_map.257 = (bf16[256,1024]{1,0:T(8,128)(2,1)}, bf16[256,1024]{1,0:T(8,128)(2,1)}, bf16[256,1024]{1,0:T(8,128)(2,1)}, bf16[256,1024]{1,0:T(8,128)(2,1)}, bf...) custom-call(bf16[2,4,512,768]{3,2,1,0:T(8,128)(2,1)} %bitcast.102, ...), custom_call_target="tpu_custom_call" | custom-call | flops 15032385536 | bytes 33554432 | tf_op jit(solution)/shard_map/pallas_call | solution.py:496
  444.3 1.5 collective-permute-start.15
  446.3 35.9 %shard_map.258 = (bf16[256,1024]{1,0:T(8,128)(2,1)}, bf16[256,1024]{1,0:T(8,128)(2,1)}, bf16[256,1024]{1,0:T(8,128)(2,1)}, bf16[256,1024]{1,0:T(8,128)(2,1)}, bf...) custom-call(bf16[2,4,512,768]{3,2,1,0:T(8,128)(2,1)} %bitcast.103, ...), custom_call_target="tpu_custom_call" | custom-call | flops 15032385536 | bytes 33554432 | tf_op jit(solution)/shard_map/pallas_call | solution.py:496
  488.2 2.8 convert_element_type.259
  493.6 3.4 fusion.19
  500.9 2.1 add_convert_fusion.4
  502.9 2.0 add_convert_fusion.5
  505.0 9.8 %convolution_convert_fusion.4 = bf16[2048,256]{1,0:T(8,128)(2,1)} fusion(bf16[4096,2048]{1,0:T(8,128)(2,1)} %bitcast.91, bf16[4096,256]{1,0:T(8,128)(2,1)S(1)} %bitcast.93), kind=kOutput, calls=%fused_computation.35 | convolution fusion | flops 4295491584 | bytes 19922944 | tf_op jit(solution)/shard_map/dot_general | solution.py:26
  516.1 7.1 %collective-permute-done.12 = bf16[256,2048]{1,0:T(8,128)(2,1)} collective-permute-done((bf16[256,2048]{1,0:T(8,128)(2,1)}, bf16[256,2048]{1,0:T(8,128)(2,1)}, u32[]{:S(2)}, u32[]{:S(2)}) %collective-permute-start.12) | collective-permute-done | bytes 1048608 | tf_op jit(solution)/shard_map/ppermute | solution.py:695
  523.2 2.4 add_bitcast_fusion.1
  525.6 2.0 add_bitcast_fusion
  527.7 2.3 fusion.12
  530.0 4.4 collective-permute-done.7
  534.4 11.2 %collective-permute-done.8 = bf16[256,1024]{1,0:T(8,128)(2,1)} collective-permute-done((bf16[256,1024]{1,0:T(8,128)(2,1)}, bf16[256,1024]{1,0:T(8,128)(2,1)}, u32[]{:S(2)}, u32[]{:S(2)}) %collective-permute-start.8) | collective-permute-done | bytes 524320 | tf_op jit(solution)/shard_map/ppermute | solution.py:695
  545.7 2.2 add_convert_fusion.3
  547.9 2.1 add_convert_fusion.2
  551.0 2.0 collective-permute-start.17
  554.1 8.9 %collective-permute-done.19 = bf16[256,1024]{1,0:T(8,128)(2,1)} collective-permute-done((bf16[256,1024]{1,0:T(8,128)(2,1)}, bf16[256,1024]{1,0:T(8,128)(2,1)}, u32[]{:S(2)}, u32[]{:S(2)}) %collective-permute-start.19) | collective-permute-done | bytes 524320 | tf_op jit(solution)/shard_map/ppermute | solution.py:695
  563.0 1.6 add_bitcast_fusion.3
  565.1 1.5 add_bitcast_fusion.2
  566.6 6.8 %collective-permute-done.17 = bf16[256,1024]{1,0:T(8,128)(2,1)} collective-permute-done((bf16[256,1024]{1,0:T(8,128)(2,1)}, bf16[256,1024]{1,0:T(8,128)(2,1)}, u32[]{:S(2)}, u32[]{:S(2)}) %collective-permute-start.17) | collective-permute-done | bytes 524320 | tf_op jit(solution)/shard_map/ppermute | solution.py:695
  573.4 1.5 add_bitcast_fusion.5
  575.8 1.5 add_bitcast_fusion.4
  578.9 2.9 convert_add_fusion.1
  581.8 16.9 %shard_map.259 = (bf16[64,8192]{1,0:T(8,128)(2,1)}, bf16[64,2048]{1,0:T(8,128)(2,1)}) custom-call(bf16[512,1024]{1,0:T(8,128)(2,1)} %reduce-scatter.9.cloned.1.call-done.refs_0_, bf16[512,256]{1,0:T(8,128)(2,1)} %reduce-scatter.11.cloned.1.call-done.refs_1_), custom_call_target="tpu_custom_call" | custom-call | flops 11900000256 | bytes 1048576 | tf_op jit(solution)/shard_map/pallas_call | solution.py:338
  598.8 1.8 convert_element_type.282
  600.6 3.8 fusion.16
  (190 shorter events, 35.3 us)
Async XLA Ops:
  7.2 133.2 %all-gather.5.cloned.1.call-start = ((), (), s32[]{:S(2)}) async-start(), calls=%async_computation.4 | async-start | bytes 5242880 | tf_op jit(solution)/shard_map/all_gather | solution.py:750
  23.5 13.9 %copy-start.30 = (bf16[64]{0:T(256)(128)(2,1)S(1)}, bf16[64]{0:T(256)(128)(2,1)}, u32[]{:S(2)}) copy-start(bf16[64]{0:T(256)(128)(2,1)} %param.29) | copy-start | bytes 388
  23.5 14.0 %copy-start = (bf16[2,256,2048]{2,1,0:T(8,128)(2,1)S(1)}, bf16[2,256,2048]{2,1,0:T(8,128)(2,1)}, u32[]{:S(2)}) copy-start(bf16[2,256,2048]{2,1,0:T(8,128)(2,1)} %refs_0_.3) | copy-start | bytes 6291460
  23.5 13.9 %copy-start.1 = (bf16[64,8192]{1,0:T(8,128)(2,1)S(1)}, bf16[64,8192]{1,0:T(8,128)(2,1)}, u32[]{:S(2)}) copy-start(bf16[64,8192]{1,0:T(8,128)(2,1)} %refs_3_.1) | copy-start | bytes 3145732
  23.6 13.9 %copy-start.2 = (bf16[64,2048]{1,0:T(8,128)(2,1)S(1)}, bf16[64,2048]{1,0:T(8,128)(2,1)}, u32[]{:S(2)}) copy-start(bf16[64,2048]{1,0:T(8,128)(2,1)} %refs_2_.1) | copy-start | bytes 786436
  23.6 151.0 %all-gather.7.cloned.1.call-start = ((), (), s32[]{:S(2)}) async-start(), calls=%async_computation.5 | async-start | bytes 3932160 | tf_op jit(solution)/shard_map/all_gather | solution.py:750
  36.2 216.0 %all-gather.9.cloned.1.call-start = ((), (), s32[]{:S(2)}) async-start(), calls=%async_computation.6 | async-start | bytes 1310720 | tf_op jit(solution)/shard_map/all_gather | solution.py:750
  37.5 96.8 %copy-start.23 = (s32[2,1024]{1,0:T(2,128)S(1)}, s32[2,1024]{1,0:T(2,128)}, u32[]{:S(2)}) copy-start(s32[2,1024]{1,0:T(2,128)} %param.16) | copy-start | bytes 24580
  134.2 159.3 %all-gather.11.cloned.1.call-start = ((), (), s32[]{:S(2)}) async-start(), calls=%async_computation.7 | async-start | bytes 5242880 | tf_op jit(solution)/shard_map/all_gather | solution.py:750
  134.3 3.7 collective-permute-start
  135.1 273.9 %reduce-scatter.5.cloned.1.call-start = ((), (), s32[]{:S(2)}) async-start(), calls=%async_computation.8 | async-start | bytes 5242880 | tf_op jit(solution)/shard_map/reduce_scatter | solution.py:855
  138.1 55.7 %collective-permute-start.1 = (bf16[2,256,2048]{2,1,0:T(8,128)(2,1)}, bf16[2,256,2048]{2,1,0:T(8,128)(2,1)}, u32[]{:S(2)}, u32[]{:S(2)}) collective-permute-start(bf16[2,256,2048]{2,1,0:T(8,128)(2,1)} %refs_5_), channel_id=1, source_target_pairs={{0,2},{1,3},{2,0},{3,1},{4,6},{5,7},{6,4},{7,5},{8,10},{9,11},{10,... | collective-permute-start | bytes 6291464 | tf_op jit(solution)/shard_map/ppermute | solution.py:695
  139.6 54.2 %collective-permute-start.2 = (bf16[2,256,2048]{2,1,0:T(8,128)(2,1)}, bf16[2,256,2048]{2,1,0:T(8,128)(2,1)}, u32[]{:S(2)}, u32[]{:S(2)}) collective-permute-start(bf16[2,256,2048]{2,1,0:T(8,128)(2,1)} %refs_5_), channel_id=1, source_target_pairs={{0,4},{1,5},{2,6},{3,7},{4,0},{5,1},{6,2},{7,3},{8,12},{9,13},{10,... | collective-permute-start | bytes 6291464 | tf_op jit(solution)/shard_map/ppermute | solution.py:695
  252.1 194.2 %reduce-scatter.7.cloned.1.call-start = ((), (), s32[]{:S(2)}) async-start(), calls=%async_computation.9 | async-start | bytes 3932160 | tf_op jit(solution)/shard_map/reduce_scatter | solution.py:855
  325.3 47.9 %collective-permute-start.3 = (bf16[256,2048]{1,0:T(8,128)(2,1)}, bf16[256,2048]{1,0:T(8,128)(2,1)S(1)}, u32[]{:S(2)}, u32[]{:S(2)}) collective-permute-start(bf16[256,2048]{1,0:T(8,128)(2,1)} %get-tuple-element.145), channel_id=1, source_target_pairs={{0,4},{1,5},{2,6},{3,7},{4,0},{5,1},{6,2},{7,3},{8,12},{9,13},{10,... | collective-permute-start | bytes 3145736 | tf_op jit(solution)/shard_map/ppermute | solution.py:695
  326.4 46.9 %collective-permute-start.4 = (bf16[256,2048]{1,0:T(8,128)(2,1)}, bf16[256,2048]{1,0:T(8,128)(2,1)}, u32[]{:S(2)}, u32[]{:S(2)}) collective-permute-start(bf16[256,2048]{1,0:T(8,128)(2,1)} %get-tuple-element.147), channel_id=1, source_target_pairs={{0,4},{1,5},{2,6},{3,7},{4,0},{5,1},{6,2},{7,3},{8,12},{9,13},{10,... | collective-permute-start | bytes 3145736 | tf_op jit(solution)/shard_map/ppermute | solution.py:695
  327.4 45.9 %collective-permute-start.5 = (bf16[256,2048]{1,0:T(8,128)(2,1)}, bf16[256,2048]{1,0:T(8,128)(2,1)}, u32[]{:S(2)}, u32[]{:S(2)}) collective-permute-start(bf16[256,2048]{1,0:T(8,128)(2,1)} %get-tuple-element.144), channel_id=1, source_target_pairs={{0,2},{1,3},{2,0},{3,1},{4,6},{5,7},{6,4},{7,5},{8,10},{9,11},{10,... | collective-permute-start | bytes 3145736 | tf_op jit(solution)/shard_map/ppermute | solution.py:695
  328.4 46.3 %collective-permute-start.6 = (bf16[256,2048]{1,0:T(8,128)(2,1)}, bf16[256,2048]{1,0:T(8,128)(2,1)}, u32[]{:S(2)}, u32[]{:S(2)}) collective-permute-start(bf16[256,2048]{1,0:T(8,128)(2,1)} %get-tuple-element.148), channel_id=1, source_target_pairs={{0,2},{1,3},{2,0},{3,1},{4,6},{5,7},{6,4},{7,5},{8,10},{9,11},{10,... | collective-permute-start | bytes 3145736 | tf_op jit(solution)/shard_map/ppermute | solution.py:695
  349.7 232.1 %reduce-scatter.9.cloned.1.call-start = ((), (), s32[]{:S(2)}) async-start(), calls=%async_computation.10 | async-start | bytes 5242880 | tf_op jit(solution)/shard_map/reduce_scatter | solution.py:855
  349.8 25.0 %copy-start.7 = (bf16[256,2048]{1,0:T(8,128)(2,1)S(1)}, bf16[256,2048]{1,0:T(8,128)(2,1)}, u32[]{:S(2)}) copy-start(bf16[256,2048]{1,0:T(8,128)(2,1)} %get-tuple-element.154) | copy-start | bytes 3145732
  349.8 28.4 %copy-start.6 = (bf16[256,2048]{1,0:T(8,128)(2,1)S(1)}, bf16[256,2048]{1,0:T(8,128)(2,1)}, u32[]{:S(2)}) copy-start(bf16[256,2048]{1,0:T(8,128)(2,1)} %get-tuple-element.150) | copy-start | bytes 3145732
  373.2 29.0 %copy-start.5 = (bf16[256,2048]{1,0:T(8,128)(2,1)}, bf16[256,2048]{1,0:T(8,128)(2,1)S(1)}, u32[]{:S(2)}) copy-start(bf16[256,2048]{1,0:T(8,128)(2,1)S(1)} %collective-permute-done.3) | copy-start | bytes 3145732
  402.3 179.6 %reduce-scatter.11.cloned.1.call-start = ((), (), s32[]{:S(2)}) async-start(), calls=%async_computation.11 | async-start | bytes 1310720 | tf_op jit(solution)/shard_map/reduce_scatter | solution.py:855
  407.9 106.9 %collective-permute-start.11 = (bf16[256,2048]{1,0:T(8,128)(2,1)}, bf16[256,2048]{1,0:T(8,128)(2,1)}, u32[]{:S(2)}, u32[]{:S(2)}) collective-permute-start(bf16[256,2048]{1,0:T(8,128)(2,1)} %add_convert_fusion.1), channel_id=1, source_target_pairs={{0,2},{1,3},{2,0},{3,1},{4,6},{5,7},{6,4},{7,5},{8,10},{9,11},{10,... | collective-permute-start | bytes 3145736 | tf_op jit(solution)/shard_map/ppermute | solution.py:695
  442.2 54.8 %collective-permute-start.13 = (bf16[256,1024]{1,0:T(8,128)(2,1)}, bf16[256,1024]{1,0:T(8,128)(2,1)}, u32[]{:S(2)}, u32[]{:S(2)}) collective-permute-start(bf16[256,1024]{1,0:T(8,128)(2,1)} %get-tuple-element.167), channel_id=1, source_target_pairs={{0,4},{1,5},{2,6},{3,7},{4,0},{5,1},{6,2},{7,3},{8,12},{9,13},{10,... | collective-permute-start | bytes 1572872 | tf_op jit(solution)/shard_map/ppermute | solution.py:695
  443.3 54.7 %collective-permute-start.14 = (bf16[256,1024]{1,0:T(8,128)(2,1)}, bf16[256,1024]{1,0:T(8,128)(2,1)}, u32[]{:S(2)}, u32[]{:S(2)}) collective-permute-start(bf16[256,1024]{1,0:T(8,128)(2,1)} %get-tuple-element.169), channel_id=1, source_target_pairs={{0,4},{1,5},{2,6},{3,7},{4,0},{5,1},{6,2},{7,3},{8,12},{9,13},{10,... | collective-permute-start | bytes 1572872 | tf_op jit(solution)/shard_map/ppermute | solution.py:695
  444.3 54.6 %collective-permute-start.15 = (bf16[256,1024]{1,0:T(8,128)(2,1)}, bf16[256,1024]{1,0:T(8,128)(2,1)}, u32[]{:S(2)}, u32[]{:S(2)}) collective-permute-start(bf16[256,1024]{1,0:T(8,128)(2,1)} %get-tuple-element.166), channel_id=1, source_target_pairs={{0,2},{1,3},{2,0},{3,1},{4,6},{5,7},{6,4},{7,5},{8,10},{9,11},{10,... | collective-permute-start | bytes 1572872 | tf_op jit(solution)/shard_map/ppermute | solution.py:695
  445.8 54.1 %collective-permute-start.16 = (bf16[256,1024]{1,0:T(8,128)(2,1)}, bf16[256,1024]{1,0:T(8,128)(2,1)}, u32[]{:S(2)}, u32[]{:S(2)}) collective-permute-start(bf16[256,1024]{1,0:T(8,128)(2,1)} %get-tuple-element.170), channel_id=1, source_target_pairs={{0,2},{1,3},{2,0},{3,1},{4,6},{5,7},{6,4},{7,5},{8,10},{9,11},{10,... | collective-permute-start | bytes 1572872 | tf_op jit(solution)/shard_map/ppermute | solution.py:695
  483.4 19.5 %copy-start.15 = (bf16[256,1024]{1,0:T(8,128)(2,1)S(1)}, bf16[256,1024]{1,0:T(8,128)(2,1)}, u32[]{:S(2)}) copy-start(bf16[256,1024]{1,0:T(8,128)(2,1)} %get-tuple-element.165) | copy-start | bytes 1572868
  488.2 16.8 %copy-start.34 = (bf16[2,2,2,2,256,256]{5,4,3,2,1,0:T(8,128)(2,1)S(1)}, bf16[2,2,2,2,256,256]{5,4,3,2,1,0:T(8,128)(2,1)}, u32[]{:S(2)}) copy-start(bf16[2,2,2,2,256,256]{5,4,3,2,1,0:T(8,128)(2,1)} %get-tuple-element.137) | copy-start | bytes 6291460
  492.3 112.1 %copy-start.40 = (f32[64]{0:T(128)}, f32[64]{0:T(128)S(1)}, u32[]{:S(2)}) copy-start(f32[64]{0:T(128)S(1)} %fusion.24) | copy-start | bytes 772
  497.0 26.2 %collective-permute-start.12 = (bf16[256,2048]{1,0:T(8,128)(2,1)}, bf16[256,2048]{1,0:T(8,128)(2,1)}, u32[]{:S(2)}, u32[]{:S(2)}) collective-permute-start(bf16[256,2048]{1,0:T(8,128)(2,1)} %add_convert_fusion), channel_id=1, source_target_pairs={{0,4},{1,5},{2,6},{3,7},{4,0},{5,1},{6,2},{7,3},{8,12},{9,13},{10,... | collective-permute-start | bytes 3145736 | tf_op jit(solution)/shard_map/ppermute | solution.py:695
  498.0 32.0 %collective-permute-start.10 = (bf16[256,1024]{1,0:T(8,128)(2,1)}, bf16[256,1024]{1,0:T(8,128)(2,1)}, u32[]{:S(2)}, u32[]{:S(2)}) collective-permute-start(bf16[256,1024]{1,0:T(8,128)(2,1)} %get-tuple-element.177), channel_id=1, source_target_pairs={{0,2},{1,3},{2,0},{3,1},{4,6},{5,7},{6,4},{7,5},{8,10},{9,11},{10,... | collective-permute-start | bytes 1572872 | tf_op jit(solution)/shard_map/ppermute | solution.py:695
  498.8 35.6 %collective-permute-start.7 = (bf16[256,1024]{1,0:T(8,128)(2,1)}, bf16[256,1024]{1,0:T(8,128)(2,1)}, u32[]{:S(2)}, u32[]{:S(2)}) collective-permute-start(bf16[256,1024]{1,0:T(8,128)(2,1)} %get-tuple-element.174), channel_id=1, source_target_pairs={{0,4},{1,5},{2,6},{3,7},{4,0},{5,1},{6,2},{7,3},{8,12},{9,13},{10,... | collective-permute-start | bytes 1572872 | tf_op jit(solution)/shard_map/ppermute | solution.py:695
  499.9 45.8 %collective-permute-start.8 = (bf16[256,1024]{1,0:T(8,128)(2,1)}, bf16[256,1024]{1,0:T(8,128)(2,1)}, u32[]{:S(2)}, u32[]{:S(2)}) collective-permute-start(bf16[256,1024]{1,0:T(8,128)(2,1)} %get-tuple-element.175), channel_id=1, source_target_pairs={{0,4},{1,5},{2,6},{3,7},{4,0},{5,1},{6,2},{7,3},{8,12},{9,13},{10,... | collective-permute-start | bytes 1572872 | tf_op jit(solution)/shard_map/ppermute | solution.py:695
  514.9 30.8 %collective-permute-start.9 = (bf16[256,1024]{1,0:T(8,128)(2,1)}, bf16[256,1024]{1,0:T(8,128)(2,1)S(1)}, u32[]{:S(2)}, u32[]{:S(2)}) collective-permute-start(bf16[256,1024]{1,0:T(8,128)(2,1)} %get-tuple-element.176), channel_id=1, source_target_pairs={{0,2},{1,3},{2,0},{3,1},{4,6},{5,7},{6,4},{7,5},{8,10},{9,11},{10,... | collective-permute-start | bytes 1572872 | tf_op jit(solution)/shard_map/ppermute | solution.py:695
  527.7 18.0 %copy-start.14 = (bf16[256,1024]{1,0:T(8,128)(2,1)S(1)}, bf16[256,1024]{1,0:T(8,128)(2,1)}, u32[]{:S(2)}) copy-start(bf16[256,1024]{1,0:T(8,128)(2,1)} %get-tuple-element.186) | copy-start | bytes 1572868
  527.7 20.2 %copy-start.13 = (bf16[256,1024]{1,0:T(8,128)(2,1)S(1)}, bf16[256,1024]{1,0:T(8,128)(2,1)}, u32[]{:S(2)}) copy-start(bf16[256,1024]{1,0:T(8,128)(2,1)} %get-tuple-element.187) | copy-start | bytes 1572868
  527.7 23.3 %copy-start.19 = (f32[1,8,8,128]{3,2,1,0:T(8,128)S(1)}, f32[1,8,8,128]{3,2,1,0:T(8,128)}, u32[]{:S(2)}) copy-start(f32[1,8,8,128]{3,2,1,0:T(8,128)} %get-tuple-element.230) | copy-start | bytes 98308
  530.0 35.1 %copy-start.12 = (bf16[256,1024]{1,0:T(8,128)(2,1)S(1)}, bf16[256,1024]{1,0:T(8,128)(2,1)}, u32[]{:S(2)}) copy-start(bf16[256,1024]{1,0:T(8,128)(2,1)} %get-tuple-element.185) | copy-start | bytes 1572868
  547.9 25.5 %copy-start.11 = (bf16[256,1024]{1,0:T(8,128)(2,1)S(1)}, bf16[256,1024]{1,0:T(8,128)(2,1)}, u32[]{:S(2)}) copy-start(bf16[256,1024]{1,0:T(8,128)(2,1)} %get-tuple-element.163) | copy-start | bytes 1572868
  547.9 15.1 %collective-permute-start.19 = (bf16[256,1024]{1,0:T(8,128)(2,1)}, bf16[256,1024]{1,0:T(8,128)(2,1)}, u32[]{:S(2)}, u32[]{:S(2)}) collective-permute-start(bf16[256,1024]{1,0:T(8,128)(2,1)} %add_convert_fusion.3), channel_id=1, source_target_pairs={{0,2},{1,3},{2,0},{3,1},{4,6},{5,7},{6,4},{7,5},{8,10},{9,11},{10,... | collective-permute-start | bytes 1572872 | tf_op jit(solution)/shard_map/ppermute | solution.py:695
  550.0 15.1 %collective-permute-start.20 = (bf16[256,1024]{1,0:T(8,128)(2,1)}, bf16[256,1024]{1,0:T(8,128)(2,1)}, u32[]{:S(2)}, u32[]{:S(2)}) collective-permute-start(bf16[256,1024]{1,0:T(8,128)(2,1)} %add_convert_fusion.2), channel_id=1, source_target_pairs={{0,4},{1,5},{2,6},{3,7},{4,0},{5,1},{6,2},{7,3},{8,12},{9,13},{10,... | collective-permute-start | bytes 1572872 | tf_op jit(solution)/shard_map/ppermute | solution.py:695
  551.0 22.4 %collective-permute-start.17 = (bf16[256,1024]{1,0:T(8,128)(2,1)}, bf16[256,1024]{1,0:T(8,128)(2,1)}, u32[]{:S(2)}, u32[]{:S(2)}) collective-permute-start(bf16[256,1024]{1,0:T(8,128)(2,1)} %add_convert_fusion.5), channel_id=1, source_target_pairs={{0,2},{1,3},{2,0},{3,1},{4,6},{5,7},{6,4},{7,5},{8,10},{9,11},{10,... | collective-permute-start | bytes 1572872 | tf_op jit(solution)/shard_map/ppermute | solution.py:695
  553.0 22.9 %collective-permute-start.18 = (bf16[256,1024]{1,0:T(8,128)(2,1)}, bf16[256,1024]{1,0:T(8,128)(2,1)}, u32[]{:S(2)}, u32[]{:S(2)}) collective-permute-start(bf16[256,1024]{1,0:T(8,128)(2,1)} %add_convert_fusion.4), channel_id=1, source_target_pairs={{0,4},{1,5},{2,6},{3,7},{4,0},{5,1},{6,2},{7,3},{8,12},{9,13},{10,... | collective-permute-start | bytes 1572872 | tf_op jit(solution)/shard_map/ppermute | solution.py:695
  581.8 18.8 %copy-start.8 = (bf16[64,8192]{1,0:T(8,128)(2,1)S(1)}, bf16[64,8192]{1,0:T(8,128)(2,1)}, u32[]{:S(2)}) copy-start(bf16[64,8192]{1,0:T(8,128)(2,1)} %refs_0_.1) | copy-start | bytes 3145732
  581.8 18.8 %copy-start.27 = (f32[64]{0:T(128)S(1)}, f32[64]{0:T(128)}, u32[]{:S(2)}) copy-start(f32[64]{0:T(128)} %copy-done.26) | copy-start | bytes 772
  581.8 18.8 %copy-start.29 = (f32[64]{0:T(128)S(1)}, f32[64]{0:T(128)}, u32[]{:S(2)}) copy-start(f32[64]{0:T(128)} %copy-done.28) | copy-start | bytes 772
  (22 other events, 185.8 us)
Sparse Core Ops, SparseCore 0:
  23.6 85.1 all-gather.4
  110.3 61.8 all-gather.6
  173.8 26.6 all-gather.8
  201.9 80.1 all-gather.10
  284.8 75.2 reduce-scatter.4
  362.3 60.8 reduce-scatter.6
  425.5 80.9 reduce-scatter.8
  554.2 24.2 reduce-scatter.10

commit v7 on v6

--- a/solution.py
+++ b/solution.py
@@ -73,10 +73,10 @@
         peer = lax.rem(me + k, lay.group)
         device = (zo, peer // lay.seq, lax.rem(peer, lay.seq))
         j = 0
-        for (parts, rows, cols), source, target in zip(plan, sources, targets, strict=True):
+        for (parts, rows, cols, first), source, target in zip(plan, sources, targets, strict=True):
             for part in range(parts):
                 wide = lambda who: pl.ds(pl.multiple_of((part * lay.group + who) * cols, 128), cols)
-                thin = pl.ds(part * cols, cols)
+                thin = pl.ds(first + part * cols, cols)
                 block = lambda who: pl.ds(pl.multiple_of(who * rows, rows), rows)
                 if back:
                     copies.append(remote(source.at[block(peer), thin], target.at[:, wide(me)], send.at[k - 1, j], recv.at[k - 1, j], device))
@@ -89,10 +89,10 @@
 def swap_own(lay, plan, me, sources, targets, sems, back):
     copies = []
     j = 0
-    for (parts, rows, cols), source, target in zip(plan, sources, targets, strict=True):
+    for (parts, rows, cols, first), source, target in zip(plan, sources, targets, strict=True):
         for part in range(parts):
             wide = pl.ds(pl.multiple_of((part * lay.group + me) * cols, 128), cols)
-            thin = pl.ds(part * cols, cols)
+            thin = pl.ds(first + part * cols, cols)
             block = pl.ds(pl.multiple_of(me * rows, rows), rows)
             if back:
                 copies.append(pltpu.make_async_copy(source.at[block, thin], target.at[:, wide], sems.at[j]))
@@ -115,8 +115,8 @@
 
 def swap_shapes(lay, plan, back):
     if back:
-        return [jax.ShapeDtypeStruct((rows, parts * lay.group * cols), BF16) for parts, rows, cols in plan]
-    return [jax.ShapeDtypeStruct((lay.group * rows, parts * cols), BF16) for parts, rows, cols in plan]
+        return [jax.ShapeDtypeStruct((rows, parts * lay.group * cols), BF16) for parts, rows, cols, _ in plan]
+    return [jax.ShapeDtypeStruct((lay.group * rows, parts * cols), BF16) for parts, rows, cols, _ in plan]
 
 
 def device_after(lay, rank, k):
@@ -285,7 +285,7 @@
 
 
 def norm_exchange(lay, plan, tokens, vec, weights):
-    count = sum(parts for parts, _, _ in plan)
+    count = sum(parts for parts, _, _, _ in plan)
     chips = lay.group // 2
     whole = jax.ShapeDtypeStruct((2, chips, *tokens.shape), BF16)
     return pl.pallas_call(
@@ -334,7 +334,7 @@
 
 
 def deal_exchange(lay, plan, arrays, back, number):
-    count = sum(parts for parts, _, _ in plan)
+    count = sum(parts for parts, _, _, _ in plan)
     return pl.pallas_call(
         functools.partial(deal_kernel, lay, plan, back),
         out_shape=swap_shapes(lay, plan, back),
@@ -359,7 +359,7 @@
     scales = take(2) if scaled else []
     sources, vec_ref = take(len(plan)), take(int(with_vec))
     outs, targets, all_ref = take(chips * batch), take(len(plan)), take(int(with_vec))
-    given, came, send, recv, out_sem = take(5)
+    given, came, act_buf, w_buf, send, recv, out_sem = take(7)
     zo, yi, s = lax.axis_index("zo"), lax.axis_index("yi"), lax.axis_index("seq")
     me = yi * lay.seq + s
     rank = zo * lay.group + me
@@ -414,6 +414,17 @@
             pl.semaphore_wait(barrier, 1)
         for rider in riders():
             rider.start()
+        at = 0
+        for k, weight in enumerate((first_w, second_w)):
+            depth = weight.shape[1]
+            if scaled:
+                line = scales[k][...]
+                gain = jnp.transpose(jnp.broadcast_to(line, (128, line.shape[1])), (1, 0))
+                for c in range(0, depth, 128):
+                    w_buf[:, at + c : at + c + 128] = (weight[:, c : c + 128].astype(F32) * gain).astype(BF16)
+            else:
+                w_buf[:, at : at + depth] = weight[...]
+            at += depth
 
     for j in range(chips):
 
@@ -421,9 +432,10 @@
         def _():
             copy(j).start()
 
-    total = dot(first_ref[0, 0], first_w[...], ((1,), (1,)))
-    other = dot(second_ref[0, 0], second_w[...], ((1,), (1,)))
-    total = total * scales[0][...] + other * scales[1][...] if scaled else total + other
+    cut = first_ref.shape[3]
+    act_buf[:, :cut] = first_ref[0, 0]
+    act_buf[:, cut:] = second_ref[0, 0]
+    total = dot(act_buf[...], w_buf[...], ((1,), (1,)))
     for j in range(chips):
 
         @pl.when(step == j)
@@ -461,7 +473,7 @@
     chips = lay.group // 2
     rows = acts[0].shape[0] // lay.group
     width = weights[0].shape[0] // cut[1]
-    count = sum(parts for parts, _, _ in plan)
+    count = sum(parts for parts, _, _, _ in plan)
     with_vec = vec is not None
 
     def act(depth):
@@ -480,9 +492,12 @@
     args += [*arrays, *([vec] if with_vec else [])]
     specs += [ANY] * (len(args) - len(specs))
     shapes = [jax.ShapeDtypeStruct((rows // batch, width), BF16)] * (chips * batch) + swap_shapes(lay, plan, True)
+    depth = sum(a.shape[1] for a in acts)
     scratch = [
         pltpu.VMEM((chips, rows, width), BF16),
         pltpu.VMEM((chips, rows, width), BF16),
+        pltpu.VMEM((rows, depth), BF16),
+        pltpu.VMEM((width, depth), BF16),
         pltpu.SemaphoreType.DMA((chips,)),
         pltpu.SemaphoreType.DMA((chips,)),
         pltpu.SemaphoreType.DMA((chips, batch)),
@@ -492,7 +507,6 @@
     if with_vec:
         shapes.append(jax.ShapeDtypeStruct((lay.count, *vec.shape), vec.dtype))
         scratch += [pltpu.SemaphoreType.DMA((lay.count - 1,))] * 2 + [pltpu.SemaphoreType.DMA]
-    depth = sum(a.shape[1] for a in acts)
     return pl.pallas_call(
         functools.partial(pair_kernel, lay, plan, with_vec, bool(scales), batch),
         grid=(2 * chips,),
@@ -639,7 +653,7 @@
             ctx_ref[c, 0, i, 0] = ctx_buf[pl.ds((c * chips + i) * length, length), :]
 
 
-def attend_back_kernel(scaling, q_ref, k_ref, v_ref, g_ref, cos_ref, sin_ref, col_ref, row_ref, lse_ref, out_ref, sum_ref,
+def attend_back_kernel(scaling, q_ref, k_ref, v_ref, dy_ref, w_ref, cos_ref, sin_ref, col_ref, row_ref, lse_ref, out_ref, sum_ref,
                        g_buf, dq_buf, dk_buf, dv_buf, cos_buf, sin_buf):
     cores, _, chips, _, length, _ = out_ref.shape
     total = q_ref.shape[1]
@@ -648,7 +662,7 @@
     sin_buf[...] = sin_all
     for c in range(cores):
         for i in range(chips):
-            g_buf[pl.ds((c * chips + i) * length, length), :] = g_ref[c, 0, i, 0]
+            g_buf[pl.ds((c * chips + i) * length, length), :] = dot(dy_ref[c, 0, i, 0], w_ref[...], ((1,), (0,))).astype(BF16)
     dk_buf[...] = jnp.zeros_like(dk_buf)
     dv_buf[...] = jnp.zeros_like(dv_buf)
 
@@ -744,7 +758,7 @@
         cols = lay.heads * HEAD_DIM
         ff_cols = ff // group
         out_cols = width // group
-        plans = {"up": (1, rows, ff_cols), "down": (1, rows, ff_cols), "qkv": (3, rows, cols), "out": (1, rows, out_cols)}
+        plans = {"up": (1, rows, ff_cols, 0), "down": (1, rows, ff_cols, 0), "qkv": (3, rows, cols, 0), "out": (1, rows, out_cols, 0)}
 
         def gather_rows(mine):
             return lax.all_gather(mine, "zo", axis=0, tiled=True)
@@ -866,19 +880,25 @@
         down_part = outer_dot(upstream, activated)
         upstream, down_part = chain((upstream, down_part))
         down_sum = scatter(down_part)
-        grad_context = dot(upstream, out_w, ((1,), (0,))).astype(BF16)
+        out_part = outer_dot(upstream, context)
+        upstream, out_part = chain((upstream, out_part))
 
         grad_packed, sum_packed = pl.pallas_call(
             functools.partial(attend_back_kernel, scaling),
             grid=(seqs,),
-            in_specs=[head_spec] * 3 + [tokens_spec, turn_spec, turn_spec, col_spec, row_spec, row_spec],
+            in_specs=[head_spec] * 3
+            + [
+                pl.BlockSpec((2, 1, chips_x, 1, length, width), lambda i: (0, i // batch, 0, i % batch, 0, 0)),
+                pl.BlockSpec((width, cols), lambda i: (0, 0), pipeline_mode=pl.Buffered(1)),
+            ]
+            + [turn_spec, turn_spec, col_spec, row_spec, row_spec],
             out_specs=[wide_spec, pl.BlockSpec((1, 1, 3 * cols), lambda i: (i, 0, 0))],
             out_shape=[jax.ShapeDtypeStruct(full, BF16), jax.ShapeDtypeStruct((seqs, 1, 3 * cols), F32)],
             scratch_shapes=[pltpu.VMEM((count, HEAD_DIM), BF16)] + [pltpu.VMEM((count, HEAD_DIM), F32)] * 3 + turn_bufs,
             compiler_params=params,
-            cost_estimate=pl.CostEstimate(flops=5 * work, bytes_accessed=24 << 20, transcendentals=seqs * count * count),
+            cost_estimate=pl.CostEstimate(flops=7 * work, bytes_accessed=40 << 20, transcendentals=seqs * count * count),
             name="attend_back",
-        )(queries, keys, values, grad_context.reshape(by_token), cosine, sine, place_col, place_row, lse)
+        )(queries, keys, values, upstream.reshape(2, sub, chips_x, batch, length, width), out_w, cosine, sine, place_col, place_row, lse)
         grad_packed = grad_packed.reshape(total, 3 * cols)
 
         acts = chain((context, activated), grad_packed)
@@ -894,7 +914,7 @@
         onward, grad_hidden = chain((far_onward(out_near, out_came), grad_hidden))
         out_parts = far_second(out_near, out_came, onward)
         up_part = outer_dot(hat, grad_hidden)
-        up_sum = scatter(up_part)
+        last_sum = scatter(jnp.concatenate([up_part, out_part], 1))
         (left,) = chain((grad_packed,), up_part)
 
         folded = (qkv_w, up_w)
@@ -918,11 +938,8 @@
         came1 = far_first(near1)
         (came0,) = chain((came0,), near1)
         onward0 = far_onward(near0, came0)
-        onward0, upstream = chain((onward0, upstream))
         parts0 = far_second(near0, came0, onward0)
-        out_part = outer_dot(upstream, context)
-        out_w_sum = scatter(out_part)
-        (out_parts,) = chain((out_parts,), out_part)
+        (out_parts,) = chain((out_parts,), onward0)
         output = (tokens.astype(F32) + add_all(out_parts) + b_out_all + b_down_all).astype(BF16)
         sums = jnp.sum(everyone.astype(F32).reshape(lay.outer, group, -1), 0)
         sum_qkv = jnp.transpose(sums[:, : 3 * cols].reshape(group, 3, cols), (1, 0, 2)).reshape(-1)
@@ -958,8 +975,10 @@
             - normal * jnp.mean(grad_normal * normal, -1, keepdims=True)
         )
 
-        up_sum, token_grad = chain((up_sum, token_grad))
-        up_raw, out_raw = deal_exchange(lay, [plans["up"], plans["out"]], [up_sum, out_w_sum], True, 3)
+        last_sum, token_grad = chain((last_sum, token_grad))
+        up_raw, out_raw = deal_exchange(
+            lay, [plans["up"], (1, rows, out_cols, ff_cols)], [last_sum, last_sum], True, 3
+        )
         up_raw = up_raw.astype(F32)
         up_grads = (
             jnp.sum(w_up.astype(F32) * up_raw, 1),

time: 618 us -> 607 us (0.982)
  other arithmetic: 49.6 us -> 42.2 us
    dot_general x8 -> x7, matrix products: 159 us -> 153 us  [dot(): lax.dot_general(left, right, (dims, ((), ())), preferred_element_type=F32)]
  transfers between devices with their start and end apart: 29 -> 28, of which waited for: 10 -> 8; matrix products, arithmetic and copies ran while one was open for 35% -> 34% of each run, Pallas kernels for 45% -> 46%
where the time goes in v7:
time: 607 us; the launch traced here: 601 us
  Pallas kernels  310 us (51%)
  matrix products  153 us (25%)
  other arithmetic  42.2 us (7%)
  waiting for transfers between devices  41.7 us (7%)
  starting transfers between devices  22.2 us (4%)
  local copies, waits for them, and re-layouts  16.4 us (3%)
  between operations  15.6 us (3%)
    dot_general x7, matrix products, dot(): lax.dot_general(left, right, (dims, ((), ())), preferred_element_type=F32)  153 us
    pallas_call x3, Pallas kernels, pair_matmul(): pl.pallas_call(functools.partial(pair_kernel, lay, plan, with_vec, bool(s...  99.9 us
    pallas_call x1, Pallas kernels, norm_exchange(): pl.pallas_call(functools.partial(norm_kernel, lay, plan), out_shape=[whol...  96.7 us
    pallas_call x3, Pallas kernels, deal_exchange(): pl.pallas_call(functools.partial(deal_kernel, lay, plan, back), out_shape...  45.4 us
    ppermute x20, waiting for transfers between devices, across(): return lax.ppermute(value, GROUP, lay.shift(*o))  39.1 us
    pallas_call x1, Pallas kernels, step(): pl.pallas_call(functools.partial(attend_kernel, lay, scaling), grid=(seqs...  34.2 us
    pallas_call x1, Pallas kernels, step(): pl.pallas_call(functools.partial(attend_back_kernel, scaling), grid=(seqs...  34.2 us
    ppermute x20, starting transfers between devices, across(): return lax.ppermute(value, GROUP, lay.shift(*o))  21.2 us
  transfers between devices with their start and end apart: 28, of which 8 were waited for; matrix products, arithmetic and copies ran while one was open for 34% of the time, Pallas kernels for 46%

profile of v7, /device:TPU:0, one launch (start us, length us, event | category | flops | bytes accessed | tf_op | source)
XLA Modules:
  0.0 601.1 jit_solution(13205209803599601098)
XLA Ops:
  7.2 16.2 %shard_map.254 = bf16[512,1024]{1,0:T(8,128)(2,1)} custom-call(bf16[64,8192]{1,0:T(8,128)(2,1)} %refs_0_.1), custom_call_target="tpu_custom_call" | custom-call | flops 11900000256 | bytes 1048576 | tf_op jit(solution)/shard_map/pallas_call | solution.py:338
  23.6 12.5 %shard_map.255 = bf16[512,768]{1,0:T(8,128)(2,1)} custom-call(bf16[64,6144]{1,0:T(8,128)(2,1)} %refs_0_.2), custom_call_target="tpu_custom_call" | custom-call | flops 11900000256 | bytes 1048576 | tf_op jit(solution)/shard_map/pallas_call | solution.py:338
  37.5 96.7 %norm_exchange.1 = (bf16[2,4,2,256,2048]{4,3,2,1,0:T(8,128)(2,1)}, bf16[2,4,2,256,2048]{4,3,2,1,0:T(8,128)(2,1)}, bf16[2,4,2,256,2048]{4,3,2,1,0:T(8,128)(2,1)},...) custom-call(bf16[2,256,2048]{2,1,0:T(8,128)(2,1)S(1)} %copy-done, ...), custom_call_target="tpu_custom_call" | custom-call | flops 70000001024 | bytes 1048576 | tf_op jit(solution)/shard_map/norm_exchange/pallas_call | solution.py:291
  135.5 2.4 collective-permute-done
  138.0 1.5 collective-permute-start.1
  140.3 28.8 %fusion.4 = (bf16[4096,1024]{1,0:T(8,128)(2,1)}, bf16[4096,1024]{1,0:T(8,128)(2,1)}) fusion(f32[1024]{0:T(1024)S(1)} %bitcast.83, bf16[4096,2048]{1,0:T(8,128)(2,1)} %bitcast.95, bf16[2048,1024]{1,0:T(8,128)(2,1)} %all-gather.5.cloned.1.call-done.refs_3_), kind=kOutput, calls=%fused_computation.5 | convolution fusion | flops 17230200832 | bytes 37752832 | tf_op jit(solution)/shard_map/dot_general | solution.py:26
  169.8 2.8 multiply_sine_fusion
  172.5 2.0 copy.32.refs_3_.col_ref
  174.5 19.3 %convolution_add_fusion = f32[4096,768]{1,0:T(8,128)} fusion(bf16[4096,2048]{1,0:T(8,128)(2,1)} %bitcast.94, bf16[2048,768]{1,0:T(8,128)(2,1)} %all-gather.7.cloned.1.call-done.refs_1_, f32[768]{0:T(1024)S(1)} %add.298), kind=kOutput, calls=%fused_computation.10 | convolution fusion | flops 12888047616 | bytes 32508928 | tf_op jit(solution)/shard_map/dot_general | solution.py:26
  193.8 34.2 %attend.1 = (bf16[4,1024,256]{2,1,0:T(8,128)(2,1)}, bf16[4,1024,256]{2,1,0:T(8,128)(2,1)}, bf16[4,1024,256]{2,1,0:T(8,128)(2,1)}, bf16[2,2,2,2,256,256]{5,4,3,2,...) custom-call(f32[2,2,2,2,256,768]{5,4,3,2,1,0:T(8,128)} %bitcast.71, ...), custom_call_target="tpu_custom_call" | custom-call | flops 4294967296 | bytes 31457280 | tf_op jit(solution)/shard_map/attend/pallas_call | solution.py:843
  228.0 24.0 %convolution_convert_fusion.1 = bf16[2048,1024]{1,0:T(8,128)(2,1)} fusion(bf16[4096,2048]{1,0:T(8,128)(2,1)} %bitcast.86, bf16[4096,1024]{1,0:T(8,128)(2,1)} %get-tuple-element.139), kind=kOutput, calls=%fused_computation.30 | convolution fusion | flops 17181966336 | bytes 29360128 | tf_op jit(solution)/shard_map/dot_general | solution.py:26
  252.1 12.4 %convolution_convert_fusion.3 = bf16[2048,256]{1,0:T(8,128)(2,1)} fusion(bf16[4096,2048]{1,0:T(8,128)(2,1)} %bitcast.87, bf16[4096,256]{1,0:T(8,128)(2,1)} %bitcast.90), kind=kOutput, calls=%fused_computation.35 | convolution fusion | flops 4295491584 | bytes 19922944 | tf_op jit(solution)/shard_map/dot_general | solution.py:26
  264.4 34.2 %attend_back.1 = (bf16[2,2,2,2,256,768]{5,4,3,2,1,0:T(8,128)(2,1)}, f32[4,1,768]{2,1,0:T(1,128)}) custom-call(bf16[4,1024,256]{2,1,0:T(8,128)(2,1)} %get-tuple-element.127.q_ref, bf16[4,1024,256]{2,1,0:T(8,128)(2,1)} %get-tuple-element.128.k_ref, bf16[4,1024,256]{2,1,0:T(8,128)(2,1)} %get-tuple-element.129.v_ref, bf16[2,2,2,2,256,2048]{5,4,3,2,1,0:T(8,128)(2,1)} %bitcast.88, ...), custom_call_target="tpu_custom_call" | custom-call | flops 15032385536 | bytes 41943040 | tf_op jit(solution)/shard_map/attend_back/pallas_call | solution.py:886
  298.6 32.2 %shard_map.256 = (bf16[256,2048]{1,0:T(8,128)(2,1)}, bf16[256,2048]{1,0:T(8,128)(2,1)}, bf16[256,2048]{1,0:T(8,128)(2,1)}, bf16[256,2048]{1,0:T(8,128)(2,1)}, bf...) custom-call(bf16[2,4,512,256]{3,2,1,0:T(8,128)(2,1)} %bitcast.91, ...), custom_call_target="tpu_custom_call" | custom-call | flops 21474836480 | bytes 33554432 | tf_op jit(solution)/shard_map/pallas_call | solution.py:510
  334.9 20.3 %convolution_convert_fusion.2 = bf16[2048,768]{1,0:T(8,128)(2,1)} fusion(bf16[4096,2048]{1,0:T(8,128)(2,1)} %bitcast.92, bf16[4096,768]{1,0:T(8,128)(2,1)} %bitcast.99), kind=kOutput, calls=%fused_computation.31 | convolution fusion | flops 12886474752 | bytes 26214400 | tf_op jit(solution)/shard_map/dot_general | solution.py:26
  355.3 25.0 %convert_reduce_fusion = (f32[1024]{0:T(1024)S(1)}, bf16[4096,1024]{1,0:T(8,128)(2,1)}) fusion(bf16[4096,1024]{1,0:T(8,128)(2,1)} %get-tuple-element.152, bf16[4096,2048]{1,0:T(8,128)(2,1)} %bitcast.89, bf16[2048,1024]{1,0:T(8,128)(2,1)} %all-gather.11.cloned.1.call-done.refs_3_), kind=kOutput, calls=%fused_computation.6 | convolution fusion | flops 17200840704 | bytes 37752832 | tf_op jit(solution)/shard_map/dot_general | solution.py:26
  380.4 3.0 add_convert_fusion
  383.3 2.6 add_convert_fusion.1
  385.9 22.8 %convolution_convert_fusion = bf16[2048,1024]{1,0:T(8,128)(2,1)S(1)} fusion(bf16[4096,2048]{1,0:T(8,128)(2,1)} %bitcast.93, bf16[4096,1024]{1,0:T(8,128)(2,1)} %get-tuple-element.157), kind=kOutput, calls=%fused_computation.29 | convolution fusion | flops 17181966336 | bytes 29360128 | tf_op jit(solution)/shard_map/dot_general | solution.py:26
  408.8 2.8 pad_maximum_fusion
  415.6 2.0 convert_reduce_fusion.2
  420.2 33.3 %shard_map.257 = (bf16[256,1024]{1,0:T(8,128)(2,1)}, bf16[256,1024]{1,0:T(8,128)(2,1)}, bf16[256,1024]{1,0:T(8,128)(2,1)}, bf16[256,1024]{1,0:T(8,128)(2,1)}, bf...) custom-call(bf16[2,4,512,768]{3,2,1,0:T(8,128)(2,1)} %bitcast.100, ...), custom_call_target="tpu_custom_call" | custom-call | flops 15032385536 | bytes 33554432 | tf_op jit(solution)/shard_map/pallas_call | solution.py:510
  453.6 1.1 collective-permute-start.13
  456.7 34.4 %shard_map.258 = (bf16[256,1024]{1,0:T(8,128)(2,1)}, bf16[256,1024]{1,0:T(8,128)(2,1)}, bf16[256,1024]{1,0:T(8,128)(2,1)}, bf16[256,1024]{1,0:T(8,128)(2,1)}, bf...) custom-call(bf16[2,4,512,768]{3,2,1,0:T(8,128)(2,1)} %bitcast.101, ...), custom_call_target="tpu_custom_call" | custom-call | flops 15032385536 | bytes 33554432 | tf_op jit(solution)/shard_map/pallas_call | solution.py:510
  491.1 1.1 reshape.159
  494.1 1.4 reshape_reshape.25
  495.5 1.4 reshape_reshape.24
  497.1 2.8 convert_element_type.255
  499.9 1.3 constant_dynamic-slice_fusion.1
  502.1 1.3 constant_dynamic-slice_fusion.2
  503.4 3.4 fusion.19
  508.9 6.5 %collective-permute-done.16 = bf16[256,1024]{1,0:T(8,128)(2,1)S(1)} collective-permute-done((bf16[256,1024]{1,0:T(8,128)(2,1)}, bf16[256,1024]{1,0:T(8,128)(2,1)S(1)}, u32[]{:S(2)}, u32[]{:S(2)}) %collective-permute-start.16) | collective-permute-done | bytes 524320 | tf_op jit(solution)/shard_map/ppermute | solution.py:709
  516.8 1.3 add_convert_fusion.5
  518.1 1.3 collective-permute-start.9
  519.4 1.7 add_bitcast_fusion.1
  521.2 2.0 add_bitcast_fusion
  523.3 2.6 fusion.12
  526.7 7.0 %collective-permute-done.8 = bf16[256,1024]{1,0:T(8,128)(2,1)S(1)} collective-permute-done((bf16[256,1024]{1,0:T(8,128)(2,1)S(1)}, bf16[256,1024]{1,0:T(8,128)(2,1)S(1)}, u32[]{:S(2)}, u32[]{:S(2)}) %collective-permute-start.8) | collective-permute-done | bytes 524320 | tf_op jit(solution)/shard_map/ppermute | solution.py:709
  533.8 4.2 collective-permute-done.9
  539.3 1.4 collective-permute-start.20
  542.6 10.4 %collective-permute-done.19 = bf16[256,1024]{1,0:T(8,128)(2,1)S(1)} collective-permute-done((bf16[256,1024]{1,0:T(8,128)(2,1)S(1)}, bf16[256,1024]{1,0:T(8,128)(2,1)S(1)}, u32[]{:S(2)}, u32[]{:S(2)}) %collective-permute-start.19) | collective-permute-done | bytes 524320 | tf_op jit(solution)/shard_map/ppermute | solution.py:709
  554.6 9.2 %collective-permute-done.17 = bf16[256,1024]{1,0:T(8,128)(2,1)S(1)} collective-permute-done((bf16[256,1024]{1,0:T(8,128)(2,1)S(1)}, bf16[256,1024]{1,0:T(8,128)(2,1)S(1)}, u32[]{:S(2)}, u32[]{:S(2)}) %collective-permute-start.17) | collective-permute-done | bytes 524320 | tf_op jit(solution)/shard_map/ppermute | solution.py:709
  563.8 1.3 add_bitcast_fusion.5
  565.1 1.3 add_bitcast_fusion.4
  568.0 2.9 convert_add_fusion.1
  571.0 16.7 %shard_map.259 = (bf16[64,8192]{1,0:T(8,128)(2,1)}, bf16[64,2048]{1,0:T(8,128)(2,1)}) custom-call(bf16[512,1280]{1,0:T(8,128)(2,1)} %reduce-scatter.8.cloned.1.call-done.refs_0_.refs_1_, bf16[512,1280]{1,0:T(8,128)(2,1)} %reduce-scatter.8.cloned.1.call-done.refs_0_.refs_1_), custom_call_target="tpu_custom_call" | custom-call | flops 11900000256 | bytes 1048576 | tf_op jit(solution)/shard_map/pallas_call | solution.py:338
  587.6 1.8 convert_element_type.278
  589.4 3.8 fusion.16
  (201 shorter events, 31.0 us)
Async XLA Ops:
  7.2 133.1 %all-gather.5.cloned.1.call-start = ((), (), s32[]{:S(2)}) async-start(), calls=%async_computation.3 | async-start | bytes 5242880 | tf_op jit(solution)/shard_map/all_gather | solution.py:764
  23.6 150.9 %all-gather.7.cloned.1.call-start = ((), (), s32[]{:S(2)}) async-start(), calls=%async_computation.4 | async-start | bytes 3932160 | tf_op jit(solution)/shard_map/all_gather | solution.py:764
  36.2 228.3 %all-gather.9.cloned.1.call-start = ((), (), s32[]{:S(2)}) async-start(), calls=%async_computation.5 | async-start | bytes 1310720 | tf_op jit(solution)/shard_map/all_gather | solution.py:764
  37.4 96.8 %copy-start.28 = (s32[2,1024]{1,0:T(2,128)S(1)}, s32[2,1024]{1,0:T(2,128)}, u32[]{:S(2)}) copy-start(s32[2,1024]{1,0:T(2,128)} %param.16) | copy-start | bytes 24580
  134.2 164.5 %all-gather.11.cloned.1.call-start = ((), (), s32[]{:S(2)}) async-start(), calls=%async_computation.6 | async-start | bytes 5242880 | tf_op jit(solution)/shard_map/all_gather | solution.py:764
  134.2 3.7 collective-permute-start
  135.0 285.2 %reduce-scatter.4.cloned.1.call-start = ((), (), s32[]{:S(2)}) async-start(), calls=%async_computation.7 | async-start | bytes 5242880 | tf_op jit(solution)/shard_map/reduce_scatter | solution.py:869
  135.2 33.9 %copy-start.21 = (f32[4,8,8,128]{3,1,2,0:T(8,128)}, f32[4,8,8,128]{3,1,2,0:T(8,128)S(1)}, u32[]{:S(2)}) copy-start(f32[4,8,8,128]{3,1,2,0:T(8,128)S(1)} %copy.42) | copy-start | bytes 393220
  138.0 55.8 %collective-permute-start.1 = (bf16[2,256,2048]{2,1,0:T(8,128)(2,1)}, bf16[2,256,2048]{2,1,0:T(8,128)(2,1)}, u32[]{:S(2)}, u32[]{:S(2)}) collective-permute-start(bf16[2,256,2048]{2,1,0:T(8,128)(2,1)} %refs_5_), channel_id=1, source_target_pairs={{0,2},{1,3},{2,0},{3,1},{4,6},{5,7},{6,4},{7,5},{8,10},{9,11},{10,... | collective-permute-start | bytes 6291464 | tf_op jit(solution)/shard_map/ppermute | solution.py:709
  139.5 54.3 %collective-permute-start.2 = (bf16[2,256,2048]{2,1,0:T(8,128)(2,1)}, bf16[2,256,2048]{2,1,0:T(8,128)(2,1)}, u32[]{:S(2)}, u32[]{:S(2)}) collective-permute-start(bf16[2,256,2048]{2,1,0:T(8,128)(2,1)} %refs_5_), channel_id=1, source_target_pairs={{0,4},{1,5},{2,6},{3,7},{4,0},{5,1},{6,2},{7,3},{8,12},{9,13},{10,... | collective-permute-start | bytes 6291464 | tf_op jit(solution)/shard_map/ppermute | solution.py:709
  252.0 204.6 %reduce-scatter.6.cloned.1.call-start = ((), (), s32[]{:S(2)}) async-start(), calls=%async_computation.8 | async-start | bytes 3932160 | tf_op jit(solution)/shard_map/reduce_scatter | solution.py:869
  330.8 49.5 %collective-permute-start.3 = (bf16[256,2048]{1,0:T(8,128)(2,1)}, bf16[256,2048]{1,0:T(8,128)(2,1)S(1)}, u32[]{:S(2)}, u32[]{:S(2)}) collective-permute-start(bf16[256,2048]{1,0:T(8,128)(2,1)} %get-tuple-element.145), channel_id=1, source_target_pairs={{0,4},{1,5},{2,6},{3,7},{4,0},{5,1},{6,2},{7,3},{8,12},{9,13},{10,... | collective-permute-start | bytes 3145736 | tf_op jit(solution)/shard_map/ppermute | solution.py:709
  331.9 48.4 %collective-permute-start.4 = (bf16[256,2048]{1,0:T(8,128)(2,1)}, bf16[256,2048]{1,0:T(8,128)(2,1)}, u32[]{:S(2)}, u32[]{:S(2)}) collective-permute-start(bf16[256,2048]{1,0:T(8,128)(2,1)} %get-tuple-element.147), channel_id=1, source_target_pairs={{0,4},{1,5},{2,6},{3,7},{4,0},{5,1},{6,2},{7,3},{8,12},{9,13},{10,... | collective-permute-start | bytes 3145736 | tf_op jit(solution)/shard_map/ppermute | solution.py:709
  332.9 47.4 %collective-permute-start.5 = (bf16[256,2048]{1,0:T(8,128)(2,1)}, bf16[256,2048]{1,0:T(8,128)(2,1)}, u32[]{:S(2)}, u32[]{:S(2)}) collective-permute-start(bf16[256,2048]{1,0:T(8,128)(2,1)} %get-tuple-element.144), channel_id=1, source_target_pairs={{0,2},{1,3},{2,0},{3,1},{4,6},{5,7},{6,4},{7,5},{8,10},{9,11},{10,... | collective-permute-start | bytes 3145736 | tf_op jit(solution)/shard_map/ppermute | solution.py:709
  334.0 46.4 %collective-permute-start.6 = (bf16[256,2048]{1,0:T(8,128)(2,1)}, bf16[256,2048]{1,0:T(8,128)(2,1)}, u32[]{:S(2)}, u32[]{:S(2)}) collective-permute-start(bf16[256,2048]{1,0:T(8,128)(2,1)} %get-tuple-element.148), channel_id=1, source_target_pairs={{0,2},{1,3},{2,0},{3,1},{4,6},{5,7},{6,4},{7,5},{8,10},{9,11},{10,... | collective-permute-start | bytes 3145736 | tf_op jit(solution)/shard_map/ppermute | solution.py:709
  355.3 215.7 %reduce-scatter.8.cloned.1.call-start = ((), (), s32[]{:S(2)}) async-start(), calls=%async_computation.9 | async-start | bytes 6553600 | tf_op jit(solution)/shard_map/reduce_scatter | solution.py:869
  355.3 25.1 %copy-start.10 = (bf16[256,2048]{1,0:T(8,128)(2,1)S(1)}, bf16[256,2048]{1,0:T(8,128)(2,1)}, u32[]{:S(2)}) copy-start(bf16[256,2048]{1,0:T(8,128)(2,1)} %get-tuple-element.154) | copy-start | bytes 3145732
  355.3 28.0 %copy-start.9 = (bf16[256,2048]{1,0:T(8,128)(2,1)S(1)}, bf16[256,2048]{1,0:T(8,128)(2,1)}, u32[]{:S(2)}) copy-start(bf16[256,2048]{1,0:T(8,128)(2,1)} %get-tuple-element.150) | copy-start | bytes 3145732
  380.3 28.4 %copy-start.6 = (bf16[256,2048]{1,0:T(8,128)(2,1)}, bf16[256,2048]{1,0:T(8,128)(2,1)S(1)}, u32[]{:S(2)}) copy-start(bf16[256,2048]{1,0:T(8,128)(2,1)S(1)} %collective-permute-done.3) | copy-start | bytes 3145732
  385.9 22.8 %copy-start.8 = (bf16[2048,256]{1,0:T(8,128)(2,1)S(1)}, bf16[2048,256]{1,0:T(8,128)(2,1)}, u32[]{:S(2)}) copy-start(bf16[2048,256]{1,0:T(8,128)(2,1)} %convolution_convert_fusion.3) | copy-start | bytes 3145732
  418.2 99.9 %collective-permute-start.11 = (bf16[256,2048]{1,0:T(8,128)(2,1)}, bf16[256,2048]{1,0:T(8,128)(2,1)}, u32[]{:S(2)}, u32[]{:S(2)}) collective-permute-start(bf16[256,2048]{1,0:T(8,128)(2,1)} %add_convert_fusion.1), channel_id=1, source_target_pairs={{0,2},{1,3},{2,0},{3,1},{4,6},{5,7},{6,4},{7,5},{8,10},{9,11},{10,... | collective-permute-start | bytes 3145736 | tf_op jit(solution)/shard_map/ppermute | solution.py:709
  419.3 100.1 %collective-permute-start.12 = (bf16[256,2048]{1,0:T(8,128)(2,1)}, bf16[256,2048]{1,0:T(8,128)(2,1)}, u32[]{:S(2)}, u32[]{:S(2)}) collective-permute-start(bf16[256,2048]{1,0:T(8,128)(2,1)} %add_convert_fusion), channel_id=1, source_target_pairs={{0,4},{1,5},{2,6},{3,7},{4,0},{5,1},{6,2},{7,3},{8,12},{9,13},{10,... | collective-permute-start | bytes 3145736 | tf_op jit(solution)/shard_map/ppermute | solution.py:709
  453.6 47.6 %collective-permute-start.13 = (bf16[256,1024]{1,0:T(8,128)(2,1)}, bf16[256,1024]{1,0:T(8,128)(2,1)}, u32[]{:S(2)}, u32[]{:S(2)}) collective-permute-start(bf16[256,1024]{1,0:T(8,128)(2,1)} %get-tuple-element.167), channel_id=1, source_target_pairs={{0,4},{1,5},{2,6},{3,7},{4,0},{5,1},{6,2},{7,3},{8,12},{9,13},{10,... | collective-permute-start | bytes 1572872 | tf_op jit(solution)/shard_map/ppermute | solution.py:709
  454.7 52.1 %collective-permute-start.14 = (bf16[256,1024]{1,0:T(8,128)(2,1)}, bf16[256,1024]{1,0:T(8,128)(2,1)}, u32[]{:S(2)}, u32[]{:S(2)}) collective-permute-start(bf16[256,1024]{1,0:T(8,128)(2,1)} %get-tuple-element.169), channel_id=1, source_target_pairs={{0,4},{1,5},{2,6},{3,7},{4,0},{5,1},{6,2},{7,3},{8,12},{9,13},{10,... | collective-permute-start | bytes 1572872 | tf_op jit(solution)/shard_map/ppermute | solution.py:709
  455.7 52.2 %collective-permute-start.15 = (bf16[256,1024]{1,0:T(8,128)(2,1)}, bf16[256,1024]{1,0:T(8,128)(2,1)}, u32[]{:S(2)}, u32[]{:S(2)}) collective-permute-start(bf16[256,1024]{1,0:T(8,128)(2,1)} %get-tuple-element.166), channel_id=1, source_target_pairs={{0,2},{1,3},{2,0},{3,1},{4,6},{5,7},{6,4},{7,5},{8,10},{9,11},{10,... | collective-permute-start | bytes 1572872 | tf_op jit(solution)/shard_map/ppermute | solution.py:709
  492.3 24.5 %copy-start.19 = (bf16[256,1024]{1,0:T(8,128)(2,1)S(1)}, bf16[256,1024]{1,0:T(8,128)(2,1)}, u32[]{:S(2)}) copy-start(bf16[256,1024]{1,0:T(8,128)(2,1)} %get-tuple-element.165) | copy-start | bytes 1572868
  497.0 18.4 %copy-start.40 = (bf16[256,1024]{1,0:T(8,128)(2,1)S(1)}, bf16[256,1024]{1,0:T(8,128)(2,1)}, u32[]{:S(2)}) copy-start(bf16[256,1024]{1,0:T(8,128)(2,1)} %get-tuple-element.175) | copy-start | bytes 1572868
  497.0 19.5 %copy-start.20 = (bf16[256,1024]{1,0:T(8,128)(2,1)S(1)}, bf16[256,1024]{1,0:T(8,128)(2,1)}, u32[]{:S(2)}) copy-start(bf16[256,1024]{1,0:T(8,128)(2,1)} %get-tuple-element.168) | copy-start | bytes 1572868
  497.1 21.1 %copy-start.39 = (bf16[256,1024]{1,0:T(8,128)(2,1)S(1)}, bf16[256,1024]{1,0:T(8,128)(2,1)}, u32[]{:S(2)}) copy-start(bf16[256,1024]{1,0:T(8,128)(2,1)} %get-tuple-element.176) | copy-start | bytes 1572868
  497.1 22.4 %copy-start.5 = (bf16[256,2048]{1,0:T(8,128)(2,1)S(1)}, bf16[256,2048]{1,0:T(8,128)(2,1)}, u32[]{:S(2)}) copy-start(bf16[256,2048]{1,0:T(8,128)(2,1)} %get-tuple-element.190) | copy-start | bytes 3145732
  497.1 22.4 %copy-start.7 = (bf16[256,2048]{1,0:T(8,128)(2,1)S(1)}, bf16[256,2048]{1,0:T(8,128)(2,1)}, u32[]{:S(2)}) copy-start(bf16[256,2048]{1,0:T(8,128)(2,1)} %copy-done.6) | copy-start | bytes 3145732
  501.2 14.3 %collective-permute-start.16 = (bf16[256,1024]{1,0:T(8,128)(2,1)}, bf16[256,1024]{1,0:T(8,128)(2,1)S(1)}, u32[]{:S(2)}, u32[]{:S(2)}) collective-permute-start(bf16[256,1024]{1,0:T(8,128)(2,1)} %get-tuple-element.170), channel_id=1, source_target_pairs={{0,2},{1,3},{2,0},{3,1},{4,6},{5,7},{6,4},{7,5},{8,10},{9,11},{10,... | collective-permute-start | bytes 1572872 | tf_op jit(solution)/shard_map/ppermute | solution.py:709
  502.1 91.1 %copy-start.47 = (f32[64]{0:T(128)}, f32[64]{0:T(128)S(1)}, u32[]{:S(2)}) copy-start(f32[64]{0:T(128)S(1)} %fusion.24) | copy-start | bytes 772
  506.8 19.9 %collective-permute-start.10 = (bf16[256,1024]{1,0:T(8,128)(2,1)S(1)}, bf16[256,1024]{1,0:T(8,128)(2,1)S(1)}, u32[]{:S(2)}, u32[]{:S(2)}) collective-permute-start(bf16[256,1024]{1,0:T(8,128)(2,1)S(1)} %copy-done.42), channel_id=1, source_target_pairs={{0,2},{1,3},{2,0},{3,1},{4,6},{5,7},{6,4},{7,5},{8,10},{9,11},{10,... | collective-permute-start | bytes 1572872 | tf_op jit(solution)/shard_map/ppermute | solution.py:709
  507.9 18.8 %collective-permute-start.7 = (bf16[256,1024]{1,0:T(8,128)(2,1)S(1)}, bf16[256,1024]{1,0:T(8,128)(2,1)S(1)}, u32[]{:S(2)}, u32[]{:S(2)}) collective-permute-start(bf16[256,1024]{1,0:T(8,128)(2,1)S(1)} %copy-done.41), channel_id=1, source_target_pairs={{0,4},{1,5},{2,6},{3,7},{4,0},{5,1},{6,2},{7,3},{8,12},{9,13},{10,... | collective-permute-start | bytes 1572872 | tf_op jit(solution)/shard_map/ppermute | solution.py:709
  515.5 18.3 %collective-permute-start.8 = (bf16[256,1024]{1,0:T(8,128)(2,1)S(1)}, bf16[256,1024]{1,0:T(8,128)(2,1)S(1)}, u32[]{:S(2)}, u32[]{:S(2)}) collective-permute-start(bf16[256,1024]{1,0:T(8,128)(2,1)S(1)} %copy-done.40), channel_id=1, source_target_pairs={{0,4},{1,5},{2,6},{3,7},{4,0},{5,1},{6,2},{7,3},{8,12},{9,13},{10,... | collective-permute-start | bytes 1572872 | tf_op jit(solution)/shard_map/ppermute | solution.py:709
  518.1 19.8 %collective-permute-start.9 = (bf16[256,1024]{1,0:T(8,128)(2,1)S(1)}, bf16[256,1024]{1,0:T(8,128)(2,1)S(1)}, u32[]{:S(2)}, u32[]{:S(2)}) collective-permute-start(bf16[256,1024]{1,0:T(8,128)(2,1)S(1)} %copy-done.39), channel_id=1, source_target_pairs={{0,2},{1,3},{2,0},{3,1},{4,6},{5,7},{6,4},{7,5},{8,10},{9,11},{10,... | collective-permute-start | bytes 1572872 | tf_op jit(solution)/shard_map/ppermute | solution.py:709
  523.3 17.5 %copy-start.24 = (f32[1,8,8,128]{3,2,1,0:T(8,128)S(1)}, f32[1,8,8,128]{3,2,1,0:T(8,128)}, u32[]{:S(2)}) copy-start(f32[1,8,8,128]{3,2,1,0:T(8,128)} %get-tuple-element.228) | copy-start | bytes 98308
  523.3 29.7 %copy-start.16 = (bf16[256,1024]{1,0:T(8,128)(2,1)S(1)}, bf16[256,1024]{1,0:T(8,128)(2,1)}, u32[]{:S(2)}) copy-start(bf16[256,1024]{1,0:T(8,128)(2,1)} %get-tuple-element.184) | copy-start | bytes 1572868
  525.9 28.3 %copy-start.15 = (bf16[256,1024]{1,0:T(8,128)(2,1)S(1)}, bf16[256,1024]{1,0:T(8,128)(2,1)}, u32[]{:S(2)}) copy-start(bf16[256,1024]{1,0:T(8,128)(2,1)} %get-tuple-element.185) | copy-start | bytes 1572868
  538.2 25.7 %copy-start.14 = (bf16[256,1024]{1,0:T(8,128)(2,1)S(1)}, bf16[256,1024]{1,0:T(8,128)(2,1)}, u32[]{:S(2)}) copy-start(bf16[256,1024]{1,0:T(8,128)(2,1)} %get-tuple-element.163) | copy-start | bytes 1572868
  538.2 14.9 %collective-permute-start.19 = (bf16[256,1024]{1,0:T(8,128)(2,1)S(1)}, bf16[256,1024]{1,0:T(8,128)(2,1)S(1)}, u32[]{:S(2)}, u32[]{:S(2)}) collective-permute-start(bf16[256,1024]{1,0:T(8,128)(2,1)S(1)} %add_convert_fusion.3), channel_id=1, source_target_pairs={{0,2},{1,3},{2,0},{3,1},{4,6},{5,7},{6,4},{7,5},{8,10},{9,11},{10,... | collective-permute-start | bytes 1572872 | tf_op jit(solution)/shard_map/ppermute | solution.py:709
  539.3 14.9 %collective-permute-start.20 = (bf16[256,1024]{1,0:T(8,128)(2,1)S(1)}, bf16[256,1024]{1,0:T(8,128)(2,1)S(1)}, u32[]{:S(2)}, u32[]{:S(2)}) collective-permute-start(bf16[256,1024]{1,0:T(8,128)(2,1)S(1)} %add_convert_fusion.2), channel_id=1, source_target_pairs={{0,4},{1,5},{2,6},{3,7},{4,0},{5,1},{6,2},{7,3},{8,12},{9,13},{10,... | collective-permute-start | bytes 1572872 | tf_op jit(solution)/shard_map/ppermute | solution.py:709
  540.8 23.1 %collective-permute-start.17 = (bf16[256,1024]{1,0:T(8,128)(2,1)S(1)}, bf16[256,1024]{1,0:T(8,128)(2,1)S(1)}, u32[]{:S(2)}, u32[]{:S(2)}) collective-permute-start(bf16[256,1024]{1,0:T(8,128)(2,1)S(1)} %add_convert_fusion.5), channel_id=1, source_target_pairs={{0,2},{1,3},{2,0},{3,1},{4,6},{5,7},{6,4},{7,5},{8,10},{9,11},{10,... | collective-permute-start | bytes 1572872 | tf_op jit(solution)/shard_map/ppermute | solution.py:709
  541.7 23.5 %collective-permute-start.18 = (bf16[256,1024]{1,0:T(8,128)(2,1)S(1)}, bf16[256,1024]{1,0:T(8,128)(2,1)S(1)}, u32[]{:S(2)}, u32[]{:S(2)}) collective-permute-start(bf16[256,1024]{1,0:T(8,128)(2,1)S(1)} %add_convert_fusion.4), channel_id=1, source_target_pairs={{0,4},{1,5},{2,6},{3,7},{4,0},{5,1},{6,2},{7,3},{8,12},{9,13},{10,... | collective-permute-start | bytes 1572872 | tf_op jit(solution)/shard_map/ppermute | solution.py:709
  570.9 18.5 %copy-start.11 = (bf16[64,8192]{1,0:T(8,128)(2,1)S(1)}, bf16[64,8192]{1,0:T(8,128)(2,1)}, u32[]{:S(2)}) copy-start(bf16[64,8192]{1,0:T(8,128)(2,1)} %refs_0_.1) | copy-start | bytes 3145732
  570.9 18.5 %copy-start.32 = (f32[64]{0:T(128)S(1)}, f32[64]{0:T(128)}, u32[]{:S(2)}) copy-start(f32[64]{0:T(128)} %copy-done.31) | copy-start | bytes 772
  570.9 18.5 %copy-start.34 = (f32[64]{0:T(128)S(1)}, f32[64]{0:T(128)}, u32[]{:S(2)}) copy-start(f32[64]{0:T(128)} %copy-done.33) | copy-start | bytes 772
  (28 other events, 249.5 us)
Sparse Core Ops, SparseCore 0:
  23.6 85.1 all-gather.4
  110.3 61.7 all-gather.6
  173.7 26.6 all-gather.8
  201.8 80.1 all-gather.10
  284.8 75.2 reduce-scatter.3
  362.2 60.8 reduce-scatter.5
  425.5 97.8 reduce-scatter.7

commit v8 on v7

--- a/solution.py
+++ b/solution.py
@@ -39,6 +39,13 @@
         src_ref=source, dst_ref=target, send_sem=send, recv_sem=recv,
         device_id=device, device_id_type=MESH,
     )
+
+
+def far_places(square, chips, batch):
+    if square and batch == 2:
+        return {(0, 0): (0, None), (0, 1): (1, None), (1, 0): (2, None), (2, 1): (3, None),
+                (2, 0): (4, 0), (3, 0): (4, 1), (1, 1): (5, 0), (3, 1): (5, 1)}
+    return {(o, m): (o * batch + m, None) for o in range(chips) for m in range(batch)}
 
 
 class Layout:
@@ -350,7 +357,7 @@
     )(*arrays)
 
 
-def pair_kernel(lay, plan, with_vec, scaled, batch, *refs):
+def pair_kernel(lay, plan, with_vec, scaled, batch, places, *refs):
     refs = list(refs)
     take = lambda k: [refs.pop(0) for _ in range(k)]
     step = pl.program_id(0)
@@ -358,7 +365,7 @@
     first_ref, first_w, second_ref, second_w = take(4)
     scales = take(2) if scaled else []
     sources, vec_ref = take(len(plan)), take(int(with_vec))
-    outs, targets, all_ref = take(chips * batch), take(len(plan)), take(int(with_vec))
+    outs, targets, all_ref = take(1 + max(k for k, _ in places.values())), take(len(plan)), take(int(with_vec))
     given, came, act_buf, w_buf, send, recv, out_sem = take(7)
     zo, yi, s = lax.axis_index("zo"), lax.axis_index("yi"), lax.axis_index("seq")
     me = yi * lay.seq + s
@@ -373,12 +380,12 @@
 
     def stores(j):
         length = came.shape[1] // batch
-        return [
-            pltpu.make_async_copy(
-                came.at[j, pl.ds(m * length, length)], outs[(j + 1) % chips * batch + m], out_sem.at[j, m]
-            )
-            for m in range(batch)
-        ]
+        copies = []
+        for m in range(batch):
+            k, at = places[((j + 1) % chips, m)]
+            target = outs[k] if at is None else outs[k].at[at]
+            copies.append(pltpu.make_async_copy(came.at[j, pl.ds(m * length, length)], target, out_sem.at[j, m]))
+        return copies
 
     def riders():
         if not plan:
@@ -491,7 +498,10 @@
         args.append(scale.reshape(1, -1))
     args += [*arrays, *([vec] if with_vec else [])]
     specs += [ANY] * (len(args) - len(specs))
-    shapes = [jax.ShapeDtypeStruct((rows // batch, width), BF16)] * (chips * batch) + swap_shapes(lay, plan, True)
+    places = far_places(lay.square, chips, batch)
+    piled = [sum(1 for k, _ in places.values() if k == i) for i in range(1 + max(k for k, _ in places.values()))]
+    piece = (rows // batch, width)
+    shapes = [jax.ShapeDtypeStruct(piece if n == 1 else (n, *piece), BF16) for n in piled] + swap_shapes(lay, plan, True)
     depth = sum(a.shape[1] for a in acts)
     scratch = [
         pltpu.VMEM((chips, rows, width), BF16),
@@ -508,7 +518,7 @@
         shapes.append(jax.ShapeDtypeStruct((lay.count, *vec.shape), vec.dtype))
         scratch += [pltpu.SemaphoreType.DMA((lay.count - 1,))] * 2 + [pltpu.SemaphoreType.DMA]
     return pl.pallas_call(
-        functools.partial(pair_kernel, lay, plan, with_vec, bool(scales), batch),
+        functools.partial(pair_kernel, lay, plan, with_vec, bool(scales), batch, places),
         grid=(2 * chips,),
         in_specs=specs,
         out_specs=[ANY] * len(shapes),
@@ -555,13 +565,13 @@
     near = take(near_count)
     q_ref, k_ref, v_ref, ctx_ref, lse_ref, dy_ref = take(6)
     q_buf, k_buf, v_buf, ctx_buf, cos_buf, sin_buf, bounce = take(7)
-    load_sem, store_sem, core_send, core_recv, on_send, on_recv = take(6)
+    load_sem, store_sem, core_send, core_recv, on_send, on_recv, fwd_send, fwd_recv = take(8)
     step, last = pl.program_id(0), pl.num_programs(0) - 1
     zo, yi, s = lax.axis_index("zo"), lax.axis_index("yi"), lax.axis_index("seq")
     x, core = s // 2, lax.rem(s, 2)
     partner = (zo, yi, x * 2 + 1 - core)
-    chips = lay.group // 2
-    half = near[0].shape[0] // 2
+    batch, length = near[0].shape[:2]
+    cuts = [(m, pl.ds(q * (length // 2), length // 2)) for m in range(batch) for q in range(2)] if lay.square else []
 
     def load(i):
         return pltpu.make_async_copy(near[i], bounce.at[i], load_sem.at[i])
@@ -570,17 +580,21 @@
         return pltpu.make_async_copy(bounce.at[i], dy_ref.at[0, i], store_sem.at[i])
 
     def to_partner(i):
-        source = near[i] if i < near_count else dy_ref.at[0, i]
-        return remote(source, dy_ref.at[1, i], core_send.at[i], core_recv.at[i], partner)
+        return remote(near[i], dy_ref.at[1, i], core_send.at[i], core_recv.at[i], partner)
 
     def onward():
-        if not lay.square:
-            return []
         over_y = (zo, lax.rem(yi + 1, lay.sub), s)
         over_x = (zo, yi, lax.rem(x + 1, lay.chips_x) * 2 + core)
         return [
-            remote(near[1].at[:half], dy_ref.at[0, 3, :half], on_send.at[0], on_recv.at[0], over_y),
-            remote(near[2].at[half:], dy_ref.at[0, 3, half:], on_send.at[1], on_recv.at[1], over_x),
+            remote(near[1 if m < batch // 2 else 2].at[m, rows], dy_ref.at[0, 3, m, rows], on_send.at[k], on_recv.at[k],
+                   over_y if m < batch // 2 else over_x)
+            for k, (m, rows) in enumerate(cuts)
+        ]
+
+    def forward():
+        return [
+            remote(dy_ref.at[0, 3, m, rows], dy_ref.at[1, 3, m, rows], fwd_send.at[k], fwd_recv.at[k], partner)
+            for k, (m, rows) in enumerate(cuts)
         ]
 
     @pl.when(step == 0)
@@ -603,16 +617,15 @@
 
     @pl.when(step == last)
     def _():
-        for copy in onward():
-            copy.wait_recv()
-        for i in range(near_count, chips):
-            to_partner(i).start()
+        for came, copy in zip(onward(), forward(), strict=True):
+            came.wait_recv()
+            copy.start()
         for i in range(near_count):
             store(i).wait()
-        for i in range(chips):
             to_partner(i).wait()
-        for copy in onward():
-            copy.wait_send()
+        for gone, copy in zip(onward(), forward(), strict=True):
+            gone.wait_send()
+            copy.wait()
 
 
 def attend_one(scaling, packed_ref, cos_ref, sin_ref, col_ref, row_ref, q_ref, k_ref, v_ref, ctx_ref, lse_ref,
@@ -653,16 +666,30 @@
             ctx_ref[c, 0, i, 0] = ctx_buf[pl.ds((c * chips + i) * length, length), :]
 
 
-def attend_back_kernel(scaling, q_ref, k_ref, v_ref, dy_ref, w_ref, cos_ref, sin_ref, col_ref, row_ref, lse_ref, out_ref, sum_ref,
-                       g_buf, dq_buf, dk_buf, dv_buf, cos_buf, sin_buf):
+def attend_back_kernel(scaling, q_ref, k_ref, v_ref, dy_ref, w_ref, ctx_ref, cos_ref, sin_ref, col_ref, row_ref, lse_ref, out_ref, sum_ref, grad_ref,
+                       g_buf, acc_buf, dq_buf, dk_buf, dv_buf, cos_buf, sin_buf):
     cores, _, chips, _, length, _ = out_ref.shape
     total = q_ref.shape[1]
     cos_all, sin_all = wide_pair(cos_ref, sin_ref)
     cos_buf[...] = cos_all
     sin_buf[...] = sin_all
-    for c in range(cores):
-        for i in range(chips):
-            g_buf[pl.ds((c * chips + i) * length, length), :] = dot(dy_ref[c, 0, i, 0], w_ref[...], ((1,), (0,))).astype(BF16)
+    upstream = dy_ref[...].reshape(total, dy_ref.shape[-1])
+    g_buf[...] = dot(upstream, w_ref[...], ((1,), (0,))).astype(BF16)
+    out_grad = dot(ctx_ref[...].reshape(total, ctx_ref.shape[-1]), upstream, ((0,), (0,)))
+    step = pl.program_id(0)
+
+    @pl.when(step == 0)
+    def _():
+        acc_buf[...] = out_grad
+
+    @pl.when(step > 0)
+    def _():
+        acc_buf[...] += out_grad
+
+    @pl.when(step == pl.num_programs(0) - 1)
+    def _():
+        grad_ref[...] = jnp.transpose(acc_buf[...], (1, 0)).astype(BF16)
+
     dk_buf[...] = jnp.zeros_like(dk_buf)
     dv_buf[...] = jnp.zeros_like(dv_buf)
 
@@ -714,28 +741,29 @@
             total = total + piece.astype(F32)
         return total
 
-    def far_first(pieces):
+    def far_first(outs):
         if square:
-            return [
-                [across(pieces[2][0], (1, 0)), across(pieces[3][0], (1, 0))],
-                [across(pieces[1][1], (0, 1)), across(pieces[3][1], (0, 1))],
+            return [across(outs[4], (1, 0)), across(outs[5], (0, 1))]
+        batch = len(outs) // (group // 2)
+        return [
+            [
+                across(outs[i * batch + m], ((-o[0]) % sub, (-o[1]) % chips_x))
+                for i, o in enumerate(lay.offsets)
+                if i
             ]
-        batch = len(pieces[0])
-        return [
-            [across(pieces[i][m], ((-o[0]) % sub, (-o[1]) % chips_x)) for i, o in enumerate(lay.offsets) if i]
             for m in range(batch)
         ]
 
-    def far_onward(pieces, came):
+    def far_onward(outs, came):
         if square:
-            return [add(pieces[1][0], came[0][1]).astype(BF16), add(pieces[2][1], came[1][1]).astype(BF16)]
+            return [add(outs[2], came[0][1]).astype(BF16), add(outs[3], came[1][1]).astype(BF16)]
         return []
 
-    def far_second(pieces, came, onward):
+    def far_second(outs, came, onward):
         if square:
             last = [across(onward[0], (0, 1)), across(onward[1], (1, 0))]
-            return [[pieces[0][m], came[m][0], last[m]] for m in range(2)]
-        return [[pieces[0][m], *came[m]] for m in range(len(came))]
+            return [[outs[m], came[m][0], last[m]] for m in range(2)]
+        return [[outs[m], *came[m]] for m in range(len(came))]
 
     def add_all(parts):
         return jnp.stack([add(*pieces) for pieces in parts])
@@ -788,7 +816,7 @@
         w_qkv_late, _ = lax.optimization_barrier((w_qkv, up_own))
         (qkv_own,) = deal_exchange(lay, [plans["qkv"]], [w_qkv_late], False, 7)
         qkv_w = gather_rows(qkv_own)
-        tokens_late, _ = lax.optimization_barrier((tokens, qkv_own))
+        tokens_late, _, places = lax.optimization_barrier((tokens, qkv_own, places))
         one, two, hat, vectors, out_own, down_own = norm_exchange(
             lay, [plans["out"], plans["down"]], tokens_late, laid(names), [w_out, w_down]
         )
@@ -804,7 +832,7 @@
         b_qkv_mine = lax.dynamic_index_in_dim(b_qkv_all.reshape(3, group, cols), me, 1, keepdims=False).reshape(-1)
         b_up_mine = lax.dynamic_index_in_dim(b_up_all.reshape(group, ff_cols), me, 0, keepdims=False)
         one, two, hat = [v.reshape(total, width) for v in (one, two, hat)]
-        cotangent, hat, places = lax.optimization_barrier((cotangent, hat, places))
+        cotangent, hat = lax.optimization_barrier((cotangent, hat))
         near_dy = [cotangent] + [across(cotangent, o) for o in lay.near[1:]]
 
         hidden = dot(two, up_w, ((1,), (0,))) + b_up_mine
@@ -855,8 +883,8 @@
             + turn_bufs
             + [pltpu.VMEM((near_count, *cotangent.shape), BF16)]
             + [pltpu.SemaphoreType.DMA((near_count,))] * 2
-            + [pltpu.SemaphoreType.DMA((chips,))] * 2
-            + [pltpu.SemaphoreType.DMA((2,))] * 2,
+            + [pltpu.SemaphoreType.DMA((near_count,))] * 2
+            + [pltpu.SemaphoreType.DMA((2 * batch,))] * 4,
             compiler_params=pltpu.CompilerParams(collective_id=8, has_side_effects=True, vmem_limit_bytes=58 << 20),
             cost_estimate=pl.CostEstimate(flops=2 * work, bytes_accessed=30 << 20, transcendentals=seqs * count * count),
             name="attend",
@@ -874,35 +902,39 @@
         def chain(values, *tokens):
             return lax.optimization_barrier((*values, *tokens))[: len(values)]
 
-        def tokens_of(pieces):
-            return [pieces[i * batch : (i + 1) * batch] for i in range(group // 2)]
-
         down_part = outer_dot(upstream, activated)
         upstream, down_part = chain((upstream, down_part))
         down_sum = scatter(down_part)
-        out_part = outer_dot(upstream, context)
-        upstream, out_part = chain((upstream, out_part))
-
-        grad_packed, sum_packed = pl.pallas_call(
+
+        grad_packed, sum_packed, out_part = pl.pallas_call(
             functools.partial(attend_back_kernel, scaling),
             grid=(seqs,),
             in_specs=[head_spec] * 3
             + [
                 pl.BlockSpec((2, 1, chips_x, 1, length, width), lambda i: (0, i // batch, 0, i % batch, 0, 0)),
                 pl.BlockSpec((width, cols), lambda i: (0, 0), pipeline_mode=pl.Buffered(1)),
+                tokens_spec,
             ]
             + [turn_spec, turn_spec, col_spec, row_spec, row_spec],
-            out_specs=[wide_spec, pl.BlockSpec((1, 1, 3 * cols), lambda i: (i, 0, 0))],
-            out_shape=[jax.ShapeDtypeStruct(full, BF16), jax.ShapeDtypeStruct((seqs, 1, 3 * cols), F32)],
-            scratch_shapes=[pltpu.VMEM((count, HEAD_DIM), BF16)] + [pltpu.VMEM((count, HEAD_DIM), F32)] * 3 + turn_bufs,
+            out_specs=[
+                wide_spec,
+                pl.BlockSpec((1, 1, 3 * cols), lambda i: (i, 0, 0)),
+                pl.BlockSpec((width, cols), lambda i: (0, 0)),
+            ],
+            out_shape=[
+                jax.ShapeDtypeStruct(full, BF16),
+                jax.ShapeDtypeStruct((seqs, 1, 3 * cols), F32),
+                jax.ShapeDtypeStruct((width, cols), BF16),
+            ],
+            scratch_shapes=[pltpu.VMEM((count, HEAD_DIM), BF16), pltpu.VMEM((cols, width), F32)] + [pltpu.VMEM((count, HEAD_DIM), F32)] * 3 + turn_bufs,
             compiler_params=params,
-            cost_estimate=pl.CostEstimate(flops=7 * work, bytes_accessed=40 << 20, transcendentals=seqs * count * count),
+            cost_estimate=pl.CostEstimate(flops=9 * work, bytes_accessed=40 << 20, transcendentals=seqs * count * count),
             name="attend_back",
-        )(queries, keys, values, upstream.reshape(2, sub, chips_x, batch, length, width), out_w, cosine, sine, place_col, place_row, lse)
+        )(queries, keys, values, upstream.reshape(2, sub, chips_x, batch, length, width), out_w, context.reshape(by_token), cosine, sine, place_col, place_row, lse)
         grad_packed = grad_packed.reshape(total, 3 * cols)
 
         acts = chain((context, activated), grad_packed)
-        out_near = tokens_of(pair_matmul(lay, acts, (out_w, down_w), batch, (0, 1), 4))
+        out_near = pair_matmul(lay, acts, (out_w, down_w), batch, (0, 1), 4)
         out_came = far_first(out_near)
         hat, out_near = chain((hat, out_near))
         qkv_part = outer_dot(hat, grad_packed)
@@ -919,22 +951,20 @@
 
         folded = (qkv_w, up_w)
         scales = (gain1_all, gain2_all)
-        left, down_sum = chain((left, down_sum))
-        *near0, down_raw = pair_matmul(
-            lay, (left, grad_hidden), folded, batch, (0, 2), 5, scales, [plans["down"]], [down_sum]
-        )
-        near0 = tokens_of(near0)
-        came0 = far_first(near0)
         own_sums = [
             jnp.sum(sum_packed, (0, 1)),
             sum_hidden,
             jnp.sum(cotangent.astype(F32), (0, 1)),
         ]
-        left, vec, qkv_sum = chain((left, laid(own_sums).astype(BF16), qkv_sum), near0)
-        *near1, qkv_raw, everyone = pair_matmul(
-            lay, (left, grad_hidden), folded, batch, (1, 2), 6, scales, [plans["qkv"]], [qkv_sum], vec
+        left, vec, down_sum = chain((left, laid(own_sums).astype(BF16), down_sum))
+        *near0, down_raw, everyone = pair_matmul(
+            lay, (left, grad_hidden), folded, batch, (0, 2), 5, scales, [plans["down"]], [down_sum], vec
         )
-        near1 = tokens_of(near1)
+        came0 = far_first(near0)
+        left, qkv_sum = chain((left, qkv_sum), near0)
+        *near1, qkv_raw = pair_matmul(
+            lay, (left, grad_hidden), folded, batch, (1, 2), 6, scales, [plans["qkv"]], [qkv_sum]
+        )
         came1 = far_first(near1)
         (came0,) = chain((came0,), near1)
         onward0 = far_onward(near0, came0)

time: 607 us -> 583 us (0.960)
  matrix products: 153 us -> 140 us
  waiting for transfers between devices: 41.7 us -> 35.6 us
    dot_general x7 -> x6, matrix products: 153 us -> 140 us  [dot(): lax.dot_general(left, right, (dims, ((), ())), preferred_element_type=F32)]
    ppermute x20 -> x14, starting transfers between devices: 21.2 us -> 15.1 us  [across(): return lax.ppermute(value, GROUP, lay.shift(*o))]
    ppermute x20 -> x14, waiting for transfers between devices: 39.1 us -> 35.4 us  [across(): return lax.ppermute(value, GROUP, lay.shift(*o))]
  transfers between devices with their start and end apart: 28 -> 22, of which waited for: 8 -> 7; matrix products, arithmetic and copies ran while one was open for 34% -> 33% of each run, Pallas kernels for 46% -> 49%
where the time goes in v8:
time: 583 us; the launch traced here: 578 us
  Pallas kernels  313 us (54%)
  matrix products  140 us (24%)
  other arithmetic  44.8 us (8%)
  waiting for transfers between devices  35.6 us (6%)
  starting transfers between devices  16.3 us (3%)
  between operations  15.6 us (3%)
  local copies, waits for them, and re-layouts  11.8 us (2%)
    dot_general x6, matrix products, dot(): lax.dot_general(left, right, (dims, ((), ())), preferred_element_type=F32)  140 us
    pallas_call x3, Pallas kernels, pair_matmul(): pl.pallas_call(functools.partial(pair_kernel, lay, plan, with_vec, bool(s...  97 us
    pallas_call x1, Pallas kernels, norm_exchange(): pl.pallas_call(functools.partial(norm_kernel, lay, plan), out_shape=[whol...  96.7 us
    pallas_call x3, Pallas kernels, deal_exchange(): pl.pallas_call(functools.partial(deal_kernel, lay, plan, back), out_shape...  45.4 us
    pallas_call x1, Pallas kernels, step(): pl.pallas_call(functools.partial(attend_back_kernel, scaling), grid=(seqs...  40 us
    ppermute x14, waiting for transfers between devices, across(): return lax.ppermute(value, GROUP, lay.shift(*o))  35.4 us
    pallas_call x1, Pallas kernels, step(): pl.pallas_call(functools.partial(attend_kernel, lay, scaling), grid=(seqs...  34.4 us
    ppermute x14, starting transfers between devices, across(): return lax.ppermute(value, GROUP, lay.shift(*o))  15.1 us
  transfers between devices with their start and end apart: 22, of which 7 were waited for; matrix products, arithmetic and copies ran while one was open for 33% of the time, Pallas kernels for 49%

profile of v8, /device:TPU:0, one launch (start us, length us, event | category | flops | bytes accessed | tf_op | source)
XLA Modules:
  0.0 577.6 jit_solution(18112271006350453700)
XLA Ops:
  7.2 16.2 %shard_map.254 = bf16[512,1024]{1,0:T(8,128)(2,1)} custom-call(bf16[64,8192]{1,0:T(8,128)(2,1)} %refs_0_.1), custom_call_target="tpu_custom_call" | custom-call | flops 11900000256 | bytes 1048576 | tf_op jit(solution)/shard_map/pallas_call | solution.py:345
  24.3 12.2 %shard_map.255 = bf16[512,768]{1,0:T(8,128)(2,1)} custom-call(bf16[64,6144]{1,0:T(8,128)(2,1)} %refs_0_.2), custom_call_target="tpu_custom_call" | custom-call | flops 11900000256 | bytes 1048576 | tf_op jit(solution)/shard_map/pallas_call | solution.py:345
  38.1 96.7 %norm_exchange.1 = (bf16[2,4,2,256,2048]{4,3,2,1,0:T(8,128)(2,1)}, bf16[2,4,2,256,2048]{4,3,2,1,0:T(8,128)(2,1)}, bf16[2,4,2,256,2048]{4,3,2,1,0:T(8,128)(2,1)},...) custom-call(bf16[2,256,2048]{2,1,0:T(8,128)(2,1)S(1)} %copy-done, ...), custom_call_target="tpu_custom_call" | custom-call | flops 70000001024 | bytes 1048576 | tf_op jit(solution)/shard_map/norm_exchange/pallas_call | solution.py:298
  135.1 1.4 collective-permute-start.1
  136.4 1.6 collective-permute-start.2
  138.5 28.7 %fusion.4 = (bf16[4096,1024]{1,0:T(8,128)(2,1)}, bf16[4096,1024]{1,0:T(8,128)(2,1)}) fusion(f32[1024]{0:T(1024)S(1)} %bitcast.115, bf16[4096,2048]{1,0:T(8,128)(2,1)} %bitcast.125, bf16[2048,1024]{1,0:T(8,128)(2,1)} %all-gather.5.cloned.1.call-done.refs_3_), kind=kOutput, calls=%fused_computation.5 | convolution fusion | flops 17230200832 | bytes 37752832 | tf_op jit(solution)/shard_map/dot_general | solution.py:26
  167.8 2.8 multiply_sine_fusion
  170.6 2.0 copy.32.refs_3_.col_ref
  172.6 19.3 %convolution_add_fusion = f32[4096,768]{1,0:T(8,128)} fusion(bf16[4096,2048]{1,0:T(8,128)(2,1)} %bitcast.124, bf16[2048,768]{1,0:T(8,128)(2,1)} %all-gather.7.cloned.1.call-done.refs_1_, f32[768]{0:T(1024)S(1)} %add.298), kind=kOutput, calls=%fused_computation.10 | convolution fusion | flops 12888047616 | bytes 32508928 | tf_op jit(solution)/shard_map/dot_general | solution.py:26
  191.8 34.4 %attend.1 = (bf16[4,1024,256]{2,1,0:T(8,128)(2,1)}, bf16[4,1024,256]{2,1,0:T(8,128)(2,1)}, bf16[4,1024,256]{2,1,0:T(8,128)(2,1)}, bf16[2,2,2,2,256,256]{5,4,3,2,...) custom-call(f32[2,2,2,2,256,768]{5,4,3,2,1,0:T(8,128)} %bitcast.103, ...), custom_call_target="tpu_custom_call" | custom-call | flops 4294967296 | bytes 31457280 | tf_op jit(solution)/shard_map/attend/pallas_call | solution.py:871
  226.2 23.8 %convolution_convert_fusion.1 = bf16[2048,1024]{1,0:T(8,128)(2,1)} fusion(bf16[4096,2048]{1,0:T(8,128)(2,1)} %bitcast.118, bf16[4096,1024]{1,0:T(8,128)(2,1)} %get-tuple-element.125), kind=kOutput, calls=%fused_computation.30 | convolution fusion | flops 17181966336 | bytes 29360128 | tf_op jit(solution)/shard_map/dot_general | solution.py:26
  253.7 2.0 convert_reduce_fusion.2
  255.7 40.0 %attend_back.1 = (bf16[2,2,2,2,256,768]{5,4,3,2,1,0:T(8,128)(2,1)}, f32[4,1,768]{2,1,0:T(1,128)}, bf16[2048,256]{1,0:T(8,128)(2,1)}) custom-call(bf16[4,1024,256]{2,1,0:T(8,128)(2,1)} %get-tuple-element.114.q_ref, bf16[4,1024,256]{2,1,0:T(8,128)(2,1)} %get-tuple-element.115.k_ref, bf16[4,1024,256]{2,1,0:T(8,128)(2,1)} %get-tuple-element.116.v_ref, ...), custom_call_target="tpu_custom_call" | custom-call | flops 19327352832 | bytes 41943040 | tf_op jit(solution)/shard_map/attend_back/pallas_call | solution.py:909
  296.5 32.1 %shard_map.256 = (bf16[256,2048]{1,0:T(8,128)(2,1)}, bf16[256,2048]{1,0:T(8,128)(2,1)}, bf16[256,2048]{1,0:T(8,128)(2,1)}, bf16[256,2048]{1,0:T(8,128)(2,1)}, bf...) custom-call(bf16[2,4,512,256]{3,2,1,0:T(8,128)(2,1)} %bitcast.121, ...), custom_call_target="tpu_custom_call" | custom-call | flops 21474836480 | bytes 33554432 | tf_op jit(solution)/shard_map/pallas_call | solution.py:520
  329.5 1.1 collective-permute-start.4
  330.6 20.3 %convolution_convert_fusion.2 = bf16[2048,768]{1,0:T(8,128)(2,1)} fusion(bf16[4096,2048]{1,0:T(8,128)(2,1)} %bitcast.122, bf16[4096,768]{1,0:T(8,128)(2,1)} %bitcast.129), kind=kOutput, calls=%fused_computation.31 | convolution fusion | flops 12886474752 | bytes 26214400 | tf_op jit(solution)/shard_map/dot_general | solution.py:26
  351.0 25.1 %convert_reduce_fusion = (f32[1024]{0:T(1024)S(1)}, bf16[4096,1024]{1,0:T(8,128)(2,1)}) fusion(bf16[4096,1024]{1,0:T(8,128)(2,1)} %get-tuple-element.136, bf16[4096,2048]{1,0:T(8,128)(2,1)} %bitcast.120, bf16[2048,1024]{1,0:T(8,128)(2,1)} %all-gather.11.cloned.1.call-done.refs_3_), kind=kOutput, calls=%fused_computation.6 | convolution fusion | flops 17200840704 | bytes 37752832 | tf_op jit(solution)/shard_map/dot_general | solution.py:26
  377.2 2.9 fusion.19
  380.0 1.4 fusion.20
  381.4 22.9 %convolution_convert_fusion = bf16[2048,1024]{1,0:T(8,128)(2,1)S(1)} fusion(bf16[4096,2048]{1,0:T(8,128)(2,1)} %bitcast.123, bf16[4096,1024]{1,0:T(8,128)(2,1)} %get-tuple-element.141), kind=kOutput, calls=%fused_computation.29 | convolution fusion | flops 17181966336 | bytes 29360128 | tf_op jit(solution)/shard_map/dot_general | solution.py:26
  405.2 1.1 collective-permute-start.8
  406.3 2.8 pad_maximum_fusion
  409.2 1.3 slice_bitcast_fusion
  410.5 1.3 slice_bitcast_fusion.1
  411.8 31.9 %shard_map.257 = (bf16[256,1024]{1,0:T(8,128)(2,1)}, bf16[256,1024]{1,0:T(8,128)(2,1)}, bf16[256,1024]{1,0:T(8,128)(2,1)}, bf16[256,1024]{1,0:T(8,128)(2,1)}, bf...) custom-call(bf16[2,4,512,768]{3,2,1,0:T(8,128)(2,1)} %bitcast.130, ...), custom_call_target="tpu_custom_call" | custom-call | flops 15032385536 | bytes 33554432 | tf_op jit(solution)/shard_map/pallas_call | solution.py:520
  445.4 33.0 %shard_map.258 = (bf16[256,1024]{1,0:T(8,128)(2,1)}, bf16[256,1024]{1,0:T(8,128)(2,1)}, bf16[256,1024]{1,0:T(8,128)(2,1)}, bf16[256,1024]{1,0:T(8,128)(2,1)}, bf...) custom-call(bf16[2,4,512,768]{3,2,1,0:T(8,128)(2,1)} %bitcast.131, ...), custom_call_target="tpu_custom_call" | custom-call | flops 15032385536 | bytes 33554432 | tf_op jit(solution)/shard_map/pallas_call | solution.py:520
  479.3 2.8 convert_element_type.285
  483.4 3.6 fusion.21
  487.0 1.5 collective-permute-start.6
  488.5 1.5 fusion.34
  490.0 1.2 fusion.35
  491.3 1.9 add_bitcast_fusion.1
  493.2 1.7 add_bitcast_fusion
  495.0 2.6 fusion.12
  497.6 6.7 %collective-permute-done.5 = bf16[2,256,1024]{2,1,0:T(8,128)(2,1)} collective-permute-done((bf16[2,256,1024]{2,1,0:T(8,128)(2,1)}, bf16[2,256,1024]{2,1,0:T(8,128)(2,1)}, u32[]{:S(2)}, u32[]{:S(2)}) %collective-permute-start.5) | collective-permute-done | bytes 1048608 | tf_op jit(solution)/shard_map/ppermute | solution.py:736
  504.3 8.4 %collective-permute-done.6 = bf16[2,256,1024]{2,1,0:T(8,128)(2,1)S(1)} collective-permute-done((bf16[2,256,1024]{2,1,0:T(8,128)(2,1)}, bf16[2,256,1024]{2,1,0:T(8,128)(2,1)S(1)}, u32[]{:S(2)}, u32[]{:S(2)}) %collective-permute-start.6) | collective-permute-done | bytes 1048608 | tf_op jit(solution)/shard_map/ppermute | solution.py:736
  512.6 1.2 fusion.27
  513.9 1.5 collective-permute-start.13
  515.6 1.1 collective-permute-start.14
  518.4 10.4 %collective-permute-done.13 = bf16[256,1024]{1,0:T(8,128)(2,1)S(1)} collective-permute-done((bf16[256,1024]{1,0:T(8,128)(2,1)S(1)}, bf16[256,1024]{1,0:T(8,128)(2,1)S(1)}, u32[]{:S(2)}, u32[]{:S(2)}) %collective-permute-start.13) | collective-permute-done | bytes 524320 | tf_op jit(solution)/shard_map/ppermute | solution.py:736
  528.8 1.3 fusion.29
  530.9 9.0 %collective-permute-done.11 = bf16[256,1024]{1,0:T(8,128)(2,1)S(1)} collective-permute-done((bf16[256,1024]{1,0:T(8,128)(2,1)S(1)}, bf16[256,1024]{1,0:T(8,128)(2,1)S(1)}, u32[]{:S(2)}, u32[]{:S(2)}) %collective-permute-start.11) | collective-permute-done | bytes 524320 | tf_op jit(solution)/shard_map/ppermute | solution.py:736
  539.9 1.3 fusion.33
  541.3 1.3 fusion.31
  544.2 2.9 convert_add_fusion.1
  547.1 17.0 %shard_map.259 = (bf16[64,8192]{1,0:T(8,128)(2,1)}, bf16[64,2048]{1,0:T(8,128)(2,1)}) custom-call(bf16[512,1280]{1,0:T(8,128)(2,1)} %reduce-scatter.8.cloned.1.call-done.refs_0_.refs_1_, bf16[512,1280]{1,0:T(8,128)(2,1)} %reduce-scatter.8.cloned.1.call-done.refs_0_.refs_1_), custom_call_target="tpu_custom_call" | custom-call | flops 11900000256 | bytes 1048576 | tf_op jit(solution)/shard_map/pallas_call | solution.py:345
  564.2 1.8 convert_element_type.314
  565.9 3.8 fusion.16
  (178 shorter events, 19.6 us)
Async XLA Ops:
  7.2 16.5 %copy-start.24 = (s32[2,1024]{1,0:T(2,128)S(1)}, s32[2,1024]{1,0:T(2,128)}, u32[]{:S(2)}) copy-start(s32[2,1024]{1,0:T(2,128)} %param.16) | copy-start | bytes 24580
  7.2 131.3 %all-gather.5.cloned.1.call-start = ((), (), s32[]{:S(2)}) async-start(), calls=%async_computation.3 | async-start | bytes 5242880 | tf_op jit(solution)/shard_map/all_gather | solution.py:792
  23.5 13.3 %copy-start.38 = (bf16[64]{0:T(256)(128)(2,1)S(1)}, bf16[64]{0:T(256)(128)(2,1)}, u32[]{:S(2)}) copy-start(bf16[64]{0:T(256)(128)(2,1)} %param.21) | copy-start | bytes 388
  23.5 13.3 %copy-start.39 = (bf16[64]{0:T(256)(128)(2,1)S(1)}, bf16[64]{0:T(256)(128)(2,1)}, u32[]{:S(2)}) copy-start(bf16[64]{0:T(256)(128)(2,1)} %param.18) | copy-start | bytes 388
  23.5 13.3 %copy-start.40 = (bf16[64]{0:T(256)(128)(2,1)S(1)}, bf16[64]{0:T(256)(128)(2,1)}, u32[]{:S(2)}) copy-start(bf16[64]{0:T(256)(128)(2,1)} %param.20) | copy-start | bytes 388
  23.5 13.4 %copy-start.33 = (bf16[64]{0:T(256)(128)(2,1)S(1)}, bf16[64]{0:T(256)(128)(2,1)}, u32[]{:S(2)}) copy-start(bf16[64]{0:T(256)(128)(2,1)} %param.29) | copy-start | bytes 388
  23.5 13.4 %copy-start.34 = (bf16[64]{0:T(256)(128)(2,1)S(1)}, bf16[64]{0:T(256)(128)(2,1)}, u32[]{:S(2)}) copy-start(bf16[64]{0:T(256)(128)(2,1)} %param.25) | copy-start | bytes 388
  23.5 13.4 %copy-start.35 = (bf16[256]{0:T(256)(128)(2,1)S(1)}, bf16[256]{0:T(256)(128)(2,1)}, u32[]{:S(2)}) copy-start(bf16[256]{0:T(256)(128)(2,1)} %param.27) | copy-start | bytes 1540
  23.5 13.4 %copy-start.36 = (bf16[192]{0:T(256)(128)(2,1)S(1)}, bf16[192]{0:T(256)(128)(2,1)}, u32[]{:S(2)}) copy-start(bf16[192]{0:T(256)(128)(2,1)} %param.23) | copy-start | bytes 1156
  23.5 14.6 %copy-start = (bf16[2,256,2048]{2,1,0:T(8,128)(2,1)S(1)}, bf16[2,256,2048]{2,1,0:T(8,128)(2,1)}, u32[]{:S(2)}) copy-start(bf16[2,256,2048]{2,1,0:T(8,128)(2,1)} %refs_0_.3) | copy-start | bytes 6291460
  23.6 14.6 %copy-start.2 = (bf16[64,8192]{1,0:T(8,128)(2,1)S(1)}, bf16[64,8192]{1,0:T(8,128)(2,1)}, u32[]{:S(2)}) copy-start(bf16[64,8192]{1,0:T(8,128)(2,1)} %refs_3_.1) | copy-start | bytes 3145732
  23.6 14.6 %copy-start.3 = (bf16[64,2048]{1,0:T(8,128)(2,1)S(1)}, bf16[64,2048]{1,0:T(8,128)(2,1)}, u32[]{:S(2)}) copy-start(bf16[64,2048]{1,0:T(8,128)(2,1)} %refs_2_.1) | copy-start | bytes 786436
  23.6 149.0 %all-gather.7.cloned.1.call-start = ((), (), s32[]{:S(2)}) async-start(), calls=%async_computation.4 | async-start | bytes 3932160 | tf_op jit(solution)/shard_map/all_gather | solution.py:792
  23.6 13.4 %collective-permute-start = (s32[2,1024]{1,0:T(2,128)S(1)}, s32[2,1024]{1,0:T(2,128)S(1)}, u32[]{:S(2)}, u32[]{:S(2)}) collective-permute-start(s32[2,1024]{1,0:T(2,128)S(1)} %copy-done.24), channel_id=1, source_target_pairs={{0,4},{4,0},{1,5},{5,1},{2,6},{6,2},{3,7},{7,3},{8,12},{12,8},{9,1... | collective-permute-start | bytes 24584 | tf_op jit(solution)/shard_map/ppermute | solution.py:799
  36.5 219.2 %all-gather.9.cloned.1.call-start = ((), (), s32[]{:S(2)}) async-start(), calls=%async_computation.5 | async-start | bytes 1310720 | tf_op jit(solution)/shard_map/all_gather | solution.py:792
  134.9 161.6 %all-gather.11.cloned.1.call-start = ((), (), s32[]{:S(2)}) async-start(), calls=%async_computation.6 | async-start | bytes 5242880 | tf_op jit(solution)/shard_map/all_gather | solution.py:792
  135.1 56.8 %collective-permute-start.1 = (bf16[2,256,2048]{2,1,0:T(8,128)(2,1)}, bf16[2,256,2048]{2,1,0:T(8,128)(2,1)}, u32[]{:S(2)}, u32[]{:S(2)}) collective-permute-start(bf16[2,256,2048]{2,1,0:T(8,128)(2,1)} %refs_5_), channel_id=1, source_target_pairs={{0,2},{1,3},{2,0},{3,1},{4,6},{5,7},{6,4},{7,5},{8,10},{9,11},{10,... | collective-permute-start | bytes 6291464 | tf_op jit(solution)/shard_map/ppermute | solution.py:736
  136.4 55.4 %collective-permute-start.2 = (bf16[2,256,2048]{2,1,0:T(8,128)(2,1)}, bf16[2,256,2048]{2,1,0:T(8,128)(2,1)}, u32[]{:S(2)}, u32[]{:S(2)}) collective-permute-start(bf16[2,256,2048]{2,1,0:T(8,128)(2,1)} %refs_5_), channel_id=1, source_target_pairs={{0,4},{1,5},{2,6},{3,7},{4,0},{5,1},{6,2},{7,3},{8,12},{9,13},{10,... | collective-permute-start | bytes 6291464 | tf_op jit(solution)/shard_map/ppermute | solution.py:736
  138.2 273.6 %reduce-scatter.4.cloned.1.call-start = ((), (), s32[]{:S(2)}) async-start(), calls=%async_computation.7 | async-start | bytes 5242880 | tf_op jit(solution)/shard_map/reduce_scatter | solution.py:897
  138.5 28.7 %copy-start.19 = (s32[1,4,4,256]{3,1,2,0:T(4,128)S(1)}, s32[1,4,4,256]{3,1,2,0:T(4,128)}, u32[]{:S(2)}) copy-start(s32[1,4,4,256]{3,1,2,0:T(4,128)} %copy.36) | copy-start | bytes 49156
  250.0 195.4 %reduce-scatter.6.cloned.1.call-start = ((), (), s32[]{:S(2)}) async-start(), calls=%async_computation.8 | async-start | bytes 3932160 | tf_op jit(solution)/shard_map/reduce_scatter | solution.py:897
  328.5 48.2 %collective-permute-start.3 = (bf16[2,256,2048]{2,1,0:T(8,128)(2,1)}, bf16[2,256,2048]{2,1,0:T(8,128)(2,1)S(1)}, u32[]{:S(2)}, u32[]{:S(2)}) collective-permute-start(bf16[2,256,2048]{2,1,0:T(8,128)(2,1)} %get-tuple-element.131), channel_id=1, source_target_pairs={{0,4},{1,5},{2,6},{3,7},{4,0},{5,1},{6,2},{7,3},{8,12},{9,13},{10,... | collective-permute-start | bytes 6291464 | tf_op jit(solution)/shard_map/ppermute | solution.py:736
  329.5 47.7 %collective-permute-start.4 = (bf16[2,256,2048]{2,1,0:T(8,128)(2,1)}, bf16[2,256,2048]{2,1,0:T(8,128)(2,1)}, u32[]{:S(2)}, u32[]{:S(2)}) collective-permute-start(bf16[2,256,2048]{2,1,0:T(8,128)(2,1)} %get-tuple-element.132), channel_id=1, source_target_pairs={{0,2},{1,3},{2,0},{3,1},{4,6},{5,7},{6,4},{7,5},{8,10},{9,11},{10,... | collective-permute-start | bytes 6291464 | tf_op jit(solution)/shard_map/ppermute | solution.py:736
  350.9 29.1 %copy-start.9 = (bf16[256,2048]{1,0:T(8,128)(2,1)S(1)}, bf16[256,2048]{1,0:T(8,128)(2,1)}, u32[]{:S(2)}) copy-start(bf16[256,2048]{1,0:T(8,128)(2,1)} %get-tuple-element.134) | copy-start | bytes 3145732
  350.9 196.2 %reduce-scatter.8.cloned.1.call-start = ((), (), s32[]{:S(2)}) async-start(), calls=%async_computation.9 | async-start | bytes 6553600 | tf_op jit(solution)/shard_map/reduce_scatter | solution.py:897
  351.0 26.2 %copy-start.10 = (bf16[256,2048]{1,0:T(8,128)(2,1)S(1)}, bf16[256,2048]{1,0:T(8,128)(2,1)}, u32[]{:S(2)}) copy-start(bf16[256,2048]{1,0:T(8,128)(2,1)} %get-tuple-element.138) | copy-start | bytes 3145732
  376.7 27.6 %copy-start.5 = (bf16[2,256,2048]{2,1,0:T(8,128)(2,1)}, bf16[2,256,2048]{2,1,0:T(8,128)(2,1)S(1)}, u32[]{:S(2)}) copy-start(bf16[2,256,2048]{2,1,0:T(8,128)(2,1)S(1)} %collective-permute-done.3) | copy-start | bytes 6291460
  381.4 24.9 %copy-start.8 = (bf16[2048,256]{1,0:T(8,128)(2,1)S(1)}, bf16[2048,256]{1,0:T(8,128)(2,1)}, u32[]{:S(2)}) copy-start(bf16[2048,256]{1,0:T(8,128)(2,1)} %get-tuple-element.178) | copy-start | bytes 3145732
  404.3 87.0 %collective-permute-start.7 = (bf16[256,2048]{1,0:T(8,128)(2,1)}, bf16[256,2048]{1,0:T(8,128)(2,1)}, u32[]{:S(2)}, u32[]{:S(2)}) collective-permute-start(bf16[256,2048]{1,0:T(8,128)(2,1)} %fusion.20), channel_id=1, source_target_pairs={{0,2},{1,3},{2,0},{3,1},{4,6},{5,7},{6,4},{7,5},{8,10},{9,11},{10,... | collective-permute-start | bytes 3145736 | tf_op jit(solution)/shard_map/ppermute | solution.py:736
  405.2 86.1 %collective-permute-start.8 = (bf16[256,2048]{1,0:T(8,128)(2,1)}, bf16[256,2048]{1,0:T(8,128)(2,1)}, u32[]{:S(2)}, u32[]{:S(2)}) collective-permute-start(bf16[256,2048]{1,0:T(8,128)(2,1)} %fusion.19), channel_id=1, source_target_pairs={{0,4},{1,5},{2,6},{3,7},{4,0},{5,1},{6,2},{7,3},{8,12},{9,13},{10,... | collective-permute-start | bytes 3145736 | tf_op jit(solution)/shard_map/ppermute | solution.py:736
  443.7 43.3 %collective-permute-start.10 = (bf16[2,256,1024]{2,1,0:T(8,128)(2,1)}, bf16[2,256,1024]{2,1,0:T(8,128)(2,1)}, u32[]{:S(2)}, u32[]{:S(2)}) collective-permute-start(bf16[2,256,1024]{2,1,0:T(8,128)(2,1)} %get-tuple-element.153), channel_id=1, source_target_pairs={{0,2},{1,3},{2,0},{3,1},{4,6},{5,7},{6,4},{7,5},{8,10},{9,11},{10,... | collective-permute-start | bytes 3145736 | tf_op jit(solution)/shard_map/ppermute | solution.py:736
  444.6 43.9 %collective-permute-start.9 = (bf16[2,256,1024]{2,1,0:T(8,128)(2,1)}, bf16[2,256,1024]{2,1,0:T(8,128)(2,1)}, u32[]{:S(2)}, u32[]{:S(2)}) collective-permute-start(bf16[2,256,1024]{2,1,0:T(8,128)(2,1)} %get-tuple-element.152), channel_id=1, source_target_pairs={{0,4},{1,5},{2,6},{3,7},{4,0},{5,1},{6,2},{7,3},{8,12},{9,13},{10,... | collective-permute-start | bytes 3145736 | tf_op jit(solution)/shard_map/ppermute | solution.py:736
  445.4 33.0 %copy-start.20 = (bf16[32,32,128]{2,1,0:T(8,128)(2,1)S(1)}, bf16[32,32,128]{2,1,0:T(8,128)(2,1)}, u32[]{:S(2)}) copy-start(bf16[32,32,128]{2,1,0:T(8,128)(2,1)} %get-tuple-element.175) | copy-start | bytes 786436
  478.6 25.7 %collective-permute-start.5 = (bf16[2,256,1024]{2,1,0:T(8,128)(2,1)}, bf16[2,256,1024]{2,1,0:T(8,128)(2,1)}, u32[]{:S(2)}, u32[]{:S(2)}) collective-permute-start(bf16[2,256,1024]{2,1,0:T(8,128)(2,1)} %get-tuple-element.156), channel_id=1, source_target_pairs={{0,4},{1,5},{2,6},{3,7},{4,0},{5,1},{6,2},{7,3},{8,12},{9,13},{10,... | collective-permute-start | bytes 3145736 | tf_op jit(solution)/shard_map/ppermute | solution.py:736
  482.8 86.9 %copy-start.41 = (f32[64]{0:T(128)}, f32[64]{0:T(128)S(1)}, u32[]{:S(2)}) copy-start(f32[64]{0:T(128)S(1)} %fusion.38) | copy-start | bytes 772
  487.0 25.6 %collective-permute-start.6 = (bf16[2,256,1024]{2,1,0:T(8,128)(2,1)}, bf16[2,256,1024]{2,1,0:T(8,128)(2,1)S(1)}, u32[]{:S(2)}, u32[]{:S(2)}) collective-permute-start(bf16[2,256,1024]{2,1,0:T(8,128)(2,1)} %get-tuple-element.157), channel_id=1, source_target_pairs={{0,2},{1,3},{2,0},{3,1},{4,6},{5,7},{6,4},{7,5},{8,10},{9,11},{10,... | collective-permute-start | bytes 3145736 | tf_op jit(solution)/shard_map/ppermute | solution.py:736
  495.0 17.6 %copy-start.17 = (bf16[256,1024]{1,0:T(8,128)(2,1)S(1)}, bf16[256,1024]{1,0:T(8,128)(2,1)}, u32[]{:S(2)}) copy-start(bf16[256,1024]{1,0:T(8,128)(2,1)} %get-tuple-element.164) | copy-start | bytes 1572868
  495.0 20.3 %copy-start.16 = (bf16[256,1024]{1,0:T(8,128)(2,1)S(1)}, bf16[256,1024]{1,0:T(8,128)(2,1)}, u32[]{:S(2)}) copy-start(bf16[256,1024]{1,0:T(8,128)(2,1)} %get-tuple-element.165) | copy-start | bytes 1572868
  495.0 33.7 %copy-start.15 = (bf16[256,1024]{1,0:T(8,128)(2,1)S(1)}, bf16[256,1024]{1,0:T(8,128)(2,1)}, u32[]{:S(2)}) copy-start(bf16[256,1024]{1,0:T(8,128)(2,1)} %get-tuple-element.162) | copy-start | bytes 1572868
  497.6 32.8 %copy-start.14 = (bf16[256,1024]{1,0:T(8,128)(2,1)S(1)}, bf16[256,1024]{1,0:T(8,128)(2,1)}, u32[]{:S(2)}) copy-start(bf16[256,1024]{1,0:T(8,128)(2,1)} %get-tuple-element.163) | copy-start | bytes 1572868
  513.9 26.0 %copy-start.13 = (bf16[256,1024]{1,0:T(8,128)(2,1)S(1)}, bf16[256,1024]{1,0:T(8,128)(2,1)}, u32[]{:S(2)}) copy-start(bf16[256,1024]{1,0:T(8,128)(2,1)} %get-tuple-element.148) | copy-start | bytes 1572868
  513.9 14.9 %collective-permute-start.13 = (bf16[256,1024]{1,0:T(8,128)(2,1)S(1)}, bf16[256,1024]{1,0:T(8,128)(2,1)S(1)}, u32[]{:S(2)}, u32[]{:S(2)}) collective-permute-start(bf16[256,1024]{1,0:T(8,128)(2,1)S(1)} %fusion.27), channel_id=1, source_target_pairs={{0,2},{1,3},{2,0},{3,1},{4,6},{5,7},{6,4},{7,5},{8,10},{9,11},{10,... | collective-permute-start | bytes 1572872 | tf_op jit(solution)/shard_map/ppermute | solution.py:736
  515.6 14.9 %collective-permute-start.14 = (bf16[256,1024]{1,0:T(8,128)(2,1)S(1)}, bf16[256,1024]{1,0:T(8,128)(2,1)S(1)}, u32[]{:S(2)}, u32[]{:S(2)}) collective-permute-start(bf16[256,1024]{1,0:T(8,128)(2,1)S(1)} %fusion.24), channel_id=1, source_target_pairs={{0,4},{1,5},{2,6},{3,7},{4,0},{5,1},{6,2},{7,3},{8,12},{9,13},{10,... | collective-permute-start | bytes 1572872 | tf_op jit(solution)/shard_map/ppermute | solution.py:736
  516.7 23.2 %collective-permute-start.11 = (bf16[256,1024]{1,0:T(8,128)(2,1)S(1)}, bf16[256,1024]{1,0:T(8,128)(2,1)S(1)}, u32[]{:S(2)}, u32[]{:S(2)}) collective-permute-start(bf16[256,1024]{1,0:T(8,128)(2,1)S(1)} %fusion.35), channel_id=1, source_target_pairs={{0,2},{1,3},{2,0},{3,1},{4,6},{5,7},{6,4},{7,5},{8,10},{9,11},{10,... | collective-permute-start | bytes 1572872 | tf_op jit(solution)/shard_map/ppermute | solution.py:736
  517.9 23.5 %collective-permute-start.12 = (bf16[256,1024]{1,0:T(8,128)(2,1)S(1)}, bf16[256,1024]{1,0:T(8,128)(2,1)S(1)}, u32[]{:S(2)}, u32[]{:S(2)}) collective-permute-start(bf16[256,1024]{1,0:T(8,128)(2,1)S(1)} %fusion.34), channel_id=1, source_target_pairs={{0,4},{1,5},{2,6},{3,7},{4,0},{5,1},{6,2},{7,3},{8,12},{9,13},{10,... | collective-permute-start | bytes 1572872 | tf_op jit(solution)/shard_map/ppermute | solution.py:736
  547.1 18.8 %copy-start.11 = (bf16[64,8192]{1,0:T(8,128)(2,1)S(1)}, bf16[64,8192]{1,0:T(8,128)(2,1)}, u32[]{:S(2)}) copy-start(bf16[64,8192]{1,0:T(8,128)(2,1)} %refs_0_.1) | copy-start | bytes 3145732
  547.1 18.8 %copy-start.30 = (f32[64]{0:T(128)S(1)}, f32[64]{0:T(128)}, u32[]{:S(2)}) copy-start(f32[64]{0:T(128)} %copy-done.29) | copy-start | bytes 772
  547.1 18.8 %copy-start.32 = (f32[64]{0:T(128)S(1)}, f32[64]{0:T(128)}, u32[]{:S(2)}) copy-start(f32[64]{0:T(128)} %copy-done.31) | copy-start | bytes 772
  (16 other events, 77.8 us)
Sparse Core Ops, SparseCore 0:
  23.6 85.1 all-gather.4
  110.3 61.8 all-gather.6
  173.7 26.7 all-gather.8
  201.9 80.0 all-gather.10
  284.7 75.2 reduce-scatter.3
  362.1 61.3 reduce-scatter.5
  425.8 96.6 reduce-scatter.7
